TPU v7x, 256 devices: a whole 4x4x8 slice. The times are simulated.
256 devices in a mesh: tm: 32 (over z, y), tok: 8 (over x, core).
Axes of the slice: x: 4, y: 4, z: 8, core: 2. Of those that a mesh axis runs over, the one named last changes fastest.
Arguments:
- states: float32 [128, 2, 256, 1152], P('tm', None, 'tok'), may hold values from -6 to 6
- noise: bfloat16 [128, 2, 256, 1152], P('tm', None, 'tok'), may hold values from -6 to 6
- x_start: float32 [2, 256, 1152], P(None, 'tok'), may hold values from -6 to 6
- timesteps: int32 [128], P('tm'), may hold values from 50 to 999
- step_mod: float32 [128, 3, 1152], P('tm'), may hold values from -40 to 40
- view_mod: float32 [8, 3, 1152], replicated, may hold values from -2 to 2
- view_ids: int32 [128, 2], P('tm'), may hold values from 0 to 7
- w_qkv: bfloat16 [1152, 3456], replicated, may hold values from -0.1875 to 0.1875
- w_out: bfloat16 [1152, 1152], replicated, may hold values from -0.1875 to 0.1875
Outputs:
- new_states: float32 [128, 2, 256, 1152], P('tm', None, 'tok')
All inputs are finite; a program needn't handle non-finite values.
Results may differ from a plain program's by a relative error of at most 0.0017.
Values may be sent and summed in bfloat16 or wider, within the bound.
No kernel may reach another device: no remote copies, remote signals or barrier semaphores. Data moves between devices by JAX's collectives and lax.ppermute only.
A program may use at most 128 MiB of HBM per device.

v0:
```python
import jax
import jax.numpy as jnp
from jax import lax
from jax.sharding import Mesh
from jax.sharding import PartitionSpec as P

HEADS = 16
SWEEPS = 2
TOK = ("tok_0", "tok_1")
TM = ("tm_0", "tm_1")


def split_up(shard, dim, peers):
    before, after = (shard.shape[:dim], shard.shape[dim + 1 :])
    return jnp.moveaxis(shard.reshape(*before, peers, -1, *after), dim, 0)


def joined_along(blocks, dim):
    dims = list(blocks.shape[1:])
    dims[dim] *= blocks.shape[0]
    return jnp.moveaxis(blocks, 0, dim).reshape(dims)


def moved_by_axis(blocks, axes, sequence):
    inside = blocks.shape[1:]
    out = blocks.reshape(*(lax.axis_size(a) for a in axes), *inside)
    for k in sequence:
        out = lax.all_to_all(out, axes[k], k, k, tiled=True)
    return out.reshape(-1, *inside)


def one_axis_at_a_time(shard, axes, sequence, split_dim, concat_dim):
    blocks = split_up(shard, split_dim, lax.axis_size(axes))
    return joined_along(moved_by_axis(blocks, axes, sequence), concat_dim)


def nothing_yet(shard, identity):
    return jnp.zeros_like(shard) + jnp.asarray(identity, shard.dtype)


def entering(shard, axes, combine, identity):
    before = start = nothing_yet(shard, identity)
    running = shard
    for axis in reversed(axes):
        peers, position = (lax.axis_size(axis), lax.axis_index(axis))
        pieces = lax.all_gather(running, axis)
        inside, running = (start, start)
        for k in range(peers):
            passed = k < position
            running = combine(running, pieces[k])
            inside = jnp.where(passed, running, inside)
        before = combine(inside, before)
    return before


def coefficients(steps_index):
    unit = steps_index.astype(jnp.float32) / 1000.0
    beta = 0.1 + 19.9 * unit
    sigma = jnp.sqrt(1.0 - jnp.exp(-(0.1 * unit + 9.95 * unit * unit)))
    coef_state = 0.5 * beta * 0.004
    coef_eps = beta * 0.004 / sigma
    coef_noise = jnp.sqrt(beta * 0.004)
    return (coef_state, coef_eps, coef_noise)


def attend_heads(queries, keys, values):
    lead = queries.shape[:-2]
    query_rows = queries.shape[-2]
    key_rows = keys.shape[-2]
    width = queries.shape[-1]
    head_size = width // HEADS
    queries = queries.reshape(lead + (query_rows, HEADS, head_size))
    keys = keys.reshape(lead + (key_rows, HEADS, head_size))
    values = values.reshape(lead + (key_rows, HEADS, head_size))
    scores = jnp.einsum(
        "...qhe,...khe->...hqk", queries, keys, preferred_element_type=jnp.float32
    ) * (1.0 / head_size**0.5)
    probs = jax.nn.softmax(scores, axis=-1).astype(jnp.bfloat16)
    attended = jnp.einsum(
        "...hqk,...khe->...qhe", probs, values, preferred_element_type=jnp.float32
    ).astype(jnp.bfloat16)
    return attended.reshape(lead + (query_rows, width))


def increments_of(latent, noise, modulation, factors, w_qkv, w_out):
    steps_here, views, tok_rows, width = latent.shape
    center = jnp.mean(latent, axis=-1, keepdims=True)
    spread = jnp.mean((latent - center) ** 2, axis=-1, keepdims=True)
    normed = (latent - center) / jnp.sqrt(spread + 1e-06)
    modulated = (
        normed * (1.0 + modulation[:, :, 1][:, :, None, :]) + modulation[:, :, 0][:, :, None, :]
    ).astype(jnp.bfloat16)
    flat_rows = modulated.reshape(steps_here * views, tok_rows, width)
    whole_rows = lax.all_to_all(flat_rows, TOK, split_axis=0, concat_axis=1, tiled=True)
    qkv = jnp.einsum("grd,de->gre", whole_rows, w_qkv, preferred_element_type=jnp.float32).astype(
        jnp.bfloat16
    )
    result_rows = attend_heads(qkv[..., :width], qkv[..., width : 2 * width], qkv[..., 2 * width :])
    returned = one_axis_at_a_time(result_rows, TOK, (1, 0), 1, 0)
    attended = returned.reshape(steps_here, views, tok_rows, width)
    projected = jnp.einsum("svrd,de->svre", attended, w_out, preferred_element_type=jnp.float32)
    denoised = latent + modulation[:, :, 2][:, :, None, :] * projected
    coef_state, coef_eps, coef_noise = factors
    return coef_state * latent + coef_eps * denoised + coef_noise * noise.astype(jnp.float32)


def per_device(states, noise, x_start, timesteps, step_mod, view_mod, view_ids, w_qkv, w_out):
    table_rows = view_mod.shape[0]
    selector = (
        view_ids[:, :, None] == jnp.arange(table_rows, dtype=jnp.int32)[None, None, :]
    ).astype(jnp.float32)
    view_terms = jnp.einsum("svn,ncd->svcd", selector, view_mod, precision=lax.Precision.HIGHEST)
    modulation = step_mod[:, None] + view_terms
    coef_state, coef_eps, coef_noise = coefficients(timesteps)
    factors = (
        coef_state[:, None, None, None],
        coef_eps[:, None, None, None],
        coef_noise[:, None, None, None],
    )
    current = states
    for sweep in range(SWEEPS):
        increments = increments_of(current, noise, modulation, factors, w_qkv, w_out)
        local_total = jnp.sum(increments, axis=0)
        lower_sum = entering(
            local_total, TM, lambda earlier, later: earlier + later, jnp.zeros_like(local_total)
        )
        running = jnp.cumsum(increments, axis=0)
        before = jnp.concatenate([jnp.zeros_like(running[:1]), running[:-1]], axis=0)
        current = x_start[None] + (lower_sum[None] + before)
    return current


def solution(mesh):
    finer = Mesh(mesh.devices.reshape(8, 4, 4, 2), ("tm_0", "tm_1", "tok_0", "tok_1"))
    placed = (
        P(TM, None, TOK, None),
        P(TM, None, TOK, None),
        P(None, TOK, None),
        P(TM),
        P(TM, None, None),
        P(),
        P(TM, None),
        P(),
        P(),
    )
    return jax.shard_map(
        per_device, mesh=finer, in_specs=placed, out_specs=P(TM, None, TOK, None), check_vma=False
    )
```

profile of v0, /device:TPU:1, one launch (start us, length us, event | category | flops | bytes accessed | tf_op | source)
XLA Modules:
  0.0 289.2 jit_solution(9496766394224943413)
XLA Ops:
  6.5 1.6 reduce_sum.72
  8.1 1.6 multiply_reduce_fusion.3
  9.8 0.3 convolution_add_fusion
  10.2 0.3 add_convert_fusion.1
  10.5 15.9 %all_to_all.38 = bf16[8,32,1152]{2,1,0:T(8,128)(2,1)S(1)} all-to-all(bf16[8,32,1152]{2,1,0:T(8,128)(2,1)S(1)} %bitcast.97), channel_id=1, replica_groups=mesh['tm_0'=8,'tm_1'=4,'tok_0'=4,'tok_1'=2] {'tok_0','tok_1'}, dimensions={0} | all-to-all | bytes 1179648 | tf_op jit(solution)/shard_map/all_to_all | solution.py:94
  26.4 5.8 %fusion.2 = bf16[1,256,3456]{2,1,0:T(8,128)(2,1)S(1)} fusion(bf16[256,1152]{1,0:T(8,128)(2,1)S(1)} %bitcast.105, bf16[1152,3456]{1,0:T(8,128)(2,1)} %param.16), kind=kOutput, calls=%fused_computation.4 | convolution fusion | flops 2039316480 | bytes 10321920 | tf_op jit(solution)/shard_map/grd,de->gre/dot_general | solution.py:95
  32.2 1.2 fusion.51
  33.3 2.1 copy.41
  35.5 2.1 copy.40
  37.6 1.1 copy.39
  38.7 4.7 %fusion.52 = (f32[16,256]{1,0:T(8,128)S(1)}, f32[16,256,256]{1,2,0:T(8,128)}) fusion(bf16[256,16,72]{0,2,1:T(8,128)(2,1)} %bitcast.101, bf16[256,16,72]{0,2,1:T(8,128)(2,1)} %bitcast.99), kind=kOutput, calls=%fused_computation.97 | convolution fusion | flops 154140928 | bytes 5390336 | tf_op jit(solution)/shard_map/sub | solution.py:78
  43.4 2.9 fusion.26
  46.3 1.7 copy.43
  48.0 2.2 reshape_transpose_reshape_reshape.6
  50.3 4.6 %all_to_all.39 = bf16[4,2,1,32,1152]{4,3,0,2,1:T(8,128)(2,1)S(1)} all-to-all(bf16[4,2,1,32,1152]{4,3,0,2,1:T(8,128)(2,1)S(1)} %copy.44), channel_id=1, replica_groups=mesh['tm_0'=8,'tm_1'=4,'tok_0'=4,'tok_1'=2] {'tok_1'}, dimensions={1} | all-to-all | bytes 1179648 | tf_op jit(solution)/shard_map/all_to_all | solution.py:28
  54.8 0.9 copy.45
  55.7 4.2 %all-to-all-start.2 = ((bf16[4,2,1,32,1152]{4,3,1,2,0:T(8,128)(2,1)}), bf16[4,2,1,32,1152]{4,3,1,2,0:T(8,128)(2,1)}, u32[]{:S(2)}, u32[]{:S(2)}) async-start(bf16[4,2,1,32,1152]{4,3,1,2,0:T(8,128)(2,1)} %copy.45), calls=%async_computation.2 | async-start | bytes 1179648 | tf_op jit(solution)/shard_map/all_to_all | solution.py:28
  60.0 9.8 %all-to-all-done.2 = bf16[4,2,1,32,1152]{4,3,1,2,0:T(8,128)(2,1)} async-done(((bf16[4,2,1,32,1152]{4,3,1,2,0:T(8,128)(2,1)}), bf16[4,2,1,32,1152]{4,3,1,2,0:T(8,128)(2,1)}, u32[]{:S(2)}, u32[]{:S(2)}) %all-to-all-start.2) | async-done | bytes 589856 | tf_op jit(solution)/shard_map/all_to_all | solution.py:28
  69.8 4.2 %fusion.53 = (f32[2,32,1152]{2,1,0:T(8,128)}, f32[4,2,32,1152]{3,2,1,0:T(8,128)}) fusion(bf16[4,2,32,1152]{3,2,1,0:T(8,128)(2,1)S(1)} %copy-done.8, f32[4]{0:T(128)S(1)} %get-tuple-element.15, f32[4,2,32,1152]{3,2,1,0:T(8,128)} %param.9, bf16[1152,1152]{1,0:T(8,128)(2,1)S(1)} %copy-done, bf16[4,2,1,32,1152]{4,3,1,2,0:T(8,128)(2,1)} %all-to-all-done.2, ...), kind=kOutput, calls=%fused_computation.98 | convolution fusion | flops 682057728 | bytes 6524976 | tf_op jit(solution)/shard_map/svrd,de->svre/dot_general | solution.py:101
  74.2 26.6 %all-gather.11.cloned.1.call-done = f32[8,32,1152]{2,1,0:T(8,128)} async-done(((f32[2,32,1152]{2,1,0:T(8,128)}), f32[8,32,1152]{2,1,0:T(8,128)}) %all-gather.11.cloned.1.call-update) | async-done | bytes 1179664 | tf_op jit(solution)/shard_map/all_gather | solution.py:46
  100.8 2.0 fusion.42
  102.9 1.4 fusion.56
  104.3 38.9 %all-gather.7.cloned.1.call-done = f32[8,2,32,1152]{3,2,1,0:T(8,128)} async-done(((f32[1,2,32,1152]{3,2,1,0:T(8,128)}), f32[8,2,32,1152]{3,2,1,0:T(8,128)}) %all-gather.7.cloned.1.call-update) | async-done | bytes 2359312 | tf_op jit(solution)/shard_map/all_gather | solution.py:46
  143.2 2.2 fusion.41
  145.5 0.2 fusion.28
  145.7 0.3 multiply_reduce_fusion.2
  146.3 0.3 add_convert_fusion
  146.6 18.7 %all_to_all.40 = bf16[8,32,1152]{2,1,0:T(8,128)(2,1)S(1)} all-to-all(bf16[8,32,1152]{2,1,0:T(8,128)(2,1)S(1)} %bitcast.98), channel_id=1, replica_groups=mesh['tm_0'=8,'tm_1'=4,'tok_0'=4,'tok_1'=2] {'tok_0','tok_1'}, dimensions={0} | all-to-all | bytes 1179648 | tf_op jit(solution)/shard_map/all_to_all | solution.py:94
  165.3 5.8 %fusion.3 = bf16[1,256,3456]{2,1,0:T(8,128)(2,1)S(1)} fusion(bf16[256,1152]{1,0:T(8,128)(2,1)S(1)} %bitcast.106, bf16[1152,3456]{1,0:T(8,128)(2,1)} %param.16), kind=kOutput, calls=%fused_computation.5 | convolution fusion | flops 2039316480 | bytes 10321920 | tf_op jit(solution)/shard_map/grd,de->gre/dot_general | solution.py:95
  171.1 1.3 fusion.50
  172.4 2.1 copy.48
  174.5 2.1 copy.47
  176.6 2.1 copy.46
  178.7 5.3 %fusion.54 = (f32[16,256]{1,0:T(8,128)}, f32[16,256,256]{1,2,0:T(8,128)}) fusion(bf16[256,16,72]{0,2,1:T(8,128)(2,1)} %bitcast.103, bf16[256,16,72]{0,2,1:T(8,128)(2,1)} %bitcast.100), kind=kOutput, calls=%fused_computation.99 | convolution fusion | flops 154140928 | bytes 5390336 | tf_op jit(solution)/shard_map/sub | solution.py:78
  184.1 3.7 %fusion.27 = bf16[1,256,16,72]{1,3,2,0:T(8,128)(2,1)} fusion(bf16[256,16,72]{0,2,1:T(8,128)(2,1)} %bitcast.104, f32[16,256,256]{1,2,0:T(8,128)} %get-tuple-element.22, f32[16,256]{1,0:T(8,128)} %get-tuple-element.21), kind=kOutput, calls=%fused_computation.34 | convolution fusion | flops 153387008 | bytes 5390336 | tf_op jit(solution)/shard_map/...hqk,...khe->...qhe/dot_general | solution.py:79
  187.7 2.6 copy.50
  190.3 2.9 %reshape_transpose_reshape_reshape.7 = bf16[4,2,1,32,1152]{4,3,1,0,2:T(8,128)(2,1)} reshape(bf16[1,256,16,72]{3,2,1,0:T(8,128)(2,1)} %copy.50) | data formatting | bytes 1179648 | tf_op jit(solution)/shard_map/reshape;transpose;reshape;reshape | solution.py:26
  193.2 1.1 copy.51
  194.3 4.6 %all_to_all.41 = bf16[4,2,1,32,1152]{4,3,0,2,1:T(8,128)(2,1)S(1)} all-to-all(bf16[4,2,1,32,1152]{4,3,0,2,1:T(8,128)(2,1)S(1)} %copy.51), channel_id=1, replica_groups=mesh['tm_0'=8,'tm_1'=4,'tok_0'=4,'tok_1'=2] {'tok_1'}, dimensions={1} | all-to-all | bytes 1179648 | tf_op jit(solution)/shard_map/all_to_all | solution.py:28
  199.0 12.1 %all_to_all.42 = bf16[4,2,1,32,1152]{4,3,1,2,0:T(8,128)(2,1)S(1)} all-to-all(bf16[4,2,1,32,1152]{4,3,1,2,0:T(8,128)(2,1)S(1)} %copy.52), channel_id=1, replica_groups=mesh['tm_0'=8,'tm_1'=4,'tok_0'=4,'tok_1'=2] {'tok_0'}, dimensions={0} | all-to-all | bytes 1179648 | tf_op jit(solution)/shard_map/all_to_all | solution.py:28
  211.1 2.9 %fusion.55 = (f32[2,32,1152]{2,1,0:T(8,128)}, f32[4,2,32,1152]{3,2,1,0:T(8,128)}) fusion(bf16[4,2,32,1152]{3,2,1,0:T(8,128)(2,1)S(1)} %copy-done.9, f32[4]{0:T(128)S(1)} %get-tuple-element.15, bf16[1152,1152]{1,0:T(8,128)(2,1)S(1)} %copy-done, bf16[4,2,1,32,1152]{4,3,1,2,0:T(8,128)(2,1)S(1)} %all_to_all.42, f32[4,2,1152]{2,1,0:T(2,128)S(1)} %copy-done.11, ...), kind=kOutput, calls=%fused_computation.100 | convolution fusion | flops 682647552 | bytes 6819888 | tf_op jit(solution)/shard_map/svrd,de->svre/dot_general | solution.py:101
  214.1 22.7 %all-gather.13.cloned.1.call-done = f32[8,32,1152]{2,1,0:T(8,128)} async-done(((f32[2,32,1152]{2,1,0:T(8,128)}), f32[8,32,1152]{2,1,0:T(8,128)}) %all-gather.13.cloned.1.call-update) | async-done | bytes 1179664 | tf_op jit(solution)/shard_map/all_gather | solution.py:46
  236.8 2.0 fusion.38
  238.9 1.4 fusion.57
  240.2 1.0 slice.185
  241.2 38.1 %all-gather.9.cloned.1.call-done = f32[8,2,32,1152]{3,2,1,0:T(8,128)} async-done(((f32[1,2,32,1152]{3,2,1,0:T(8,128)}), f32[8,2,32,1152]{3,2,1,0:T(8,128)}) %all-gather.9.cloned.1.call-update) | async-done | bytes 2359312 | tf_op jit(solution)/shard_map/all_gather | solution.py:46
  279.3 2.2 fusion.37
  281.5 1.1 add_add_fusion
  (60 shorter events, 0.9 us)
Async XLA Ops:
  6.5 63.3 %copy-start = (bf16[1152,1152]{1,0:T(8,128)(2,1)S(1)}, bf16[1152,1152]{1,0:T(8,128)(2,1)}, u32[]{:S(2)}) copy-start(bf16[1152,1152]{1,0:T(8,128)(2,1)} %param.17) | copy-start | bytes 7962628
  6.5 3.2 %copy-start.18 = (s32[4,2]{0,1:T(2,128)S(1)}, s32[4,2]{0,1:T(2,128)}, u32[]{:S(2)}) copy-start(s32[4,2]{0,1:T(2,128)} %param.15) | copy-start | bytes 100
  6.5 3.2 %copy-start.16 = (f32[8,3,1152]{2,0,1:T(8,128)S(1)}, f32[8,3,1152]{2,0,1:T(8,128)}, u32[]{:S(2)}) copy-start(f32[8,3,1152]{2,0,1:T(8,128)} %param.14) | copy-start | bytes 331780
  6.5 3.3 %copy-start.17 = (f32[4,3,1152]{2,0,1:T(4,128)S(1)}, f32[4,3,1152]{2,0,1:T(4,128)}, u32[]{:S(2)}) copy-start(f32[4,3,1152]{2,0,1:T(4,128)} %param.13) | copy-start | bytes 165892
  8.1 2.1 copy-start.1
  10.1 16.2 %copy-start.12 = (f32[4,2,1152]{2,1,0:T(2,128)}, f32[4,2,1152]{2,1,0:T(2,128)S(1)}, u32[]{:S(2)}) copy-start(f32[4,2,1152]{2,1,0:T(2,128)S(1)} %copy.38) | copy-start | bytes 110596
  10.2 16.2 %copy-start.14 = (f32[4,2,1152]{2,1,0:T(2,128)}, f32[4,2,1152]{2,1,0:T(2,128)S(1)}, u32[]{:S(2)}) copy-start(f32[4,2,1152]{2,1,0:T(2,128)S(1)} %copy.37) | copy-start | bytes 110596
  54.8 5.1 %copy-start.19 = (s32[4]{0:T(128)S(1)}, s32[4]{0:T(128)}, u32[]{:S(2)}) copy-start(s32[4]{0:T(128)} %param.12) | copy-start | bytes 52
  54.8 15.0 %copy-start.8 = (bf16[4,2,32,1152]{3,2,1,0:T(8,128)(2,1)S(1)}, bf16[4,2,32,1152]{3,2,1,0:T(8,128)(2,1)}, u32[]{:S(2)}) copy-start(bf16[4,2,32,1152]{3,2,1,0:T(8,128)(2,1)} %param.10) | copy-start | bytes 1769476
  55.7 14.1 %all-to-all-start.2 = ((bf16[4,2,1,32,1152]{4,3,1,2,0:T(8,128)(2,1)}), bf16[4,2,1,32,1152]{4,3,1,2,0:T(8,128)(2,1)}, u32[]{:S(2)}, u32[]{:S(2)}) async-start(bf16[4,2,1,32,1152]{4,3,1,2,0:T(8,128)(2,1)} %copy.45), calls=%async_computation.2 | async-start | bytes 1179648 | tf_op jit(solution)/shard_map/all_to_all | solution.py:28
  59.9 40.9 %all-gather.11.cloned.1.call-start = ((), (), s32[]{:S(2)}) async-start(), calls=%async_computation.8 | async-start | bytes 1474560 | tf_op jit(solution)/shard_map/all_gather | solution.py:46
  60.0 14.1 %copy-start.10 = (f32[4,2,1152]{2,1,0:T(2,128)}, f32[4,2,1152]{2,1,0:T(2,128)S(1)}, u32[]{:S(2)}) copy-start(f32[4,2,1152]{2,1,0:T(2,128)S(1)} %copy.36) | copy-start | bytes 110596
  74.1 69.1 %all-gather.7.cloned.1.call-start = ((), (), s32[]{:S(2)}) async-start(), calls=%async_computation.6 | async-start | bytes 2654208 | tf_op jit(solution)/shard_map/all_gather | solution.py:46
  102.8 134.1 %all-gather.13.cloned.1.call-start = ((), (), s32[]{:S(2)}) async-start(), calls=%async_computation.9 | async-start | bytes 1474560 | tf_op jit(solution)/shard_map/all_gather | solution.py:46
  143.2 2.2 copy-start.4
  145.4 0.7 copy-start.2
  145.4 0.8 copy-start.13
  145.4 0.8 copy-start.15
  198.9 12.2 %copy-start.3 = (f32[2,32,1152]{2,1,0:T(8,128)S(1)}, f32[2,32,1152]{2,1,0:T(8,128)}, u32[]{:S(2)}) copy-start(f32[2,32,1152]{2,1,0:T(8,128)} %copy-done.2) | copy-start | bytes 884740
  198.9 12.2 %copy-start.5 = (f32[2,32,1152]{2,1,0:T(8,128)S(1)}, f32[2,32,1152]{2,1,0:T(8,128)}, u32[]{:S(2)}) copy-start(f32[2,32,1152]{2,1,0:T(8,128)} %param.11) | copy-start | bytes 884740
  198.9 12.2 %copy-start.9 = (bf16[4,2,32,1152]{3,2,1,0:T(8,128)(2,1)S(1)}, bf16[4,2,32,1152]{3,2,1,0:T(8,128)(2,1)}, u32[]{:S(2)}) copy-start(bf16[4,2,32,1152]{3,2,1,0:T(8,128)(2,1)} %param.10) | copy-start | bytes 1769476
  198.9 12.2 %copy-start.11 = (f32[4,2,1152]{2,1,0:T(2,128)S(1)}, f32[4,2,1152]{2,1,0:T(2,128)}, u32[]{:S(2)}) copy-start(f32[4,2,1152]{2,1,0:T(2,128)} %copy-done.10) | copy-start | bytes 110596
  214.1 65.2 %all-gather.9.cloned.1.call-start = ((), (), s32[]{:S(2)}) async-start(), calls=%async_computation.7 | async-start | bytes 2654208 | tf_op jit(solution)/shard_map/all_gather | solution.py:46
  241.2 40.3 %copy-start.6 = (f32[2,32,1152]{2,1,0:T(8,128)S(1)}, f32[2,32,1152]{2,1,0:T(8,128)}, u32[]{:S(2)}) copy-start(f32[2,32,1152]{2,1,0:T(8,128)} %param.11) | copy-start | bytes 884740
  279.3 2.3 copy-start.7
Sparse Core Ops, SparseCore 0:
  74.2 26.4 all-gather.10
  102.9 40.2 all-gather.6
  214.2 22.6 all-gather.12
  239.0 40.2 all-gather.8
where the time goes:
time: 293 us; the launch traced here: 289 us
  waiting for transfers between devices  136 us (46%)
  blocking collectives  55.9 us (19%)
  matrix products  35.6 us (12%)
  local copies, waits for them, and re-layouts  27.1 us (9%)
  other arithmetic  16.6 us (6%)
  between operations  13.5 us (5%)
  starting transfers between devices  4.32 us (1%)
    all_gather x4, waiting for transfers between devices, entering(): pieces = lax.all_gather(running, axis)  126 us
    all_to_all x2, blocking collectives, increments_of(): lax.all_to_all(flat_rows, TOK, split_axis=0, concat_axis=1, tiled=True)  34.6 us
    all_to_all x3, blocking collectives, moved_by_axis(): out = lax.all_to_all(out, axes[k], k, k, tiled=True)  21.3 us
    dot_general x2, matrix products, increments_of(): jnp.einsum('grd,de->gre', whole_rows, w_qkv, preferred_element_type=jnp.f...  11.6 us
    sub x2, matrix products, attend_heads(): probs = jax.nn.softmax(scores, axis=-1).astype(jnp.bfloat16)  10 us
    all_to_all x1, waiting for transfers between devices, moved_by_axis(): out = lax.all_to_all(out, axes[k], k, k, tiled=True)  9.85 us
    dot_general x2, matrix products, increments_of(): jnp.einsum('svrd,de->svre', attended, w_out, preferred_element_type=jnp.f...  7.2 us
    slice x4, local copies, waits for them, and re-layouts, increments_of(): qkv[..., width:2 * width]  6.69 us
  transfers between devices with their start and end apart: 5, of which 5 were waited for; matrix products, arithmetic and copies ran while one was open for 1% of the time, Pallas kernels for 0%

commit v1 on v0

v1 whole, which is shorter than its diff:
```python
import jax
import jax.numpy as jnp
from jax import lax
from jax.experimental import pallas as pl
from jax.experimental.pallas import tpu as pltpu
from jax.sharding import Mesh
from jax.sharding import PartitionSpec as P

HEADS = 16
SWEEPS = 2
LANES = 128
VMEM = pl.BlockSpec(memory_space=pltpu.VMEM)
SMEM = pl.BlockSpec(memory_space=pltpu.SMEM)


def shifted(value, axis, shift):
    size = lax.axis_size(axis)
    return lax.ppermute(value, axis, [(i, (i + shift) % size) for i in range(size)])


def from_below(value, axis, shift):
    size = lax.axis_size(axis)
    return lax.ppermute(value, axis, [(i, i + shift) for i in range(size - shift)])


def call(body, outs, specs, *args, scratch=()):
    return pl.pallas_call(
        body,
        out_shape=outs,
        in_specs=specs,
        out_specs=jax.tree.map(lambda _: VMEM, outs),
        scratch_shapes=list(scratch),
        compiler_params=pltpu.CompilerParams(vmem_limit_bytes=48 * 2**20),
    )(*args)


def normed_rows(rows, shift, scale):
    center = jnp.mean(rows, axis=-1, keepdims=True)
    off = rows - center
    spread = jnp.mean(off * off, axis=-1, keepdims=True)
    normed = off / jnp.sqrt(spread + 1e-06)
    return (normed * (1.0 + scale) + shift).astype(jnp.bfloat16)


def modulation_row(where_ref, step_ref, view_ref, step, part):
    return step_ref[step, part : part + 1, :] + view_ref[where_ref[2 + step], part : part + 1, :]


def enter_body(where_ref, mine_ref, peer_ref, step_ref, view_ref, x_ref, *mod_refs):
    place = where_ref[0]
    steps = mine_ref.shape[0]
    for r in range(steps):
        step = lax.rem(place + r, steps)
        shift = modulation_row(where_ref, step_ref, view_ref, step, 0)
        scale = modulation_row(where_ref, step_ref, view_ref, step, 1)
        rows = jnp.concatenate([mine_ref[step], peer_ref[step]], axis=0)
        x_ref[step] = rows
        mod_refs[r][...] = normed_rows(rows, shift, scale)


def resume_body(where_ref, start_ref, before_ref, l0, l1, l2, l3, step_ref, view_ref, x_ref, *rest):
    mod_refs, base_ref = rest[:-1], rest[-1]
    place, spot = where_ref[0], where_ref[1]
    steps = before_ref.shape[0]
    lower = (l0, l1, l2, l3)
    part = l0.shape[0]
    for r in range(len(lower)):
        rows = pl.ds(pl.multiple_of(lax.rem(spot + len(lower) - r, len(lower)) * part, part), part)
        base_ref[rows, :] = lower[r][...]
    for r in range(steps):
        step = lax.rem(place + r, steps)
        rows = start_ref[...] + (base_ref[...] + before_ref[step])
        x_ref[step] = rows
        if mod_refs:
            shift = modulation_row(where_ref, step_ref, view_ref, step, 0)
            scale = modulation_row(where_ref, step_ref, view_ref, step, 1)
            mod_refs[r][...] = normed_rows(rows, shift, scale)


def attend_body(a0, a1, a2, a3, w_ref, mask_ref, o0, o1, o2, o3, rows_ref, qkv_ref):
    pieces = (a0, a1, a2, a3)
    part, width = a0.shape
    for r in range(4):
        rows_ref[r * part : (r + 1) * part, :] = pieces[r][...]
    qkv_ref[...] = jnp.dot(
        rows_ref[...], w_ref[...], preferred_element_type=jnp.float32
    ).astype(jnp.bfloat16)
    size = width // HEADS
    tiles = [None] * (width // LANES)
    for h in range(HEADS):
        first = h * size // LANES
        last = ((h + 1) * size - 1) // LANES
        low, high = first * LANES, (last + 1) * LANES
        q = qkv_ref[:, low:high] * mask_ref[h : h + 1, low:high]
        k = qkv_ref[:, width + low : width + high]
        v = qkv_ref[:, 2 * width + low : 2 * width + high]
        scores = lax.dot_general(
            q, k, (((1,), (1,)), ((), ())), preferred_element_type=jnp.float32
        ) * (1.0 / size**0.5)
        top = jnp.max(scores, axis=-1, keepdims=True)
        powers = jnp.exp(scores - top)
        probs = (powers / jnp.sum(powers, axis=-1, keepdims=True)).astype(jnp.bfloat16)
        out = jnp.dot(probs, v, preferred_element_type=jnp.float32)
        for t in range(first, last + 1):
            piece = out[:, t * LANES - low : (t + 1) * LANES - low]
            if tiles[t] is not None:
                lane = lax.broadcasted_iota(jnp.int32, piece.shape, 1) + t * LANES
                piece = jnp.where(lane >= h * size, piece, tiles[t])
            tiles[t] = piece
    outs = (o0, o1, o2, o3)
    for t, tile in enumerate(tiles):
        tile = tile.astype(jnp.bfloat16)
        for r in range(4):
            outs[r][:, t * LANES : (t + 1) * LANES] = tile[r * part : (r + 1) * part]


def project_body(
    where_ref, coef_ref, a0, a1, a2, a3, w_ref, x_ref, mine_ref, peer_ref, step_ref, view_ref, before_ref, *rest
):
    total_refs, rows_ref, proj_ref, total_ref = rest[:-3], rest[-3], rest[-2], rest[-1]
    place, spot = where_ref[0], where_ref[1]
    pieces = (a0, a1, a2, a3)
    part = a0.shape[0]
    steps = len(pieces)
    for r in range(steps):
        rows = pl.ds(pl.multiple_of(lax.rem(place + r, steps) * part, part), part)
        rows_ref[rows, :] = pieces[r][...]
    proj_ref[...] = jnp.dot(rows_ref[...], w_ref[...], preferred_element_type=jnp.float32)
    running = None
    for step in range(steps):
        gate = modulation_row(where_ref, step_ref, view_ref, step, 2)
        rows = x_ref[step]
        denoised = rows + gate * proj_ref[step * part : (step + 1) * part, :]
        drawn = jnp.concatenate([mine_ref[step], peer_ref[step]], axis=0).astype(jnp.float32)
        increment = coef_ref[0, step] * rows + coef_ref[1, step] * denoised + coef_ref[2, step] * drawn
        before_ref[step] = jnp.zeros_like(increment) if running is None else running
        running = increment if running is None else running + increment
    total_ref[...] = running
    share = total_refs[0].shape[0]
    for r in range(len(total_refs)):
        rows = pl.ds(pl.multiple_of(lax.rem(spot + r, len(total_refs)) * share, share), share)
        total_refs[r][...] = total_ref[rows, :]


def coefficients(steps_index):
    unit = steps_index.astype(jnp.float32) / 1000.0
    beta = 0.1 + 19.9 * unit
    sigma = jnp.sqrt(1.0 - jnp.exp(-(0.1 * unit + 9.95 * unit * unit)))
    coef_state = 0.5 * beta * 0.004
    coef_eps = beta * 0.004 / sigma
    coef_noise = jnp.sqrt(beta * 0.004)
    return (coef_state, coef_eps, coef_noise)


def earlier_sum(totals):
    spot = lax.axis_index("y")
    peers = lax.axis_size("y")
    mine = [totals[0]] + [shifted(totals[r], "y", r) for r in range(1, peers)]
    held = []
    for p in range(peers):
        r = lax.rem(spot - p + peers, peers)
        value = mine[0]
        for k in range(1, peers):
            value = jnp.where(r == k, mine[k], value)
        held.append(value)
    inside = [jnp.zeros_like(held[0])]
    for p in range(peers):
        inside.append(inside[-1] + held[p])
    running = inside.pop()
    below = jnp.zeros_like(running)
    shift = 1
    while shift < lax.axis_size("z"):
        passed = from_below(running, "z", shift)
        below = below + passed
        running = running + passed
        shift *= 2
    lower = []
    for r in range(peers):
        p = lax.rem(spot + r, peers)
        value = inside[0]
        for k in range(1, peers):
            value = jnp.where(p == k, inside[k], value)
        lower.append(value + below)
    return [lower[0]] + [shifted(lower[r], "y", r) for r in range(1, peers)]


def per_device(states, noise, x_start, timesteps, step_mod, view_mod, view_ids, w_qkv, w_out):
    steps, views, part, width = states.shape
    place, spot, core = (lax.axis_index(a) for a in ("x", "y", "c"))
    other = 1 - core
    f32, bf16 = jnp.float32, jnp.bfloat16
    rows = 2 * part

    def own(a, axis):
        return lax.dynamic_index_in_dim(a, core, axis, keepdims=False)

    def from_peer(a, axis):
        return shifted(lax.dynamic_index_in_dim(a, other, axis, keepdims=False), "c", 1)

    where = jnp.concatenate([jnp.stack([place, spot]).astype(jnp.int32), own(view_ids, 1)])
    coefs = jnp.stack(coefficients(timesteps))
    start = jnp.concatenate([own(x_start, 0), from_peer(x_start, 0)], axis=0)
    noise_mine, noise_peer = own(noise, 1), from_peer(noise, 1)
    size = width // HEADS
    column = jnp.arange(width, dtype=jnp.int32)[None, :]
    head = jnp.arange(HEADS, dtype=jnp.int32)[:, None]
    mask = ((column >= head * size) & (column < (head + 1) * size)).astype(bf16)

    x_shape = jax.ShapeDtypeStruct((steps, rows, width), f32)
    piece = jax.ShapeDtypeStruct((rows, width), bf16)
    share = jax.ShapeDtypeStruct((rows // lax.axis_size("y"), width), f32)
    x, *mods = call(
        enter_body,
        [x_shape] + [piece] * steps,
        [SMEM] + [VMEM] * 4,
        where,
        own(states, 1),
        from_peer(states, 1),
        step_mod,
        view_mod,
    )
    for sweep in range(SWEEPS):
        arrived = [mods[0]] + [shifted(mods[r], "x", r) for r in range(1, steps)]
        attended = call(
            attend_body,
            [piece] * steps,
            [VMEM] * 6,
            *arrived,
            w_qkv,
            mask,
            scratch=[pltpu.VMEM((steps * rows, width), bf16), pltpu.VMEM((steps * rows, 3 * width), bf16)],
        )
        back = [attended[0]] + [shifted(attended[r], "x", -r) for r in range(1, steps)]
        before, *totals = call(
            project_body,
            [x_shape] + [share] * lax.axis_size("y"),
            [SMEM] * 2 + [VMEM] * 10,
            where,
            coefs,
            *back,
            w_out,
            x,
            noise_mine,
            noise_peer,
            step_mod,
            view_mod,
            scratch=[
                pltpu.VMEM((steps * rows, width), bf16),
                pltpu.VMEM((steps * rows, width), f32),
                pltpu.VMEM((rows, width), f32),
            ],
        )
        lower = earlier_sum(totals)
        more = sweep + 1 < SWEEPS
        x, *mods = call(
            resume_body,
            [x_shape] + ([piece] * steps if more else []),
            [SMEM] + [VMEM] * 8,
            where,
            start,
            before,
            *lower,
            step_mod,
            view_mod,
            scratch=[pltpu.VMEM((rows, width), f32)],
        )
    mine, given = x[:, :part], shifted(x[:, part:], "c", 1)
    low = jnp.where(core == 0, mine, given)
    high = jnp.where(core == 0, given, mine)
    return jnp.stack([low, high], axis=1)


def solution(mesh):
    finer = Mesh(mesh.devices.reshape(8, 4, 4, 2), ("z", "y", "x", "c"))
    tm, tok = ("z", "y"), ("x", "c")
    placed = (
        P(tm, None, tok, None),
        P(tm, None, tok, None),
        P(None, tok, None),
        P(tm),
        P(tm, None, None),
        P(),
        P(tm, None),
        P(),
        P(),
    )
    return jax.shard_map(
        per_device, mesh=finer, in_specs=placed, out_specs=P(tm, None, tok, None), check_vma=False
    )
```

time: 293 us -> 164 us (0.56); the launches traced: 289 us -> 164 us
  waiting for transfers between devices: 136 us -> 49.3 us
  starting transfers between devices: 4.32 us -> 85.9 us
  blocking collectives: 55.9 us -> 0 us
  matrix products: 35.6 us -> 0 us
  Pallas kernels: 0 us -> 24.9 us
  local copies, waits for them, and re-layouts: 27.1 us -> 2.69 us
  other arithmetic: 16.6 us -> 0.69 us
  between operations: 13.5 us -> 0.29 us
    all_gather x4 -> x0, waiting for transfers between devices: 126 us -> none  [entering(): pieces = lax.all_gather(running, axis)]
    ppermute x0 -> x34, starting transfers between devices: none -> 85.9 us  [the longest x28 51.1 us: shifted(): lax.ppermute(value, axis, [(i, (i + shift) % size) for i in range(size)])]
    all_to_all x5 -> x0, blocking collectives: 55.9 us -> none  [the longest x2 34.6 us: increments_of(): lax.all_to_all(flat_rows, TOK, split_axis=0, concat_axis=1, tiled=True)]
    ppermute x0 -> x34, waiting for transfers between devices: none -> 49.3 us  [the longest x28 42.4 us: shifted(): lax.ppermute(value, axis, [(i, (i + shift) % size) for i in range(size)])]
    dot_general x7 -> x0, matrix products: 25.6 us -> none  [the longest x2 11.6 us: increments_of(): jnp.einsum('grd,de->gre', whole_rows, w_qkv, preferred_element_type=jnp.f...]
    pallas_call x0 -> x7, Pallas kernels: none -> 24.9 us  [call(): pl.pallas_call(body, out_shape=outs, in_specs=specs, out_specs=jax.tree.m...]
    slice x10 -> x1, local copies, waits for them, and re-layouts: 15.1 us -> 0.04 us  [per_device(): mine, given = (x[:, :part], shifted(x[:, part:], 'c', 1))]
    sub x2 -> x0, matrix products: 10 us -> none  [attend_heads(): probs = jax.nn.softmax(scores, axis=-1).astype(jnp.bfloat16)]
  transfers between devices with their start and end apart: 5 -> 34, of which waited for: 5 -> 28; matrix products, arithmetic and copies ran while one was open for 1% -> 0% of each run, Pallas kernels for 0% -> 6%
where the time goes in v1:
time: 164 us
  starting transfers between devices  85.9 us (52%)
  waiting for transfers between devices  49.3 us (30%)
  Pallas kernels  24.9 us (15%)
  local copies, waits for them, and re-layouts  2.69 us (2%)
    ppermute x28, starting transfers between devices, shifted(): lax.ppermute(value, axis, [(i, (i + shift) % size) for i in range(size)])  51.1 us
    ppermute x28, waiting for transfers between devices, shifted(): lax.ppermute(value, axis, [(i, (i + shift) % size) for i in range(size)])  42.4 us
    ppermute x6, starting transfers between devices, from_below(): lax.ppermute(value, axis, [(i, i + shift) for i in range(size - shift)])  34.7 us
    pallas_call x7, Pallas kernels, call(): pl.pallas_call(body, out_shape=outs, in_specs=specs, out_specs=jax.tree.m...  24.9 us
    ppermute x6, waiting for transfers between devices, from_below(): lax.ppermute(value, axis, [(i, i + shift) for i in range(size - shift)])  6.94 us
  transfers between devices with their start and end apart: 34, of which 28 were waited for; matrix products, arithmetic and copies ran while one was open for 0% of the time, Pallas kernels for 6%

profile of v1, /device:TPU:1, one launch (start us, length us, event | category | flops | bytes accessed | tf_op | source)
XLA Modules:
  0.0 163.7 jit_solution(11702326659487667153)
XLA Ops:
  0.0 1.4 dynamic-slice_bitcast_fusion
  1.4 3.3 %collective-permute-start.1 = (f32[4,32,1152]{2,1,0:T(8,128)S(1)}, f32[4,32,1152]{2,1,0:T(8,128)S(1)}, u32[]{:S(2)}, u32[]{:S(2)}) collective-permute-start(f32[4,32,1152]{2,1,0:T(8,128)S(1)} %get-tuple-element.75), channel_id=1, source_target_pairs={{0,1},{1,0},{2,3},{3,2},{4,5},{5,4},{6,7},{7,6},{8,9},{9,8},{10,11... | collective-permute-start | bytes 1769480 | tf_op jit(solution)/shard_map/ppermute | solution.py:18
  5.1 1.3 collective-permute-done.1.peer_ref
  6.3 1.0 shard_map.91
  7.5 1.9 %collective-permute-start.3 = (bf16[64,1152]{1,0:T(8,128)(2,1)S(1)}, bf16[64,1152]{1,0:T(8,128)(2,1)S(1)}, u32[]{:S(2)}, u32[]{:S(2)}) collective-permute-start(bf16[64,1152]{1,0:T(8,128)(2,1)S(1)} %get-tuple-element.35), channel_id=1, source_target_pairs={{0,4},{2,6},{4,0},{6,2},{1,5},{3,7},{5,1},{7,3},{8,12},{10,14},{12... | collective-permute-start | bytes 442376 | tf_op jit(solution)/shard_map/ppermute | solution.py:18
  9.4 1.2 collective-permute-start.4
  10.6 3.8 %collective-permute-done.2.a1 = bf16[64,1152]{1,0:T(8,128)(2,1)S(1)} collective-permute-done((bf16[64,1152]{1,0:T(8,128)(2,1)S(1)}, bf16[64,1152]{1,0:T(8,128)(2,1)S(1)}, u32[]{:S(2)}, u32[]{:S(2)}) %collective-permute-start.2) | collective-permute-done | bytes 147488 | tf_op jit(solution)/shard_map/ppermute | solution.py:18
  14.4 1.8 %collective-permute-done.3.a2 = bf16[64,1152]{1,0:T(8,128)(2,1)S(1)} collective-permute-done((bf16[64,1152]{1,0:T(8,128)(2,1)S(1)}, bf16[64,1152]{1,0:T(8,128)(2,1)S(1)}, u32[]{:S(2)}, u32[]{:S(2)}) %collective-permute-start.3) | collective-permute-done | bytes 147488 | tf_op jit(solution)/shard_map/ppermute | solution.py:18
  17.2 8.1 %shard_map.92 = (bf16[64,1152]{1,0:T(8,128)(2,1)S(1)}, bf16[64,1152]{1,0:T(8,128)(2,1)S(1)}, bf16[64,1152]{1,0:T(8,128)(2,1)S(1)}, bf16[64,1152]{1,0:T(8,128)(2,1)S(1)}) custom-call(bf16[64,1152]{1,0:T(8,128)(2,1)S(1)} %get-tuple-element.33.a0, bf16[64,1152]{1,0:T(8,128)(2,1)S(1)} %collective-permute-done.2.a1, ...), custom_call_target="tpu_custom_call" | custom-call | tf_op jit(solution)/shard_map/pallas_call | solution.py:27
  25.3 3.4 %collective-permute-start.5 = (bf16[64,1152]{1,0:T(8,128)(2,1)S(1)}, bf16[64,1152]{1,0:T(8,128)(2,1)S(1)}, u32[]{:S(2)}, u32[]{:S(2)}) collective-permute-start(bf16[64,1152]{1,0:T(8,128)(2,1)S(1)} %get-tuple-element.38), channel_id=1, source_target_pairs={{0,6},{2,0},{4,2},{6,4},{1,7},{3,1},{5,3},{7,5},{8,14},{10,8},{12,... | collective-permute-start | bytes 442376 | tf_op jit(solution)/shard_map/ppermute | solution.py:18
  29.4 5.3 %collective-permute-done.5.a1 = bf16[64,1152]{1,0:T(8,128)(2,1)S(1)} collective-permute-done((bf16[64,1152]{1,0:T(8,128)(2,1)S(1)}, bf16[64,1152]{1,0:T(8,128)(2,1)S(1)}, u32[]{:S(2)}, u32[]{:S(2)}) %collective-permute-start.5) | collective-permute-done | bytes 147488 | tf_op jit(solution)/shard_map/ppermute | solution.py:18
  34.9 3.6 %collective-permute-done.7.a3 = bf16[64,1152]{1,0:T(8,128)(2,1)S(1)} collective-permute-done((bf16[64,1152]{1,0:T(8,128)(2,1)S(1)}, bf16[64,1152]{1,0:T(8,128)(2,1)S(1)}, u32[]{:S(2)}, u32[]{:S(2)}) %collective-permute-start.7) | collective-permute-done | bytes 147488 | tf_op jit(solution)/shard_map/ppermute | solution.py:18
  38.6 2.9 %shard_map.93 = (f32[4,64,1152]{2,1,0:T(8,128)S(1)}, f32[16,1152]{1,0:T(8,128)S(1)}, f32[16,1152]{1,0:T(8,128)S(1)}, f32[16,1152]{1,0:T(8,128)S(1)}, f32[16,1152]{1,0:T(8,128)S(1)}) custom-call(s32[6]{0:T(128)S(1)} %pad_add_fusion.where_ref, f32[3,4]{1,0:T(4,128)S(1)} %pad_maximum_fusion.2.coef_ref, bf16[64,1152]{1,0:T(8,128)(2,1)S(1)} %get-tuple-element.37.a0, ...), custom_call_target="tpu_custom_call" | custom-call | tf_op jit(solution)/shard_map/pallas_call | solution.py:27
  43.4 1.5 collective-permute-done.9
  44.9 2.2 %collective-permute-done.10 = f32[16,1152]{1,0:T(8,128)S(1)} collective-permute-done((f32[16,1152]{1,0:T(8,128)S(1)}, f32[16,1152]{1,0:T(8,128)S(1)}, u32[]{:S(2)}, u32[]{:S(2)}) %collective-permute-start.10) | collective-permute-done | bytes 73760 | tf_op jit(solution)/shard_map/ppermute | solution.py:18
  47.9 3.5 %collective-permute-start.12 = (f32[16,1152]{1,0:T(8,128)S(1)}, f32[16,1152]{1,0:T(8,128)S(1)}, u32[]{:S(2)}, u32[]{:S(2)}) collective-permute-start(f32[16,1152]{1,0:T(8,128)S(1)} %get-tuple-element.69), channel_id=1, source_target_pairs={{0,32},{32,64},{64,96},{96,128},{128,160},{160,192},{192,224},{1,3... | collective-permute-start | bytes 221192 | tf_op jit(solution)/shard_map/ppermute | solution.py:23
  51.5 1.4 collective-permute-done.12
  52.9 5.1 %collective-permute-start.13 = (f32[16,1152]{1,0:T(8,128)S(1)}, f32[16,1152]{1,0:T(8,128)S(1)}, u32[]{:S(2)}, u32[]{:S(2)}) collective-permute-start(f32[16,1152]{1,0:T(8,128)S(1)} %add.141), channel_id=1, source_target_pairs={{0,64},{32,96},{64,128},{96,160},{128,192},{160,224},{1,65},{33,97... | collective-permute-start | bytes 221192 | tf_op jit(solution)/shard_map/ppermute | solution.py:23
  57.9 1.4 collective-permute-done.13
  59.3 10.9 %collective-permute-start.14 = (f32[16,1152]{1,0:T(8,128)S(1)}, f32[16,1152]{1,0:T(8,128)S(1)}, u32[]{:S(2)}, u32[]{:S(2)}) collective-permute-start(f32[16,1152]{1,0:T(8,128)S(1)} %add.143), channel_id=1, source_target_pairs={{0,128},{32,160},{64,192},{96,224},{1,129},{33,161},{65,193},{97,2... | collective-permute-start | bytes 221192 | tf_op jit(solution)/shard_map/ppermute | solution.py:23
  70.3 5.1 %collective-permute-start = (f32[32,1152]{1,0:T(8,128)S(1)}, f32[32,1152]{1,0:T(8,128)S(1)}, u32[]{:S(2)}, u32[]{:S(2)}) collective-permute-start(f32[32,1152]{1,0:T(8,128)S(1)} %get-tuple-element.86), channel_id=1, source_target_pairs={{0,1},{1,0},{2,3},{3,2},{4,5},{5,4},{6,7},{7,6},{8,9},{9,8},{10,11... | collective-permute-start | bytes 442376 | tf_op jit(solution)/shard_map/ppermute | solution.py:18
  75.5 1.0 collective-permute-start.16
  76.5 2.7 %collective-permute-start.17 = (f32[16,1152]{1,0:T(8,128)S(1)}, f32[16,1152]{1,0:T(8,128)S(1)}, u32[]{:S(2)}, u32[]{:S(2)}) collective-permute-start(f32[16,1152]{1,0:T(8,128)S(1)} %get-tuple-element.67), channel_id=1, source_target_pairs={{0,24},{8,0},{16,8},{24,16},{1,25},{9,1},{17,9},{25,17},{2,26},{10... | collective-permute-start | bytes 221192 | tf_op jit(solution)/shard_map/ppermute | solution.py:18
  79.2 1.1 collective-permute-done.16.l2
  81.1 1.1 shard_map.94
  82.3 1.5 collective-permute-start.19
  83.8 1.2 collective-permute-start.20
  85.1 4.0 %collective-permute-done.18.a1 = bf16[64,1152]{1,0:T(8,128)(2,1)S(1)} collective-permute-done((bf16[64,1152]{1,0:T(8,128)(2,1)S(1)}, bf16[64,1152]{1,0:T(8,128)(2,1)S(1)}, u32[]{:S(2)}, u32[]{:S(2)}) %collective-permute-start.18) | collective-permute-done | bytes 147488 | tf_op jit(solution)/shard_map/ppermute | solution.py:18
  90.0 8.1 %shard_map.95 = (bf16[64,1152]{1,0:T(8,128)(2,1)S(1)}, bf16[64,1152]{1,0:T(8,128)(2,1)S(1)}, bf16[64,1152]{1,0:T(8,128)(2,1)S(1)}, bf16[64,1152]{1,0:T(8,128)(2,1)S(1)}) custom-call(bf16[64,1152]{1,0:T(8,128)(2,1)S(1)} %get-tuple-element.47.a0, bf16[64,1152]{1,0:T(8,128)(2,1)S(1)} %collective-permute-done.18.a1, ...), custom_call_target="tpu_custom_call" | custom-call | tf_op jit(solution)/shard_map/pallas_call | solution.py:27
  98.1 2.1 %collective-permute-start.21 = (bf16[64,1152]{1,0:T(8,128)(2,1)S(1)}, bf16[64,1152]{1,0:T(8,128)(2,1)S(1)}, u32[]{:S(2)}, u32[]{:S(2)}) collective-permute-start(bf16[64,1152]{1,0:T(8,128)(2,1)S(1)} %get-tuple-element.52), channel_id=1, source_target_pairs={{0,6},{2,0},{4,2},{6,4},{1,7},{3,1},{5,3},{7,5},{8,14},{10,8},{12,... | collective-permute-start | bytes 442376 | tf_op jit(solution)/shard_map/ppermute | solution.py:18
  100.9 3.0 %collective-permute-done.21.a1 = bf16[64,1152]{1,0:T(8,128)(2,1)S(1)} collective-permute-done((bf16[64,1152]{1,0:T(8,128)(2,1)S(1)}, bf16[64,1152]{1,0:T(8,128)(2,1)S(1)}, u32[]{:S(2)}, u32[]{:S(2)}) %collective-permute-start.21) | collective-permute-done | bytes 147488 | tf_op jit(solution)/shard_map/ppermute | solution.py:18
  103.9 1.9 %collective-permute-done.22.a2 = bf16[64,1152]{1,0:T(8,128)(2,1)S(1)} collective-permute-done((bf16[64,1152]{1,0:T(8,128)(2,1)S(1)}, bf16[64,1152]{1,0:T(8,128)(2,1)S(1)}, u32[]{:S(2)}, u32[]{:S(2)}) %collective-permute-start.22) | collective-permute-done | bytes 147488 | tf_op jit(solution)/shard_map/ppermute | solution.py:18
  105.8 1.2 collective-permute-done.23.a3
  107.0 2.9 %shard_map.96 = (f32[4,64,1152]{2,1,0:T(8,128)S(1)}, f32[16,1152]{1,0:T(8,128)S(1)}, f32[16,1152]{1,0:T(8,128)S(1)}, f32[16,1152]{1,0:T(8,128)S(1)}, f32[16,1152]{1,0:T(8,128)S(1)}) custom-call(s32[6]{0:T(128)S(1)} %pad_add_fusion.where_ref, f32[3,4]{1,0:T(4,128)S(1)} %pad_maximum_fusion.2.coef_ref, bf16[64,1152]{1,0:T(8,128)(2,1)S(1)} %get-tuple-element.51.a0, ...), custom_call_target="tpu_custom_call" | custom-call | tf_op jit(solution)/shard_map/pallas_call | solution.py:27
  109.9 2.9 %collective-permute-start.24 = (f32[16,1152]{1,0:T(8,128)S(1)}, f32[16,1152]{1,0:T(8,128)S(1)}, u32[]{:S(2)}, u32[]{:S(2)}) collective-permute-start(f32[16,1152]{1,0:T(8,128)S(1)} %get-tuple-element.57), channel_id=1, source_target_pairs={{0,24},{8,0},{16,8},{24,16},{1,25},{9,1},{17,9},{25,17},{2,26},{10... | collective-permute-start | bytes 221192 | tf_op jit(solution)/shard_map/ppermute | solution.py:18
  113.5 1.4 collective-permute-done.24
  114.9 2.7 %collective-permute-done.25 = f32[16,1152]{1,0:T(8,128)S(1)} collective-permute-done((f32[16,1152]{1,0:T(8,128)S(1)}, f32[16,1152]{1,0:T(8,128)S(1)}, u32[]{:S(2)}, u32[]{:S(2)}) %collective-permute-start.25) | collective-permute-done | bytes 73760 | tf_op jit(solution)/shard_map/ppermute | solution.py:18
  118.3 1.7 %collective-permute-start.27 = (f32[16,1152]{1,0:T(8,128)S(1)}, f32[16,1152]{1,0:T(8,128)S(1)}, u32[]{:S(2)}, u32[]{:S(2)}) collective-permute-start(f32[16,1152]{1,0:T(8,128)S(1)} %get-tuple-element.63), channel_id=1, source_target_pairs={{0,32},{32,64},{64,96},{96,128},{128,160},{160,192},{192,224},{1,3... | collective-permute-start | bytes 221192 | tf_op jit(solution)/shard_map/ppermute | solution.py:23
  120.0 1.4 collective-permute-done.27
  121.4 3.7 %collective-permute-start.28 = (f32[16,1152]{1,0:T(8,128)S(1)}, f32[16,1152]{1,0:T(8,128)S(1)}, u32[]{:S(2)}, u32[]{:S(2)}) collective-permute-start(f32[16,1152]{1,0:T(8,128)S(1)} %add.152), channel_id=1, source_target_pairs={{0,64},{32,96},{64,128},{96,160},{128,192},{160,224},{1,65},{33,97... | collective-permute-start | bytes 221192 | tf_op jit(solution)/shard_map/ppermute | solution.py:23
  125.1 1.4 collective-permute-done.28
  126.5 9.8 %collective-permute-start.29 = (f32[16,1152]{1,0:T(8,128)S(1)}, f32[16,1152]{1,0:T(8,128)S(1)}, u32[]{:S(2)}, u32[]{:S(2)}) collective-permute-start(f32[16,1152]{1,0:T(8,128)S(1)} %add.154), channel_id=1, source_target_pairs={{0,128},{32,160},{64,192},{96,224},{1,129},{33,161},{65,193},{97,2... | collective-permute-start | bytes 221192 | tf_op jit(solution)/shard_map/ppermute | solution.py:23
  136.3 1.4 collective-permute-done.29
  137.8 1.3 collective-permute-start.31
  139.2 2.5 %collective-permute-start.32 = (f32[16,1152]{1,0:T(8,128)S(1)}, f32[16,1152]{1,0:T(8,128)S(1)}, u32[]{:S(2)}, u32[]{:S(2)}) collective-permute-start(f32[16,1152]{1,0:T(8,128)S(1)} %get-tuple-element.61), channel_id=1, source_target_pairs={{0,24},{8,0},{16,8},{24,16},{1,25},{9,1},{17,9},{25,17},{2,26},{10... | collective-permute-start | bytes 221192 | tf_op jit(solution)/shard_map/ppermute | solution.py:18
  144.3 16.5 %collective-permute-start.33 = (f32[4,32,1152]{2,1,0:T(8,128)S(1)}, f32[4,32,1152]{2,1,0:T(8,128)S(1)}, u32[]{:S(2)}, u32[]{:S(2)}) collective-permute-start(f32[4,32,1152]{2,1,0:T(8,128)S(1)} %slice.9), channel_id=1, source_target_pairs={{0,1},{1,0},{2,3},{3,2},{4,5},{5,4},{6,7},{7,6},{8,9},{9,8},{10,11... | collective-permute-start | bytes 1769480 | tf_op jit(solution)/shard_map/ppermute | solution.py:18
  160.8 1.6 collective-permute-done.33
  162.6 1.1 copy.20
  (65 shorter events, 12.1 us)
Async XLA Ops:
  0.0 5.0 %copy-start = (s32[4,2]{0,1:T(2,128)S(1)}, s32[4,2]{0,1:T(2,128)}, u32[]{:S(2)}) copy-start(s32[4,2]{0,1:T(2,128)} %param.15) | copy-start | bytes 100
  0.0 4.7 %copy-start.1 = (bf16[4,2,32,1152]{3,2,1,0:T(8,128)(2,1)S(1)}, bf16[4,2,32,1152]{3,2,1,0:T(8,128)(2,1)}, u32[]{:S(2)}) copy-start(bf16[4,2,32,1152]{3,2,1,0:T(8,128)(2,1)} %param.10) | copy-start | bytes 1769476
  1.4 3.5 %copy-start.4 = (f32[4,3,1152]{2,0,1:T(4,128)S(1)}, f32[4,3,1152]{2,0,1:T(4,128)}, u32[]{:S(2)}) copy-start(f32[4,3,1152]{2,0,1:T(4,128)} %param.13) | copy-start | bytes 165892
  1.4 3.5 %copy-start.3 = (f32[8,3,1152]{2,0,1:T(8,128)S(1)}, f32[8,3,1152]{2,0,1:T(8,128)}, u32[]{:S(2)}) copy-start(f32[8,3,1152]{2,0,1:T(8,128)} %param.14) | copy-start | bytes 331780
  1.4 4.9 %collective-permute-start.1 = (f32[4,32,1152]{2,1,0:T(8,128)S(1)}, f32[4,32,1152]{2,1,0:T(8,128)S(1)}, u32[]{:S(2)}, u32[]{:S(2)}) collective-permute-start(f32[4,32,1152]{2,1,0:T(8,128)S(1)} %get-tuple-element.75), channel_id=1, source_target_pairs={{0,1},{1,0},{2,3},{3,2},{4,5},{5,4},{6,7},{7,6},{8,9},{9,8},{10,11... | collective-permute-start | bytes 1769480 | tf_op jit(solution)/shard_map/ppermute | solution.py:18
  4.8 24.7 %collective-permute-start.8 = (bf16[4,32,1152]{2,1,0:T(8,128)(2,1)S(1)}, bf16[4,32,1152]{2,1,0:T(8,128)(2,1)S(1)}, u32[]{:S(2)}, u32[]{:S(2)}) collective-permute-start(bf16[4,32,1152]{2,1,0:T(8,128)(2,1)S(1)} %get-tuple-element.77), channel_id=1, source_target_pairs={{0,1},{1,0},{2,3},{3,2},{4,5},{5,4},{6,7},{7,6},{8,9},{9,8},{10,11... | collective-permute-start | bytes 884744 | tf_op jit(solution)/shard_map/ppermute | solution.py:18
  7.4 7.0 %collective-permute-start.2 = (bf16[64,1152]{1,0:T(8,128)(2,1)S(1)}, bf16[64,1152]{1,0:T(8,128)(2,1)S(1)}, u32[]{:S(2)}, u32[]{:S(2)}) collective-permute-start(bf16[64,1152]{1,0:T(8,128)(2,1)S(1)} %get-tuple-element.34), channel_id=1, source_target_pairs={{0,2},{2,4},{4,6},{6,0},{1,3},{3,5},{5,7},{7,1},{8,10},{10,12},{12... | collective-permute-start | bytes 442376 | tf_op jit(solution)/shard_map/ppermute | solution.py:18
  7.5 8.7 %collective-permute-start.3 = (bf16[64,1152]{1,0:T(8,128)(2,1)S(1)}, bf16[64,1152]{1,0:T(8,128)(2,1)S(1)}, u32[]{:S(2)}, u32[]{:S(2)}) collective-permute-start(bf16[64,1152]{1,0:T(8,128)(2,1)S(1)} %get-tuple-element.35), channel_id=1, source_target_pairs={{0,4},{2,6},{4,0},{6,2},{1,5},{3,7},{5,1},{7,3},{8,12},{10,14},{12... | collective-permute-start | bytes 442376 | tf_op jit(solution)/shard_map/ppermute | solution.py:18
  9.4 7.8 %collective-permute-start.4 = (bf16[64,1152]{1,0:T(8,128)(2,1)S(1)}, bf16[64,1152]{1,0:T(8,128)(2,1)S(1)}, u32[]{:S(2)}, u32[]{:S(2)}) collective-permute-start(bf16[64,1152]{1,0:T(8,128)(2,1)S(1)} %get-tuple-element.36), channel_id=1, source_target_pairs={{0,6},{2,0},{4,2},{6,4},{1,7},{3,1},{5,3},{7,5},{8,14},{10,8},{12,... | collective-permute-start | bytes 442376 | tf_op jit(solution)/shard_map/ppermute | solution.py:18
  17.2 12.2 %copy-start.5 = (s32[4]{0:T(128)S(1)}, s32[4]{0:T(128)}, u32[]{:S(2)}) copy-start(s32[4]{0:T(128)} %param.12) | copy-start | bytes 52
  25.3 9.5 %collective-permute-start.5 = (bf16[64,1152]{1,0:T(8,128)(2,1)S(1)}, bf16[64,1152]{1,0:T(8,128)(2,1)S(1)}, u32[]{:S(2)}, u32[]{:S(2)}) collective-permute-start(bf16[64,1152]{1,0:T(8,128)(2,1)S(1)} %get-tuple-element.38), channel_id=1, source_target_pairs={{0,6},{2,0},{4,2},{6,4},{1,7},{3,1},{5,3},{7,5},{8,14},{10,8},{12,... | collective-permute-start | bytes 442376 | tf_op jit(solution)/shard_map/ppermute | solution.py:18
  28.7 6.2 %collective-permute-start.6 = (bf16[64,1152]{1,0:T(8,128)(2,1)S(1)}, bf16[64,1152]{1,0:T(8,128)(2,1)S(1)}, u32[]{:S(2)}, u32[]{:S(2)}) collective-permute-start(bf16[64,1152]{1,0:T(8,128)(2,1)S(1)} %get-tuple-element.39), channel_id=1, source_target_pairs={{0,4},{2,6},{4,0},{6,2},{1,5},{3,7},{5,1},{7,3},{8,12},{10,14},{12... | collective-permute-start | bytes 442376 | tf_op jit(solution)/shard_map/ppermute | solution.py:18
  28.7 9.8 %collective-permute-start.7 = (bf16[64,1152]{1,0:T(8,128)(2,1)S(1)}, bf16[64,1152]{1,0:T(8,128)(2,1)S(1)}, u32[]{:S(2)}, u32[]{:S(2)}) collective-permute-start(bf16[64,1152]{1,0:T(8,128)(2,1)S(1)} %get-tuple-element.40), channel_id=1, source_target_pairs={{0,2},{2,4},{4,6},{6,0},{1,3},{3,5},{5,7},{7,1},{8,10},{10,12},{12... | collective-permute-start | bytes 442376 | tf_op jit(solution)/shard_map/ppermute | solution.py:18
  41.5 28.8 %copy-start.2 = (f32[2,32,1152]{2,1,0:T(8,128)S(1)}, f32[2,32,1152]{2,1,0:T(8,128)}, u32[]{:S(2)}) copy-start(f32[2,32,1152]{2,1,0:T(8,128)} %param.11) | copy-start | bytes 884740
  41.5 3.5 %collective-permute-start.9 = (f32[16,1152]{1,0:T(8,128)S(1)}, f32[16,1152]{1,0:T(8,128)S(1)}, u32[]{:S(2)}, u32[]{:S(2)}) collective-permute-start(f32[16,1152]{1,0:T(8,128)S(1)} %get-tuple-element.43), channel_id=1, source_target_pairs={{0,24},{8,0},{16,8},{24,16},{1,25},{9,1},{17,9},{25,17},{2,26},{10... | collective-permute-start | bytes 221192 | tf_op jit(solution)/shard_map/ppermute | solution.py:18
  42.4 4.8 %collective-permute-start.10 = (f32[16,1152]{1,0:T(8,128)S(1)}, f32[16,1152]{1,0:T(8,128)S(1)}, u32[]{:S(2)}, u32[]{:S(2)}) collective-permute-start(f32[16,1152]{1,0:T(8,128)S(1)} %get-tuple-element.44), channel_id=1, source_target_pairs={{0,16},{8,24},{16,0},{24,8},{1,17},{9,25},{17,1},{25,9},{2,18},{10... | collective-permute-start | bytes 221192 | tf_op jit(solution)/shard_map/ppermute | solution.py:18
  42.7 5.1 %collective-permute-start.11 = (f32[16,1152]{1,0:T(8,128)S(1)}, f32[16,1152]{1,0:T(8,128)S(1)}, u32[]{:S(2)}, u32[]{:S(2)}) collective-permute-start(f32[16,1152]{1,0:T(8,128)S(1)} %get-tuple-element.45), channel_id=1, source_target_pairs={{0,8},{8,16},{16,24},{24,0},{1,9},{9,17},{17,25},{25,1},{2,10},{10... | collective-permute-start | bytes 221192 | tf_op jit(solution)/shard_map/ppermute | solution.py:18
  47.9 4.9 %collective-permute-start.12 = (f32[16,1152]{1,0:T(8,128)S(1)}, f32[16,1152]{1,0:T(8,128)S(1)}, u32[]{:S(2)}, u32[]{:S(2)}) collective-permute-start(f32[16,1152]{1,0:T(8,128)S(1)} %get-tuple-element.69), channel_id=1, source_target_pairs={{0,32},{32,64},{64,96},{96,128},{128,160},{160,192},{192,224},{1,3... | collective-permute-start | bytes 221192 | tf_op jit(solution)/shard_map/ppermute | solution.py:23
  52.9 6.5 %collective-permute-start.13 = (f32[16,1152]{1,0:T(8,128)S(1)}, f32[16,1152]{1,0:T(8,128)S(1)}, u32[]{:S(2)}, u32[]{:S(2)}) collective-permute-start(f32[16,1152]{1,0:T(8,128)S(1)} %add.141), channel_id=1, source_target_pairs={{0,64},{32,96},{64,128},{96,160},{128,192},{160,224},{1,65},{33,97... | collective-permute-start | bytes 221192 | tf_op jit(solution)/shard_map/ppermute | solution.py:23
  59.3 16.1 %collective-permute-start.14 = (f32[16,1152]{1,0:T(8,128)S(1)}, f32[16,1152]{1,0:T(8,128)S(1)}, u32[]{:S(2)}, u32[]{:S(2)}) collective-permute-start(f32[16,1152]{1,0:T(8,128)S(1)} %add.143), channel_id=1, source_target_pairs={{0,128},{32,160},{64,192},{96,224},{1,129},{33,161},{65,193},{97,2... | collective-permute-start | bytes 221192 | tf_op jit(solution)/shard_map/ppermute | solution.py:23
  70.3 8.9 %collective-permute-start = (f32[32,1152]{1,0:T(8,128)S(1)}, f32[32,1152]{1,0:T(8,128)S(1)}, u32[]{:S(2)}, u32[]{:S(2)}) collective-permute-start(f32[32,1152]{1,0:T(8,128)S(1)} %get-tuple-element.86), channel_id=1, source_target_pairs={{0,1},{1,0},{2,3},{3,2},{4,5},{5,4},{6,7},{7,6},{8,9},{9,8},{10,11... | collective-permute-start | bytes 442376 | tf_op jit(solution)/shard_map/ppermute | solution.py:18
  75.5 4.8 %collective-permute-start.16 = (f32[16,1152]{1,0:T(8,128)S(1)}, f32[16,1152]{1,0:T(8,128)S(1)}, u32[]{:S(2)}, u32[]{:S(2)}) collective-permute-start(f32[16,1152]{1,0:T(8,128)S(1)} %get-tuple-element.82), channel_id=1, source_target_pairs={{0,16},{8,24},{16,0},{24,8},{1,17},{9,25},{17,1},{25,9},{2,18},{10... | collective-permute-start | bytes 221192 | tf_op jit(solution)/shard_map/ppermute | solution.py:18
  76.5 4.5 %collective-permute-start.15 = (f32[16,1152]{1,0:T(8,128)S(1)}, f32[16,1152]{1,0:T(8,128)S(1)}, u32[]{:S(2)}, u32[]{:S(2)}) collective-permute-start(f32[16,1152]{1,0:T(8,128)S(1)} %get-tuple-element.83), channel_id=1, source_target_pairs={{0,8},{8,16},{16,24},{24,0},{1,9},{9,17},{17,25},{25,1},{2,10},{10... | collective-permute-start | bytes 221192 | tf_op jit(solution)/shard_map/ppermute | solution.py:18
  76.5 4.5 %collective-permute-start.17 = (f32[16,1152]{1,0:T(8,128)S(1)}, f32[16,1152]{1,0:T(8,128)S(1)}, u32[]{:S(2)}, u32[]{:S(2)}) collective-permute-start(f32[16,1152]{1,0:T(8,128)S(1)} %get-tuple-element.67), channel_id=1, source_target_pairs={{0,24},{8,0},{16,8},{24,16},{1,25},{9,1},{17,9},{25,17},{2,26},{10... | collective-permute-start | bytes 221192 | tf_op jit(solution)/shard_map/ppermute | solution.py:18
  82.2 6.9 %collective-permute-start.18 = (bf16[64,1152]{1,0:T(8,128)(2,1)S(1)}, bf16[64,1152]{1,0:T(8,128)(2,1)S(1)}, u32[]{:S(2)}, u32[]{:S(2)}) collective-permute-start(bf16[64,1152]{1,0:T(8,128)(2,1)S(1)} %get-tuple-element.48), channel_id=1, source_target_pairs={{0,2},{2,4},{4,6},{6,0},{1,3},{3,5},{5,7},{7,1},{8,10},{10,12},{12... | collective-permute-start | bytes 442376 | tf_op jit(solution)/shard_map/ppermute | solution.py:18
  82.3 6.8 %collective-permute-start.19 = (bf16[64,1152]{1,0:T(8,128)(2,1)S(1)}, bf16[64,1152]{1,0:T(8,128)(2,1)S(1)}, u32[]{:S(2)}, u32[]{:S(2)}) collective-permute-start(bf16[64,1152]{1,0:T(8,128)(2,1)S(1)} %get-tuple-element.49), channel_id=1, source_target_pairs={{0,4},{2,6},{4,0},{6,2},{1,5},{3,7},{5,1},{7,3},{8,12},{10,14},{12... | collective-permute-start | bytes 442376 | tf_op jit(solution)/shard_map/ppermute | solution.py:18
  83.8 6.2 %collective-permute-start.20 = (bf16[64,1152]{1,0:T(8,128)(2,1)S(1)}, bf16[64,1152]{1,0:T(8,128)(2,1)S(1)}, u32[]{:S(2)}, u32[]{:S(2)}) collective-permute-start(bf16[64,1152]{1,0:T(8,128)(2,1)S(1)} %get-tuple-element.50), channel_id=1, source_target_pairs={{0,6},{2,0},{4,2},{6,4},{1,7},{3,1},{5,3},{7,5},{8,14},{10,8},{12,... | collective-permute-start | bytes 442376 | tf_op jit(solution)/shard_map/ppermute | solution.py:18
  98.1 5.8 %collective-permute-start.21 = (bf16[64,1152]{1,0:T(8,128)(2,1)S(1)}, bf16[64,1152]{1,0:T(8,128)(2,1)S(1)}, u32[]{:S(2)}, u32[]{:S(2)}) collective-permute-start(bf16[64,1152]{1,0:T(8,128)(2,1)S(1)} %get-tuple-element.52), channel_id=1, source_target_pairs={{0,6},{2,0},{4,2},{6,4},{1,7},{3,1},{5,3},{7,5},{8,14},{10,8},{12,... | collective-permute-start | bytes 442376 | tf_op jit(solution)/shard_map/ppermute | solution.py:18
  100.2 5.6 %collective-permute-start.22 = (bf16[64,1152]{1,0:T(8,128)(2,1)S(1)}, bf16[64,1152]{1,0:T(8,128)(2,1)S(1)}, u32[]{:S(2)}, u32[]{:S(2)}) collective-permute-start(bf16[64,1152]{1,0:T(8,128)(2,1)S(1)} %get-tuple-element.53), channel_id=1, source_target_pairs={{0,4},{2,6},{4,0},{6,2},{1,5},{3,7},{5,1},{7,3},{8,12},{10,14},{12... | collective-permute-start | bytes 442376 | tf_op jit(solution)/shard_map/ppermute | solution.py:18
  100.2 6.8 %collective-permute-start.23 = (bf16[64,1152]{1,0:T(8,128)(2,1)S(1)}, bf16[64,1152]{1,0:T(8,128)(2,1)S(1)}, u32[]{:S(2)}, u32[]{:S(2)}) collective-permute-start(bf16[64,1152]{1,0:T(8,128)(2,1)S(1)} %get-tuple-element.54), channel_id=1, source_target_pairs={{0,2},{2,4},{4,6},{6,0},{1,3},{3,5},{5,7},{7,1},{8,10},{10,12},{12... | collective-permute-start | bytes 442376 | tf_op jit(solution)/shard_map/ppermute | solution.py:18
  109.9 5.0 %collective-permute-start.24 = (f32[16,1152]{1,0:T(8,128)S(1)}, f32[16,1152]{1,0:T(8,128)S(1)}, u32[]{:S(2)}, u32[]{:S(2)}) collective-permute-start(f32[16,1152]{1,0:T(8,128)S(1)} %get-tuple-element.57), channel_id=1, source_target_pairs={{0,24},{8,0},{16,8},{24,16},{1,25},{9,1},{17,9},{25,17},{2,26},{10... | collective-permute-start | bytes 221192 | tf_op jit(solution)/shard_map/ppermute | solution.py:18
  112.9 4.8 %collective-permute-start.25 = (f32[16,1152]{1,0:T(8,128)S(1)}, f32[16,1152]{1,0:T(8,128)S(1)}, u32[]{:S(2)}, u32[]{:S(2)}) collective-permute-start(f32[16,1152]{1,0:T(8,128)S(1)} %get-tuple-element.58), channel_id=1, source_target_pairs={{0,16},{8,24},{16,0},{24,8},{1,17},{9,25},{17,1},{25,9},{2,18},{10... | collective-permute-start | bytes 221192 | tf_op jit(solution)/shard_map/ppermute | solution.py:18
  113.0 5.2 %collective-permute-start.26 = (f32[16,1152]{1,0:T(8,128)S(1)}, f32[16,1152]{1,0:T(8,128)S(1)}, u32[]{:S(2)}, u32[]{:S(2)}) collective-permute-start(f32[16,1152]{1,0:T(8,128)S(1)} %get-tuple-element.59), channel_id=1, source_target_pairs={{0,8},{8,16},{16,24},{24,0},{1,9},{9,17},{17,25},{25,1},{2,10},{10... | collective-permute-start | bytes 221192 | tf_op jit(solution)/shard_map/ppermute | solution.py:18
  118.3 3.1 %collective-permute-start.27 = (f32[16,1152]{1,0:T(8,128)S(1)}, f32[16,1152]{1,0:T(8,128)S(1)}, u32[]{:S(2)}, u32[]{:S(2)}) collective-permute-start(f32[16,1152]{1,0:T(8,128)S(1)} %get-tuple-element.63), channel_id=1, source_target_pairs={{0,32},{32,64},{64,96},{96,128},{128,160},{160,192},{192,224},{1,3... | collective-permute-start | bytes 221192 | tf_op jit(solution)/shard_map/ppermute | solution.py:23
  121.4 5.1 %collective-permute-start.28 = (f32[16,1152]{1,0:T(8,128)S(1)}, f32[16,1152]{1,0:T(8,128)S(1)}, u32[]{:S(2)}, u32[]{:S(2)}) collective-permute-start(f32[16,1152]{1,0:T(8,128)S(1)} %add.152), channel_id=1, source_target_pairs={{0,64},{32,96},{64,128},{96,160},{128,192},{160,224},{1,65},{33,97... | collective-permute-start | bytes 221192 | tf_op jit(solution)/shard_map/ppermute | solution.py:23
  126.5 11.2 %collective-permute-start.29 = (f32[16,1152]{1,0:T(8,128)S(1)}, f32[16,1152]{1,0:T(8,128)S(1)}, u32[]{:S(2)}, u32[]{:S(2)}) collective-permute-start(f32[16,1152]{1,0:T(8,128)S(1)} %add.154), channel_id=1, source_target_pairs={{0,128},{32,160},{64,192},{96,224},{1,129},{33,161},{65,193},{97,2... | collective-permute-start | bytes 221192 | tf_op jit(solution)/shard_map/ppermute | solution.py:23
  137.8 4.8 %collective-permute-start.31 = (f32[16,1152]{1,0:T(8,128)S(1)}, f32[16,1152]{1,0:T(8,128)S(1)}, u32[]{:S(2)}, u32[]{:S(2)}) collective-permute-start(f32[16,1152]{1,0:T(8,128)S(1)} %get-tuple-element.79), channel_id=1, source_target_pairs={{0,16},{8,24},{16,0},{24,8},{1,17},{9,25},{17,1},{25,9},{2,18},{10... | collective-permute-start | bytes 221192 | tf_op jit(solution)/shard_map/ppermute | solution.py:18
  139.0 4.4 %collective-permute-start.30 = (f32[16,1152]{1,0:T(8,128)S(1)}, f32[16,1152]{1,0:T(8,128)S(1)}, u32[]{:S(2)}, u32[]{:S(2)}) collective-permute-start(f32[16,1152]{1,0:T(8,128)S(1)} %get-tuple-element.80), channel_id=1, source_target_pairs={{0,8},{8,16},{16,24},{24,0},{1,9},{9,17},{17,25},{25,1},{2,10},{10... | collective-permute-start | bytes 221192 | tf_op jit(solution)/shard_map/ppermute | solution.py:18
  139.2 4.2 %collective-permute-start.32 = (f32[16,1152]{1,0:T(8,128)S(1)}, f32[16,1152]{1,0:T(8,128)S(1)}, u32[]{:S(2)}, u32[]{:S(2)}) collective-permute-start(f32[16,1152]{1,0:T(8,128)S(1)} %get-tuple-element.61), channel_id=1, source_target_pairs={{0,24},{8,0},{16,8},{24,16},{1,25},{9,1},{17,9},{25,17},{2,26},{10... | collective-permute-start | bytes 221192 | tf_op jit(solution)/shard_map/ppermute | solution.py:18
  144.3 18.2 %collective-permute-start.33 = (f32[4,32,1152]{2,1,0:T(8,128)S(1)}, f32[4,32,1152]{2,1,0:T(8,128)S(1)}, u32[]{:S(2)}, u32[]{:S(2)}) collective-permute-start(f32[4,32,1152]{2,1,0:T(8,128)S(1)} %slice.9), channel_id=1, source_target_pairs={{0,1},{1,0},{2,3},{3,2},{4,5},{5,4},{6,7},{7,6},{8,9},{9,8},{10,11... | collective-permute-start | bytes 1769480 | tf_op jit(solution)/shard_map/ppermute | solution.py:18

commit v2 on v1

--- a/solution.py
+++ b/solution.py
@@ -9,6 +9,10 @@
 HEADS = 16
 SWEEPS = 2
 LANES = 128
+BLOCKS = 4
+LOG2E = 1.4426950408889634
+HALF = ("v", "u", "y")
+PLANES = ("w", "v", "u")
 VMEM = pl.BlockSpec(memory_space=pltpu.VMEM)
 SMEM = pl.BlockSpec(memory_space=pltpu.SMEM)
 
@@ -16,11 +20,6 @@
 def shifted(value, axis, shift):
     size = lax.axis_size(axis)
     return lax.ppermute(value, axis, [(i, (i + shift) % size) for i in range(size)])
-
-
-def from_below(value, axis, shift):
-    size = lax.axis_size(axis)
-    return lax.ppermute(value, axis, [(i, i + shift) for i in range(size - shift)])
 
 
 def call(body, outs, specs, *args, scratch=()):
@@ -58,15 +57,18 @@
         mod_refs[r][...] = normed_rows(rows, shift, scale)
 
 
-def resume_body(where_ref, start_ref, before_ref, l0, l1, l2, l3, step_ref, view_ref, x_ref, *rest):
+def block_rows(flip, block, blocks, part):
+    place = block + flip * (blocks - 1 - 2 * block)
+    return pl.ds(pl.multiple_of(place * part, part), part)
+
+
+def resume_body(where_ref, start_ref, before_ref, lower_ref, step_ref, view_ref, x_ref, *rest):
     mod_refs, base_ref = rest[:-1], rest[-1]
-    place, spot = where_ref[0], where_ref[1]
+    place, flip = where_ref[0], where_ref[1]
     steps = before_ref.shape[0]
-    lower = (l0, l1, l2, l3)
-    part = l0.shape[0]
-    for r in range(len(lower)):
-        rows = pl.ds(pl.multiple_of(lax.rem(spot + len(lower) - r, len(lower)) * part, part), part)
-        base_ref[rows, :] = lower[r][...]
+    part = lower_ref.shape[0] // BLOCKS
+    for block in range(BLOCKS):
+        base_ref[block * part : (block + 1) * part, :] = lower_ref[block_rows(flip, block, BLOCKS, part), :]
     for r in range(steps):
         step = lax.rem(place + r, steps)
         rows = start_ref[...] + (base_ref[...] + before_ref[step])
@@ -94,13 +96,11 @@
         q = qkv_ref[:, low:high] * mask_ref[h : h + 1, low:high]
         k = qkv_ref[:, width + low : width + high]
         v = qkv_ref[:, 2 * width + low : 2 * width + high]
-        scores = lax.dot_general(
-            q, k, (((1,), (1,)), ((), ())), preferred_element_type=jnp.float32
-        ) * (1.0 / size**0.5)
+        scores = lax.dot_general(q, k, (((1,), (1,)), ((), ())), preferred_element_type=jnp.float32)
         top = jnp.max(scores, axis=-1, keepdims=True)
-        powers = jnp.exp(scores - top)
-        probs = (powers / jnp.sum(powers, axis=-1, keepdims=True)).astype(jnp.bfloat16)
-        out = jnp.dot(probs, v, preferred_element_type=jnp.float32)
+        powers = jnp.exp2((scores - top) * (LOG2E / size**0.5))
+        share = 1.0 / jnp.sum(powers, axis=-1, keepdims=True)
+        out = jnp.dot(powers.astype(jnp.bfloat16), v, preferred_element_type=jnp.float32) * share
         for t in range(first, last + 1):
             piece = out[:, t * LANES - low : (t + 1) * LANES - low]
             if tiles[t] is not None:
@@ -115,10 +115,24 @@
 
 
 def project_body(
-    where_ref, coef_ref, a0, a1, a2, a3, w_ref, x_ref, mine_ref, peer_ref, step_ref, view_ref, before_ref, *rest
+    where_ref,
+    coef_ref,
+    a0,
+    a1,
+    a2,
+    a3,
+    w_ref,
+    x_ref,
+    mine_ref,
+    peer_ref,
+    step_ref,
+    view_ref,
+    before_ref,
+    total_ref,
+    rows_ref,
+    proj_ref,
 ):
-    total_refs, rows_ref, proj_ref, total_ref = rest[:-3], rest[-3], rest[-2], rest[-1]
-    place, spot = where_ref[0], where_ref[1]
+    place, flip = where_ref[0], where_ref[1]
     pieces = (a0, a1, a2, a3)
     part = a0.shape[0]
     steps = len(pieces)
@@ -135,11 +149,9 @@
         increment = coef_ref[0, step] * rows + coef_ref[1, step] * denoised + coef_ref[2, step] * drawn
         before_ref[step] = jnp.zeros_like(increment) if running is None else running
         running = increment if running is None else running + increment
-    total_ref[...] = running
-    share = total_refs[0].shape[0]
-    for r in range(len(total_refs)):
-        rows = pl.ds(pl.multiple_of(lax.rem(spot + r, len(total_refs)) * share, share), share)
-        total_refs[r][...] = total_ref[rows, :]
+    share = part // BLOCKS
+    for block in range(BLOCKS):
+        total_ref[block_rows(flip, block, BLOCKS, share), :] = running[block * share : (block + 1) * share]
 
 
 def coefficients(steps_index):
@@ -152,41 +164,35 @@
     return (coef_state, coef_eps, coef_noise)
 
 
-def earlier_sum(totals):
-    spot = lax.axis_index("y")
-    peers = lax.axis_size("y")
-    mine = [totals[0]] + [shifted(totals[r], "y", r) for r in range(1, peers)]
-    held = []
-    for p in range(peers):
-        r = lax.rem(spot - p + peers, peers)
-        value = mine[0]
-        for k in range(1, peers):
-            value = jnp.where(r == k, mine[k], value)
-        held.append(value)
-    inside = [jnp.zeros_like(held[0])]
-    for p in range(peers):
-        inside.append(inside[-1] + held[p])
-    running = inside.pop()
-    below = jnp.zeros_like(running)
-    shift = 1
-    while shift < lax.axis_size("z"):
-        passed = from_below(running, "z", shift)
-        below = below + passed
-        running = running + passed
-        shift *= 2
-    lower = []
-    for r in range(peers):
-        p = lax.rem(spot + r, peers)
-        value = inside[0]
-        for k in range(1, peers):
-            value = jnp.where(p == k, inside[k], value)
-        lower.append(value + below)
-    return [lower[0]] + [shifted(lower[r], "y", r) for r in range(1, peers)]
+def inside_body(held_ref, before_ref, all_ref):
+    running = jnp.zeros(held_ref.shape[1:], held_ref.dtype)
+    for q in range(held_ref.shape[0]):
+        before_ref[q] = running
+        running = running + held_ref[q]
+    all_ref[...] = running
+
+
+def earlier_sum(total):
+    places = lax.axis_size(HALF)
+    rows, width = total.shape
+    shares = total.reshape(places, rows // places, width)
+    held = lax.all_to_all(shares, HALF, 0, 0, tiled=True)
+    before, whole = call(
+        inside_body,
+        [jax.ShapeDtypeStruct(shares.shape, total.dtype), jax.ShapeDtypeStruct(shares.shape[1:], total.dtype)],
+        [VMEM],
+        held,
+    )
+    planes = lax.axis_size(PLANES)
+    below = lax.ppermute(whole, PLANES, [(i, planes - 1 - i) for i in range(planes)])
+    below = jnp.where(lax.axis_index("w") == 1, below, jnp.zeros_like(below))
+    lower = lax.all_to_all(before + below[None], HALF, 0, 0, tiled=True)
+    return lower.reshape(rows, width)
 
 
 def per_device(states, noise, x_start, timesteps, step_mod, view_mod, view_ids, w_qkv, w_out):
     steps, views, part, width = states.shape
-    place, spot, core = (lax.axis_index(a) for a in ("x", "y", "c"))
+    place, flip, core = (lax.axis_index(a) for a in ("x", "w", "c"))
     other = 1 - core
     f32, bf16 = jnp.float32, jnp.bfloat16
     rows = 2 * part
@@ -197,7 +203,7 @@
     def from_peer(a, axis):
         return shifted(lax.dynamic_index_in_dim(a, other, axis, keepdims=False), "c", 1)
 
-    where = jnp.concatenate([jnp.stack([place, spot]).astype(jnp.int32), own(view_ids, 1)])
+    where = jnp.concatenate([jnp.stack([place, flip]).astype(jnp.int32), own(view_ids, 1)])
     coefs = jnp.stack(coefficients(timesteps))
     start = jnp.concatenate([own(x_start, 0), from_peer(x_start, 0)], axis=0)
     noise_mine, noise_peer = own(noise, 1), from_peer(noise, 1)
@@ -208,7 +214,7 @@
 
     x_shape = jax.ShapeDtypeStruct((steps, rows, width), f32)
     piece = jax.ShapeDtypeStruct((rows, width), bf16)
-    share = jax.ShapeDtypeStruct((rows // lax.axis_size("y"), width), f32)
+    total_shape = jax.ShapeDtypeStruct((rows, width), f32)
     x, *mods = call(
         enter_body,
         [x_shape] + [piece] * steps,
@@ -231,9 +237,9 @@
             scratch=[pltpu.VMEM((steps * rows, width), bf16), pltpu.VMEM((steps * rows, 3 * width), bf16)],
         )
         back = [attended[0]] + [shifted(attended[r], "x", -r) for r in range(1, steps)]
-        before, *totals = call(
+        before, total = call(
             project_body,
-            [x_shape] + [share] * lax.axis_size("y"),
+            [x_shape, total_shape],
             [SMEM] * 2 + [VMEM] * 10,
             where,
             coefs,
@@ -247,19 +253,18 @@
             scratch=[
                 pltpu.VMEM((steps * rows, width), bf16),
                 pltpu.VMEM((steps * rows, width), f32),
-                pltpu.VMEM((rows, width), f32),
             ],
         )
-        lower = earlier_sum(totals)
+        lower = earlier_sum(total)
         more = sweep + 1 < SWEEPS
         x, *mods = call(
             resume_body,
             [x_shape] + ([piece] * steps if more else []),
-            [SMEM] + [VMEM] * 8,
+            [SMEM] + [VMEM] * 5,
             where,
             start,
             before,
-            *lower,
+            lower,
             step_mod,
             view_mod,
             scratch=[pltpu.VMEM((rows, width), f32)],
@@ -271,8 +276,8 @@
 
 
 def solution(mesh):
-    finer = Mesh(mesh.devices.reshape(8, 4, 4, 2), ("z", "y", "x", "c"))
-    tm, tok = ("z", "y"), ("x", "c")
+    finer = Mesh(mesh.devices.reshape(2, 2, 2, 4, 4, 2), ("w", "v", "u", "y", "x", "c"))
+    tm, tok = ("w", "v", "u", "y"), ("x", "c")
     placed = (
         P(tm, None, tok, None),
         P(tm, None, tok, None),

time: 164 us -> 148 us (0.902)
  starting transfers between devices: 85.9 us -> 40.6 us
  blocking collectives: 0 us -> 40.5 us
  waiting for transfers between devices: 49.3 us -> 39 us
  Pallas kernels: 24.9 us -> 23.2 us
    all_to_all x0 -> x3, blocking collectives: none -> 40.5 us  [the longest x2 27.7 us: earlier_sum(): held = lax.all_to_all(shares, HALF, 0, 0, tiled=True)]
    ppermute x6 -> x2, starting transfers between devices: 34.7 us -> 4.92 us  [earlier_sum(): lax.ppermute(whole, PLANES, [(i, planes - 1 - i) for i in range(planes)])]
    ppermute x28 -> x16, starting transfers between devices: 51.1 us -> 30.7 us  [shifted(): lax.ppermute(value, axis, [(i, (i + shift) % size) for i in range(size)])]
    ppermute x28 -> x16, waiting for transfers between devices: 42.4 us -> 30.4 us  [shifted(): lax.ppermute(value, axis, [(i, (i + shift) % size) for i in range(size)])]
    all_to_all x0 -> x1, starting transfers between devices: none -> 4.92 us  [earlier_sum(): lower = lax.all_to_all(before + below[None], HALF, 0, 0, tiled=True)]
    all_to_all x0 -> x1, waiting for transfers between devices: none -> 4.9 us  [earlier_sum(): lower = lax.all_to_all(before + below[None], HALF, 0, 0, tiled=True)]
    ppermute x6 -> x2, waiting for transfers between devices: 6.94 us -> 3.65 us  [earlier_sum(): lax.ppermute(whole, PLANES, [(i, planes - 1 - i) for i in range(planes)])]
    pallas_call x7 -> x9, Pallas kernels: 24.9 us -> 23.2 us  [call(): pl.pallas_call(body, out_shape=outs, in_specs=specs, out_specs=jax.tree.m...]
  transfers between devices with their start and end apart: 34 -> 19, of which waited for: 28 -> 17; matrix products, arithmetic and copies ran while one was open for 0% -> 0% of each run, Pallas kernels for 6% -> 6%
where the time goes in v2:
time: 148 us
  starting transfers between devices  40.6 us (27%)
  blocking collectives  40.5 us (27%)
  waiting for transfers between devices  39 us (26%)
  Pallas kernels  23.2 us (16%)
  local copies, waits for them, and re-layouts  3.08 us (2%)
    ppermute x16, starting transfers between devices, shifted(): lax.ppermute(value, axis, [(i, (i + shift) % size) for i in range(size)])  30.7 us
    ppermute x16, waiting for transfers between devices, shifted(): lax.ppermute(value, axis, [(i, (i + shift) % size) for i in range(size)])  30.4 us
    all_to_all x2, blocking collectives, earlier_sum(): held = lax.all_to_all(shares, HALF, 0, 0, tiled=True)  27.7 us
    pallas_call x9, Pallas kernels, call(): pl.pallas_call(body, out_shape=outs, in_specs=specs, out_specs=jax.tree.m...  23.2 us
    all_to_all x1, blocking collectives, earlier_sum(): lower = lax.all_to_all(before + below[None], HALF, 0, 0, tiled=True)  12.9 us
    all_to_all x1, starting transfers between devices, earlier_sum(): lower = lax.all_to_all(before + below[None], HALF, 0, 0, tiled=True)  4.92 us
    ppermute x2, starting transfers between devices, earlier_sum(): lax.ppermute(whole, PLANES, [(i, planes - 1 - i) for i in range(planes)])  4.92 us
    all_to_all x1, waiting for transfers between devices, earlier_sum(): lower = lax.all_to_all(before + below[None], HALF, 0, 0, tiled=True)  4.9 us
  transfers between devices with their start and end apart: 19, of which 17 were waited for; matrix products, arithmetic and copies ran while one was open for 0% of the time, Pallas kernels for 6%

profile of v2, /device:TPU:1, one launch (start us, length us, event | category | flops | bytes accessed | tf_op | source)
XLA Modules:
  0.0 147.7 jit_solution(12898997106271805256)
XLA Ops:
  0.0 1.4 dynamic-slice_bitcast_fusion
  1.4 3.3 %collective-permute-start.1 = (f32[4,32,1152]{2,1,0:T(8,128)S(1)}, f32[4,32,1152]{2,1,0:T(8,128)S(1)}, u32[]{:S(2)}, u32[]{:S(2)}) collective-permute-start(f32[4,32,1152]{2,1,0:T(8,128)S(1)} %get-tuple-element.59), channel_id=1, source_target_pairs={{0,1},{1,0},{2,3},{3,2},{4,5},{5,4},{6,7},{7,6},{8,9},{9,8},{10,11... | collective-permute-start | bytes 1769480 | tf_op jit(solution)/shard_map/ppermute | solution.py:22
  4.8 0.1 collective-permute-start.8
  5.1 1.3 collective-permute-done.1.peer_ref
  6.3 1.0 shard_map.91
  7.5 1.9 %collective-permute-start.3 = (bf16[64,1152]{1,0:T(8,128)(2,1)S(1)}, bf16[64,1152]{1,0:T(8,128)(2,1)S(1)}, u32[]{:S(2)}, u32[]{:S(2)}) collective-permute-start(bf16[64,1152]{1,0:T(8,128)(2,1)S(1)} %get-tuple-element.33), channel_id=1, source_target_pairs={{0,4},{2,6},{4,0},{6,2},{1,5},{3,7},{5,1},{7,3},{8,12},{10,14},{12... | collective-permute-start | bytes 442376 | tf_op jit(solution)/shard_map/ppermute | solution.py:22
  9.4 1.2 collective-permute-start.4
  10.6 3.8 %collective-permute-done.2.a1 = bf16[64,1152]{1,0:T(8,128)(2,1)S(1)} collective-permute-done((bf16[64,1152]{1,0:T(8,128)(2,1)S(1)}, bf16[64,1152]{1,0:T(8,128)(2,1)S(1)}, u32[]{:S(2)}, u32[]{:S(2)}) %collective-permute-start.2) | collective-permute-done | bytes 147488 | tf_op jit(solution)/shard_map/ppermute | solution.py:22
  14.4 1.8 %collective-permute-done.3.a2 = bf16[64,1152]{1,0:T(8,128)(2,1)S(1)} collective-permute-done((bf16[64,1152]{1,0:T(8,128)(2,1)S(1)}, bf16[64,1152]{1,0:T(8,128)(2,1)S(1)}, u32[]{:S(2)}, u32[]{:S(2)}) %collective-permute-start.3) | collective-permute-done | bytes 147488 | tf_op jit(solution)/shard_map/ppermute | solution.py:22
  16.2 1.0 collective-permute-done.4.a3
  17.2 7.2 %shard_map.92 = (bf16[64,1152]{1,0:T(8,128)(2,1)S(1)}, bf16[64,1152]{1,0:T(8,128)(2,1)S(1)}, bf16[64,1152]{1,0:T(8,128)(2,1)S(1)}, bf16[64,1152]{1,0:T(8,128)(2,1)S(1)}) custom-call(bf16[64,1152]{1,0:T(8,128)(2,1)S(1)} %get-tuple-element.31.a0, bf16[64,1152]{1,0:T(8,128)(2,1)S(1)} %collective-permute-done.2.a1, ...), custom_call_target="tpu_custom_call" | custom-call | tf_op jit(solution)/shard_map/pallas_call | solution.py:26
  24.4 3.4 %collective-permute-start.5 = (bf16[64,1152]{1,0:T(8,128)(2,1)S(1)}, bf16[64,1152]{1,0:T(8,128)(2,1)S(1)}, u32[]{:S(2)}, u32[]{:S(2)}) collective-permute-start(bf16[64,1152]{1,0:T(8,128)(2,1)S(1)} %get-tuple-element.36), channel_id=1, source_target_pairs={{0,6},{2,0},{4,2},{6,4},{1,7},{3,1},{5,3},{7,5},{8,14},{10,8},{12,... | collective-permute-start | bytes 442376 | tf_op jit(solution)/shard_map/ppermute | solution.py:22
  27.9 0.7 collective-permute-start.7
  28.6 5.3 %collective-permute-done.5.a1 = bf16[64,1152]{1,0:T(8,128)(2,1)S(1)} collective-permute-done((bf16[64,1152]{1,0:T(8,128)(2,1)S(1)}, bf16[64,1152]{1,0:T(8,128)(2,1)S(1)}, u32[]{:S(2)}, u32[]{:S(2)}) %collective-permute-start.5) | collective-permute-done | bytes 147488 | tf_op jit(solution)/shard_map/ppermute | solution.py:22
  33.9 0.2 collective-permute-done.6.a2
  34.1 3.6 %collective-permute-done.7.a3 = bf16[64,1152]{1,0:T(8,128)(2,1)S(1)} collective-permute-done((bf16[64,1152]{1,0:T(8,128)(2,1)S(1)}, bf16[64,1152]{1,0:T(8,128)(2,1)S(1)}, u32[]{:S(2)}, u32[]{:S(2)}) %collective-permute-start.7) | collective-permute-done | bytes 147488 | tf_op jit(solution)/shard_map/ppermute | solution.py:22
  37.7 2.9 %shard_map.93 = (f32[4,64,1152]{2,1,0:T(8,128)S(1)}, f32[64,1152]{1,0:T(8,128)S(1)}) custom-call(s32[6]{0:T(128)S(1)} %pad_add_fusion.where_ref, f32[3,4]{1,0:T(4,128)S(1)} %pad_maximum_fusion.2.coef_ref, bf16[64,1152]{1,0:T(8,128)(2,1)S(1)} %get-tuple-element.35.a0, bf16[64,1152]{1,0:T(8,128)(2,1)S(1)} %collective-permute-done.5.a1, ...), custom_call_target="tpu_custom_call" | custom-call | tf_op jit(solution)/shard_map/pallas_call | solution.py:26
  40.6 0.1 reshape.26
  40.7 15.8 %all_to_all.20.held_ref = f32[16,4,1152]{2,1,0:T(4,128)S(1)} all-to-all(f32[16,4,1152]{2,1,0:T(4,128)S(1)} %reshape.26), channel_id=1, replica_groups=mesh['w'=2,'v'=2,'u'=2,'y'=4,'x'=4,'c'=2] {'v','u','y'}, dimensions={0} | all-to-all | bytes 589824 | tf_op jit(solution)/shard_map/all_to_all | solution.py:179
  56.6 3.2 %collective-permute-start.9 = (f32[4,1152]{1,0:T(4,128)S(1)}, f32[4,1152]{1,0:T(4,128)S(1)}, u32[]{:S(2)}, u32[]{:S(2)}) collective-permute-start(f32[4,1152]{1,0:T(4,128)S(1)} %get-tuple-element.43), channel_id=1, source_target_pairs={{0,224},{32,192},{64,160},{96,128},{128,96},{160,64},{192,32},{224... | collective-permute-start | bytes 55304 | tf_op jit(solution)/shard_map/ppermute | solution.py:187
  59.8 1.2 collective-permute-done.9
  60.9 0.7 broadcast_add_fusion.1
  61.7 4.9 %all-to-all-start.1 = ((f32[16,4,1152]{2,1,0:T(4,128)}), f32[16,4,1152]{2,1,0:T(4,128)S(1)}, u32[]{:S(2)}, u32[]{:S(2)}) async-start(f32[16,4,1152]{2,1,0:T(4,128)} %bitcast.28), calls=%async_computation.1 | async-start | bytes 589824 | tf_op jit(solution)/shard_map/all_to_all | solution.py:189
  66.7 3.3 %collective-permute-start = (f32[32,1152]{1,0:T(8,128)S(1)}, f32[32,1152]{1,0:T(8,128)S(1)}, u32[]{:S(2)}, u32[]{:S(2)}) collective-permute-start(f32[32,1152]{1,0:T(8,128)S(1)} %get-tuple-element.64), channel_id=1, source_target_pairs={{0,1},{1,0},{2,3},{3,2},{4,5},{5,4},{6,7},{7,6},{8,9},{9,8},{10,11... | collective-permute-start | bytes 442376 | tf_op jit(solution)/shard_map/ppermute | solution.py:22
  70.0 1.0 collective-permute-done
  71.0 4.9 %all-to-all-done.1 = f32[16,4,1152]{2,1,0:T(4,128)S(1)} async-done(((f32[16,4,1152]{2,1,0:T(4,128)}), f32[16,4,1152]{2,1,0:T(4,128)S(1)}, u32[]{:S(2)}, u32[]{:S(2)}) %all-to-all-start.1) | async-done | bytes 294944 | tf_op jit(solution)/shard_map/all_to_all | solution.py:189
  75.9 0.1 reshape.27.lower_ref
  76.0 1.1 shard_map.95
  77.2 0.6 collective-permute-start.11
  77.8 2.1 %collective-permute-start.12 = (bf16[64,1152]{1,0:T(8,128)(2,1)S(1)}, bf16[64,1152]{1,0:T(8,128)(2,1)S(1)}, u32[]{:S(2)}, u32[]{:S(2)}) collective-permute-start(bf16[64,1152]{1,0:T(8,128)(2,1)S(1)} %get-tuple-element.47), channel_id=1, source_target_pairs={{0,6},{2,0},{4,2},{6,4},{1,7},{3,1},{5,3},{7,5},{8,14},{10,8},{12,... | collective-permute-start | bytes 442376 | tf_op jit(solution)/shard_map/ppermute | solution.py:22
  79.9 4.1 %collective-permute-done.10.a1 = bf16[64,1152]{1,0:T(8,128)(2,1)S(1)} collective-permute-done((bf16[64,1152]{1,0:T(8,128)(2,1)S(1)}, bf16[64,1152]{1,0:T(8,128)(2,1)S(1)}, u32[]{:S(2)}, u32[]{:S(2)}) %collective-permute-start.10) | collective-permute-done | bytes 147488 | tf_op jit(solution)/shard_map/ppermute | solution.py:22
  84.0 0.6 collective-permute-done.12.a3
  84.6 7.2 %shard_map.96 = (bf16[64,1152]{1,0:T(8,128)(2,1)S(1)}, bf16[64,1152]{1,0:T(8,128)(2,1)S(1)}, bf16[64,1152]{1,0:T(8,128)(2,1)S(1)}, bf16[64,1152]{1,0:T(8,128)(2,1)S(1)}) custom-call(bf16[64,1152]{1,0:T(8,128)(2,1)S(1)} %get-tuple-element.44.a0, bf16[64,1152]{1,0:T(8,128)(2,1)S(1)} %collective-permute-done.10.a1, ...), custom_call_target="tpu_custom_call" | custom-call | tf_op jit(solution)/shard_map/pallas_call | solution.py:26
  91.8 2.1 %collective-permute-start.13 = (bf16[64,1152]{1,0:T(8,128)(2,1)S(1)}, bf16[64,1152]{1,0:T(8,128)(2,1)S(1)}, u32[]{:S(2)}, u32[]{:S(2)}) collective-permute-start(bf16[64,1152]{1,0:T(8,128)(2,1)S(1)} %get-tuple-element.49), channel_id=1, source_target_pairs={{0,6},{2,0},{4,2},{6,4},{1,7},{3,1},{5,3},{7,5},{8,14},{10,8},{12,... | collective-permute-start | bytes 442376 | tf_op jit(solution)/shard_map/ppermute | solution.py:22
  94.0 0.7 collective-permute-start.15
  94.7 3.0 %collective-permute-done.13.a1 = bf16[64,1152]{1,0:T(8,128)(2,1)S(1)} collective-permute-done((bf16[64,1152]{1,0:T(8,128)(2,1)S(1)}, bf16[64,1152]{1,0:T(8,128)(2,1)S(1)}, u32[]{:S(2)}, u32[]{:S(2)}) %collective-permute-start.13) | collective-permute-done | bytes 147488 | tf_op jit(solution)/shard_map/ppermute | solution.py:22
  97.6 1.9 %collective-permute-done.14.a2 = bf16[64,1152]{1,0:T(8,128)(2,1)S(1)} collective-permute-done((bf16[64,1152]{1,0:T(8,128)(2,1)S(1)}, bf16[64,1152]{1,0:T(8,128)(2,1)S(1)}, u32[]{:S(2)}, u32[]{:S(2)}) %collective-permute-start.14) | collective-permute-done | bytes 147488 | tf_op jit(solution)/shard_map/ppermute | solution.py:22
  99.6 1.2 collective-permute-done.15.a3
  100.8 2.9 %shard_map.97 = (f32[4,64,1152]{2,1,0:T(8,128)S(1)}, f32[64,1152]{1,0:T(8,128)S(1)}) custom-call(s32[6]{0:T(128)S(1)} %pad_add_fusion.where_ref, f32[3,4]{1,0:T(4,128)S(1)} %pad_maximum_fusion.2.coef_ref, bf16[64,1152]{1,0:T(8,128)(2,1)S(1)} %get-tuple-element.48.a0, bf16[64,1152]{1,0:T(8,128)(2,1)S(1)} %collective-permute-done.13.a1, ...), custom_call_target="tpu_custom_call" | custom-call | tf_op jit(solution)/shard_map/pallas_call | solution.py:26
  103.8 11.9 %all_to_all.21.held_ref = f32[16,4,1152]{2,1,0:T(4,128)S(1)} all-to-all(f32[16,4,1152]{2,1,0:T(4,128)S(1)} %reshape.28), channel_id=1, replica_groups=mesh['w'=2,'v'=2,'u'=2,'y'=4,'x'=4,'c'=2] {'v','u','y'}, dimensions={0} | all-to-all | bytes 589824 | tf_op jit(solution)/shard_map/all_to_all | solution.py:179
  115.6 1.7 %collective-permute-start.16 = (f32[4,1152]{1,0:T(4,128)S(1)}, f32[4,1152]{1,0:T(4,128)S(1)}, u32[]{:S(2)}, u32[]{:S(2)}) collective-permute-start(f32[4,1152]{1,0:T(4,128)S(1)} %get-tuple-element.56), channel_id=1, source_target_pairs={{0,224},{32,192},{64,160},{96,128},{128,96},{160,64},{192,32},{224... | collective-permute-start | bytes 55304 | tf_op jit(solution)/shard_map/ppermute | solution.py:187
  117.4 2.5 %collective-permute-done.16 = f32[4,1152]{1,0:T(4,128)S(1)} collective-permute-done((f32[4,1152]{1,0:T(4,128)S(1)}, f32[4,1152]{1,0:T(4,128)S(1)}, u32[]{:S(2)}, u32[]{:S(2)}) %collective-permute-start.16) | collective-permute-done | bytes 18464 | tf_op jit(solution)/shard_map/ppermute | solution.py:187
  119.9 12.9 %all_to_all.22 = f32[16,4,1152]{2,1,0:T(4,128)S(1)} all-to-all(f32[16,4,1152]{2,1,0:T(4,128)S(1)} %bitcast.34), channel_id=1, replica_groups=mesh['w'=2,'v'=2,'u'=2,'y'=4,'x'=4,'c'=2] {'v','u','y'}, dimensions={0} | all-to-all | bytes 589824 | tf_op jit(solution)/shard_map/all_to_all | solution.py:189
  132.8 0.1 reshape.29.lower_ref
  132.9 0.8 shard_map.99
  133.7 11.2 %collective-permute-start.17 = (f32[4,32,1152]{2,1,0:T(8,128)S(1)}, f32[4,32,1152]{2,1,0:T(8,128)S(1)}, u32[]{:S(2)}, u32[]{:S(2)}) collective-permute-start(f32[4,32,1152]{2,1,0:T(8,128)S(1)} %slice.9), channel_id=1, source_target_pairs={{0,1},{1,0},{2,3},{3,2},{4,5},{5,4},{6,7},{7,6},{8,9},{9,8},{10,11... | collective-permute-start | bytes 1769480 | tf_op jit(solution)/shard_map/ppermute | solution.py:22
  144.8 1.6 %collective-permute-done.17 = f32[4,32,1152]{2,1,0:T(8,128)S(1)} collective-permute-done((f32[4,32,1152]{2,1,0:T(8,128)S(1)}, f32[4,32,1152]{2,1,0:T(8,128)S(1)}, u32[]{:S(2)}, u32[]{:S(2)}) %collective-permute-start.17) | collective-permute-done | bytes 589856 | tf_op jit(solution)/shard_map/ppermute | solution.py:22
  146.7 1.1 copy.20
  (40 shorter events, 0.9 us)
Async XLA Ops:
  0.0 5.0 %copy-start = (s32[4,2]{0,1:T(2,128)S(1)}, s32[4,2]{0,1:T(2,128)}, u32[]{:S(2)}) copy-start(s32[4,2]{0,1:T(2,128)} %param.15) | copy-start | bytes 100
  0.0 4.7 %copy-start.1 = (bf16[4,2,32,1152]{3,2,1,0:T(8,128)(2,1)S(1)}, bf16[4,2,32,1152]{3,2,1,0:T(8,128)(2,1)}, u32[]{:S(2)}) copy-start(bf16[4,2,32,1152]{3,2,1,0:T(8,128)(2,1)} %param.10) | copy-start | bytes 1769476
  1.4 3.5 %copy-start.4 = (f32[4,3,1152]{2,0,1:T(4,128)S(1)}, f32[4,3,1152]{2,0,1:T(4,128)}, u32[]{:S(2)}) copy-start(f32[4,3,1152]{2,0,1:T(4,128)} %param.13) | copy-start | bytes 165892
  1.4 3.5 %copy-start.3 = (f32[8,3,1152]{2,0,1:T(8,128)S(1)}, f32[8,3,1152]{2,0,1:T(8,128)}, u32[]{:S(2)}) copy-start(f32[8,3,1152]{2,0,1:T(8,128)} %param.14) | copy-start | bytes 331780
  1.4 4.9 %collective-permute-start.1 = (f32[4,32,1152]{2,1,0:T(8,128)S(1)}, f32[4,32,1152]{2,1,0:T(8,128)S(1)}, u32[]{:S(2)}, u32[]{:S(2)}) collective-permute-start(f32[4,32,1152]{2,1,0:T(8,128)S(1)} %get-tuple-element.59), channel_id=1, source_target_pairs={{0,1},{1,0},{2,3},{3,2},{4,5},{5,4},{6,7},{7,6},{8,9},{9,8},{10,11... | collective-permute-start | bytes 1769480 | tf_op jit(solution)/shard_map/ppermute | solution.py:22
  4.8 23.8 %collective-permute-start.8 = (bf16[4,32,1152]{2,1,0:T(8,128)(2,1)S(1)}, bf16[4,32,1152]{2,1,0:T(8,128)(2,1)S(1)}, u32[]{:S(2)}, u32[]{:S(2)}) collective-permute-start(bf16[4,32,1152]{2,1,0:T(8,128)(2,1)S(1)} %get-tuple-element.61), channel_id=1, source_target_pairs={{0,1},{1,0},{2,3},{3,2},{4,5},{5,4},{6,7},{7,6},{8,9},{9,8},{10,11... | collective-permute-start | bytes 884744 | tf_op jit(solution)/shard_map/ppermute | solution.py:22
  7.4 7.0 %collective-permute-start.2 = (bf16[64,1152]{1,0:T(8,128)(2,1)S(1)}, bf16[64,1152]{1,0:T(8,128)(2,1)S(1)}, u32[]{:S(2)}, u32[]{:S(2)}) collective-permute-start(bf16[64,1152]{1,0:T(8,128)(2,1)S(1)} %get-tuple-element.32), channel_id=1, source_target_pairs={{0,2},{2,4},{4,6},{6,0},{1,3},{3,5},{5,7},{7,1},{8,10},{10,12},{12... | collective-permute-start | bytes 442376 | tf_op jit(solution)/shard_map/ppermute | solution.py:22
  7.5 8.7 %collective-permute-start.3 = (bf16[64,1152]{1,0:T(8,128)(2,1)S(1)}, bf16[64,1152]{1,0:T(8,128)(2,1)S(1)}, u32[]{:S(2)}, u32[]{:S(2)}) collective-permute-start(bf16[64,1152]{1,0:T(8,128)(2,1)S(1)} %get-tuple-element.33), channel_id=1, source_target_pairs={{0,4},{2,6},{4,0},{6,2},{1,5},{3,7},{5,1},{7,3},{8,12},{10,14},{12... | collective-permute-start | bytes 442376 | tf_op jit(solution)/shard_map/ppermute | solution.py:22
  9.4 7.8 %collective-permute-start.4 = (bf16[64,1152]{1,0:T(8,128)(2,1)S(1)}, bf16[64,1152]{1,0:T(8,128)(2,1)S(1)}, u32[]{:S(2)}, u32[]{:S(2)}) collective-permute-start(bf16[64,1152]{1,0:T(8,128)(2,1)S(1)} %get-tuple-element.34), channel_id=1, source_target_pairs={{0,6},{2,0},{4,2},{6,4},{1,7},{3,1},{5,3},{7,5},{8,14},{10,8},{12,... | collective-permute-start | bytes 442376 | tf_op jit(solution)/shard_map/ppermute | solution.py:22
  17.2 11.4 %copy-start.5 = (s32[4]{0:T(128)S(1)}, s32[4]{0:T(128)}, u32[]{:S(2)}) copy-start(s32[4]{0:T(128)} %param.12) | copy-start | bytes 52
  24.4 9.5 %collective-permute-start.5 = (bf16[64,1152]{1,0:T(8,128)(2,1)S(1)}, bf16[64,1152]{1,0:T(8,128)(2,1)S(1)}, u32[]{:S(2)}, u32[]{:S(2)}) collective-permute-start(bf16[64,1152]{1,0:T(8,128)(2,1)S(1)} %get-tuple-element.36), channel_id=1, source_target_pairs={{0,6},{2,0},{4,2},{6,4},{1,7},{3,1},{5,3},{7,5},{8,14},{10,8},{12,... | collective-permute-start | bytes 442376 | tf_op jit(solution)/shard_map/ppermute | solution.py:22
  27.9 6.2 %collective-permute-start.6 = (bf16[64,1152]{1,0:T(8,128)(2,1)S(1)}, bf16[64,1152]{1,0:T(8,128)(2,1)S(1)}, u32[]{:S(2)}, u32[]{:S(2)}) collective-permute-start(bf16[64,1152]{1,0:T(8,128)(2,1)S(1)} %get-tuple-element.37), channel_id=1, source_target_pairs={{0,4},{2,6},{4,0},{6,2},{1,5},{3,7},{5,1},{7,3},{8,12},{10,14},{12... | collective-permute-start | bytes 442376 | tf_op jit(solution)/shard_map/ppermute | solution.py:22
  27.9 9.8 %collective-permute-start.7 = (bf16[64,1152]{1,0:T(8,128)(2,1)S(1)}, bf16[64,1152]{1,0:T(8,128)(2,1)S(1)}, u32[]{:S(2)}, u32[]{:S(2)}) collective-permute-start(bf16[64,1152]{1,0:T(8,128)(2,1)S(1)} %get-tuple-element.38), channel_id=1, source_target_pairs={{0,2},{2,4},{4,6},{6,0},{1,3},{3,5},{5,7},{7,1},{8,10},{10,12},{12... | collective-permute-start | bytes 442376 | tf_op jit(solution)/shard_map/ppermute | solution.py:22
  56.5 10.1 %copy-start.2 = (f32[2,32,1152]{2,1,0:T(8,128)S(1)}, f32[2,32,1152]{2,1,0:T(8,128)}, u32[]{:S(2)}) copy-start(f32[2,32,1152]{2,1,0:T(8,128)} %param.11) | copy-start | bytes 884740
  56.6 4.4 %collective-permute-start.9 = (f32[4,1152]{1,0:T(4,128)S(1)}, f32[4,1152]{1,0:T(4,128)S(1)}, u32[]{:S(2)}, u32[]{:S(2)}) collective-permute-start(f32[4,1152]{1,0:T(4,128)S(1)} %get-tuple-element.43), channel_id=1, source_target_pairs={{0,224},{32,192},{64,160},{96,128},{128,96},{160,64},{192,32},{224... | collective-permute-start | bytes 55304 | tf_op jit(solution)/shard_map/ppermute | solution.py:187
  61.7 14.2 %all-to-all-start.1 = ((f32[16,4,1152]{2,1,0:T(4,128)}), f32[16,4,1152]{2,1,0:T(4,128)S(1)}, u32[]{:S(2)}, u32[]{:S(2)}) async-start(f32[16,4,1152]{2,1,0:T(4,128)} %bitcast.28), calls=%async_computation.1 | async-start | bytes 589824 | tf_op jit(solution)/shard_map/all_to_all | solution.py:189
  66.7 4.3 %collective-permute-start = (f32[32,1152]{1,0:T(8,128)S(1)}, f32[32,1152]{1,0:T(8,128)S(1)}, u32[]{:S(2)}, u32[]{:S(2)}) collective-permute-start(f32[32,1152]{1,0:T(8,128)S(1)} %get-tuple-element.64), channel_id=1, source_target_pairs={{0,1},{1,0},{2,3},{3,2},{4,5},{5,4},{6,7},{7,6},{8,9},{9,8},{10,11... | collective-permute-start | bytes 442376 | tf_op jit(solution)/shard_map/ppermute | solution.py:22
  77.1 6.9 %collective-permute-start.10 = (bf16[64,1152]{1,0:T(8,128)(2,1)S(1)}, bf16[64,1152]{1,0:T(8,128)(2,1)S(1)}, u32[]{:S(2)}, u32[]{:S(2)}) collective-permute-start(bf16[64,1152]{1,0:T(8,128)(2,1)S(1)} %get-tuple-element.45), channel_id=1, source_target_pairs={{0,2},{2,4},{4,6},{6,0},{1,3},{3,5},{5,7},{7,1},{8,10},{10,12},{12... | collective-permute-start | bytes 442376 | tf_op jit(solution)/shard_map/ppermute | solution.py:22
  77.2 6.8 %collective-permute-start.11 = (bf16[64,1152]{1,0:T(8,128)(2,1)S(1)}, bf16[64,1152]{1,0:T(8,128)(2,1)S(1)}, u32[]{:S(2)}, u32[]{:S(2)}) collective-permute-start(bf16[64,1152]{1,0:T(8,128)(2,1)S(1)} %get-tuple-element.46), channel_id=1, source_target_pairs={{0,4},{2,6},{4,0},{6,2},{1,5},{3,7},{5,1},{7,3},{8,12},{10,14},{12... | collective-permute-start | bytes 442376 | tf_op jit(solution)/shard_map/ppermute | solution.py:22
  77.8 6.8 %collective-permute-start.12 = (bf16[64,1152]{1,0:T(8,128)(2,1)S(1)}, bf16[64,1152]{1,0:T(8,128)(2,1)S(1)}, u32[]{:S(2)}, u32[]{:S(2)}) collective-permute-start(bf16[64,1152]{1,0:T(8,128)(2,1)S(1)} %get-tuple-element.47), channel_id=1, source_target_pairs={{0,6},{2,0},{4,2},{6,4},{1,7},{3,1},{5,3},{7,5},{8,14},{10,8},{12,... | collective-permute-start | bytes 442376 | tf_op jit(solution)/shard_map/ppermute | solution.py:22
  91.8 5.8 %collective-permute-start.13 = (bf16[64,1152]{1,0:T(8,128)(2,1)S(1)}, bf16[64,1152]{1,0:T(8,128)(2,1)S(1)}, u32[]{:S(2)}, u32[]{:S(2)}) collective-permute-start(bf16[64,1152]{1,0:T(8,128)(2,1)S(1)} %get-tuple-element.49), channel_id=1, source_target_pairs={{0,6},{2,0},{4,2},{6,4},{1,7},{3,1},{5,3},{7,5},{8,14},{10,8},{12,... | collective-permute-start | bytes 442376 | tf_op jit(solution)/shard_map/ppermute | solution.py:22
  94.0 5.6 %collective-permute-start.14 = (bf16[64,1152]{1,0:T(8,128)(2,1)S(1)}, bf16[64,1152]{1,0:T(8,128)(2,1)S(1)}, u32[]{:S(2)}, u32[]{:S(2)}) collective-permute-start(bf16[64,1152]{1,0:T(8,128)(2,1)S(1)} %get-tuple-element.50), channel_id=1, source_target_pairs={{0,4},{2,6},{4,0},{6,2},{1,5},{3,7},{5,1},{7,3},{8,12},{10,14},{12... | collective-permute-start | bytes 442376 | tf_op jit(solution)/shard_map/ppermute | solution.py:22
  94.0 6.8 %collective-permute-start.15 = (bf16[64,1152]{1,0:T(8,128)(2,1)S(1)}, bf16[64,1152]{1,0:T(8,128)(2,1)S(1)}, u32[]{:S(2)}, u32[]{:S(2)}) collective-permute-start(bf16[64,1152]{1,0:T(8,128)(2,1)S(1)} %get-tuple-element.51), channel_id=1, source_target_pairs={{0,2},{2,4},{4,6},{6,0},{1,3},{3,5},{5,7},{7,1},{8,10},{10,12},{12... | collective-permute-start | bytes 442376 | tf_op jit(solution)/shard_map/ppermute | solution.py:22
  115.6 4.2 %collective-permute-start.16 = (f32[4,1152]{1,0:T(4,128)S(1)}, f32[4,1152]{1,0:T(4,128)S(1)}, u32[]{:S(2)}, u32[]{:S(2)}) collective-permute-start(f32[4,1152]{1,0:T(4,128)S(1)} %get-tuple-element.56), channel_id=1, source_target_pairs={{0,224},{32,192},{64,160},{96,128},{128,96},{160,64},{192,32},{224... | collective-permute-start | bytes 55304 | tf_op jit(solution)/shard_map/ppermute | solution.py:187
  133.7 12.8 %collective-permute-start.17 = (f32[4,32,1152]{2,1,0:T(8,128)S(1)}, f32[4,32,1152]{2,1,0:T(8,128)S(1)}, u32[]{:S(2)}, u32[]{:S(2)}) collective-permute-start(f32[4,32,1152]{2,1,0:T(8,128)S(1)} %slice.9), channel_id=1, source_target_pairs={{0,1},{1,0},{2,3},{3,2},{4,5},{5,4},{6,7},{7,6},{8,9},{9,8},{10,11... | collective-permute-start | bytes 1769480 | tf_op jit(solution)/shard_map/ppermute | solution.py:22

commit v3 on v2

v3 whole, which is shorter than its diff:
```python
import jax
import jax.numpy as jnp
from jax import lax
from jax.experimental import pallas as pl
from jax.experimental.pallas import tpu as pltpu
from jax.sharding import Mesh
from jax.sharding import PartitionSpec as P

HEADS = 16
SWEEPS = 2
LANES = 128
BLOCKS = 4
LOG2E = 1.4426950408889634
HALF = ("v", "u", "y")
PLANES = ("w", "v", "u")
VMEM = pl.BlockSpec(memory_space=pltpu.VMEM)
SMEM = pl.BlockSpec(memory_space=pltpu.SMEM)


def shifted(value, axis, shift):
    size = lax.axis_size(axis)
    return lax.ppermute(value, axis, [(i, (i + shift) % size) for i in range(size)])


def call(body, outs, specs, *args, scratch=()):
    return pl.pallas_call(
        body,
        out_shape=outs,
        in_specs=specs,
        out_specs=jax.tree.map(lambda _: VMEM, outs),
        scratch_shapes=list(scratch),
        compiler_params=pltpu.CompilerParams(vmem_limit_bytes=16 * 2**20),
    )(*args)


def normed_rows(rows, shift, scale):
    center = jnp.mean(rows, axis=-1, keepdims=True)
    off = rows - center
    spread = jnp.mean(off * off, axis=-1, keepdims=True)
    normed = off / jnp.sqrt(spread + 1e-06)
    return (normed * (1.0 + scale) + shift).astype(jnp.bfloat16)


def modulation_row(where_ref, step_ref, view_ref, step, part):
    return step_ref[step, part : part + 1, :] + view_ref[where_ref[3 + step], part : part + 1, :]


def enter_body(where_ref, mine_ref, start_mine, peer_ref, step_ref, view_ref, x_ref, start_ref, *mod_refs):
    place = where_ref[0]
    start_ref[...] = jnp.concatenate([start_mine[...], peer_ref[mine_ref.shape[0]]], axis=0)
    steps = mine_ref.shape[0]
    for r in range(steps):
        step = lax.rem(place + r, steps)
        shift = modulation_row(where_ref, step_ref, view_ref, step, 0)
        scale = modulation_row(where_ref, step_ref, view_ref, step, 1)
        rows = jnp.concatenate([mine_ref[step], peer_ref[step]], axis=0)
        x_ref[step] = rows
        mod_refs[r][...] = normed_rows(rows, shift, scale)


def block_rows(flip, block, blocks, part):
    place = block + flip * (blocks - 1 - 2 * block)
    return pl.ds(pl.multiple_of(place * part, part), part)


def resume_body(
    where_ref, start_ref, mine_before, peer_before, lower_ref, step_ref, view_ref, x_ref, *rest
):
    mod_refs, base_ref = rest[:-1], rest[-1]
    place, flip = where_ref[0], where_ref[1]
    steps = mine_before.shape[0]
    part = lower_ref.shape[0] // BLOCKS
    for block in range(BLOCKS):
        base_ref[block * part : (block + 1) * part, :] = lower_ref[block_rows(flip, block, BLOCKS, part), :]
    for r in range(steps):
        step = lax.rem(place + r, steps)
        before = jnp.concatenate([mine_before[step], peer_before[step]], axis=0)
        rows = start_ref[...] + (base_ref[...] + before)
        x_ref[step] = rows
        shift = modulation_row(where_ref, step_ref, view_ref, step, 0)
        scale = modulation_row(where_ref, step_ref, view_ref, step, 1)
        mod_refs[r][...] = normed_rows(rows, shift, scale)


def finish_body(where_ref, start_ref, mine_before, peer_before, mine_lower, peer_lower, out_ref):
    flip, core = where_ref[1], where_ref[2]
    blocks = BLOCKS // 2
    part = mine_lower.shape[0] // blocks
    for view, before_ref, lower_ref in ((core, mine_before, mine_lower), (1 - core, peer_before, peer_lower)):
        for block in range(blocks):
            rows = slice(block * part, (block + 1) * part)
            base = lower_ref[block_rows(flip, block, blocks, part), :]
            for step in range(before_ref.shape[0]):
                out_ref[step, view, rows, :] = start_ref[view, rows, :] + (base + before_ref[step, rows, :])


def project_rows(rows, w_ref):
    return jnp.dot(rows, w_ref[...], preferred_element_type=jnp.float32).astype(jnp.bfloat16)


def first_body(a0, w_ref, qkv_ref):
    qkv_ref[...] = project_rows(a0[...], w_ref)


def attend(q_ref, kv_ref, mask_ref, outs):
    width = mask_ref.shape[1]
    part = outs[0].shape[0]
    size = width // HEADS
    tiles = [None] * (width // LANES)
    for h in range(HEADS):
        first = h * size // LANES
        last = ((h + 1) * size - 1) // LANES
        low, high = first * LANES, (last + 1) * LANES
        q = q_ref[:, low:high] * mask_ref[h : h + 1, low:high]
        k = kv_ref[:, width + low : width + high]
        v = kv_ref[:, 2 * width + low : 2 * width + high]
        scores = lax.dot_general(q, k, (((1,), (1,)), ((), ())), preferred_element_type=jnp.float32)
        top = jnp.max(scores, axis=-1, keepdims=True)
        powers = jnp.exp2((scores - top) * (LOG2E / size**0.5))
        share = 1.0 / jnp.sum(powers, axis=-1, keepdims=True)
        out = jnp.dot(powers.astype(jnp.bfloat16), v, preferred_element_type=jnp.float32) * share
        for t in range(first, last + 1):
            piece = out[:, t * LANES - low : (t + 1) * LANES - low]
            if tiles[t] is not None:
                lane = lax.broadcasted_iota(jnp.int32, piece.shape, 1) + t * LANES
                piece = jnp.where(lane >= h * size, piece, tiles[t])
            tiles[t] = piece
    for t, tile in enumerate(tiles):
        tile = tile.astype(jnp.bfloat16)
        for r, out in enumerate(outs):
            out[:, t * LANES : (t + 1) * LANES] = tile[r * part : (r + 1) * part]


def others_body(first_ref, a1, a2, a3, w_ref, mask_ref, o1, o2, o3, qkv_ref, rows_ref):
    part = a1.shape[0]
    for r, piece in enumerate((a1, a2, a3)):
        rows_ref[r * part : (r + 1) * part, :] = piece[...]
    qkv_ref[: 3 * part, :] = project_rows(rows_ref[...], w_ref)
    qkv_ref[3 * part :, :] = first_ref[...]
    attend(qkv_ref.at[: 3 * part], qkv_ref, mask_ref, (o1, o2, o3))


def own_body(first_ref, qkv_ref, mask_ref, o0):
    attend(first_ref, qkv_ref, mask_ref, (o0,))


def base_body(coef_ref, x_ref, mine_ref, peer_ref, base_ref):
    for step in range(x_ref.shape[0]):
        rows = x_ref[step]
        drawn = jnp.concatenate([mine_ref[step], peer_ref[step]], axis=0).astype(jnp.float32)
        base_ref[step] = (coef_ref[0, step] + coef_ref[1, step]) * rows + coef_ref[2, step] * drawn


def project_body(
    where_ref,
    coef_ref,
    a0,
    a1,
    a2,
    a3,
    w_ref,
    base_ref,
    step_ref,
    view_ref,
    mine_before,
    peer_before,
    total_ref,
    rows_ref,
    proj_ref,
):
    place, flip = where_ref[0], where_ref[1]
    pieces = (a0, a1, a2, a3)
    part = a0.shape[0]
    half = part // 2
    steps = len(pieces)
    for r in range(steps):
        rows = pl.ds(pl.multiple_of(lax.rem(place + r, steps) * part, part), part)
        rows_ref[rows, :] = pieces[r][...]
    proj_ref[...] = jnp.dot(rows_ref[...], w_ref[...], preferred_element_type=jnp.float32)
    running = jnp.zeros((part, proj_ref.shape[1]), jnp.float32)
    for step in range(steps):
        gate = modulation_row(where_ref, step_ref, view_ref, step, 2) * coef_ref[1, step]
        mine_before[step] = running[:half]
        peer_before[step] = running[half:]
        running = running + (base_ref[step] + gate * proj_ref[step * part : (step + 1) * part, :])
    share = part // BLOCKS
    for block in range(BLOCKS):
        total_ref[block_rows(flip, block, BLOCKS, share), :] = running[block * share : (block + 1) * share]


def coefficients(steps_index):
    unit = steps_index.astype(jnp.float32) / 1000.0
    beta = 0.1 + 19.9 * unit
    sigma = jnp.sqrt(1.0 - jnp.exp(-(0.1 * unit + 9.95 * unit * unit)))
    coef_state = 0.5 * beta * 0.004
    coef_eps = beta * 0.004 / sigma
    coef_noise = jnp.sqrt(beta * 0.004)
    return (coef_state, coef_eps, coef_noise)


def inside_body(held_ref, before_ref, all_ref):
    running = jnp.zeros(held_ref.shape[1:], held_ref.dtype)
    for q in range(held_ref.shape[0]):
        before_ref[q] = running
        running = running + held_ref[q]
    all_ref[...] = running


def earlier_sum(total, beside=None):
    places = lax.axis_size(HALF)
    rows, width = total.shape
    shares = total.reshape(places, rows // places, width)
    held = lax.all_to_all(shares, HALF, 0, 0, tiled=True)
    before, whole = call(
        inside_body,
        [jax.ShapeDtypeStruct(shares.shape, total.dtype), jax.ShapeDtypeStruct(shares.shape[1:], total.dtype)],
        [VMEM],
        held,
    )
    planes = lax.axis_size(PLANES)
    below = lax.ppermute(whole, PLANES, [(i, planes - 1 - i) for i in range(planes)])
    if beside is not None:
        below, beside = lax.optimization_barrier((below, shifted(beside, "c", 1)))
    below = jnp.where(lax.axis_index("w") == 1, below, jnp.zeros_like(below))
    lower = lax.all_to_all(before + below[None], HALF, 0, 0, tiled=True)
    return lower, beside


def per_device(states, noise, x_start, timesteps, step_mod, view_mod, view_ids, w_qkv, w_out):
    steps, views, part, width = states.shape
    place, flip, core = (lax.axis_index(a) for a in ("x", "w", "c"))
    other = 1 - core
    f32, bf16 = jnp.float32, jnp.bfloat16
    rows = 2 * part

    def own(a, axis):
        return lax.dynamic_index_in_dim(a, core, axis, keepdims=False)

    def given(a, axis):
        return lax.dynamic_index_in_dim(a, other, axis, keepdims=False)

    def shape(*dims, kind=f32):
        return jax.ShapeDtypeStruct(dims, kind)

    swapped = shifted(jnp.concatenate([given(states, 1), given(x_start, 0)[None]], axis=0), "c", 1)
    states_mine, start_mine = own(states, 1), own(x_start, 0)
    noise_mine, noise_peer = own(noise, 1), shifted(given(noise, 1), "c", 1)
    where = jnp.concatenate([jnp.stack([place, flip, core]).astype(jnp.int32), own(view_ids, 1)])
    coefs = jnp.stack(coefficients(timesteps))
    size = width // HEADS
    column = jnp.arange(width, dtype=jnp.int32)[None, :]
    head = jnp.arange(HEADS, dtype=jnp.int32)[:, None]
    mask = ((column >= head * size) & (column < (head + 1) * size)).astype(bf16)

    x_shape = shape(steps, rows, width)
    half = shape(steps, part, width)
    piece = shape(rows, width, kind=bf16)
    x, start, *mods = call(
        enter_body,
        [x_shape, shape(rows, width)] + [piece] * steps,
        [SMEM] + [VMEM] * 5,
        where,
        states_mine,
        start_mine,
        swapped,
        step_mod,
        view_mod,
    )
    for sweep in range(SWEEPS):
        arrived = [shifted(mods[r], "x", r) for r in range(1, steps)]
        first = call(first_body, shape(rows, 3 * width, kind=bf16), [VMEM] * 2, mods[0], w_qkv)
        *attended, qkv = call(
            others_body,
            [piece] * (steps - 1) + [shape(steps * rows, 3 * width, kind=bf16)],
            [VMEM] * 6,
            first,
            *arrived,
            w_qkv,
            mask,
            scratch=[pltpu.VMEM(((steps - 1) * rows, width), bf16)],
        )
        back = [shifted(attended[r - 1], "x", -r) for r in range(1, steps)]
        kept = call(own_body, piece, [VMEM] * 3, first, qkv, mask)
        base = call(base_body, x_shape, [SMEM] + [VMEM] * 3, coefs, x, noise_mine, noise_peer)
        mine_before, peer_before, total = call(
            project_body,
            [half, half, shape(rows, width)],
            [SMEM] * 2 + [VMEM] * 8,
            where,
            coefs,
            kept,
            *back,
            w_out,
            base,
            step_mod,
            view_mod,
            scratch=[pltpu.VMEM((steps * rows, width), bf16), pltpu.VMEM((steps * rows, width), f32)],
        )
        if sweep + 1 == SWEEPS:
            break
        lower, _ = earlier_sum(total)
        x, *mods = call(
            resume_body,
            [x_shape] + [piece] * steps,
            [SMEM] + [VMEM] * 6,
            where,
            start,
            mine_before,
            peer_before,
            lower.reshape(rows, width),
            step_mod,
            view_mod,
            scratch=[pltpu.VMEM((rows, width), f32)],
        )
    lower, peer_before = earlier_sum(total, peer_before)
    places = lower.shape[0] // 2
    lower_mine = lax.dynamic_slice_in_dim(lower, flip * places, places)
    lower_peer = shifted(lax.dynamic_slice_in_dim(lower, (1 - flip) * places, places), "c", 1)
    return call(
        finish_body,
        shape(*states.shape),
        [SMEM] + [VMEM] * 5,
        where,
        x_start,
        mine_before,
        peer_before,
        lower_mine.reshape(part, width),
        lower_peer.reshape(part, width),
    )


def solution(mesh):
    finer = Mesh(mesh.devices.reshape(2, 2, 2, 4, 4, 2), ("w", "v", "u", "y", "x", "c"))
    tm, tok = ("w", "v", "u", "y"), ("x", "c")
    placed = (
        P(tm, None, tok, None),
        P(tm, None, tok, None),
        P(None, tok, None),
        P(tm),
        P(tm, None, None),
        P(),
        P(tm, None),
        P(),
        P(),
    )
    return jax.shard_map(
        per_device, mesh=finer, in_specs=placed, out_specs=P(tm, None, tok, None), check_vma=False
    )
```

time: 148 us -> 157 us (1.061)
  local copies, waits for them, and re-layouts: 3.08 us -> 22.3 us
  waiting for transfers between devices: 39 us -> 21.9 us
  Pallas kernels: 23.2 us -> 28.1 us
  blocking collectives: 40.5 us -> 43.2 us
  starting transfers between devices: 40.6 us -> 38 us
    ppermute x16, waiting for transfers between devices: 30.4 us -> 10.2 us  [shifted(): lax.ppermute(value, axis, [(i, (i + shift) % size) for i in range(size)])]
    unnamed x16 -> x50, local copies, waits for them, and re-layouts: 0.1 us -> 16 us
    pallas_call x9 -> x15, Pallas kernels: 23.2 us -> 28.1 us  [call(): pl.pallas_call(body, out_shape=outs, in_specs=specs, out_specs=jax.tree.m...]
    all_to_all x1, waiting for transfers between devices: 4.9 us -> 9.19 us  [earlier_sum(): lower = lax.all_to_all(before + below[None], HALF, 0, 0, tiled=True)]
    ppermute x16, starting transfers between devices: 30.7 us -> 27.6 us  [shifted(): lax.ppermute(value, axis, [(i, (i + shift) % size) for i in range(size)])]
    reshape x2, local copies, waits for them, and re-layouts: 0.17 us -> 2.83 us  [earlier_sum(): shares = total.reshape(places, rows // places, width)]
    reshape x2 -> x3, local copies, waits for them, and re-layouts: 0.2 us -> 1.91 us  [the longest x1 1.8 us: per_device(): lower.reshape(rows, width)]
  transfers between devices with their start and end apart: 19 -> 19, of which waited for: 17 -> 12; matrix products, arithmetic and copies ran while one was open for 0% -> 1% of each run, Pallas kernels for 6% -> 10%
where the time goes in v3:
time: 157 us; the launch traced here: 156 us
  blocking collectives  43.2 us (28%)
  starting transfers between devices  38 us (24%)
  Pallas kernels  28.1 us (18%)
  local copies, waits for them, and re-layouts  22.3 us (14%)
  waiting for transfers between devices  21.9 us (14%)
  other arithmetic  1.98 us (1%)
    all_to_all x2, blocking collectives, earlier_sum(): held = lax.all_to_all(shares, HALF, 0, 0, tiled=True)  29.1 us
    pallas_call x15, Pallas kernels, call(): pl.pallas_call(body, out_shape=outs, in_specs=specs, out_specs=jax.tree.m...  28.1 us
    ppermute x16, starting transfers between devices, shifted(): lax.ppermute(value, axis, [(i, (i + shift) % size) for i in range(size)])  27.6 us
    unnamed x50, local copies, waits for them, and re-layouts  16 us
    all_to_all x1, blocking collectives, earlier_sum(): lower = lax.all_to_all(before + below[None], HALF, 0, 0, tiled=True)  14.1 us
    ppermute x16, waiting for transfers between devices, shifted(): lax.ppermute(value, axis, [(i, (i + shift) % size) for i in range(size)])  10.2 us
    all_to_all x1, waiting for transfers between devices, earlier_sum(): lower = lax.all_to_all(before + below[None], HALF, 0, 0, tiled=True)  9.19 us
    ppermute x2, starting transfers between devices, earlier_sum(): lax.ppermute(whole, PLANES, [(i, planes - 1 - i) for i in range(planes)])  5.81 us
  transfers between devices with their start and end apart: 19, of which 12 were waited for; matrix products, arithmetic and copies ran while one was open for 1% of the time, Pallas kernels for 10%

profile of v3, /device:TPU:1, one launch (start us, length us, event | category | flops | bytes accessed | tf_op | source)
XLA Modules:
  0.0 155.8 jit_solution(7730036324701998753)
XLA Ops:
  0.0 1.4 dynamic-slice_bitcast_fusion
  1.5 3.3 %collective-permute-start = (f32[5,32,1152]{2,1,0:T(8,128)S(1)}, f32[5,32,1152]{2,1,0:T(8,128)S(1)}, u32[]{:S(2)}, u32[]{:S(2)}) collective-permute-start(f32[5,32,1152]{2,1,0:T(8,128)S(1)} %pad_maximum_fusion), channel_id=1, source_target_pairs={{0,1},{1,0},{2,3},{3,2},{4,5},{5,4},{6,7},{7,6},{8,9},{9,8},{10,11... | collective-permute-start | bytes 2211848 | tf_op jit(solution)/shard_map/ppermute | solution.py:22
  4.9 0.9 collective-permute-start.7
  6.6 1.0 shard_map.91
  8.4 2.0 %collective-permute-start.2 = (bf16[64,1152]{1,0:T(8,128)(2,1)S(1)}, bf16[64,1152]{1,0:T(8,128)(2,1)S(1)}, u32[]{:S(2)}, u32[]{:S(2)}) collective-permute-start(bf16[64,1152]{1,0:T(8,128)(2,1)S(1)} %get-tuple-element.39), channel_id=1, source_target_pairs={{0,4},{2,6},{4,0},{6,2},{1,5},{3,7},{5,1},{7,3},{8,12},{10,14},{12... | collective-permute-start | bytes 442376 | tf_op jit(solution)/shard_map/ppermute | solution.py:22
  10.4 1.2 collective-permute-start.3
  11.6 3.3 %copy-done.1 = bf16[1152,3456]{1,0:T(8,128)(2,1)S(1)} copy-done((bf16[1152,3456]{1,0:T(8,128)(2,1)S(1)}, bf16[1152,3456]{1,0:T(8,128)(2,1)}, u32[]{:S(2)}) %copy-start.1) | copy-done | bytes 7962648
  14.9 1.3 shard_map.92.first_ref
  16.2 0.9 collective-permute-done.2.a2
  17.1 1.0 collective-permute-done.3.a3
  18.1 4.8 %shard_map.93 = (bf16[64,1152]{1,0:T(8,128)(2,1)S(1)}, bf16[64,1152]{1,0:T(8,128)(2,1)S(1)}, bf16[64,1152]{1,0:T(8,128)(2,1)S(1)}, bf16[256,3456]{1,0:T(8,128)(2,1)S(1)}) custom-call(bf16[64,3456]{1,0:T(8,128)(2,1)S(1)} %shard_map.92.first_ref, bf16[64,1152]{1,0:T(8,128)(2,1)S(1)} %collective-permute-done.1.a1, ...), custom_call_target="tpu_custom_call" | custom-call | tf_op jit(solution)/shard_map/pallas_call | solution.py:26
  22.9 3.4 %collective-permute-start.4 = (bf16[64,1152]{1,0:T(8,128)(2,1)S(1)}, bf16[64,1152]{1,0:T(8,128)(2,1)S(1)}, u32[]{:S(2)}, u32[]{:S(2)}) collective-permute-start(bf16[64,1152]{1,0:T(8,128)(2,1)S(1)} %get-tuple-element.42), channel_id=1, source_target_pairs={{0,6},{2,0},{4,2},{6,4},{1,7},{3,1},{5,3},{7,5},{8,14},{10,8},{12,... | collective-permute-start | bytes 442376 | tf_op jit(solution)/shard_map/ppermute | solution.py:22
  27.9 3.2 %shard_map.94.a0 = bf16[64,1152]{1,0:T(8,128)(2,1)S(1)} custom-call(bf16[64,3456]{1,0:T(8,128)(2,1)S(1)} %shard_map.92.first_ref, bf16[256,3456]{1,0:T(8,128)(2,1)S(1)} %get-tuple-element.41.qkv_ref, bf16[16,1152]{1,0:T(8,128)(2,1)S(1)} %fusion.1.mask_ref), custom_call_target="tpu_custom_call" | custom-call | tf_op jit(solution)/shard_map/pallas_call | solution.py:26
  31.0 1.3 collective-permute-done.4.a1
  32.6 3.6 %collective-permute-done.6.a3 = bf16[64,1152]{1,0:T(8,128)(2,1)S(1)} collective-permute-done((bf16[64,1152]{1,0:T(8,128)(2,1)S(1)}, bf16[64,1152]{1,0:T(8,128)(2,1)S(1)}, u32[]{:S(2)}, u32[]{:S(2)}) %collective-permute-start.6) | collective-permute-done | bytes 147488 | tf_op jit(solution)/shard_map/ppermute | solution.py:22
  36.2 1.7 %shard_map.96 = (f32[4,32,1152]{2,1,0:T(8,128)S(1)}, f32[4,32,1152]{2,1,0:T(8,128)S(1)}, f32[64,1152]{1,0:T(8,128)S(1)}) custom-call(s32[7]{0:T(128)S(1)} %pad_add_fusion.where_ref, f32[3,4]{1,0:T(4,128)S(1)} %pad_maximum_fusion.1.coef_ref, bf16[64,1152]{1,0:T(8,128)(2,1)S(1)} %shard_map.94.a0, bf16[64,1152]{1,0:T(8,128)(2,1)S(1)} %collective-permute-done.4.a1, ...), custom_call_target="tpu_custom_call" | custom-call | tf_op jit(solution)/shard_map/pallas_call | solution.py:26
  40.3 1.8 %reshape.29 = f32[16,4,1152]{2,1,0:T(4,128)} reshape(f32[64,1152]{1,0:T(8,128)} %copy-done.16) | data formatting | bytes 589824 | tf_op jit(solution)/shard_map/reshape | solution.py:212
  42.0 15.7 %all_to_all.20.held_ref = f32[16,4,1152]{2,1,0:T(4,128)S(1)} all-to-all(f32[16,4,1152]{2,1,0:T(4,128)} %reshape.29), channel_id=1, replica_groups=mesh['w'=2,'v'=2,'u'=2,'y'=4,'x'=4,'c'=2] {'v','u','y'}, dimensions={0} | all-to-all | bytes 589824 | tf_op jit(solution)/shard_map/all_to_all | solution.py:213
  58.5 3.3 %collective-permute-start.8 = (f32[4,1152]{1,0:T(4,128)S(1)}, f32[4,1152]{1,0:T(4,128)S(1)}, u32[]{:S(2)}, u32[]{:S(2)}) collective-permute-start(f32[4,1152]{1,0:T(4,128)S(1)} %get-tuple-element.50), channel_id=1, source_target_pairs={{0,224},{32,192},{64,160},{96,128},{128,96},{160,64},{192,32},{224... | collective-permute-start | bytes 55304 | tf_op jit(solution)/shard_map/ppermute | solution.py:221
  61.8 1.1 collective-permute-done.8
  62.9 1.0 broadcast_add_fusion.1
  63.9 14.1 %all_to_all.21 = f32[16,4,1152]{2,1,0:T(4,128)} all-to-all(f32[16,4,1152]{2,1,0:T(4,128)S(1)} %bitcast.29), channel_id=1, replica_groups=mesh['w'=2,'v'=2,'u'=2,'y'=4,'x'=4,'c'=2] {'v','u','y'}, dimensions={0} | all-to-all | bytes 589824 | tf_op jit(solution)/shard_map/all_to_all | solution.py:225
  78.0 1.8 %reshape.30.lower_ref = f32[64,1152]{1,0:T(8,128)} reshape(f32[16,4,1152]{2,1,0:T(4,128)} %all_to_all.21) | data formatting | bytes 589824 | tf_op jit(solution)/shard_map/reshape | solution.py:310
  79.8 1.0 copy-done.7
  80.8 1.1 copy-done.11
  81.9 1.1 copy-done.13
  82.9 1.0 copy-done.18
  83.9 1.1 shard_map.98
  85.0 1.0 collective-permute-start.10
  86.0 1.5 collective-permute-start.9
  87.5 3.3 %copy-done.3 = bf16[1152,3456]{1,0:T(8,128)(2,1)S(1)} copy-done((bf16[1152,3456]{1,0:T(8,128)(2,1)S(1)}, bf16[1152,3456]{1,0:T(8,128)(2,1)}, u32[]{:S(2)}) %copy-start.3) | copy-done | bytes 7962648
  90.8 1.3 shard_map.99.first_ref
  92.2 4.8 %shard_map.100 = (bf16[64,1152]{1,0:T(8,128)(2,1)S(1)}, bf16[64,1152]{1,0:T(8,128)(2,1)S(1)}, bf16[64,1152]{1,0:T(8,128)(2,1)S(1)}, bf16[256,3456]{1,0:T(8,128)(2,1)S(1)}) custom-call(bf16[64,3456]{1,0:T(8,128)(2,1)S(1)} %shard_map.99.first_ref, bf16[64,1152]{1,0:T(8,128)(2,1)S(1)} %collective-permute-done.9.a1, ...), custom_call_target="tpu_custom_call" | custom-call | tf_op jit(solution)/shard_map/pallas_call | solution.py:26
  96.9 1.5 collective-permute-start.12
  98.4 0.9 collective-permute-start.13
  100.9 3.2 %shard_map.101.a0 = bf16[64,1152]{1,0:T(8,128)(2,1)S(1)} custom-call(bf16[64,3456]{1,0:T(8,128)(2,1)S(1)} %shard_map.99.first_ref, bf16[256,3456]{1,0:T(8,128)(2,1)S(1)} %get-tuple-element.55.qkv_ref, bf16[16,1152]{1,0:T(8,128)(2,1)S(1)} %fusion.1.mask_ref), custom_call_target="tpu_custom_call" | custom-call | tf_op jit(solution)/shard_map/pallas_call | solution.py:26
  104.1 1.4 collective-permute-done.14.a3
  105.5 2.5 %shard_map.103 = (f32[4,32,1152]{2,1,0:T(8,128)S(1)}, f32[4,32,1152]{2,1,0:T(8,128)}, f32[64,1152]{1,0:T(8,128)S(1)}) custom-call(s32[7]{0:T(128)S(1)} %pad_add_fusion.where_ref, f32[3,4]{1,0:T(4,128)S(1)} %pad_maximum_fusion.1.coef_ref, bf16[64,1152]{1,0:T(8,128)(2,1)S(1)} %shard_map.101.a0, bf16[64,1152]{1,0:T(8,128)(2,1)S(1)} %collective-permute-done.12.a1, ...), custom_call_target="tpu_custom_call" | custom-call | tf_op jit(solution)/shard_map/pallas_call | solution.py:26
  109.5 6.3 %collective-permute-start.16 = (f32[4,32,1152]{2,1,0:T(8,128)}, f32[4,32,1152]{2,1,0:T(8,128)S(1)}, u32[]{:S(2)}, u32[]{:S(2)}) collective-permute-start(f32[4,32,1152]{2,1,0:T(8,128)} %get-tuple-element.63), channel_id=1, source_target_pairs={{0,1},{1,0},{2,3},{3,2},{4,5},{5,4},{6,7},{7,6},{8,9},{9,8},{10,11... | collective-permute-start | bytes 1769480 | tf_op jit(solution)/shard_map/ppermute | solution.py:22
  115.8 1.0 reshape.31
  116.9 13.4 %all_to_all.22.held_ref = f32[16,4,1152]{2,1,0:T(4,128)S(1)} all-to-all(f32[16,4,1152]{2,1,0:T(4,128)S(1)} %reshape.31), channel_id=1, replica_groups=mesh['w'=2,'v'=2,'u'=2,'y'=4,'x'=4,'c'=2] {'v','u','y'}, dimensions={0} | all-to-all | bytes 589824 | tf_op jit(solution)/shard_map/all_to_all | solution.py:213
  130.3 2.5 %collective-permute-start.15 = (f32[4,1152]{1,0:T(4,128)S(1)}, f32[4,1152]{1,0:T(4,128)S(1)}, u32[]{:S(2)}, u32[]{:S(2)}) collective-permute-start(f32[4,1152]{1,0:T(4,128)S(1)} %get-tuple-element.62), channel_id=1, source_target_pairs={{0,224},{32,192},{64,160},{96,128},{128,96},{160,64},{192,32},{224... | collective-permute-start | bytes 55304 | tf_op jit(solution)/shard_map/ppermute | solution.py:221
  132.8 1.4 collective-permute-done.15
  135.0 4.6 %all-to-all-start.3 = ((f32[16,4,1152]{2,1,0:T(4,128)}), f32[16,4,1152]{2,1,0:T(4,128)S(1)}, u32[]{:S(2)}, u32[]{:S(2)}) async-start(f32[16,4,1152]{2,1,0:T(4,128)} %bitcast.26), calls=%async_computation.3 | async-start | bytes 589824 | tf_op jit(solution)/shard_map/all_to_all | solution.py:225
  139.6 9.2 %all-to-all-done.3 = f32[16,4,1152]{2,1,0:T(4,128)S(1)} async-done(((f32[16,4,1152]{2,1,0:T(4,128)}), f32[16,4,1152]{2,1,0:T(4,128)S(1)}, u32[]{:S(2)}, u32[]{:S(2)}) %all-to-all-start.3) | async-done | bytes 294944 | tf_op jit(solution)/shard_map/all_to_all | solution.py:225
  148.8 4.2 %collective-permute-start.17 = (f32[8,4,1152]{2,1,0:T(4,128)S(1)}, f32[8,4,1152]{2,1,0:T(4,128)S(1)}, u32[]{:S(2)}, u32[]{:S(2)}) collective-permute-start(f32[8,4,1152]{2,1,0:T(4,128)S(1)} %get-tuple-element.71), channel_id=1, source_target_pairs={{0,1},{1,0},{2,3},{3,2},{4,5},{5,4},{6,7},{7,6},{8,9},{9,8},{10,11... | collective-permute-start | bytes 442376 | tf_op jit(solution)/shard_map/ppermute | solution.py:22
  153.0 1.0 collective-permute-done.17
  154.0 1.7 %shard_map.105 = f32[4,2,32,1152]{3,2,1,0:T(8,128)} custom-call(s32[7]{0:T(128)S(1)} %pad_add_fusion.where_ref, f32[2,32,1152]{2,1,0:T(8,128)S(1)} %copy-done.6, f32[4,32,1152]{2,1,0:T(8,128)S(1)} %copy-done.9, f32[4,32,1152]{2,1,0:T(8,128)S(1)} %collective-permute-done.16.peer_before, f32[32,1152]{1,0:T(8,128)S(1)} %reshape.32.mine_lower, ...), custom_call_target="tpu_custom_call" | custom-call | tf_op jit(solution)/shard_map/pallas_call | solution.py:26
  (78 shorter events, 10.6 us)
Async XLA Ops:
  0.0 5.9 %copy-start = (s32[4,2]{0,1:T(2,128)S(1)}, s32[4,2]{0,1:T(2,128)}, u32[]{:S(2)}) copy-start(s32[4,2]{0,1:T(2,128)} %param.15) | copy-start | bytes 100
  0.0 1.4 copy-start.5
  1.4 3.4 %copy-start.19 = (bf16[4,2,32,1152]{3,2,1,0:T(8,128)(2,1)S(1)}, bf16[4,2,32,1152]{3,2,1,0:T(8,128)(2,1)}, u32[]{:S(2)}) copy-start(bf16[4,2,32,1152]{3,2,1,0:T(8,128)(2,1)} %param.10) | copy-start | bytes 1769476
  1.4 4.4 %copy-start.20 = (f32[8,3,1152]{2,0,1:T(8,128)S(1)}, f32[8,3,1152]{2,0,1:T(8,128)}, u32[]{:S(2)}) copy-start(f32[8,3,1152]{2,0,1:T(8,128)} %param.14) | copy-start | bytes 331780
  1.4 4.4 %copy-start.21 = (f32[4,3,1152]{2,0,1:T(4,128)S(1)}, f32[4,3,1152]{2,0,1:T(4,128)}, u32[]{:S(2)}) copy-start(f32[4,3,1152]{2,0,1:T(4,128)} %param.13) | copy-start | bytes 165892
  1.5 5.1 %collective-permute-start = (f32[5,32,1152]{2,1,0:T(8,128)S(1)}, f32[5,32,1152]{2,1,0:T(8,128)S(1)}, u32[]{:S(2)}, u32[]{:S(2)}) collective-permute-start(f32[5,32,1152]{2,1,0:T(8,128)S(1)} %pad_maximum_fusion), channel_id=1, source_target_pairs={{0,1},{1,0},{2,3},{3,2},{4,5},{5,4},{6,7},{7,6},{8,9},{9,8},{10,11... | collective-permute-start | bytes 2211848 | tf_op jit(solution)/shard_map/ppermute | solution.py:22
  4.9 22.2 %collective-permute-start.7 = (bf16[4,32,1152]{2,1,0:T(8,128)(2,1)S(1)}, bf16[4,32,1152]{2,1,0:T(8,128)(2,1)S(1)}, u32[]{:S(2)}, u32[]{:S(2)}) collective-permute-start(bf16[4,32,1152]{2,1,0:T(8,128)(2,1)S(1)} %get-tuple-element.69), channel_id=1, source_target_pairs={{0,1},{1,0},{2,3},{3,2},{4,5},{5,4},{6,7},{7,6},{8,9},{9,8},{10,11... | collective-permute-start | bytes 884744 | tf_op jit(solution)/shard_map/ppermute | solution.py:22
  7.7 0.7 copy-start.17
  8.4 7.8 %collective-permute-start.1 = (bf16[64,1152]{1,0:T(8,128)(2,1)S(1)}, bf16[64,1152]{1,0:T(8,128)(2,1)S(1)}, u32[]{:S(2)}, u32[]{:S(2)}) collective-permute-start(bf16[64,1152]{1,0:T(8,128)(2,1)S(1)} %get-tuple-element.38), channel_id=1, source_target_pairs={{0,2},{2,4},{4,6},{6,0},{1,3},{3,5},{5,7},{7,1},{8,10},{10,12},{12... | collective-permute-start | bytes 442376 | tf_op jit(solution)/shard_map/ppermute | solution.py:22
  8.4 8.7 %collective-permute-start.2 = (bf16[64,1152]{1,0:T(8,128)(2,1)S(1)}, bf16[64,1152]{1,0:T(8,128)(2,1)S(1)}, u32[]{:S(2)}, u32[]{:S(2)}) collective-permute-start(bf16[64,1152]{1,0:T(8,128)(2,1)S(1)} %get-tuple-element.39), channel_id=1, source_target_pairs={{0,4},{2,6},{4,0},{6,2},{1,5},{3,7},{5,1},{7,3},{8,12},{10,14},{12... | collective-permute-start | bytes 442376 | tf_op jit(solution)/shard_map/ppermute | solution.py:22
  10.4 7.8 %collective-permute-start.3 = (bf16[64,1152]{1,0:T(8,128)(2,1)S(1)}, bf16[64,1152]{1,0:T(8,128)(2,1)S(1)}, u32[]{:S(2)}, u32[]{:S(2)}) collective-permute-start(bf16[64,1152]{1,0:T(8,128)(2,1)S(1)} %get-tuple-element.40), channel_id=1, source_target_pairs={{0,6},{2,0},{4,2},{6,4},{1,7},{3,1},{5,3},{7,5},{8,14},{10,8},{12,... | collective-permute-start | bytes 442376 | tf_op jit(solution)/shard_map/ppermute | solution.py:22
  11.6 3.3 %copy-start.1 = (bf16[1152,3456]{1,0:T(8,128)(2,1)S(1)}, bf16[1152,3456]{1,0:T(8,128)(2,1)}, u32[]{:S(2)}) copy-start(bf16[1152,3456]{1,0:T(8,128)(2,1)} %w_ref.10) | copy-start | bytes 23887876
  14.9 3.3 %copy-start.2 = (bf16[1152,3456]{1,0:T(8,128)(2,1)S(1)}, bf16[1152,3456]{1,0:T(8,128)(2,1)}, u32[]{:S(2)}) copy-start(bf16[1152,3456]{1,0:T(8,128)(2,1)} %w_ref.10) | copy-start | bytes 23887876
  16.2 10.8 %copy-start.22 = (s32[4]{0:T(128)S(1)}, s32[4]{0:T(128)}, u32[]{:S(2)}) copy-start(s32[4]{0:T(128)} %param.12) | copy-start | bytes 52
  22.9 9.5 %collective-permute-start.4 = (bf16[64,1152]{1,0:T(8,128)(2,1)S(1)}, bf16[64,1152]{1,0:T(8,128)(2,1)S(1)}, u32[]{:S(2)}, u32[]{:S(2)}) collective-permute-start(bf16[64,1152]{1,0:T(8,128)(2,1)S(1)} %get-tuple-element.42), channel_id=1, source_target_pairs={{0,6},{2,0},{4,2},{6,4},{1,7},{3,1},{5,3},{7,5},{8,14},{10,8},{12,... | collective-permute-start | bytes 442376 | tf_op jit(solution)/shard_map/ppermute | solution.py:22
  26.4 6.2 %collective-permute-start.5 = (bf16[64,1152]{1,0:T(8,128)(2,1)S(1)}, bf16[64,1152]{1,0:T(8,128)(2,1)S(1)}, u32[]{:S(2)}, u32[]{:S(2)}) collective-permute-start(bf16[64,1152]{1,0:T(8,128)(2,1)S(1)} %get-tuple-element.43), channel_id=1, source_target_pairs={{0,4},{2,6},{4,0},{6,2},{1,5},{3,7},{5,1},{7,3},{8,12},{10,14},{12... | collective-permute-start | bytes 442376 | tf_op jit(solution)/shard_map/ppermute | solution.py:22
  26.4 9.8 %collective-permute-start.6 = (bf16[64,1152]{1,0:T(8,128)(2,1)S(1)}, bf16[64,1152]{1,0:T(8,128)(2,1)S(1)}, u32[]{:S(2)}, u32[]{:S(2)}) collective-permute-start(bf16[64,1152]{1,0:T(8,128)(2,1)S(1)} %get-tuple-element.44), channel_id=1, source_target_pairs={{0,2},{2,4},{4,6},{6,0},{1,3},{3,5},{5,7},{7,1},{8,10},{10,12},{12... | collective-permute-start | bytes 442376 | tf_op jit(solution)/shard_map/ppermute | solution.py:22
  27.1 9.1 %copy-start.4 = (bf16[1152,1152]{1,0:T(8,128)(2,1)S(1)}, bf16[1152,1152]{1,0:T(8,128)(2,1)}, u32[]{:S(2)}) copy-start(bf16[1152,1152]{1,0:T(8,128)(2,1)} %w_ref.11) | copy-start | bytes 7962628
  37.9 0.8 copy-start.10
  38.7 0.8 copy-start.12
  39.5 0.7 copy-start.16
  57.8 0.7 copy-start.14
  58.5 4.4 %collective-permute-start.8 = (f32[4,1152]{1,0:T(4,128)S(1)}, f32[4,1152]{1,0:T(4,128)S(1)}, u32[]{:S(2)}, u32[]{:S(2)}) collective-permute-start(f32[4,1152]{1,0:T(4,128)S(1)} %get-tuple-element.50), channel_id=1, source_target_pairs={{0,224},{32,192},{64,160},{96,128},{128,96},{160,64},{192,32},{224... | collective-permute-start | bytes 55304 | tf_op jit(solution)/shard_map/ppermute | solution.py:221
  79.8 1.0 copy-start.7
  80.8 1.1 copy-start.11
  81.9 1.1 copy-start.13
  82.9 1.0 copy-start.18
  85.0 7.1 %collective-permute-start.10 = (bf16[64,1152]{1,0:T(8,128)(2,1)S(1)}, bf16[64,1152]{1,0:T(8,128)(2,1)S(1)}, u32[]{:S(2)}, u32[]{:S(2)}) collective-permute-start(bf16[64,1152]{1,0:T(8,128)(2,1)S(1)} %get-tuple-element.53), channel_id=1, source_target_pairs={{0,4},{2,6},{4,0},{6,2},{1,5},{3,7},{5,1},{7,3},{8,12},{10,14},{12... | collective-permute-start | bytes 442376 | tf_op jit(solution)/shard_map/ppermute | solution.py:22
  86.0 6.1 %collective-permute-start.11 = (bf16[64,1152]{1,0:T(8,128)(2,1)S(1)}, bf16[64,1152]{1,0:T(8,128)(2,1)S(1)}, u32[]{:S(2)}, u32[]{:S(2)}) collective-permute-start(bf16[64,1152]{1,0:T(8,128)(2,1)S(1)} %get-tuple-element.54), channel_id=1, source_target_pairs={{0,6},{2,0},{4,2},{6,4},{1,7},{3,1},{5,3},{7,5},{8,14},{10,8},{12,... | collective-permute-start | bytes 442376 | tf_op jit(solution)/shard_map/ppermute | solution.py:22
  86.0 6.1 %collective-permute-start.9 = (bf16[64,1152]{1,0:T(8,128)(2,1)S(1)}, bf16[64,1152]{1,0:T(8,128)(2,1)S(1)}, u32[]{:S(2)}, u32[]{:S(2)}) collective-permute-start(bf16[64,1152]{1,0:T(8,128)(2,1)S(1)} %get-tuple-element.52), channel_id=1, source_target_pairs={{0,2},{2,4},{4,6},{6,0},{1,3},{3,5},{5,7},{7,1},{8,10},{10,12},{12... | collective-permute-start | bytes 442376 | tf_op jit(solution)/shard_map/ppermute | solution.py:22
  87.5 3.3 %copy-start.3 = (bf16[1152,3456]{1,0:T(8,128)(2,1)S(1)}, bf16[1152,3456]{1,0:T(8,128)(2,1)}, u32[]{:S(2)}) copy-start(bf16[1152,3456]{1,0:T(8,128)(2,1)} %w_ref.10) | copy-start | bytes 23887876
  96.9 7.1 %collective-permute-start.12 = (bf16[64,1152]{1,0:T(8,128)(2,1)S(1)}, bf16[64,1152]{1,0:T(8,128)(2,1)S(1)}, u32[]{:S(2)}, u32[]{:S(2)}) collective-permute-start(bf16[64,1152]{1,0:T(8,128)(2,1)S(1)} %get-tuple-element.56), channel_id=1, source_target_pairs={{0,6},{2,0},{4,2},{6,4},{1,7},{3,1},{5,3},{7,5},{8,14},{10,8},{12,... | collective-permute-start | bytes 442376 | tf_op jit(solution)/shard_map/ppermute | solution.py:22
  98.4 5.6 %collective-permute-start.13 = (bf16[64,1152]{1,0:T(8,128)(2,1)S(1)}, bf16[64,1152]{1,0:T(8,128)(2,1)S(1)}, u32[]{:S(2)}, u32[]{:S(2)}) collective-permute-start(bf16[64,1152]{1,0:T(8,128)(2,1)S(1)} %get-tuple-element.57), channel_id=1, source_target_pairs={{0,4},{2,6},{4,0},{6,2},{1,5},{3,7},{5,1},{7,3},{8,12},{10,14},{12... | collective-permute-start | bytes 442376 | tf_op jit(solution)/shard_map/ppermute | solution.py:22
  99.3 6.2 %collective-permute-start.14 = (bf16[64,1152]{1,0:T(8,128)(2,1)S(1)}, bf16[64,1152]{1,0:T(8,128)(2,1)S(1)}, u32[]{:S(2)}, u32[]{:S(2)}) collective-permute-start(bf16[64,1152]{1,0:T(8,128)(2,1)S(1)} %get-tuple-element.58), channel_id=1, source_target_pairs={{0,2},{2,4},{4,6},{6,0},{1,3},{3,5},{5,7},{7,1},{8,10},{10,12},{12... | collective-permute-start | bytes 442376 | tf_op jit(solution)/shard_map/ppermute | solution.py:22
  108.0 0.8 copy-start.8
  108.8 0.7 copy-start.15
  109.5 24.7 %collective-permute-start.16 = (f32[4,32,1152]{2,1,0:T(8,128)}, f32[4,32,1152]{2,1,0:T(8,128)S(1)}, u32[]{:S(2)}, u32[]{:S(2)}) collective-permute-start(f32[4,32,1152]{2,1,0:T(8,128)} %get-tuple-element.63), channel_id=1, source_target_pairs={{0,1},{1,0},{2,3},{3,2},{4,5},{5,4},{6,7},{7,6},{8,9},{9,8},{10,11... | collective-permute-start | bytes 1769480 | tf_op jit(solution)/shard_map/ppermute | solution.py:22
  130.3 3.9 %collective-permute-start.15 = (f32[4,1152]{1,0:T(4,128)S(1)}, f32[4,1152]{1,0:T(4,128)S(1)}, u32[]{:S(2)}, u32[]{:S(2)}) collective-permute-start(f32[4,1152]{1,0:T(4,128)S(1)} %get-tuple-element.62), channel_id=1, source_target_pairs={{0,224},{32,192},{64,160},{96,128},{128,96},{160,64},{192,32},{224... | collective-permute-start | bytes 55304 | tf_op jit(solution)/shard_map/ppermute | solution.py:221
  134.2 19.8 %copy-start.6 = (f32[2,32,1152]{2,1,0:T(8,128)S(1)}, f32[2,32,1152]{2,1,0:T(8,128)}, u32[]{:S(2)}) copy-start(f32[2,32,1152]{2,1,0:T(8,128)} %start_ref.1) | copy-start | bytes 884740
  134.2 19.8 %copy-start.9 = (f32[4,32,1152]{2,1,0:T(8,128)S(1)}, f32[4,32,1152]{2,1,0:T(8,128)}, u32[]{:S(2)}) copy-start(f32[4,32,1152]{2,1,0:T(8,128)} %copy-done.8) | copy-start | bytes 1769476
  135.0 13.8 %all-to-all-start.3 = ((f32[16,4,1152]{2,1,0:T(4,128)}), f32[16,4,1152]{2,1,0:T(4,128)S(1)}, u32[]{:S(2)}, u32[]{:S(2)}) async-start(f32[16,4,1152]{2,1,0:T(4,128)} %bitcast.26), calls=%async_computation.3 | async-start | bytes 589824 | tf_op jit(solution)/shard_map/all_to_all | solution.py:225
  148.8 5.2 %collective-permute-start.17 = (f32[8,4,1152]{2,1,0:T(4,128)S(1)}, f32[8,4,1152]{2,1,0:T(4,128)S(1)}, u32[]{:S(2)}, u32[]{:S(2)}) collective-permute-start(f32[8,4,1152]{2,1,0:T(4,128)S(1)} %get-tuple-element.71), channel_id=1, source_target_pairs={{0,1},{1,0},{2,3},{3,2},{4,5},{5,4},{6,7},{7,6},{8,9},{9,8},{10,11... | collective-permute-start | bytes 442376 | tf_op jit(solution)/shard_map/ppermute | solution.py:22

commit v4 on v3

--- a/solution.py
+++ b/solution.py
@@ -9,7 +9,7 @@
 HEADS = 16
 SWEEPS = 2
 LANES = 128
-BLOCKS = 4
+PLANE_GROUPS = 4
 LOG2E = 1.4426950408889634
 HALF = ("v", "u", "y")
 PLANES = ("w", "v", "u")
@@ -58,9 +58,10 @@
         mod_refs[r][...] = normed_rows(rows, shift, scale)
 
 
-def block_rows(flip, block, blocks, part):
-    place = block + flip * (blocks - 1 - 2 * block)
-    return pl.ds(pl.multiple_of(place * part, part), part)
+def share_place(flip, q, places):
+    inner = places // PLANE_GROUPS
+    block = q // inner
+    return (block + flip * (PLANE_GROUPS - 1 - 2 * block)) * inner + q % inner
 
 
 def resume_body(
@@ -69,9 +70,9 @@
     mod_refs, base_ref = rest[:-1], rest[-1]
     place, flip = where_ref[0], where_ref[1]
     steps = mine_before.shape[0]
-    part = lower_ref.shape[0] // BLOCKS
-    for block in range(BLOCKS):
-        base_ref[block * part : (block + 1) * part, :] = lower_ref[block_rows(flip, block, BLOCKS, part), :]
+    places, share, _ = lower_ref.shape
+    for q in range(places):
+        base_ref[q * share : (q + 1) * share, :] = lower_ref[share_place(flip, q, places)]
     for r in range(steps):
         step = lax.rem(place + r, steps)
         before = jnp.concatenate([mine_before[step], peer_before[step]], axis=0)
@@ -82,16 +83,16 @@
         mod_refs[r][...] = normed_rows(rows, shift, scale)
 
 
-def finish_body(where_ref, start_ref, mine_before, peer_before, mine_lower, peer_lower, out_ref):
+def finish_body(where_ref, start_ref, mine_before, peer_before, mine_lower, peer_lower, out_ref, base_ref):
     flip, core = where_ref[1], where_ref[2]
-    blocks = BLOCKS // 2
-    part = mine_lower.shape[0] // blocks
-    for view, before_ref, lower_ref in ((core, mine_before, mine_lower), (1 - core, peer_before, peer_lower)):
-        for block in range(blocks):
-            rows = slice(block * part, (block + 1) * part)
-            base = lower_ref[block_rows(flip, block, blocks, part), :]
-            for step in range(before_ref.shape[0]):
-                out_ref[step, view, rows, :] = start_ref[view, rows, :] + (base + before_ref[step, rows, :])
+    places, share, _ = mine_lower.shape
+    half = places // 2
+    sides = ((core, 0, mine_before, mine_lower), (1 - core, half, peer_before, peer_lower))
+    for view, low, before_ref, lower_ref in sides:
+        for q in range(half):
+            base_ref[q * share : (q + 1) * share, :] = lower_ref[share_place(flip, low + q, places)]
+        for step in range(before_ref.shape[0]):
+            out_ref[step, view] = start_ref[view] + (base_ref[...] + before_ref[step])
 
 
 def project_rows(rows, w_ref):
@@ -183,9 +184,9 @@
         mine_before[step] = running[:half]
         peer_before[step] = running[half:]
         running = running + (base_ref[step] + gate * proj_ref[step * part : (step + 1) * part, :])
-    share = part // BLOCKS
-    for block in range(BLOCKS):
-        total_ref[block_rows(flip, block, BLOCKS, share), :] = running[block * share : (block + 1) * share]
+    places, share, _ = total_ref.shape
+    for q in range(places):
+        total_ref[share_place(flip, q, places)] = running[q * share : (q + 1) * share]
 
 
 def coefficients(steps_index):
@@ -206,24 +207,22 @@
     all_ref[...] = running
 
 
-def earlier_sum(total, beside=None):
-    places = lax.axis_size(HALF)
-    rows, width = total.shape
-    shares = total.reshape(places, rows // places, width)
+def below_body(where_ref, before_ref, below_ref, out_ref):
+    below = jnp.where(where_ref[1] == 1, below_ref[...], 0.0)
+    for q in range(before_ref.shape[0]):
+        out_ref[q] = before_ref[q] + below
+
+
+def earlier_sum(where, shares, beside=None):
     held = lax.all_to_all(shares, HALF, 0, 0, tiled=True)
-    before, whole = call(
-        inside_body,
-        [jax.ShapeDtypeStruct(shares.shape, total.dtype), jax.ShapeDtypeStruct(shares.shape[1:], total.dtype)],
-        [VMEM],
-        held,
-    )
+    whole = jax.ShapeDtypeStruct(shares.shape, shares.dtype)
+    before, total = call(inside_body, [whole, jax.ShapeDtypeStruct(shares.shape[1:], shares.dtype)], [VMEM], held)
     planes = lax.axis_size(PLANES)
-    below = lax.ppermute(whole, PLANES, [(i, planes - 1 - i) for i in range(planes)])
+    below = lax.ppermute(total, PLANES, [(i, planes - 1 - i) for i in range(planes)])
     if beside is not None:
         below, beside = lax.optimization_barrier((below, shifted(beside, "c", 1)))
-    below = jnp.where(lax.axis_index("w") == 1, below, jnp.zeros_like(below))
-    lower = lax.all_to_all(before + below[None], HALF, 0, 0, tiled=True)
-    return lower, beside
+    sums = call(below_body, whole, [SMEM] + [VMEM] * 2, where, before, below)
+    return lax.all_to_all(sums, HALF, 0, 0, tiled=True), beside
 
 
 def per_device(states, noise, x_start, timesteps, step_mod, view_mod, view_ids, w_qkv, w_out):
@@ -254,6 +253,7 @@
 
     x_shape = shape(steps, rows, width)
     half = shape(steps, part, width)
+    places = lax.axis_size(HALF)
     piece = shape(rows, width, kind=bf16)
     x, start, *mods = call(
         enter_body,
@@ -284,7 +284,7 @@
         base = call(base_body, x_shape, [SMEM] + [VMEM] * 3, coefs, x, noise_mine, noise_peer)
         mine_before, peer_before, total = call(
             project_body,
-            [half, half, shape(rows, width)],
+            [half, half, shape(places, rows // places, width)],
             [SMEM] * 2 + [VMEM] * 8,
             where,
             coefs,
@@ -298,7 +298,7 @@
         )
         if sweep + 1 == SWEEPS:
             break
-        lower, _ = earlier_sum(total)
+        lower, _ = earlier_sum(where, total)
         x, *mods = call(
             resume_body,
             [x_shape] + [piece] * steps,
@@ -307,15 +307,12 @@
             start,
             mine_before,
             peer_before,
-            lower.reshape(rows, width),
+            lower,
             step_mod,
             view_mod,
             scratch=[pltpu.VMEM((rows, width), f32)],
         )
-    lower, peer_before = earlier_sum(total, peer_before)
-    places = lower.shape[0] // 2
-    lower_mine = lax.dynamic_slice_in_dim(lower, flip * places, places)
-    lower_peer = shifted(lax.dynamic_slice_in_dim(lower, (1 - flip) * places, places), "c", 1)
+    lower, peer_before = earlier_sum(where, total, peer_before)
     return call(
         finish_body,
         shape(*states.shape),
@@ -324,8 +321,9 @@
         x_start,
         mine_before,
         peer_before,
-        lower_mine.reshape(part, width),
-        lower_peer.reshape(part, width),
+        lower,
+        shifted(lower, "c", 1),
+        scratch=[pltpu.VMEM((part, width), f32)],
     )
 
 

time: 157 us -> 141 us (0.90)
  local copies, waits for them, and re-layouts: 22.3 us -> 5.63 us
  blocking collectives: 43.2 us -> 57.2 us
  starting transfers between devices: 38 us -> 32 us
  waiting for transfers between devices: 21.9 us -> 16.5 us
  other arithmetic: 1.98 us -> 0.24 us
    all_to_all x1 -> x2, blocking collectives: 14.1 us -> 27.6 us  [earlier_sum(): return (lax.all_to_all(sums, HALF, 0, 0, tiled=True), beside)]
    unnamed x50 -> x18, local copies, waits for them, and re-layouts: 16 us -> 4.17 us
    all_to_all x1 -> x0, waiting for transfers between devices: 9.19 us -> none  [earlier_sum(): lower = lax.all_to_all(before + below[None], HALF, 0, 0, tiled=True)]
    reshape x5 -> x0, local copies, waits for them, and re-layouts: 4.73 us -> none  [the longest x2 2.83 us: earlier_sum(): shares = total.reshape(places, rows // places, width)]
    all_to_all x1 -> x0, starting transfers between devices: 4.58 us -> none  [earlier_sum(): lower = lax.all_to_all(before + below[None], HALF, 0, 0, tiled=True)]
    ppermute x16, waiting for transfers between devices: 10.2 us -> 14 us  [shifted(): lax.ppermute(value, axis, [(i, (i + shift) % size) for i in range(size)])]
    add x2 -> x0, other arithmetic: 1.73 us -> none  [earlier_sum(): lower = lax.all_to_all(before + below[None], HALF, 0, 0, tiled=True)]
    pallas_call x15 -> x17, Pallas kernels: 28.1 us -> 28.8 us  [call(): pl.pallas_call(body, out_shape=outs, in_specs=specs, out_specs=jax.tree.m...]
  transfers between devices with their start and end apart: 19 -> 18, of which waited for: 12 -> 12; matrix products, arithmetic and copies ran while one was open for 1% -> 1% of each run, Pallas kernels for 10% -> 12%
where the time goes in v4:
time: 141 us
  blocking collectives  57.2 us (41%)
  starting transfers between devices  32 us (23%)
  Pallas kernels  28.8 us (20%)
  waiting for transfers between devices  16.5 us (12%)
  local copies, waits for them, and re-layouts  5.63 us (4%)
    all_to_all x2, blocking collectives, earlier_sum(): held = lax.all_to_all(shares, HALF, 0, 0, tiled=True)  29.5 us
    pallas_call x17, Pallas kernels, call(): pl.pallas_call(body, out_shape=outs, in_specs=specs, out_specs=jax.tree.m...  28.8 us
    all_to_all x2, blocking collectives, earlier_sum(): return (lax.all_to_all(sums, HALF, 0, 0, tiled=True), beside)  27.6 us
    ppermute x16, starting transfers between devices, shifted(): lax.ppermute(value, axis, [(i, (i + shift) % size) for i in range(size)])  26.3 us
    ppermute x16, waiting for transfers between devices, shifted(): lax.ppermute(value, axis, [(i, (i + shift) % size) for i in range(size)])  14 us
    ppermute x2, starting transfers between devices, earlier_sum(): lax.ppermute(total, PLANES, [(i, planes - 1 - i) for i in range(planes)])  5.66 us
    unnamed x18, local copies, waits for them, and re-layouts  4.17 us
  transfers between devices with their start and end apart: 18, of which 12 were waited for; matrix products, arithmetic and copies ran while one was open for 1% of the time, Pallas kernels for 12%

profile of v4, /device:TPU:1, one launch (start us, length us, event | category | flops | bytes accessed | tf_op | source)
XLA Modules:
  0.0 140.6 jit_solution(15571868119032659873)
XLA Ops:
  0.0 1.4 dynamic-slice_bitcast_fusion
  1.5 3.3 %collective-permute-start = (f32[5,32,1152]{2,1,0:T(8,128)S(1)}, f32[5,32,1152]{2,1,0:T(8,128)S(1)}, u32[]{:S(2)}, u32[]{:S(2)}) collective-permute-start(f32[5,32,1152]{2,1,0:T(8,128)S(1)} %pad_maximum_fusion), channel_id=1, source_target_pairs={{0,1},{1,0},{2,3},{3,2},{4,5},{5,4},{6,7},{7,6},{8,9},{9,8},{10,11... | collective-permute-start | bytes 2211848 | tf_op jit(solution)/shard_map/ppermute | solution.py:22
  4.9 0.9 collective-permute-start.7
  5.8 0.8 copy.10.step_ref
  6.8 1.0 shard_map.91
  7.9 1.9 %collective-permute-start.2 = (bf16[64,1152]{1,0:T(8,128)(2,1)S(1)}, bf16[64,1152]{1,0:T(8,128)(2,1)S(1)}, u32[]{:S(2)}, u32[]{:S(2)}) collective-permute-start(bf16[64,1152]{1,0:T(8,128)(2,1)S(1)} %get-tuple-element.39), channel_id=1, source_target_pairs={{0,4},{2,6},{4,0},{6,2},{1,5},{3,7},{5,1},{7,3},{8,12},{10,14},{12... | collective-permute-start | bytes 442376 | tf_op jit(solution)/shard_map/ppermute | solution.py:22
  9.9 1.2 collective-permute-start.3
  11.1 3.3 %copy-done.1 = bf16[1152,3456]{1,0:T(8,128)(2,1)S(1)} copy-done((bf16[1152,3456]{1,0:T(8,128)(2,1)S(1)}, bf16[1152,3456]{1,0:T(8,128)(2,1)}, u32[]{:S(2)}) %copy-start.1) | copy-done | bytes 7962648
  14.4 1.4 shard_map.92.first_ref
  15.8 1.0 collective-permute-done.2.a2
  16.8 1.0 collective-permute-done.3.a3
  17.8 4.8 %shard_map.93 = (bf16[64,1152]{1,0:T(8,128)(2,1)S(1)}, bf16[64,1152]{1,0:T(8,128)(2,1)S(1)}, bf16[64,1152]{1,0:T(8,128)(2,1)S(1)}, bf16[256,3456]{1,0:T(8,128)(2,1)S(1)}) custom-call(bf16[64,3456]{1,0:T(8,128)(2,1)S(1)} %shard_map.92.first_ref, bf16[64,1152]{1,0:T(8,128)(2,1)S(1)} %collective-permute-done.1.a1, ...), custom_call_target="tpu_custom_call" | custom-call | tf_op jit(solution)/shard_map/pallas_call | solution.py:26
  22.6 3.3 %collective-permute-start.4 = (bf16[64,1152]{1,0:T(8,128)(2,1)S(1)}, bf16[64,1152]{1,0:T(8,128)(2,1)S(1)}, u32[]{:S(2)}, u32[]{:S(2)}) collective-permute-start(bf16[64,1152]{1,0:T(8,128)(2,1)S(1)} %get-tuple-element.42), channel_id=1, source_target_pairs={{0,6},{2,0},{4,2},{6,4},{1,7},{3,1},{5,3},{7,5},{8,14},{10,8},{12,... | collective-permute-start | bytes 442376 | tf_op jit(solution)/shard_map/ppermute | solution.py:22
  25.9 0.7 collective-permute-start.6
  26.7 0.8 shard_map.95.base_ref
  27.4 3.2 %shard_map.94.a0 = bf16[64,1152]{1,0:T(8,128)(2,1)S(1)} custom-call(bf16[64,3456]{1,0:T(8,128)(2,1)S(1)} %shard_map.92.first_ref, bf16[256,3456]{1,0:T(8,128)(2,1)S(1)} %get-tuple-element.41.qkv_ref, bf16[16,1152]{1,0:T(8,128)(2,1)S(1)} %fusion.1.mask_ref), custom_call_target="tpu_custom_call" | custom-call | tf_op jit(solution)/shard_map/pallas_call | solution.py:26
  30.6 1.3 collective-permute-done.4.a1
  32.2 3.6 %collective-permute-done.6.a3 = bf16[64,1152]{1,0:T(8,128)(2,1)S(1)} collective-permute-done((bf16[64,1152]{1,0:T(8,128)(2,1)S(1)}, bf16[64,1152]{1,0:T(8,128)(2,1)S(1)}, u32[]{:S(2)}, u32[]{:S(2)}) %collective-permute-start.6) | collective-permute-done | bytes 147488 | tf_op jit(solution)/shard_map/ppermute | solution.py:22
  35.8 1.7 %shard_map.96 = (f32[4,32,1152]{2,1,0:T(8,128)S(1)}, f32[4,32,1152]{2,1,0:T(8,128)S(1)}, f32[16,4,1152]{2,1,0:T(4,128)S(1)}) custom-call(s32[7]{0:T(128)S(1)} %pad_add_fusion.where_ref, f32[3,4]{1,0:T(4,128)S(1)} %pad_maximum_fusion.1.coef_ref, bf16[64,1152]{1,0:T(8,128)(2,1)S(1)} %shard_map.94.a0, bf16[64,1152]{1,0:T(8,128)(2,1)S(1)} %collective-permute-done.4.a1, ...), custom_call_target="tpu_custom_call" | custom-call | tf_op jit(solution)/shard_map/pallas_call | solution.py:26
  37.5 16.2 %all_to_all.20.held_ref = f32[16,4,1152]{2,1,0:T(4,128)S(1)} all-to-all(f32[16,4,1152]{2,1,0:T(4,128)S(1)} %get-tuple-element.48), channel_id=1, replica_groups=mesh['w'=2,'v'=2,'u'=2,'y'=4,'x'=4,'c'=2] {'v','u','y'}, dimensions={0} | all-to-all | bytes 589824 | tf_op jit(solution)/shard_map/all_to_all | solution.py:217
  53.7 3.1 %collective-permute-start.8 = (f32[4,1152]{1,0:T(4,128)S(1)}, f32[4,1152]{1,0:T(4,128)S(1)}, u32[]{:S(2)}, u32[]{:S(2)}) collective-permute-start(f32[4,1152]{1,0:T(4,128)S(1)} %get-tuple-element.50), channel_id=1, source_target_pairs={{0,224},{32,192},{64,160},{96,128},{128,96},{160,64},{192,32},{224... | collective-permute-start | bytes 55304 | tf_op jit(solution)/shard_map/ppermute | solution.py:221
  56.8 1.2 collective-permute-done.8.below_ref
  57.9 0.6 shard_map.98
  58.5 14.0 %all_to_all.21.lower_ref = f32[16,4,1152]{2,1,0:T(4,128)S(1)} all-to-all(f32[16,4,1152]{2,1,0:T(4,128)S(1)} %shard_map.98), channel_id=1, replica_groups=mesh['w'=2,'v'=2,'u'=2,'y'=4,'x'=4,'c'=2] {'v','u','y'}, dimensions={0} | all-to-all | bytes 589824 | tf_op jit(solution)/shard_map/all_to_all | solution.py:225
  72.5 1.1 shard_map.99
  73.7 0.7 collective-permute-start.10
  74.4 1.5 %collective-permute-start.9 = (bf16[64,1152]{1,0:T(8,128)(2,1)S(1)}, bf16[64,1152]{1,0:T(8,128)(2,1)S(1)}, u32[]{:S(2)}, u32[]{:S(2)}) collective-permute-start(bf16[64,1152]{1,0:T(8,128)(2,1)S(1)} %get-tuple-element.52), channel_id=1, source_target_pairs={{0,2},{2,4},{4,6},{6,0},{1,3},{3,5},{5,7},{7,1},{8,10},{10,12},{12... | collective-permute-start | bytes 442376 | tf_op jit(solution)/shard_map/ppermute | solution.py:22
  75.8 1.4 shard_map.100.first_ref
  77.2 2.1 %collective-permute-done.10.a2 = bf16[64,1152]{1,0:T(8,128)(2,1)S(1)} collective-permute-done((bf16[64,1152]{1,0:T(8,128)(2,1)S(1)}, bf16[64,1152]{1,0:T(8,128)(2,1)S(1)}, u32[]{:S(2)}, u32[]{:S(2)}) %collective-permute-start.10) | collective-permute-done | bytes 147488 | tf_op jit(solution)/shard_map/ppermute | solution.py:22
  79.4 1.5 %collective-permute-done.9.a1 = bf16[64,1152]{1,0:T(8,128)(2,1)S(1)} collective-permute-done((bf16[64,1152]{1,0:T(8,128)(2,1)S(1)}, bf16[64,1152]{1,0:T(8,128)(2,1)S(1)}, u32[]{:S(2)}, u32[]{:S(2)}) %collective-permute-start.9) | collective-permute-done | bytes 147488 | tf_op jit(solution)/shard_map/ppermute | solution.py:22
  80.8 4.8 %shard_map.101 = (bf16[64,1152]{1,0:T(8,128)(2,1)S(1)}, bf16[64,1152]{1,0:T(8,128)(2,1)S(1)}, bf16[64,1152]{1,0:T(8,128)(2,1)S(1)}, bf16[256,3456]{1,0:T(8,128)(2,1)S(1)}) custom-call(bf16[64,3456]{1,0:T(8,128)(2,1)S(1)} %shard_map.100.first_ref, bf16[64,1152]{1,0:T(8,128)(2,1)S(1)} %collective-permute-done.9.a1, ...), custom_call_target="tpu_custom_call" | custom-call | tf_op jit(solution)/shard_map/pallas_call | solution.py:26
  85.7 0.4 collective-permute-start.12
  86.0 0.6 collective-permute-start.13
  86.7 0.6 collective-permute-start.14
  87.2 0.7 shard_map.103.base_ref
  88.0 3.2 %shard_map.102.a0 = bf16[64,1152]{1,0:T(8,128)(2,1)S(1)} custom-call(bf16[64,3456]{1,0:T(8,128)(2,1)S(1)} %shard_map.100.first_ref, bf16[256,3456]{1,0:T(8,128)(2,1)S(1)} %get-tuple-element.55.qkv_ref, bf16[16,1152]{1,0:T(8,128)(2,1)S(1)} %fusion.1.mask_ref), custom_call_target="tpu_custom_call" | custom-call | tf_op jit(solution)/shard_map/pallas_call | solution.py:26
  91.2 0.5 collective-permute-done.13.a2
  91.7 1.5 %collective-permute-done.14.a3 = bf16[64,1152]{1,0:T(8,128)(2,1)S(1)} collective-permute-done((bf16[64,1152]{1,0:T(8,128)(2,1)S(1)}, bf16[64,1152]{1,0:T(8,128)(2,1)S(1)}, u32[]{:S(2)}, u32[]{:S(2)}) %collective-permute-start.14) | collective-permute-done | bytes 147488 | tf_op jit(solution)/shard_map/ppermute | solution.py:22
  93.1 1.7 %shard_map.104 = (f32[4,32,1152]{2,1,0:T(8,128)S(1)}, f32[4,32,1152]{2,1,0:T(8,128)S(1)}, f32[16,4,1152]{2,1,0:T(4,128)S(1)}) custom-call(s32[7]{0:T(128)S(1)} %pad_add_fusion.where_ref, f32[3,4]{1,0:T(4,128)S(1)} %pad_maximum_fusion.1.coef_ref, bf16[64,1152]{1,0:T(8,128)(2,1)S(1)} %shard_map.102.a0, bf16[64,1152]{1,0:T(8,128)(2,1)S(1)} %collective-permute-done.12.a1, ...), custom_call_target="tpu_custom_call" | custom-call | tf_op jit(solution)/shard_map/pallas_call | solution.py:26
  94.8 7.2 %collective-permute-start.16 = (f32[4,32,1152]{2,1,0:T(8,128)S(1)}, f32[4,32,1152]{2,1,0:T(8,128)S(1)}, u32[]{:S(2)}, u32[]{:S(2)}) collective-permute-start(f32[4,32,1152]{2,1,0:T(8,128)S(1)} %get-tuple-element.63), channel_id=1, source_target_pairs={{0,1},{1,0},{2,3},{3,2},{4,5},{5,4},{6,7},{7,6},{8,9},{9,8},{10,11... | collective-permute-start | bytes 1769480 | tf_op jit(solution)/shard_map/ppermute | solution.py:22
  102.0 13.3 %all_to_all.22.held_ref = f32[16,4,1152]{2,1,0:T(4,128)S(1)} all-to-all(f32[16,4,1152]{2,1,0:T(4,128)S(1)} %get-tuple-element.61), channel_id=1, replica_groups=mesh['w'=2,'v'=2,'u'=2,'y'=4,'x'=4,'c'=2] {'v','u','y'}, dimensions={0} | all-to-all | bytes 589824 | tf_op jit(solution)/shard_map/all_to_all | solution.py:217
  115.4 2.6 %collective-permute-start.15 = (f32[4,1152]{1,0:T(4,128)S(1)}, f32[4,1152]{1,0:T(4,128)S(1)}, u32[]{:S(2)}, u32[]{:S(2)}) collective-permute-start(f32[4,1152]{1,0:T(4,128)S(1)} %get-tuple-element.62), channel_id=1, source_target_pairs={{0,224},{32,192},{64,160},{96,128},{128,96},{160,64},{192,32},{224... | collective-permute-start | bytes 55304 | tf_op jit(solution)/shard_map/ppermute | solution.py:221
  118.0 1.3 collective-permute-done.15.below_ref
  119.3 0.6 shard_map.106
  119.9 13.6 %all_to_all.23.mine_lower = f32[16,4,1152]{2,1,0:T(4,128)S(1)} all-to-all(f32[16,4,1152]{2,1,0:T(4,128)S(1)} %shard_map.106), channel_id=1, replica_groups=mesh['w'=2,'v'=2,'u'=2,'y'=4,'x'=4,'c'=2] {'v','u','y'}, dimensions={0} | all-to-all | bytes 589824 | tf_op jit(solution)/shard_map/all_to_all | solution.py:225
  133.5 4.1 %collective-permute-start.17 = (f32[16,4,1152]{2,1,0:T(4,128)S(1)}, f32[16,4,1152]{2,1,0:T(4,128)S(1)}, u32[]{:S(2)}, u32[]{:S(2)}) collective-permute-start(f32[16,4,1152]{2,1,0:T(4,128)S(1)} %all_to_all.23.mine_lower), channel_id=1, source_target_pairs={{0,1},{1,0},{2,3},{3,2},{4,5},{5,4},{6,7},{7,6},{8,9},{9,8},{10,11... | collective-permute-start | bytes 884744 | tf_op jit(solution)/shard_map/ppermute | solution.py:22
  137.6 1.2 collective-permute-done.17.peer_lower
  138.8 1.8 %shard_map.107 = f32[4,2,32,1152]{3,2,1,0:T(8,128)} custom-call(s32[7]{0:T(128)S(1)} %pad_add_fusion.where_ref, f32[2,32,1152]{2,1,0:T(8,128)S(1)} %copy-done.4, f32[4,32,1152]{2,1,0:T(8,128)S(1)} %get-tuple-element.60.mine_before, f32[4,32,1152]{2,1,0:T(8,128)S(1)} %collective-permute-done.16.peer_before, f32[16,4,1152]{2,1,0:T(4,128)S(1)} %all_to_all.23.mine_lower, ...), custom_call_target="tpu_custom_call" | custom-call | tf_op jit(solution)/shard_map/pallas_call | solution.py:26
  (37 shorter events, 0.8 us)
Async XLA Ops:
  0.0 6.7 %copy-start = (s32[4,2]{0,1:T(2,128)S(1)}, s32[4,2]{0,1:T(2,128)}, u32[]{:S(2)}) copy-start(s32[4,2]{0,1:T(2,128)} %param.15) | copy-start | bytes 100
  0.0 1.4 copy-start.4
  1.4 3.4 %copy-start.5 = (bf16[4,2,32,1152]{3,2,1,0:T(8,128)(2,1)S(1)}, bf16[4,2,32,1152]{3,2,1,0:T(8,128)(2,1)}, u32[]{:S(2)}) copy-start(bf16[4,2,32,1152]{3,2,1,0:T(8,128)(2,1)} %param.10) | copy-start | bytes 1769476
  1.4 4.4 %copy-start.6 = (f32[8,3,1152]{2,0,1:T(8,128)S(1)}, f32[8,3,1152]{2,0,1:T(8,128)}, u32[]{:S(2)}) copy-start(f32[8,3,1152]{2,0,1:T(8,128)} %param.14) | copy-start | bytes 331780
  1.5 5.3 %collective-permute-start = (f32[5,32,1152]{2,1,0:T(8,128)S(1)}, f32[5,32,1152]{2,1,0:T(8,128)S(1)}, u32[]{:S(2)}, u32[]{:S(2)}) collective-permute-start(f32[5,32,1152]{2,1,0:T(8,128)S(1)} %pad_maximum_fusion), channel_id=1, source_target_pairs={{0,1},{1,0},{2,3},{3,2},{4,5},{5,4},{6,7},{7,6},{8,9},{9,8},{10,11... | collective-permute-start | bytes 2211848 | tf_op jit(solution)/shard_map/ppermute | solution.py:22
  4.9 21.8 %collective-permute-start.7 = (bf16[4,32,1152]{2,1,0:T(8,128)(2,1)S(1)}, bf16[4,32,1152]{2,1,0:T(8,128)(2,1)S(1)}, u32[]{:S(2)}, u32[]{:S(2)}) collective-permute-start(bf16[4,32,1152]{2,1,0:T(8,128)(2,1)S(1)} %get-tuple-element.69), channel_id=1, source_target_pairs={{0,1},{1,0},{2,3},{3,2},{4,5},{5,4},{6,7},{7,6},{8,9},{9,8},{10,11... | collective-permute-start | bytes 884744 | tf_op jit(solution)/shard_map/ppermute | solution.py:22
  7.8 7.9 %collective-permute-start.1 = (bf16[64,1152]{1,0:T(8,128)(2,1)S(1)}, bf16[64,1152]{1,0:T(8,128)(2,1)S(1)}, u32[]{:S(2)}, u32[]{:S(2)}) collective-permute-start(bf16[64,1152]{1,0:T(8,128)(2,1)S(1)} %get-tuple-element.38), channel_id=1, source_target_pairs={{0,2},{2,4},{4,6},{6,0},{1,3},{3,5},{5,7},{7,1},{8,10},{10,12},{12... | collective-permute-start | bytes 442376 | tf_op jit(solution)/shard_map/ppermute | solution.py:22
  7.9 8.9 %collective-permute-start.2 = (bf16[64,1152]{1,0:T(8,128)(2,1)S(1)}, bf16[64,1152]{1,0:T(8,128)(2,1)S(1)}, u32[]{:S(2)}, u32[]{:S(2)}) collective-permute-start(bf16[64,1152]{1,0:T(8,128)(2,1)S(1)} %get-tuple-element.39), channel_id=1, source_target_pairs={{0,4},{2,6},{4,0},{6,2},{1,5},{3,7},{5,1},{7,3},{8,12},{10,14},{12... | collective-permute-start | bytes 442376 | tf_op jit(solution)/shard_map/ppermute | solution.py:22
  9.9 7.9 %collective-permute-start.3 = (bf16[64,1152]{1,0:T(8,128)(2,1)S(1)}, bf16[64,1152]{1,0:T(8,128)(2,1)S(1)}, u32[]{:S(2)}, u32[]{:S(2)}) collective-permute-start(bf16[64,1152]{1,0:T(8,128)(2,1)S(1)} %get-tuple-element.40), channel_id=1, source_target_pairs={{0,6},{2,0},{4,2},{6,4},{1,7},{3,1},{5,3},{7,5},{8,14},{10,8},{12,... | collective-permute-start | bytes 442376 | tf_op jit(solution)/shard_map/ppermute | solution.py:22
  11.1 3.3 %copy-start.1 = (bf16[1152,3456]{1,0:T(8,128)(2,1)S(1)}, bf16[1152,3456]{1,0:T(8,128)(2,1)}, u32[]{:S(2)}) copy-start(bf16[1152,3456]{1,0:T(8,128)(2,1)} %w_ref.10) | copy-start | bytes 23887876
  14.4 3.4 %copy-start.2 = (bf16[1152,3456]{1,0:T(8,128)(2,1)S(1)}, bf16[1152,3456]{1,0:T(8,128)(2,1)}, u32[]{:S(2)}) copy-start(bf16[1152,3456]{1,0:T(8,128)(2,1)} %w_ref.10) | copy-start | bytes 23887876
  15.8 10.8 %copy-start.7 = (s32[4]{0:T(128)S(1)}, s32[4]{0:T(128)}, u32[]{:S(2)}) copy-start(s32[4]{0:T(128)} %param.12) | copy-start | bytes 52
  22.6 9.3 %collective-permute-start.4 = (bf16[64,1152]{1,0:T(8,128)(2,1)S(1)}, bf16[64,1152]{1,0:T(8,128)(2,1)S(1)}, u32[]{:S(2)}, u32[]{:S(2)}) collective-permute-start(bf16[64,1152]{1,0:T(8,128)(2,1)S(1)} %get-tuple-element.42), channel_id=1, source_target_pairs={{0,6},{2,0},{4,2},{6,4},{1,7},{3,1},{5,3},{7,5},{8,14},{10,8},{12,... | collective-permute-start | bytes 442376 | tf_op jit(solution)/shard_map/ppermute | solution.py:22
  25.9 6.2 %collective-permute-start.5 = (bf16[64,1152]{1,0:T(8,128)(2,1)S(1)}, bf16[64,1152]{1,0:T(8,128)(2,1)S(1)}, u32[]{:S(2)}, u32[]{:S(2)}) collective-permute-start(bf16[64,1152]{1,0:T(8,128)(2,1)S(1)} %get-tuple-element.43), channel_id=1, source_target_pairs={{0,4},{2,6},{4,0},{6,2},{1,5},{3,7},{5,1},{7,3},{8,12},{10,14},{12... | collective-permute-start | bytes 442376 | tf_op jit(solution)/shard_map/ppermute | solution.py:22
  25.9 9.8 %collective-permute-start.6 = (bf16[64,1152]{1,0:T(8,128)(2,1)S(1)}, bf16[64,1152]{1,0:T(8,128)(2,1)S(1)}, u32[]{:S(2)}, u32[]{:S(2)}) collective-permute-start(bf16[64,1152]{1,0:T(8,128)(2,1)S(1)} %get-tuple-element.44), channel_id=1, source_target_pairs={{0,2},{2,4},{4,6},{6,0},{1,3},{3,5},{5,7},{7,1},{8,10},{10,12},{12... | collective-permute-start | bytes 442376 | tf_op jit(solution)/shard_map/ppermute | solution.py:22
  26.7 9.1 %copy-start.3 = (bf16[1152,1152]{1,0:T(8,128)(2,1)S(1)}, bf16[1152,1152]{1,0:T(8,128)(2,1)}, u32[]{:S(2)}) copy-start(bf16[1152,1152]{1,0:T(8,128)(2,1)} %w_ref.11) | copy-start | bytes 7962628
  53.7 4.2 %collective-permute-start.8 = (f32[4,1152]{1,0:T(4,128)S(1)}, f32[4,1152]{1,0:T(4,128)S(1)}, u32[]{:S(2)}, u32[]{:S(2)}) collective-permute-start(f32[4,1152]{1,0:T(4,128)S(1)} %get-tuple-element.50), channel_id=1, source_target_pairs={{0,224},{32,192},{64,160},{96,128},{128,96},{160,64},{192,32},{224... | collective-permute-start | bytes 55304 | tf_op jit(solution)/shard_map/ppermute | solution.py:221
  73.7 5.7 %collective-permute-start.10 = (bf16[64,1152]{1,0:T(8,128)(2,1)S(1)}, bf16[64,1152]{1,0:T(8,128)(2,1)S(1)}, u32[]{:S(2)}, u32[]{:S(2)}) collective-permute-start(bf16[64,1152]{1,0:T(8,128)(2,1)S(1)} %get-tuple-element.53), channel_id=1, source_target_pairs={{0,4},{2,6},{4,0},{6,2},{1,5},{3,7},{5,1},{7,3},{8,12},{10,14},{12... | collective-permute-start | bytes 442376 | tf_op jit(solution)/shard_map/ppermute | solution.py:22
  74.3 5.0 %collective-permute-start.11 = (bf16[64,1152]{1,0:T(8,128)(2,1)S(1)}, bf16[64,1152]{1,0:T(8,128)(2,1)S(1)}, u32[]{:S(2)}, u32[]{:S(2)}) collective-permute-start(bf16[64,1152]{1,0:T(8,128)(2,1)S(1)} %get-tuple-element.54), channel_id=1, source_target_pairs={{0,6},{2,0},{4,2},{6,4},{1,7},{3,1},{5,3},{7,5},{8,14},{10,8},{12,... | collective-permute-start | bytes 442376 | tf_op jit(solution)/shard_map/ppermute | solution.py:22
  74.4 6.5 %collective-permute-start.9 = (bf16[64,1152]{1,0:T(8,128)(2,1)S(1)}, bf16[64,1152]{1,0:T(8,128)(2,1)S(1)}, u32[]{:S(2)}, u32[]{:S(2)}) collective-permute-start(bf16[64,1152]{1,0:T(8,128)(2,1)S(1)} %get-tuple-element.52), channel_id=1, source_target_pairs={{0,2},{2,4},{4,6},{6,0},{1,3},{3,5},{5,7},{7,1},{8,10},{10,12},{12... | collective-permute-start | bytes 442376 | tf_op jit(solution)/shard_map/ppermute | solution.py:22
  85.7 5.5 %collective-permute-start.12 = (bf16[64,1152]{1,0:T(8,128)(2,1)S(1)}, bf16[64,1152]{1,0:T(8,128)(2,1)S(1)}, u32[]{:S(2)}, u32[]{:S(2)}) collective-permute-start(bf16[64,1152]{1,0:T(8,128)(2,1)S(1)} %get-tuple-element.56), channel_id=1, source_target_pairs={{0,6},{2,0},{4,2},{6,4},{1,7},{3,1},{5,3},{7,5},{8,14},{10,8},{12,... | collective-permute-start | bytes 442376 | tf_op jit(solution)/shard_map/ppermute | solution.py:22
  86.0 5.6 %collective-permute-start.13 = (bf16[64,1152]{1,0:T(8,128)(2,1)S(1)}, bf16[64,1152]{1,0:T(8,128)(2,1)S(1)}, u32[]{:S(2)}, u32[]{:S(2)}) collective-permute-start(bf16[64,1152]{1,0:T(8,128)(2,1)S(1)} %get-tuple-element.57), channel_id=1, source_target_pairs={{0,4},{2,6},{4,0},{6,2},{1,5},{3,7},{5,1},{7,3},{8,12},{10,14},{12... | collective-permute-start | bytes 442376 | tf_op jit(solution)/shard_map/ppermute | solution.py:22
  86.7 6.5 %collective-permute-start.14 = (bf16[64,1152]{1,0:T(8,128)(2,1)S(1)}, bf16[64,1152]{1,0:T(8,128)(2,1)S(1)}, u32[]{:S(2)}, u32[]{:S(2)}) collective-permute-start(bf16[64,1152]{1,0:T(8,128)(2,1)S(1)} %get-tuple-element.58), channel_id=1, source_target_pairs={{0,2},{2,4},{4,6},{6,0},{1,3},{3,5},{5,7},{7,1},{8,10},{10,12},{12... | collective-permute-start | bytes 442376 | tf_op jit(solution)/shard_map/ppermute | solution.py:22
  94.8 24.5 %collective-permute-start.16 = (f32[4,32,1152]{2,1,0:T(8,128)S(1)}, f32[4,32,1152]{2,1,0:T(8,128)S(1)}, u32[]{:S(2)}, u32[]{:S(2)}) collective-permute-start(f32[4,32,1152]{2,1,0:T(8,128)S(1)} %get-tuple-element.63), channel_id=1, source_target_pairs={{0,1},{1,0},{2,3},{3,2},{4,5},{5,4},{6,7},{7,6},{8,9},{9,8},{10,11... | collective-permute-start | bytes 1769480 | tf_op jit(solution)/shard_map/ppermute | solution.py:22
  115.4 3.9 %collective-permute-start.15 = (f32[4,1152]{1,0:T(4,128)S(1)}, f32[4,1152]{1,0:T(4,128)S(1)}, u32[]{:S(2)}, u32[]{:S(2)}) collective-permute-start(f32[4,1152]{1,0:T(4,128)S(1)} %get-tuple-element.62), channel_id=1, source_target_pairs={{0,224},{32,192},{64,160},{96,128},{128,96},{160,64},{192,32},{224... | collective-permute-start | bytes 55304 | tf_op jit(solution)/shard_map/ppermute | solution.py:221
  133.5 5.3 %collective-permute-start.17 = (f32[16,4,1152]{2,1,0:T(4,128)S(1)}, f32[16,4,1152]{2,1,0:T(4,128)S(1)}, u32[]{:S(2)}, u32[]{:S(2)}) collective-permute-start(f32[16,4,1152]{2,1,0:T(4,128)S(1)} %all_to_all.23.mine_lower), channel_id=1, source_target_pairs={{0,1},{1,0},{2,3},{3,2},{4,5},{5,4},{6,7},{7,6},{8,9},{9,8},{10,11... | collective-permute-start | bytes 884744 | tf_op jit(solution)/shard_map/ppermute | solution.py:22

commit v5 on v4

--- a/solution.py
+++ b/solution.py
@@ -9,10 +9,9 @@
 HEADS = 16
 SWEEPS = 2
 LANES = 128
-PLANE_GROUPS = 4
 LOG2E = 1.4426950408889634
-HALF = ("v", "u", "y")
-PLANES = ("w", "v", "u")
+SHARES = ("u", "y")
+GROUPS = ("w", "v")
 VMEM = pl.BlockSpec(memory_space=pltpu.VMEM)
 SMEM = pl.BlockSpec(memory_space=pltpu.SMEM)
 
@@ -58,21 +57,15 @@
         mod_refs[r][...] = normed_rows(rows, shift, scale)
 
 
-def share_place(flip, q, places):
-    inner = places // PLANE_GROUPS
-    block = q // inner
-    return (block + flip * (PLANE_GROUPS - 1 - 2 * block)) * inner + q % inner
-
-
 def resume_body(
     where_ref, start_ref, mine_before, peer_before, lower_ref, step_ref, view_ref, x_ref, *rest
 ):
     mod_refs, base_ref = rest[:-1], rest[-1]
-    place, flip = where_ref[0], where_ref[1]
+    place = where_ref[0]
     steps = mine_before.shape[0]
     places, share, _ = lower_ref.shape
     for q in range(places):
-        base_ref[q * share : (q + 1) * share, :] = lower_ref[share_place(flip, q, places)]
+        base_ref[q * share : (q + 1) * share, :] = lower_ref[q]
     for r in range(steps):
         step = lax.rem(place + r, steps)
         before = jnp.concatenate([mine_before[step], peer_before[step]], axis=0)
@@ -84,13 +77,13 @@
 
 
 def finish_body(where_ref, start_ref, mine_before, peer_before, mine_lower, peer_lower, out_ref, base_ref):
-    flip, core = where_ref[1], where_ref[2]
+    core = where_ref[2]
     places, share, _ = mine_lower.shape
     half = places // 2
     sides = ((core, 0, mine_before, mine_lower), (1 - core, half, peer_before, peer_lower))
     for view, low, before_ref, lower_ref in sides:
         for q in range(half):
-            base_ref[q * share : (q + 1) * share, :] = lower_ref[share_place(flip, low + q, places)]
+            base_ref[q * share : (q + 1) * share, :] = lower_ref[low + q]
         for step in range(before_ref.shape[0]):
             out_ref[step, view] = start_ref[view] + (base_ref[...] + before_ref[step])
 
@@ -169,7 +162,7 @@
     rows_ref,
     proj_ref,
 ):
-    place, flip = where_ref[0], where_ref[1]
+    place = where_ref[0]
     pieces = (a0, a1, a2, a3)
     part = a0.shape[0]
     half = part // 2
@@ -186,7 +179,7 @@
         running = running + (base_ref[step] + gate * proj_ref[step * part : (step + 1) * part, :])
     places, share, _ = total_ref.shape
     for q in range(places):
-        total_ref[share_place(flip, q, places)] = running[q * share : (q + 1) * share]
+        total_ref[q] = running[q * share : (q + 1) * share]
 
 
 def coefficients(steps_index):
@@ -207,27 +200,30 @@
     all_ref[...] = running
 
 
-def below_body(where_ref, before_ref, below_ref, out_ref):
-    below = jnp.where(where_ref[1] == 1, below_ref[...], 0.0)
+def below_body(where_ref, before_ref, *refs):
+    passed, out_ref = refs[:-1], refs[-1]
+    group = where_ref[1]
+    below = jnp.zeros(before_ref.shape[1:], before_ref.dtype)
+    for shift, ref in enumerate(passed, 1):
+        below = below + jnp.where(shift <= group, ref[...], 0.0)
     for q in range(before_ref.shape[0]):
         out_ref[q] = before_ref[q] + below
 
 
 def earlier_sum(where, shares, beside=None):
-    held = lax.all_to_all(shares, HALF, 0, 0, tiled=True)
+    held = lax.all_to_all(shares, SHARES, 0, 0, tiled=True)
     whole = jax.ShapeDtypeStruct(shares.shape, shares.dtype)
     before, total = call(inside_body, [whole, jax.ShapeDtypeStruct(shares.shape[1:], shares.dtype)], [VMEM], held)
-    planes = lax.axis_size(PLANES)
-    below = lax.ppermute(total, PLANES, [(i, planes - 1 - i) for i in range(planes)])
+    passed = [shifted(total, GROUPS, shift) for shift in range(1, lax.axis_size(GROUPS))]
     if beside is not None:
-        below, beside = lax.optimization_barrier((below, shifted(beside, "c", 1)))
-    sums = call(below_body, whole, [SMEM] + [VMEM] * 2, where, before, below)
-    return lax.all_to_all(sums, HALF, 0, 0, tiled=True), beside
+        passed[0], beside = lax.optimization_barrier((passed[0], shifted(beside, "c", 1)))
+    sums = call(below_body, whole, [SMEM] + [VMEM] * (1 + len(passed)), where, before, *passed)
+    return lax.all_to_all(sums, SHARES, 0, 0, tiled=True), beside
 
 
 def per_device(states, noise, x_start, timesteps, step_mod, view_mod, view_ids, w_qkv, w_out):
     steps, views, part, width = states.shape
-    place, flip, core = (lax.axis_index(a) for a in ("x", "w", "c"))
+    place, group, core = (lax.axis_index(a) for a in ("x", GROUPS, "c"))
     other = 1 - core
     f32, bf16 = jnp.float32, jnp.bfloat16
     rows = 2 * part
@@ -244,7 +240,7 @@
     swapped = shifted(jnp.concatenate([given(states, 1), given(x_start, 0)[None]], axis=0), "c", 1)
     states_mine, start_mine = own(states, 1), own(x_start, 0)
     noise_mine, noise_peer = own(noise, 1), shifted(given(noise, 1), "c", 1)
-    where = jnp.concatenate([jnp.stack([place, flip, core]).astype(jnp.int32), own(view_ids, 1)])
+    where = jnp.concatenate([jnp.stack([place, group, core]).astype(jnp.int32), own(view_ids, 1)])
     coefs = jnp.stack(coefficients(timesteps))
     size = width // HEADS
     column = jnp.arange(width, dtype=jnp.int32)[None, :]
@@ -253,7 +249,7 @@
 
     x_shape = shape(steps, rows, width)
     half = shape(steps, part, width)
-    places = lax.axis_size(HALF)
+    places = lax.axis_size(SHARES)
     piece = shape(rows, width, kind=bf16)
     x, start, *mods = call(
         enter_body,

time: 141 us -> 138 us (0.979)
  blocking collectives: 57.2 us -> 37.8 us
  starting transfers between devices: 32 us -> 44.5 us
  waiting for transfers between devices: 16.5 us -> 20.3 us
    all_to_all x4, blocking collectives: 57.2 us -> 37.8 us  [the longest x2 19.6 us: earlier_sum(): held = lax.all_to_all(shares, SHARES, 0, 0, tiled=True)]
    ppermute x16 -> x22, starting transfers between devices: 26.3 us -> 44.5 us  [shifted(): lax.ppermute(value, axis, [(i, (i + shift) % size) for i in range(size)])]
    ppermute x16 -> x22, waiting for transfers between devices: 14 us -> 20.3 us  [shifted(): lax.ppermute(value, axis, [(i, (i + shift) % size) for i in range(size)])]
    ppermute x2 -> x0, starting transfers between devices: 5.66 us -> none  [earlier_sum(): lax.ppermute(total, PLANES, [(i, planes - 1 - i) for i in range(planes)])]
    ppermute x2 -> x0, waiting for transfers between devices: 2.49 us -> none  [earlier_sum(): lax.ppermute(total, PLANES, [(i, planes - 1 - i) for i in range(planes)])]
    unnamed x18 -> x20, local copies, waits for them, and re-layouts: 4.17 us -> 3.36 us
  transfers between devices with their start and end apart: 18 -> 22, of which waited for: 12 -> 14; matrix products, arithmetic and copies ran while one was open for 1% -> 1% of each run, Pallas kernels for 12% -> 12%
where the time goes in v5:
time: 138 us; the launch traced here: 137 us
  starting transfers between devices  44.5 us (32%)
  blocking collectives  37.8 us (27%)
  Pallas kernels  28.5 us (21%)
  waiting for transfers between devices  20.3 us (15%)
  local copies, waits for them, and re-layouts  5.52 us (4%)
    ppermute x22, starting transfers between devices, shifted(): lax.ppermute(value, axis, [(i, (i + shift) % size) for i in range(size)])  44.5 us
    pallas_call x17, Pallas kernels, call(): pl.pallas_call(body, out_shape=outs, in_specs=specs, out_specs=jax.tree.m...  28.5 us
    ppermute x22, waiting for transfers between devices, shifted(): lax.ppermute(value, axis, [(i, (i + shift) % size) for i in range(size)])  20.3 us
    all_to_all x2, blocking collectives, earlier_sum(): held = lax.all_to_all(shares, SHARES, 0, 0, tiled=True)  19.6 us
    all_to_all x2, blocking collectives, earlier_sum(): return (lax.all_to_all(sums, SHARES, 0, 0, tiled=True), beside)  18.2 us
    unnamed x20, local copies, waits for them, and re-layouts  3.36 us
  transfers between devices with their start and end apart: 22, of which 14 were waited for; matrix products, arithmetic and copies ran while one was open for 1% of the time, Pallas kernels for 12%

profile of v5, /device:TPU:1, one launch (start us, length us, event | category | flops | bytes accessed | tf_op | source)
XLA Modules:
  0.0 137.3 jit_solution(17574021124080103256)
XLA Ops:
  0.0 1.4 dynamic-slice_bitcast_fusion
  1.5 3.3 %collective-permute-start = (f32[5,32,1152]{2,1,0:T(8,128)S(1)}, f32[5,32,1152]{2,1,0:T(8,128)S(1)}, u32[]{:S(2)}, u32[]{:S(2)}) collective-permute-start(f32[5,32,1152]{2,1,0:T(8,128)S(1)} %pad_maximum_fusion), channel_id=1, source_target_pairs={{0,1},{1,0},{2,3},{3,2},{4,5},{5,4},{6,7},{7,6},{8,9},{9,8},{10,11... | collective-permute-start | bytes 2211848 | tf_op jit(solution)/shard_map/ppermute | solution.py:21
  4.8 0.8 dynamic-slice_bitcast_fusion.2
  5.6 0.8 collective-permute-start.7
  6.6 1.0 shard_map.91
  7.8 1.9 %collective-permute-start.2 = (bf16[64,1152]{1,0:T(8,128)(2,1)S(1)}, bf16[64,1152]{1,0:T(8,128)(2,1)S(1)}, u32[]{:S(2)}, u32[]{:S(2)}) collective-permute-start(bf16[64,1152]{1,0:T(8,128)(2,1)S(1)} %get-tuple-element.39), channel_id=1, source_target_pairs={{0,4},{2,6},{4,0},{6,2},{1,5},{3,7},{5,1},{7,3},{8,12},{10,14},{12... | collective-permute-start | bytes 442376 | tf_op jit(solution)/shard_map/ppermute | solution.py:21
  9.7 1.2 collective-permute-start.3
  11.0 3.3 %copy-done.1 = bf16[1152,3456]{1,0:T(8,128)(2,1)S(1)} copy-done((bf16[1152,3456]{1,0:T(8,128)(2,1)S(1)}, bf16[1152,3456]{1,0:T(8,128)(2,1)}, u32[]{:S(2)}) %copy-start.1) | copy-done | bytes 7962648
  14.2 1.4 %shard_map.92.first_ref = bf16[64,3456]{1,0:T(8,128)(2,1)S(1)} custom-call(bf16[64,1152]{1,0:T(8,128)(2,1)S(1)} %get-tuple-element.37.a0, bf16[1152,3456]{1,0:T(8,128)(2,1)S(1)} %copy-done.1), custom_call_target="tpu_custom_call" | custom-call | tf_op jit(solution)/shard_map/pallas_call | solution.py:25
  15.6 0.8 collective-permute-done.2.a2
  16.5 1.0 collective-permute-done.3.a3
  17.5 4.8 %shard_map.93 = (bf16[64,1152]{1,0:T(8,128)(2,1)S(1)}, bf16[64,1152]{1,0:T(8,128)(2,1)S(1)}, bf16[64,1152]{1,0:T(8,128)(2,1)S(1)}, bf16[256,3456]{1,0:T(8,128)(2,1)S(1)}) custom-call(bf16[64,3456]{1,0:T(8,128)(2,1)S(1)} %shard_map.92.first_ref, bf16[64,1152]{1,0:T(8,128)(2,1)S(1)} %collective-permute-done.1.a1, ...), custom_call_target="tpu_custom_call" | custom-call | tf_op jit(solution)/shard_map/pallas_call | solution.py:25
  22.3 3.4 %collective-permute-start.4 = (bf16[64,1152]{1,0:T(8,128)(2,1)S(1)}, bf16[64,1152]{1,0:T(8,128)(2,1)S(1)}, u32[]{:S(2)}, u32[]{:S(2)}) collective-permute-start(bf16[64,1152]{1,0:T(8,128)(2,1)S(1)} %get-tuple-element.42), channel_id=1, source_target_pairs={{0,6},{2,0},{4,2},{6,4},{1,7},{3,1},{5,3},{7,5},{8,14},{10,8},{12,... | collective-permute-start | bytes 442376 | tf_op jit(solution)/shard_map/ppermute | solution.py:21
  25.8 0.7 collective-permute-start.6
  26.5 0.7 shard_map.95.base_ref
  27.3 3.2 %shard_map.94.a0 = bf16[64,1152]{1,0:T(8,128)(2,1)S(1)} custom-call(bf16[64,3456]{1,0:T(8,128)(2,1)S(1)} %shard_map.92.first_ref, bf16[256,3456]{1,0:T(8,128)(2,1)S(1)} %get-tuple-element.41.qkv_ref, bf16[16,1152]{1,0:T(8,128)(2,1)S(1)} %fusion.1.mask_ref), custom_call_target="tpu_custom_call" | custom-call | tf_op jit(solution)/shard_map/pallas_call | solution.py:25
  30.4 1.3 collective-permute-done.4.a1
  32.0 3.6 %collective-permute-done.6.a3 = bf16[64,1152]{1,0:T(8,128)(2,1)S(1)} collective-permute-done((bf16[64,1152]{1,0:T(8,128)(2,1)S(1)}, bf16[64,1152]{1,0:T(8,128)(2,1)S(1)}, u32[]{:S(2)}, u32[]{:S(2)}) %collective-permute-start.6) | collective-permute-done | bytes 147488 | tf_op jit(solution)/shard_map/ppermute | solution.py:21
  35.6 1.6 %shard_map.96 = (f32[4,32,1152]{2,1,0:T(8,128)S(1)}, f32[4,32,1152]{2,1,0:T(8,128)S(1)}, f32[8,8,1152]{2,1,0:T(8,128)S(1)}) custom-call(s32[7]{0:T(128)S(1)} %pad_add_fusion.where_ref, f32[3,4]{1,0:T(4,128)S(1)} %pad_maximum_fusion.1.coef_ref, bf16[64,1152]{1,0:T(8,128)(2,1)S(1)} %shard_map.94.a0, bf16[64,1152]{1,0:T(8,128)(2,1)S(1)} %collective-permute-done.4.a1, ...), custom_call_target="tpu_custom_call" | custom-call | tf_op jit(solution)/shard_map/pallas_call | solution.py:25
  37.3 9.7 %all_to_all.20.held_ref = f32[8,8,1152]{2,1,0:T(8,128)S(1)} all-to-all(f32[8,8,1152]{2,1,0:T(8,128)S(1)} %get-tuple-element.48), channel_id=1, replica_groups=mesh['w'=2,'v'=2,'u'=2,'y'=4,'x'=4,'c'=2] {'u','y'}, dimensions={0} | all-to-all | bytes 589824 | tf_op jit(solution)/shard_map/all_to_all | solution.py:214
  47.0 5.2 %collective-permute-start.10 = (f32[8,1152]{1,0:T(8,128)S(1)}, f32[8,1152]{1,0:T(8,128)S(1)}, u32[]{:S(2)}, u32[]{:S(2)}) collective-permute-start(f32[8,1152]{1,0:T(8,128)S(1)} %get-tuple-element.50), channel_id=1, source_target_pairs={{0,192},{64,0},{128,64},{192,128},{1,193},{65,1},{129,65},{193,129... | collective-permute-start | bytes 110600 | tf_op jit(solution)/shard_map/ppermute | solution.py:21
  52.2 3.2 %collective-permute-start.9 = (f32[8,1152]{1,0:T(8,128)S(1)}, f32[8,1152]{1,0:T(8,128)S(1)}, u32[]{:S(2)}, u32[]{:S(2)}) collective-permute-start(f32[8,1152]{1,0:T(8,128)S(1)} %get-tuple-element.50), channel_id=1, source_target_pairs={{0,128},{64,192},{128,0},{192,64},{1,129},{65,193},{129,1},{193,65... | collective-permute-start | bytes 110600 | tf_op jit(solution)/shard_map/ppermute | solution.py:21
  55.4 1.7 %collective-permute-done.8.refs_0_ = f32[8,1152]{1,0:T(8,128)S(1)} collective-permute-done((f32[8,1152]{1,0:T(8,128)S(1)}, f32[8,1152]{1,0:T(8,128)S(1)}, u32[]{:S(2)}, u32[]{:S(2)}) %collective-permute-start.8) | collective-permute-done | bytes 36896 | tf_op jit(solution)/shard_map/ppermute | solution.py:21
  57.1 1.8 %collective-permute-done.9.refs_1_ = f32[8,1152]{1,0:T(8,128)S(1)} collective-permute-done((f32[8,1152]{1,0:T(8,128)S(1)}, f32[8,1152]{1,0:T(8,128)S(1)}, u32[]{:S(2)}, u32[]{:S(2)}) %collective-permute-start.9) | collective-permute-done | bytes 36896 | tf_op jit(solution)/shard_map/ppermute | solution.py:21
  59.5 8.9 %all_to_all.21.lower_ref = f32[8,8,1152]{2,1,0:T(8,128)S(1)} all-to-all(f32[8,8,1152]{2,1,0:T(8,128)S(1)} %shard_map.98), channel_id=1, replica_groups=mesh['w'=2,'v'=2,'u'=2,'y'=4,'x'=4,'c'=2] {'u','y'}, dimensions={0} | all-to-all | bytes 589824 | tf_op jit(solution)/shard_map/all_to_all | solution.py:221
  68.4 1.1 shard_map.99
  69.6 1.0 collective-permute-start.12
  70.6 2.0 %collective-permute-start.13 = (bf16[64,1152]{1,0:T(8,128)(2,1)S(1)}, bf16[64,1152]{1,0:T(8,128)(2,1)S(1)}, u32[]{:S(2)}, u32[]{:S(2)}) collective-permute-start(bf16[64,1152]{1,0:T(8,128)(2,1)S(1)} %get-tuple-element.54), channel_id=1, source_target_pairs={{0,6},{2,0},{4,2},{6,4},{1,7},{3,1},{5,3},{7,5},{8,14},{10,8},{12,... | collective-permute-start | bytes 442376 | tf_op jit(solution)/shard_map/ppermute | solution.py:21
  72.6 1.3 shard_map.100.first_ref
  73.9 2.4 %collective-permute-done.11.a1 = bf16[64,1152]{1,0:T(8,128)(2,1)S(1)} collective-permute-done((bf16[64,1152]{1,0:T(8,128)(2,1)S(1)}, bf16[64,1152]{1,0:T(8,128)(2,1)S(1)}, u32[]{:S(2)}, u32[]{:S(2)}) %collective-permute-start.11) | collective-permute-done | bytes 147488 | tf_op jit(solution)/shard_map/ppermute | solution.py:21
  76.9 4.8 %shard_map.101 = (bf16[64,1152]{1,0:T(8,128)(2,1)S(1)}, bf16[64,1152]{1,0:T(8,128)(2,1)S(1)}, bf16[64,1152]{1,0:T(8,128)(2,1)S(1)}, bf16[256,3456]{1,0:T(8,128)(2,1)S(1)}) custom-call(bf16[64,3456]{1,0:T(8,128)(2,1)S(1)} %shard_map.100.first_ref, bf16[64,1152]{1,0:T(8,128)(2,1)S(1)} %collective-permute-done.11.a1, ...), custom_call_target="tpu_custom_call" | custom-call | tf_op jit(solution)/shard_map/pallas_call | solution.py:25
  81.8 2.5 %collective-permute-start.14 = (bf16[64,1152]{1,0:T(8,128)(2,1)S(1)}, bf16[64,1152]{1,0:T(8,128)(2,1)S(1)}, u32[]{:S(2)}, u32[]{:S(2)}) collective-permute-start(bf16[64,1152]{1,0:T(8,128)(2,1)S(1)} %get-tuple-element.56), channel_id=1, source_target_pairs={{0,6},{2,0},{4,2},{6,4},{1,7},{3,1},{5,3},{7,5},{8,14},{10,8},{12,... | collective-permute-start | bytes 442376 | tf_op jit(solution)/shard_map/ppermute | solution.py:21
  84.9 0.7 shard_map.103.base_ref
  85.7 3.2 %shard_map.102.a0 = bf16[64,1152]{1,0:T(8,128)(2,1)S(1)} custom-call(bf16[64,3456]{1,0:T(8,128)(2,1)S(1)} %shard_map.100.first_ref, bf16[256,3456]{1,0:T(8,128)(2,1)S(1)} %get-tuple-element.55.qkv_ref, bf16[16,1152]{1,0:T(8,128)(2,1)S(1)} %fusion.1.mask_ref), custom_call_target="tpu_custom_call" | custom-call | tf_op jit(solution)/shard_map/pallas_call | solution.py:25
  88.9 1.0 collective-permute-done.15.a2
  89.8 1.2 collective-permute-done.16.a3
  91.0 1.6 %shard_map.104 = (f32[4,32,1152]{2,1,0:T(8,128)S(1)}, f32[4,32,1152]{2,1,0:T(8,128)S(1)}, f32[8,8,1152]{2,1,0:T(8,128)S(1)}) custom-call(s32[7]{0:T(128)S(1)} %pad_add_fusion.where_ref, f32[3,4]{1,0:T(4,128)S(1)} %pad_maximum_fusion.1.coef_ref, bf16[64,1152]{1,0:T(8,128)(2,1)S(1)} %shard_map.102.a0, bf16[64,1152]{1,0:T(8,128)(2,1)S(1)} %collective-permute-done.14.a1, ...), custom_call_target="tpu_custom_call" | custom-call | tf_op jit(solution)/shard_map/pallas_call | solution.py:25
  92.7 8.4 %collective-permute-start.18 = (f32[4,32,1152]{2,1,0:T(8,128)S(1)}, f32[4,32,1152]{2,1,0:T(8,128)S(1)}, u32[]{:S(2)}, u32[]{:S(2)}) collective-permute-start(f32[4,32,1152]{2,1,0:T(8,128)S(1)} %get-tuple-element.63), channel_id=1, source_target_pairs={{0,1},{1,0},{2,3},{3,2},{4,5},{5,4},{6,7},{7,6},{8,9},{9,8},{10,11... | collective-permute-start | bytes 1769480 | tf_op jit(solution)/shard_map/ppermute | solution.py:21
  101.1 10.0 %all_to_all.22.held_ref = f32[8,8,1152]{2,1,0:T(8,128)S(1)} all-to-all(f32[8,8,1152]{2,1,0:T(8,128)S(1)} %get-tuple-element.61), channel_id=1, replica_groups=mesh['w'=2,'v'=2,'u'=2,'y'=4,'x'=4,'c'=2] {'u','y'}, dimensions={0} | all-to-all | bytes 589824 | tf_op jit(solution)/shard_map/all_to_all | solution.py:214
  111.1 1.4 %collective-permute-start.17 = (f32[8,1152]{1,0:T(8,128)S(1)}, f32[8,1152]{1,0:T(8,128)S(1)}, u32[]{:S(2)}, u32[]{:S(2)}) collective-permute-start(f32[8,1152]{1,0:T(8,128)S(1)} %get-tuple-element.62), channel_id=1, source_target_pairs={{0,64},{64,128},{128,192},{192,0},{1,65},{65,129},{129,193},{193,1... | collective-permute-start | bytes 110600 | tf_op jit(solution)/shard_map/ppermute | solution.py:21
  112.5 4.3 %collective-permute-start.19 = (f32[8,1152]{1,0:T(8,128)S(1)}, f32[8,1152]{1,0:T(8,128)S(1)}, u32[]{:S(2)}, u32[]{:S(2)}) collective-permute-start(f32[8,1152]{1,0:T(8,128)S(1)} %get-tuple-element.62), channel_id=1, source_target_pairs={{0,128},{64,192},{128,0},{192,64},{1,129},{65,193},{129,1},{193,65... | collective-permute-start | bytes 110600 | tf_op jit(solution)/shard_map/ppermute | solution.py:21
  116.7 1.1 collective-permute-start.20
  117.9 1.4 %collective-permute-done.19.refs_1_ = f32[8,1152]{1,0:T(8,128)S(1)} collective-permute-done((f32[8,1152]{1,0:T(8,128)S(1)}, f32[8,1152]{1,0:T(8,128)S(1)}, u32[]{:S(2)}, u32[]{:S(2)}) %collective-permute-start.19) | collective-permute-done | bytes 36896 | tf_op jit(solution)/shard_map/ppermute | solution.py:21
  119.3 1.9 %collective-permute-done.20.refs_2_ = f32[8,1152]{1,0:T(8,128)S(1)} collective-permute-done((f32[8,1152]{1,0:T(8,128)S(1)}, f32[8,1152]{1,0:T(8,128)S(1)}, u32[]{:S(2)}, u32[]{:S(2)}) %collective-permute-start.20) | collective-permute-done | bytes 36896 | tf_op jit(solution)/shard_map/ppermute | solution.py:21
  121.8 9.3 %all_to_all.23.mine_lower = f32[8,8,1152]{2,1,0:T(8,128)S(1)} all-to-all(f32[8,8,1152]{2,1,0:T(8,128)S(1)} %shard_map.106), channel_id=1, replica_groups=mesh['w'=2,'v'=2,'u'=2,'y'=4,'x'=4,'c'=2] {'u','y'}, dimensions={0} | all-to-all | bytes 589824 | tf_op jit(solution)/shard_map/all_to_all | solution.py:221
  131.1 3.3 %collective-permute-start.21 = (f32[8,8,1152]{2,1,0:T(8,128)S(1)}, f32[8,8,1152]{2,1,0:T(8,128)S(1)}, u32[]{:S(2)}, u32[]{:S(2)}) collective-permute-start(f32[8,8,1152]{2,1,0:T(8,128)S(1)} %all_to_all.23.mine_lower), channel_id=1, source_target_pairs={{0,1},{1,0},{2,3},{3,2},{4,5},{5,4},{6,7},{7,6},{8,9},{9,8},{10,11... | collective-permute-start | bytes 884744 | tf_op jit(solution)/shard_map/ppermute | solution.py:21
  134.3 1.2 collective-permute-done.21.peer_lower
  135.6 1.7 %shard_map.107 = f32[4,2,32,1152]{3,2,1,0:T(8,128)} custom-call(s32[7]{0:T(128)S(1)} %pad_add_fusion.where_ref, f32[2,32,1152]{2,1,0:T(8,128)S(1)} %copy-done.4, f32[4,32,1152]{2,1,0:T(8,128)S(1)} %get-tuple-element.60.mine_before, f32[4,32,1152]{2,1,0:T(8,128)S(1)} %collective-permute-done.18.peer_before, f32[8,8,1152]{2,1,0:T(8,128)S(1)} %all_to_all.23.mine_lower, ...), custom_call_target="tpu_custom_call" | custom-call | tf_op jit(solution)/shard_map/pallas_call | solution.py:25
  (47 shorter events, 3.3 us)
Async XLA Ops:
  0.0 6.5 %copy-start = (s32[4,2]{0,1:T(2,128)S(1)}, s32[4,2]{0,1:T(2,128)}, u32[]{:S(2)}) copy-start(s32[4,2]{0,1:T(2,128)} %param.15) | copy-start | bytes 100
  0.0 1.4 %copy-start.4 = (f32[2,32,1152]{2,1,0:T(8,128)S(1)}, f32[2,32,1152]{2,1,0:T(8,128)}, u32[]{:S(2)}) copy-start(f32[2,32,1152]{2,1,0:T(8,128)} %start_ref.1) | copy-start | bytes 884740
  1.4 3.4 %copy-start.5 = (bf16[4,2,32,1152]{3,2,1,0:T(8,128)(2,1)S(1)}, bf16[4,2,32,1152]{3,2,1,0:T(8,128)(2,1)}, u32[]{:S(2)}) copy-start(bf16[4,2,32,1152]{3,2,1,0:T(8,128)(2,1)} %param.10) | copy-start | bytes 1769476
  1.4 5.0 %copy-start.6 = (f32[8,3,1152]{2,0,1:T(8,128)S(1)}, f32[8,3,1152]{2,0,1:T(8,128)}, u32[]{:S(2)}) copy-start(f32[8,3,1152]{2,0,1:T(8,128)} %param.14) | copy-start | bytes 331780
  1.4 5.0 %copy-start.7 = (f32[4,3,1152]{2,0,1:T(4,128)S(1)}, f32[4,3,1152]{2,0,1:T(4,128)}, u32[]{:S(2)}) copy-start(f32[4,3,1152]{2,0,1:T(4,128)} %param.13) | copy-start | bytes 165892
  1.5 5.1 %collective-permute-start = (f32[5,32,1152]{2,1,0:T(8,128)S(1)}, f32[5,32,1152]{2,1,0:T(8,128)S(1)}, u32[]{:S(2)}, u32[]{:S(2)}) collective-permute-start(f32[5,32,1152]{2,1,0:T(8,128)S(1)} %pad_maximum_fusion), channel_id=1, source_target_pairs={{0,1},{1,0},{2,3},{3,2},{4,5},{5,4},{6,7},{7,6},{8,9},{9,8},{10,11... | collective-permute-start | bytes 2211848 | tf_op jit(solution)/shard_map/ppermute | solution.py:21
  5.6 20.9 %collective-permute-start.7 = (bf16[4,32,1152]{2,1,0:T(8,128)(2,1)}, bf16[4,32,1152]{2,1,0:T(8,128)(2,1)S(1)}, u32[]{:S(2)}, u32[]{:S(2)}) collective-permute-start(bf16[4,32,1152]{2,1,0:T(8,128)(2,1)} %get-tuple-element.69), channel_id=1, source_target_pairs={{0,1},{1,0},{2,3},{3,2},{4,5},{5,4},{6,7},{7,6},{8,9},{9,8},{10,11... | collective-permute-start | bytes 884744 | tf_op jit(solution)/shard_map/ppermute | solution.py:21
  7.7 8.0 %collective-permute-start.1 = (bf16[64,1152]{1,0:T(8,128)(2,1)S(1)}, bf16[64,1152]{1,0:T(8,128)(2,1)S(1)}, u32[]{:S(2)}, u32[]{:S(2)}) collective-permute-start(bf16[64,1152]{1,0:T(8,128)(2,1)S(1)} %get-tuple-element.38), channel_id=1, source_target_pairs={{0,2},{2,4},{4,6},{6,0},{1,3},{3,5},{5,7},{7,1},{8,10},{10,12},{12... | collective-permute-start | bytes 442376 | tf_op jit(solution)/shard_map/ppermute | solution.py:21
  7.8 8.7 %collective-permute-start.2 = (bf16[64,1152]{1,0:T(8,128)(2,1)S(1)}, bf16[64,1152]{1,0:T(8,128)(2,1)S(1)}, u32[]{:S(2)}, u32[]{:S(2)}) collective-permute-start(bf16[64,1152]{1,0:T(8,128)(2,1)S(1)} %get-tuple-element.39), channel_id=1, source_target_pairs={{0,4},{2,6},{4,0},{6,2},{1,5},{3,7},{5,1},{7,3},{8,12},{10,14},{12... | collective-permute-start | bytes 442376 | tf_op jit(solution)/shard_map/ppermute | solution.py:21
  9.7 7.8 %collective-permute-start.3 = (bf16[64,1152]{1,0:T(8,128)(2,1)S(1)}, bf16[64,1152]{1,0:T(8,128)(2,1)S(1)}, u32[]{:S(2)}, u32[]{:S(2)}) collective-permute-start(bf16[64,1152]{1,0:T(8,128)(2,1)S(1)} %get-tuple-element.40), channel_id=1, source_target_pairs={{0,6},{2,0},{4,2},{6,4},{1,7},{3,1},{5,3},{7,5},{8,14},{10,8},{12,... | collective-permute-start | bytes 442376 | tf_op jit(solution)/shard_map/ppermute | solution.py:21
  11.0 3.3 %copy-start.1 = (bf16[1152,3456]{1,0:T(8,128)(2,1)S(1)}, bf16[1152,3456]{1,0:T(8,128)(2,1)}, u32[]{:S(2)}) copy-start(bf16[1152,3456]{1,0:T(8,128)(2,1)} %w_ref.10) | copy-start | bytes 23887876
  14.2 3.3 %copy-start.2 = (bf16[1152,3456]{1,0:T(8,128)(2,1)S(1)}, bf16[1152,3456]{1,0:T(8,128)(2,1)}, u32[]{:S(2)}) copy-start(bf16[1152,3456]{1,0:T(8,128)(2,1)} %w_ref.10) | copy-start | bytes 23887876
  15.6 10.8 %copy-start.8 = (s32[4]{0:T(128)S(1)}, s32[4]{0:T(128)}, u32[]{:S(2)}) copy-start(s32[4]{0:T(128)} %param.12) | copy-start | bytes 52
  22.3 9.5 %collective-permute-start.4 = (bf16[64,1152]{1,0:T(8,128)(2,1)S(1)}, bf16[64,1152]{1,0:T(8,128)(2,1)S(1)}, u32[]{:S(2)}, u32[]{:S(2)}) collective-permute-start(bf16[64,1152]{1,0:T(8,128)(2,1)S(1)} %get-tuple-element.42), channel_id=1, source_target_pairs={{0,6},{2,0},{4,2},{6,4},{1,7},{3,1},{5,3},{7,5},{8,14},{10,8},{12,... | collective-permute-start | bytes 442376 | tf_op jit(solution)/shard_map/ppermute | solution.py:21
  25.8 6.2 %collective-permute-start.5 = (bf16[64,1152]{1,0:T(8,128)(2,1)S(1)}, bf16[64,1152]{1,0:T(8,128)(2,1)S(1)}, u32[]{:S(2)}, u32[]{:S(2)}) collective-permute-start(bf16[64,1152]{1,0:T(8,128)(2,1)S(1)} %get-tuple-element.43), channel_id=1, source_target_pairs={{0,4},{2,6},{4,0},{6,2},{1,5},{3,7},{5,1},{7,3},{8,12},{10,14},{12... | collective-permute-start | bytes 442376 | tf_op jit(solution)/shard_map/ppermute | solution.py:21
  25.8 9.8 %collective-permute-start.6 = (bf16[64,1152]{1,0:T(8,128)(2,1)S(1)}, bf16[64,1152]{1,0:T(8,128)(2,1)S(1)}, u32[]{:S(2)}, u32[]{:S(2)}) collective-permute-start(bf16[64,1152]{1,0:T(8,128)(2,1)S(1)} %get-tuple-element.44), channel_id=1, source_target_pairs={{0,2},{2,4},{4,6},{6,0},{1,3},{3,5},{5,7},{7,1},{8,10},{10,12},{12... | collective-permute-start | bytes 442376 | tf_op jit(solution)/shard_map/ppermute | solution.py:21
  26.5 9.1 %copy-start.3 = (bf16[1152,1152]{1,0:T(8,128)(2,1)S(1)}, bf16[1152,1152]{1,0:T(8,128)(2,1)}, u32[]{:S(2)}) copy-start(bf16[1152,1152]{1,0:T(8,128)(2,1)} %w_ref.11) | copy-start | bytes 7962628
  47.0 8.5 %collective-permute-start.10 = (f32[8,1152]{1,0:T(8,128)S(1)}, f32[8,1152]{1,0:T(8,128)S(1)}, u32[]{:S(2)}, u32[]{:S(2)}) collective-permute-start(f32[8,1152]{1,0:T(8,128)S(1)} %get-tuple-element.50), channel_id=1, source_target_pairs={{0,192},{64,0},{128,64},{192,128},{1,193},{65,1},{129,65},{193,129... | collective-permute-start | bytes 110600 | tf_op jit(solution)/shard_map/ppermute | solution.py:21
  52.2 4.9 %collective-permute-start.8 = (f32[8,1152]{1,0:T(8,128)S(1)}, f32[8,1152]{1,0:T(8,128)S(1)}, u32[]{:S(2)}, u32[]{:S(2)}) collective-permute-start(f32[8,1152]{1,0:T(8,128)S(1)} %get-tuple-element.50), channel_id=1, source_target_pairs={{0,64},{64,128},{128,192},{192,0},{1,65},{65,129},{129,193},{193,1... | collective-permute-start | bytes 110600 | tf_op jit(solution)/shard_map/ppermute | solution.py:21
  52.2 6.7 %collective-permute-start.9 = (f32[8,1152]{1,0:T(8,128)S(1)}, f32[8,1152]{1,0:T(8,128)S(1)}, u32[]{:S(2)}, u32[]{:S(2)}) collective-permute-start(f32[8,1152]{1,0:T(8,128)S(1)} %get-tuple-element.50), channel_id=1, source_target_pairs={{0,128},{64,192},{128,0},{192,64},{1,129},{65,193},{129,1},{193,65... | collective-permute-start | bytes 110600 | tf_op jit(solution)/shard_map/ppermute | solution.py:21
  69.5 6.9 %collective-permute-start.11 = (bf16[64,1152]{1,0:T(8,128)(2,1)S(1)}, bf16[64,1152]{1,0:T(8,128)(2,1)S(1)}, u32[]{:S(2)}, u32[]{:S(2)}) collective-permute-start(bf16[64,1152]{1,0:T(8,128)(2,1)S(1)} %get-tuple-element.52), channel_id=1, source_target_pairs={{0,2},{2,4},{4,6},{6,0},{1,3},{3,5},{5,7},{7,1},{8,10},{10,12},{12... | collective-permute-start | bytes 442376 | tf_op jit(solution)/shard_map/ppermute | solution.py:21
  69.6 6.8 %collective-permute-start.12 = (bf16[64,1152]{1,0:T(8,128)(2,1)S(1)}, bf16[64,1152]{1,0:T(8,128)(2,1)S(1)}, u32[]{:S(2)}, u32[]{:S(2)}) collective-permute-start(bf16[64,1152]{1,0:T(8,128)(2,1)S(1)} %get-tuple-element.53), channel_id=1, source_target_pairs={{0,4},{2,6},{4,0},{6,2},{1,5},{3,7},{5,1},{7,3},{8,12},{10,14},{12... | collective-permute-start | bytes 442376 | tf_op jit(solution)/shard_map/ppermute | solution.py:21
  70.6 6.3 %collective-permute-start.13 = (bf16[64,1152]{1,0:T(8,128)(2,1)S(1)}, bf16[64,1152]{1,0:T(8,128)(2,1)S(1)}, u32[]{:S(2)}, u32[]{:S(2)}) collective-permute-start(bf16[64,1152]{1,0:T(8,128)(2,1)S(1)} %get-tuple-element.54), channel_id=1, source_target_pairs={{0,6},{2,0},{4,2},{6,4},{1,7},{3,1},{5,3},{7,5},{8,14},{10,8},{12,... | collective-permute-start | bytes 442376 | tf_op jit(solution)/shard_map/ppermute | solution.py:21
  81.8 7.1 %collective-permute-start.14 = (bf16[64,1152]{1,0:T(8,128)(2,1)S(1)}, bf16[64,1152]{1,0:T(8,128)(2,1)S(1)}, u32[]{:S(2)}, u32[]{:S(2)}) collective-permute-start(bf16[64,1152]{1,0:T(8,128)(2,1)S(1)} %get-tuple-element.56), channel_id=1, source_target_pairs={{0,6},{2,0},{4,2},{6,4},{1,7},{3,1},{5,3},{7,5},{8,14},{10,8},{12,... | collective-permute-start | bytes 442376 | tf_op jit(solution)/shard_map/ppermute | solution.py:21
  84.2 5.6 %collective-permute-start.15 = (bf16[64,1152]{1,0:T(8,128)(2,1)S(1)}, bf16[64,1152]{1,0:T(8,128)(2,1)S(1)}, u32[]{:S(2)}, u32[]{:S(2)}) collective-permute-start(bf16[64,1152]{1,0:T(8,128)(2,1)S(1)} %get-tuple-element.57), channel_id=1, source_target_pairs={{0,4},{2,6},{4,0},{6,2},{1,5},{3,7},{5,1},{7,3},{8,12},{10,14},{12... | collective-permute-start | bytes 442376 | tf_op jit(solution)/shard_map/ppermute | solution.py:21
  84.2 6.8 %collective-permute-start.16 = (bf16[64,1152]{1,0:T(8,128)(2,1)S(1)}, bf16[64,1152]{1,0:T(8,128)(2,1)S(1)}, u32[]{:S(2)}, u32[]{:S(2)}) collective-permute-start(bf16[64,1152]{1,0:T(8,128)(2,1)S(1)} %get-tuple-element.58), channel_id=1, source_target_pairs={{0,2},{2,4},{4,6},{6,0},{1,3},{3,5},{5,7},{7,1},{8,10},{10,12},{12... | collective-permute-start | bytes 442376 | tf_op jit(solution)/shard_map/ppermute | solution.py:21
  92.7 25.2 %collective-permute-start.18 = (f32[4,32,1152]{2,1,0:T(8,128)S(1)}, f32[4,32,1152]{2,1,0:T(8,128)S(1)}, u32[]{:S(2)}, u32[]{:S(2)}) collective-permute-start(f32[4,32,1152]{2,1,0:T(8,128)S(1)} %get-tuple-element.63), channel_id=1, source_target_pairs={{0,1},{1,0},{2,3},{3,2},{4,5},{5,4},{6,7},{7,6},{8,9},{9,8},{10,11... | collective-permute-start | bytes 1769480 | tf_op jit(solution)/shard_map/ppermute | solution.py:21
  111.1 6.8 %collective-permute-start.17 = (f32[8,1152]{1,0:T(8,128)S(1)}, f32[8,1152]{1,0:T(8,128)S(1)}, u32[]{:S(2)}, u32[]{:S(2)}) collective-permute-start(f32[8,1152]{1,0:T(8,128)S(1)} %get-tuple-element.62), channel_id=1, source_target_pairs={{0,64},{64,128},{128,192},{192,0},{1,65},{65,129},{129,193},{193,1... | collective-permute-start | bytes 110600 | tf_op jit(solution)/shard_map/ppermute | solution.py:21
  112.5 6.8 %collective-permute-start.19 = (f32[8,1152]{1,0:T(8,128)S(1)}, f32[8,1152]{1,0:T(8,128)S(1)}, u32[]{:S(2)}, u32[]{:S(2)}) collective-permute-start(f32[8,1152]{1,0:T(8,128)S(1)} %get-tuple-element.62), channel_id=1, source_target_pairs={{0,128},{64,192},{128,0},{192,64},{1,129},{65,193},{129,1},{193,65... | collective-permute-start | bytes 110600 | tf_op jit(solution)/shard_map/ppermute | solution.py:21
  116.7 4.5 %collective-permute-start.20 = (f32[8,1152]{1,0:T(8,128)S(1)}, f32[8,1152]{1,0:T(8,128)S(1)}, u32[]{:S(2)}, u32[]{:S(2)}) collective-permute-start(f32[8,1152]{1,0:T(8,128)S(1)} %get-tuple-element.62), channel_id=1, source_target_pairs={{0,192},{64,0},{128,64},{192,128},{1,193},{65,1},{129,65},{193,129... | collective-permute-start | bytes 110600 | tf_op jit(solution)/shard_map/ppermute | solution.py:21
  131.1 4.5 %collective-permute-start.21 = (f32[8,8,1152]{2,1,0:T(8,128)S(1)}, f32[8,8,1152]{2,1,0:T(8,128)S(1)}, u32[]{:S(2)}, u32[]{:S(2)}) collective-permute-start(f32[8,8,1152]{2,1,0:T(8,128)S(1)} %all_to_all.23.mine_lower), channel_id=1, source_target_pairs={{0,1},{1,0},{2,3},{3,2},{4,5},{5,4},{6,7},{7,6},{8,9},{9,8},{10,11... | collective-permute-start | bytes 884744 | tf_op jit(solution)/shard_map/ppermute | solution.py:21

commit v6 on v5

--- a/solution.py
+++ b/solution.py
@@ -5,6 +5,7 @@
 from jax.experimental.pallas import tpu as pltpu
 from jax.sharding import Mesh
 from jax.sharding import PartitionSpec as P
+
 
 HEADS = 16
 SWEEPS = 2
@@ -21,12 +22,19 @@
     return lax.ppermute(value, axis, [(i, (i + shift) % size) for i in range(size)])
 
 
-def call(body, outs, specs, *args, scratch=()):
+def spread(values, axis, sign=1):
+    moved = []
+    for k, value in enumerate(values, 1):
+        moved.append(shifted(value, axis, sign * k))
+    return moved
+
+
+def call(body, outs, specs, *args, scratch=(), out_spec=VMEM):
     return pl.pallas_call(
         body,
         out_shape=outs,
         in_specs=specs,
-        out_specs=jax.tree.map(lambda _: VMEM, outs),
+        out_specs=jax.tree.map(lambda _: out_spec, outs),
         scratch_shapes=list(scratch),
         compiler_params=pltpu.CompilerParams(vmem_limit_bytes=16 * 2**20),
     )(*args)
@@ -76,16 +84,26 @@
         mod_refs[r][...] = normed_rows(rows, shift, scale)
 
 
-def finish_body(where_ref, start_ref, mine_before, peer_before, mine_lower, peer_lower, out_ref, base_ref):
+def finish_body(
+    where_ref, start_ref, mine_before, peer_before, mine_lower, peer_lower, out_ref, base_ref, rows_ref, sems
+):
     core = where_ref[2]
     places, share, _ = mine_lower.shape
     half = places // 2
     sides = ((core, 0, mine_before, mine_lower), (1 - core, half, peer_before, peer_lower))
-    for view, low, before_ref, lower_ref in sides:
+    copies = []
+    for side, (view, low, before_ref, lower_ref) in enumerate(sides):
         for q in range(half):
-            base_ref[q * share : (q + 1) * share, :] = lower_ref[low + q]
+            rows = slice(q * share, (q + 1) * share)
+            base_ref[rows, :] = lower_ref[low + q]
         for step in range(before_ref.shape[0]):
-            out_ref[step, view] = start_ref[view] + (base_ref[...] + before_ref[step])
+            rows_ref[side, step] = start_ref[view] + (base_ref[...] + before_ref[step])
+            copies.append(
+                pltpu.make_async_copy(rows_ref.at[side, step], out_ref.at[step, view], sems.at[side, step])
+            )
+            copies[-1].start()
+    for copy in copies:
+        copy.wait()
 
 
 def project_rows(rows, w_ref):
@@ -214,14 +232,14 @@
     held = lax.all_to_all(shares, SHARES, 0, 0, tiled=True)
     whole = jax.ShapeDtypeStruct(shares.shape, shares.dtype)
     before, total = call(inside_body, [whole, jax.ShapeDtypeStruct(shares.shape[1:], shares.dtype)], [VMEM], held)
-    passed = [shifted(total, GROUPS, shift) for shift in range(1, lax.axis_size(GROUPS))]
+    passed = spread([total] * (lax.axis_size(GROUPS) - 1), GROUPS)
     if beside is not None:
         passed[0], beside = lax.optimization_barrier((passed[0], shifted(beside, "c", 1)))
     sums = call(below_body, whole, [SMEM] + [VMEM] * (1 + len(passed)), where, before, *passed)
     return lax.all_to_all(sums, SHARES, 0, 0, tiled=True), beside
 
 
-def per_device(states, noise, x_start, timesteps, step_mod, view_mod, view_ids, w_qkv, w_out):
+def device_program(states, noise, x_start, timesteps, step_mod, view_mod, view_ids, w_qkv, w_out):
     steps, views, part, width = states.shape
     place, group, core = (lax.axis_index(a) for a in ("x", GROUPS, "c"))
     other = 1 - core
@@ -239,7 +257,6 @@
 
     swapped = shifted(jnp.concatenate([given(states, 1), given(x_start, 0)[None]], axis=0), "c", 1)
     states_mine, start_mine = own(states, 1), own(x_start, 0)
-    noise_mine, noise_peer = own(noise, 1), shifted(given(noise, 1), "c", 1)
     where = jnp.concatenate([jnp.stack([place, group, core]).astype(jnp.int32), own(view_ids, 1)])
     coefs = jnp.stack(coefficients(timesteps))
     size = width // HEADS
@@ -262,8 +279,10 @@
         step_mod,
         view_mod,
     )
+    drawn, _ = lax.optimization_barrier((noise, mods[0]))
+    noise_mine, noise_peer = own(drawn, 1), shifted(given(drawn, 1), "c", 1)
     for sweep in range(SWEEPS):
-        arrived = [shifted(mods[r], "x", r) for r in range(1, steps)]
+        arrived = spread(mods[1:], "x")
         first = call(first_body, shape(rows, 3 * width, kind=bf16), [VMEM] * 2, mods[0], w_qkv)
         *attended, qkv = call(
             others_body,
@@ -275,7 +294,7 @@
             mask,
             scratch=[pltpu.VMEM(((steps - 1) * rows, width), bf16)],
         )
-        back = [shifted(attended[r - 1], "x", -r) for r in range(1, steps)]
+        back = spread(attended, "x", -1)
         kept = call(own_body, piece, [VMEM] * 3, first, qkv, mask)
         base = call(base_body, x_shape, [SMEM] + [VMEM] * 3, coefs, x, noise_mine, noise_peer)
         mine_before, peer_before, total = call(
@@ -319,7 +338,12 @@
         peer_before,
         lower,
         shifted(lower, "c", 1),
-        scratch=[pltpu.VMEM((part, width), f32)],
+        scratch=[
+            pltpu.VMEM((part, width), f32),
+            pltpu.VMEM((views, steps, part, width), f32),
+            pltpu.SemaphoreType.DMA((views, steps)),
+        ],
+        out_spec=pl.BlockSpec(memory_space=pl.ANY),
     )
 
 
@@ -338,5 +362,5 @@
         P(),
     )
     return jax.shard_map(
-        per_device, mesh=finer, in_specs=placed, out_specs=P(tm, None, tok, None), check_vma=False
+        device_program, mesh=finer, in_specs=placed, out_specs=P(tm, None, tok, None), check_vma=False
     )

time: 138 us -> 137 us (level)
  starting transfers between devices: 44.5 us -> 46.2 us
    ppermute x22, starting transfers between devices: 44.5 us -> 46.2 us  [shifted(): lax.ppermute(value, axis, [(i, (i + shift) % size) for i in range(size)])]
  transfers between devices with their start and end apart: 22 -> 22, of which waited for: 14 -> 14; matrix products, arithmetic and copies ran while one was open for 1% -> 0% of each run, Pallas kernels for 12% -> 11%
where the time goes in v6:
time: 137 us
  starting transfers between devices  46.2 us (34%)
  blocking collectives  37.6 us (27%)
  Pallas kernels  28.5 us (21%)
  waiting for transfers between devices  19 us (14%)
  local copies, waits for them, and re-layouts  4.91 us (4%)
    ppermute x22, starting transfers between devices, shifted(): lax.ppermute(value, axis, [(i, (i + shift) % size) for i in range(size)])  46.2 us
    pallas_call x17, Pallas kernels, call(): pl.pallas_call(body, out_shape=outs, in_specs=specs, out_specs=jax.tree.m...  28.5 us
    all_to_all x2, blocking collectives, earlier_sum(): held = lax.all_to_all(shares, SHARES, 0, 0, tiled=True)  19.6 us
    ppermute x22, waiting for transfers between devices, shifted(): lax.ppermute(value, axis, [(i, (i + shift) % size) for i in range(size)])  19 us
    all_to_all x2, blocking collectives, earlier_sum(): return (lax.all_to_all(sums, SHARES, 0, 0, tiled=True), beside)  18.1 us
    unnamed x20, local copies, waits for them, and re-layouts  3.45 us
  transfers between devices with their start and end apart: 22, of which 14 were waited for; matrix products, arithmetic and copies ran while one was open for 0% of the time, Pallas kernels for 11%

profile of v6, /device:TPU:1, one launch (start us, length us, event | category | flops | bytes accessed | tf_op | source)
XLA Modules:
  0.0 136.9 jit_solution(14046560595370854133)
XLA Ops:
  0.0 1.4 dynamic-slice_bitcast_fusion
  1.5 3.3 %collective-permute-start = (f32[5,32,1152]{2,1,0:T(8,128)S(1)}, f32[5,32,1152]{2,1,0:T(8,128)S(1)}, u32[]{:S(2)}, u32[]{:S(2)}) collective-permute-start(f32[5,32,1152]{2,1,0:T(8,128)S(1)} %pad_maximum_fusion), channel_id=1, source_target_pairs={{0,1},{1,0},{2,3},{3,2},{4,5},{5,4},{6,7},{7,6},{8,9},{9,8},{10,11... | collective-permute-start | bytes 2211848 | tf_op jit(solution)/shard_map/ppermute | solution.py:22
  5.1 1.6 %collective-permute-done.peer_ref = f32[5,32,1152]{2,1,0:T(8,128)S(1)} collective-permute-done((f32[5,32,1152]{2,1,0:T(8,128)S(1)}, f32[5,32,1152]{2,1,0:T(8,128)S(1)}, u32[]{:S(2)}, u32[]{:S(2)}) %collective-permute-start) | collective-permute-done | bytes 737312 | tf_op jit(solution)/shard_map/ppermute | solution.py:22
  6.6 1.0 shard_map.91
  7.8 1.9 %collective-permute-start.2 = (bf16[64,1152]{1,0:T(8,128)(2,1)S(1)}, bf16[64,1152]{1,0:T(8,128)(2,1)S(1)}, u32[]{:S(2)}, u32[]{:S(2)}) collective-permute-start(bf16[64,1152]{1,0:T(8,128)(2,1)S(1)} %get-tuple-element.40), channel_id=1, source_target_pairs={{0,4},{2,6},{4,0},{6,2},{1,5},{3,7},{5,1},{7,3},{8,12},{10,14},{12... | collective-permute-start | bytes 442376 | tf_op jit(solution)/shard_map/ppermute | solution.py:22
  9.7 1.2 collective-permute-start.3
  10.9 3.3 %copy-done.1 = bf16[1152,3456]{1,0:T(8,128)(2,1)S(1)} copy-done((bf16[1152,3456]{1,0:T(8,128)(2,1)S(1)}, bf16[1152,3456]{1,0:T(8,128)(2,1)}, u32[]{:S(2)}) %copy-start.1) | copy-done | bytes 7962648
  14.1 1.4 %shard_map.92.first_ref = bf16[64,3456]{1,0:T(8,128)(2,1)S(1)} custom-call(bf16[64,1152]{1,0:T(8,128)(2,1)S(1)} %get-tuple-element.38.a0, bf16[1152,3456]{1,0:T(8,128)(2,1)S(1)} %copy-done.1), custom_call_target="tpu_custom_call" | custom-call | tf_op jit(solution)/shard_map/pallas_call | solution.py:33
  15.6 1.3 collective-permute-start.7
  17.6 4.8 %shard_map.93 = (bf16[64,1152]{1,0:T(8,128)(2,1)S(1)}, bf16[64,1152]{1,0:T(8,128)(2,1)S(1)}, bf16[64,1152]{1,0:T(8,128)(2,1)S(1)}, bf16[256,3456]{1,0:T(8,128)(2,1)S(1)}) custom-call(bf16[64,3456]{1,0:T(8,128)(2,1)S(1)} %shard_map.92.first_ref, bf16[64,1152]{1,0:T(8,128)(2,1)S(1)} %collective-permute-done.1.a1, ...), custom_call_target="tpu_custom_call" | custom-call | tf_op jit(solution)/shard_map/pallas_call | solution.py:33
  22.4 3.4 %collective-permute-start.4 = (bf16[64,1152]{1,0:T(8,128)(2,1)S(1)}, bf16[64,1152]{1,0:T(8,128)(2,1)S(1)}, u32[]{:S(2)}, u32[]{:S(2)}) collective-permute-start(bf16[64,1152]{1,0:T(8,128)(2,1)S(1)} %get-tuple-element.43), channel_id=1, source_target_pairs={{0,6},{2,0},{4,2},{6,4},{1,7},{3,1},{5,3},{7,5},{8,14},{10,8},{12,... | collective-permute-start | bytes 442376 | tf_op jit(solution)/shard_map/ppermute | solution.py:22
  25.8 0.7 collective-permute-start.6
  26.5 3.2 %shard_map.94.a0 = bf16[64,1152]{1,0:T(8,128)(2,1)S(1)} custom-call(bf16[64,3456]{1,0:T(8,128)(2,1)S(1)} %shard_map.92.first_ref, bf16[256,3456]{1,0:T(8,128)(2,1)S(1)} %get-tuple-element.42.qkv_ref, bf16[16,1152]{1,0:T(8,128)(2,1)S(1)} %fusion.1.mask_ref), custom_call_target="tpu_custom_call" | custom-call | tf_op jit(solution)/shard_map/pallas_call | solution.py:33
  29.7 0.8 shard_map.95.base_ref
  30.4 1.3 collective-permute-done.4.a1
  32.0 3.6 %collective-permute-done.6.a3 = bf16[64,1152]{1,0:T(8,128)(2,1)S(1)} collective-permute-done((bf16[64,1152]{1,0:T(8,128)(2,1)S(1)}, bf16[64,1152]{1,0:T(8,128)(2,1)S(1)}, u32[]{:S(2)}, u32[]{:S(2)}) %collective-permute-start.6) | collective-permute-done | bytes 147488 | tf_op jit(solution)/shard_map/ppermute | solution.py:22
  35.6 1.6 %shard_map.96 = (f32[4,32,1152]{2,1,0:T(8,128)S(1)}, f32[4,32,1152]{2,1,0:T(8,128)S(1)}, f32[8,8,1152]{2,1,0:T(8,128)S(1)}) custom-call(s32[7]{0:T(128)S(1)} %pad_add_fusion.where_ref, f32[3,4]{1,0:T(4,128)S(1)} %pad_maximum_fusion.1.coef_ref, bf16[64,1152]{1,0:T(8,128)(2,1)S(1)} %shard_map.94.a0, bf16[64,1152]{1,0:T(8,128)(2,1)S(1)} %collective-permute-done.4.a1, ...), custom_call_target="tpu_custom_call" | custom-call | tf_op jit(solution)/shard_map/pallas_call | solution.py:33
  37.3 9.6 %all_to_all.20.held_ref = f32[8,8,1152]{2,1,0:T(8,128)S(1)} all-to-all(f32[8,8,1152]{2,1,0:T(8,128)S(1)} %get-tuple-element.50), channel_id=1, replica_groups=mesh['w'=2,'v'=2,'u'=2,'y'=4,'x'=4,'c'=2] {'u','y'}, dimensions={0} | all-to-all | bytes 589824 | tf_op jit(solution)/shard_map/all_to_all | solution.py:232
  46.9 3.1 %collective-permute-start.8 = (f32[8,1152]{1,0:T(8,128)S(1)}, f32[8,1152]{1,0:T(8,128)S(1)}, u32[]{:S(2)}, u32[]{:S(2)}) collective-permute-start(f32[8,1152]{1,0:T(8,128)S(1)} %get-tuple-element.52), channel_id=1, source_target_pairs={{0,64},{64,128},{128,192},{192,0},{1,65},{65,129},{129,193},{193,1... | collective-permute-start | bytes 110600 | tf_op jit(solution)/shard_map/ppermute | solution.py:22
  50.0 4.2 %collective-permute-start.9 = (f32[8,1152]{1,0:T(8,128)S(1)}, f32[8,1152]{1,0:T(8,128)S(1)}, u32[]{:S(2)}, u32[]{:S(2)}) collective-permute-start(f32[8,1152]{1,0:T(8,128)S(1)} %get-tuple-element.52), channel_id=1, source_target_pairs={{0,128},{64,192},{128,0},{192,64},{1,129},{65,193},{129,1},{193,65... | collective-permute-start | bytes 110600 | tf_op jit(solution)/shard_map/ppermute | solution.py:22
  54.2 2.4 %collective-permute-start.10 = (f32[8,1152]{1,0:T(8,128)S(1)}, f32[8,1152]{1,0:T(8,128)S(1)}, u32[]{:S(2)}, u32[]{:S(2)}) collective-permute-start(f32[8,1152]{1,0:T(8,128)S(1)} %get-tuple-element.52), channel_id=1, source_target_pairs={{0,192},{64,0},{128,64},{192,128},{1,193},{65,1},{129,65},{193,129... | collective-permute-start | bytes 110600 | tf_op jit(solution)/shard_map/ppermute | solution.py:22
  57.1 1.3 collective-permute-done.10.refs_2_
  58.9 9.1 %all_to_all.21.lower_ref = f32[8,8,1152]{2,1,0:T(8,128)S(1)} all-to-all(f32[8,8,1152]{2,1,0:T(8,128)S(1)} %shard_map.98), channel_id=1, replica_groups=mesh['w'=2,'v'=2,'u'=2,'y'=4,'x'=4,'c'=2] {'u','y'}, dimensions={0} | all-to-all | bytes 589824 | tf_op jit(solution)/shard_map/all_to_all | solution.py:239
  68.1 1.1 shard_map.99
  69.3 1.6 %collective-permute-start.12 = (bf16[64,1152]{1,0:T(8,128)(2,1)S(1)}, bf16[64,1152]{1,0:T(8,128)(2,1)S(1)}, u32[]{:S(2)}, u32[]{:S(2)}) collective-permute-start(bf16[64,1152]{1,0:T(8,128)(2,1)S(1)} %get-tuple-element.55), channel_id=1, source_target_pairs={{0,4},{2,6},{4,0},{6,2},{1,5},{3,7},{5,1},{7,3},{8,12},{10,14},{12... | collective-permute-start | bytes 442376 | tf_op jit(solution)/shard_map/ppermute | solution.py:22
  70.9 2.0 %collective-permute-start.13 = (bf16[64,1152]{1,0:T(8,128)(2,1)S(1)}, bf16[64,1152]{1,0:T(8,128)(2,1)S(1)}, u32[]{:S(2)}, u32[]{:S(2)}) collective-permute-start(bf16[64,1152]{1,0:T(8,128)(2,1)S(1)} %get-tuple-element.56), channel_id=1, source_target_pairs={{0,6},{2,0},{4,2},{6,4},{1,7},{3,1},{5,3},{7,5},{8,14},{10,8},{12,... | collective-permute-start | bytes 442376 | tf_op jit(solution)/shard_map/ppermute | solution.py:22
  72.9 1.3 shard_map.100.first_ref
  74.2 1.8 %collective-permute-done.11.a1 = bf16[64,1152]{1,0:T(8,128)(2,1)S(1)} collective-permute-done((bf16[64,1152]{1,0:T(8,128)(2,1)S(1)}, bf16[64,1152]{1,0:T(8,128)(2,1)S(1)}, u32[]{:S(2)}, u32[]{:S(2)}) %collective-permute-start.11) | collective-permute-done | bytes 147488 | tf_op jit(solution)/shard_map/ppermute | solution.py:22
  76.0 0.6 collective-permute-done.13.a3
  76.6 4.8 %shard_map.101 = (bf16[64,1152]{1,0:T(8,128)(2,1)S(1)}, bf16[64,1152]{1,0:T(8,128)(2,1)S(1)}, bf16[64,1152]{1,0:T(8,128)(2,1)S(1)}, bf16[256,3456]{1,0:T(8,128)(2,1)S(1)}) custom-call(bf16[64,3456]{1,0:T(8,128)(2,1)S(1)} %shard_map.100.first_ref, bf16[64,1152]{1,0:T(8,128)(2,1)S(1)} %collective-permute-done.11.a1, ...), custom_call_target="tpu_custom_call" | custom-call | tf_op jit(solution)/shard_map/pallas_call | solution.py:33
  81.4 2.5 %collective-permute-start.14 = (bf16[64,1152]{1,0:T(8,128)(2,1)S(1)}, bf16[64,1152]{1,0:T(8,128)(2,1)S(1)}, u32[]{:S(2)}, u32[]{:S(2)}) collective-permute-start(bf16[64,1152]{1,0:T(8,128)(2,1)S(1)} %get-tuple-element.58), channel_id=1, source_target_pairs={{0,6},{2,0},{4,2},{6,4},{1,7},{3,1},{5,3},{7,5},{8,14},{10,8},{12,... | collective-permute-start | bytes 442376 | tf_op jit(solution)/shard_map/ppermute | solution.py:22
  83.9 0.6 collective-permute-start.15
  84.6 0.7 shard_map.103.base_ref
  85.3 3.2 %shard_map.102.a0 = bf16[64,1152]{1,0:T(8,128)(2,1)S(1)} custom-call(bf16[64,3456]{1,0:T(8,128)(2,1)S(1)} %shard_map.100.first_ref, bf16[256,3456]{1,0:T(8,128)(2,1)S(1)} %get-tuple-element.57.qkv_ref, bf16[16,1152]{1,0:T(8,128)(2,1)S(1)} %fusion.1.mask_ref), custom_call_target="tpu_custom_call" | custom-call | tf_op jit(solution)/shard_map/pallas_call | solution.py:33
  88.5 1.0 collective-permute-done.15.a2
  89.5 1.5 %collective-permute-done.16.a3 = bf16[64,1152]{1,0:T(8,128)(2,1)S(1)} collective-permute-done((bf16[64,1152]{1,0:T(8,128)(2,1)S(1)}, bf16[64,1152]{1,0:T(8,128)(2,1)S(1)}, u32[]{:S(2)}, u32[]{:S(2)}) %collective-permute-start.16) | collective-permute-done | bytes 147488 | tf_op jit(solution)/shard_map/ppermute | solution.py:22
  91.0 1.6 %shard_map.104 = (f32[4,32,1152]{2,1,0:T(8,128)S(1)}, f32[4,32,1152]{2,1,0:T(8,128)S(1)}, f32[8,8,1152]{2,1,0:T(8,128)S(1)}) custom-call(s32[7]{0:T(128)S(1)} %pad_add_fusion.where_ref, f32[3,4]{1,0:T(4,128)S(1)} %pad_maximum_fusion.1.coef_ref, bf16[64,1152]{1,0:T(8,128)(2,1)S(1)} %shard_map.102.a0, bf16[64,1152]{1,0:T(8,128)(2,1)S(1)} %collective-permute-done.14.a1, ...), custom_call_target="tpu_custom_call" | custom-call | tf_op jit(solution)/shard_map/pallas_call | solution.py:33
  92.6 8.0 %collective-permute-start.18 = (f32[4,32,1152]{2,1,0:T(8,128)S(1)}, f32[4,32,1152]{2,1,0:T(8,128)S(1)}, u32[]{:S(2)}, u32[]{:S(2)}) collective-permute-start(f32[4,32,1152]{2,1,0:T(8,128)S(1)} %get-tuple-element.65), channel_id=1, source_target_pairs={{0,1},{1,0},{2,3},{3,2},{4,5},{5,4},{6,7},{7,6},{8,9},{9,8},{10,11... | collective-permute-start | bytes 1769480 | tf_op jit(solution)/shard_map/ppermute | solution.py:22
  100.6 10.0 %all_to_all.22.held_ref = f32[8,8,1152]{2,1,0:T(8,128)S(1)} all-to-all(f32[8,8,1152]{2,1,0:T(8,128)S(1)} %get-tuple-element.63), channel_id=1, replica_groups=mesh['w'=2,'v'=2,'u'=2,'y'=4,'x'=4,'c'=2] {'u','y'}, dimensions={0} | all-to-all | bytes 589824 | tf_op jit(solution)/shard_map/all_to_all | solution.py:232
  110.6 1.6 %collective-permute-start.17 = (f32[8,1152]{1,0:T(8,128)S(1)}, f32[8,1152]{1,0:T(8,128)S(1)}, u32[]{:S(2)}, u32[]{:S(2)}) collective-permute-start(f32[8,1152]{1,0:T(8,128)S(1)} %get-tuple-element.64), channel_id=1, source_target_pairs={{0,64},{64,128},{128,192},{192,0},{1,65},{65,129},{129,193},{193,1... | collective-permute-start | bytes 110600 | tf_op jit(solution)/shard_map/ppermute | solution.py:22
  112.2 4.0 %collective-permute-start.19 = (f32[8,1152]{1,0:T(8,128)S(1)}, f32[8,1152]{1,0:T(8,128)S(1)}, u32[]{:S(2)}, u32[]{:S(2)}) collective-permute-start(f32[8,1152]{1,0:T(8,128)S(1)} %get-tuple-element.64), channel_id=1, source_target_pairs={{0,128},{64,192},{128,0},{192,64},{1,129},{65,193},{129,1},{193,65... | collective-permute-start | bytes 110600 | tf_op jit(solution)/shard_map/ppermute | solution.py:22
  116.3 0.6 collective-permute-start.20
  116.9 2.5 %collective-permute-done.19.refs_1_ = f32[8,1152]{1,0:T(8,128)S(1)} collective-permute-done((f32[8,1152]{1,0:T(8,128)S(1)}, f32[8,1152]{1,0:T(8,128)S(1)}, u32[]{:S(2)}, u32[]{:S(2)}) %collective-permute-start.19) | collective-permute-done | bytes 36896 | tf_op jit(solution)/shard_map/ppermute | solution.py:22
  119.4 1.3 collective-permute-done.20.refs_2_
  121.3 8.9 %all_to_all.23.mine_lower = f32[8,8,1152]{2,1,0:T(8,128)S(1)} all-to-all(f32[8,8,1152]{2,1,0:T(8,128)S(1)} %shard_map.106), channel_id=1, replica_groups=mesh['w'=2,'v'=2,'u'=2,'y'=4,'x'=4,'c'=2] {'u','y'}, dimensions={0} | all-to-all | bytes 589824 | tf_op jit(solution)/shard_map/all_to_all | solution.py:239
  130.2 3.6 %collective-permute-start.21 = (f32[8,8,1152]{2,1,0:T(8,128)S(1)}, f32[8,8,1152]{2,1,0:T(8,128)S(1)}, u32[]{:S(2)}, u32[]{:S(2)}) collective-permute-start(f32[8,8,1152]{2,1,0:T(8,128)S(1)} %all_to_all.23.mine_lower), channel_id=1, source_target_pairs={{0,1},{1,0},{2,3},{3,2},{4,5},{5,4},{6,7},{7,6},{8,9},{9,8},{10,11... | collective-permute-start | bytes 884744 | tf_op jit(solution)/shard_map/ppermute | solution.py:22
  133.9 1.2 collective-permute-done.21.peer_lower
  135.1 1.6 %shard_map.107 = f32[4,2,32,1152]{3,2,1,0:T(8,128)} custom-call(s32[7]{0:T(128)S(1)} %pad_add_fusion.where_ref, f32[2,32,1152]{2,1,0:T(8,128)S(1)} %copy-done.4, f32[4,32,1152]{2,1,0:T(8,128)S(1)} %get-tuple-element.62.mine_before, f32[4,32,1152]{2,1,0:T(8,128)S(1)} %collective-permute-done.18.peer_before, f32[8,8,1152]{2,1,0:T(8,128)S(1)} %all_to_all.23.mine_lower, ...), custom_call_target="tpu_custom_call" | custom-call | tf_op jit(solution)/shard_map/pallas_call | solution.py:33
  (47 shorter events, 3.3 us)
Async XLA Ops:
  0.0 4.9 %copy-start = (s32[4,2]{0,1:T(2,128)S(1)}, s32[4,2]{0,1:T(2,128)}, u32[]{:S(2)}) copy-start(s32[4,2]{0,1:T(2,128)} %param.15) | copy-start | bytes 100
  0.0 1.4 %copy-start.4 = (f32[2,32,1152]{2,1,0:T(8,128)S(1)}, f32[2,32,1152]{2,1,0:T(8,128)}, u32[]{:S(2)}) copy-start(f32[2,32,1152]{2,1,0:T(8,128)} %start_ref.1) | copy-start | bytes 884740
  1.4 3.4 %copy-start.7 = (f32[4,3,1152]{2,0,1:T(4,128)S(1)}, f32[4,3,1152]{2,0,1:T(4,128)}, u32[]{:S(2)}) copy-start(f32[4,3,1152]{2,0,1:T(4,128)} %param.13) | copy-start | bytes 165892
  1.4 3.4 %copy-start.6 = (f32[8,3,1152]{2,0,1:T(8,128)S(1)}, f32[8,3,1152]{2,0,1:T(8,128)}, u32[]{:S(2)}) copy-start(f32[8,3,1152]{2,0,1:T(8,128)} %param.14) | copy-start | bytes 331780
  1.5 5.1 %collective-permute-start = (f32[5,32,1152]{2,1,0:T(8,128)S(1)}, f32[5,32,1152]{2,1,0:T(8,128)S(1)}, u32[]{:S(2)}, u32[]{:S(2)}) collective-permute-start(f32[5,32,1152]{2,1,0:T(8,128)S(1)} %pad_maximum_fusion), channel_id=1, source_target_pairs={{0,1},{1,0},{2,3},{3,2},{4,5},{5,4},{6,7},{7,6},{8,9},{9,8},{10,11... | collective-permute-start | bytes 2211848 | tf_op jit(solution)/shard_map/ppermute | solution.py:22
  7.7 9.2 %collective-permute-start.1 = (bf16[64,1152]{1,0:T(8,128)(2,1)S(1)}, bf16[64,1152]{1,0:T(8,128)(2,1)S(1)}, u32[]{:S(2)}, u32[]{:S(2)}) collective-permute-start(bf16[64,1152]{1,0:T(8,128)(2,1)S(1)} %get-tuple-element.39), channel_id=1, source_target_pairs={{0,2},{2,4},{4,6},{6,0},{1,3},{3,5},{5,7},{7,1},{8,10},{10,12},{12... | collective-permute-start | bytes 442376 | tf_op jit(solution)/shard_map/ppermute | solution.py:22
  7.8 9.2 %collective-permute-start.2 = (bf16[64,1152]{1,0:T(8,128)(2,1)S(1)}, bf16[64,1152]{1,0:T(8,128)(2,1)S(1)}, u32[]{:S(2)}, u32[]{:S(2)}) collective-permute-start(bf16[64,1152]{1,0:T(8,128)(2,1)S(1)} %get-tuple-element.40), channel_id=1, source_target_pairs={{0,4},{2,6},{4,0},{6,2},{1,5},{3,7},{5,1},{7,3},{8,12},{10,14},{12... | collective-permute-start | bytes 442376 | tf_op jit(solution)/shard_map/ppermute | solution.py:22
  9.7 7.8 %collective-permute-start.3 = (bf16[64,1152]{1,0:T(8,128)(2,1)S(1)}, bf16[64,1152]{1,0:T(8,128)(2,1)S(1)}, u32[]{:S(2)}, u32[]{:S(2)}) collective-permute-start(bf16[64,1152]{1,0:T(8,128)(2,1)S(1)} %get-tuple-element.41), channel_id=1, source_target_pairs={{0,6},{2,0},{4,2},{6,4},{1,7},{3,1},{5,3},{7,5},{8,14},{10,8},{12,... | collective-permute-start | bytes 442376 | tf_op jit(solution)/shard_map/ppermute | solution.py:22
  10.9 3.3 %copy-start.1 = (bf16[1152,3456]{1,0:T(8,128)(2,1)S(1)}, bf16[1152,3456]{1,0:T(8,128)(2,1)}, u32[]{:S(2)}) copy-start(bf16[1152,3456]{1,0:T(8,128)(2,1)} %w_ref.10) | copy-start | bytes 23887876
  14.1 1.4 %copy-start.5 = (bf16[4,2,32,1152]{3,2,1,0:T(8,128)(2,1)S(1)}, bf16[4,2,32,1152]{3,2,1,0:T(8,128)(2,1)}, u32[]{:S(2)}) copy-start(bf16[4,2,32,1152]{3,2,1,0:T(8,128)(2,1)} %param.10) | copy-start | bytes 1769476
  14.1 3.5 %copy-start.2 = (bf16[1152,3456]{1,0:T(8,128)(2,1)S(1)}, bf16[1152,3456]{1,0:T(8,128)(2,1)}, u32[]{:S(2)}) copy-start(bf16[1152,3456]{1,0:T(8,128)(2,1)} %w_ref.10) | copy-start | bytes 23887876
  15.6 10.9 %copy-start.8 = (s32[4]{0:T(128)S(1)}, s32[4]{0:T(128)}, u32[]{:S(2)}) copy-start(s32[4]{0:T(128)} %param.12) | copy-start | bytes 52
  15.6 14.1 %collective-permute-start.7 = (bf16[4,32,1152]{2,1,0:T(8,128)(2,1)S(1)}, bf16[4,32,1152]{2,1,0:T(8,128)(2,1)S(1)}, u32[]{:S(2)}, u32[]{:S(2)}) collective-permute-start(bf16[4,32,1152]{2,1,0:T(8,128)(2,1)S(1)} %get-tuple-element.71), channel_id=1, source_target_pairs={{0,1},{1,0},{2,3},{3,2},{4,5},{5,4},{6,7},{7,6},{8,9},{9,8},{10,11... | collective-permute-start | bytes 884744 | tf_op jit(solution)/shard_map/ppermute | solution.py:22
  22.4 9.4 %collective-permute-start.4 = (bf16[64,1152]{1,0:T(8,128)(2,1)S(1)}, bf16[64,1152]{1,0:T(8,128)(2,1)S(1)}, u32[]{:S(2)}, u32[]{:S(2)}) collective-permute-start(bf16[64,1152]{1,0:T(8,128)(2,1)S(1)} %get-tuple-element.43), channel_id=1, source_target_pairs={{0,6},{2,0},{4,2},{6,4},{1,7},{3,1},{5,3},{7,5},{8,14},{10,8},{12,... | collective-permute-start | bytes 442376 | tf_op jit(solution)/shard_map/ppermute | solution.py:22
  25.8 6.2 %collective-permute-start.5 = (bf16[64,1152]{1,0:T(8,128)(2,1)S(1)}, bf16[64,1152]{1,0:T(8,128)(2,1)S(1)}, u32[]{:S(2)}, u32[]{:S(2)}) collective-permute-start(bf16[64,1152]{1,0:T(8,128)(2,1)S(1)} %get-tuple-element.44), channel_id=1, source_target_pairs={{0,4},{2,6},{4,0},{6,2},{1,5},{3,7},{5,1},{7,3},{8,12},{10,14},{12... | collective-permute-start | bytes 442376 | tf_op jit(solution)/shard_map/ppermute | solution.py:22
  25.8 9.8 %collective-permute-start.6 = (bf16[64,1152]{1,0:T(8,128)(2,1)S(1)}, bf16[64,1152]{1,0:T(8,128)(2,1)S(1)}, u32[]{:S(2)}, u32[]{:S(2)}) collective-permute-start(bf16[64,1152]{1,0:T(8,128)(2,1)S(1)} %get-tuple-element.45), channel_id=1, source_target_pairs={{0,2},{2,4},{4,6},{6,0},{1,3},{3,5},{5,7},{7,1},{8,10},{10,12},{12... | collective-permute-start | bytes 442376 | tf_op jit(solution)/shard_map/ppermute | solution.py:22
  29.7 5.9 %copy-start.3 = (bf16[1152,1152]{1,0:T(8,128)(2,1)S(1)}, bf16[1152,1152]{1,0:T(8,128)(2,1)}, u32[]{:S(2)}) copy-start(bf16[1152,1152]{1,0:T(8,128)(2,1)} %w_ref.11) | copy-start | bytes 7962628
  46.9 9.7 %collective-permute-start.8 = (f32[8,1152]{1,0:T(8,128)S(1)}, f32[8,1152]{1,0:T(8,128)S(1)}, u32[]{:S(2)}, u32[]{:S(2)}) collective-permute-start(f32[8,1152]{1,0:T(8,128)S(1)} %get-tuple-element.52), channel_id=1, source_target_pairs={{0,64},{64,128},{128,192},{192,0},{1,65},{65,129},{129,193},{193,1... | collective-permute-start | bytes 110600 | tf_op jit(solution)/shard_map/ppermute | solution.py:22
  50.0 7.1 %collective-permute-start.9 = (f32[8,1152]{1,0:T(8,128)S(1)}, f32[8,1152]{1,0:T(8,128)S(1)}, u32[]{:S(2)}, u32[]{:S(2)}) collective-permute-start(f32[8,1152]{1,0:T(8,128)S(1)} %get-tuple-element.52), channel_id=1, source_target_pairs={{0,128},{64,192},{128,0},{192,64},{1,129},{65,193},{129,1},{193,65... | collective-permute-start | bytes 110600 | tf_op jit(solution)/shard_map/ppermute | solution.py:22
  54.2 4.2 %collective-permute-start.10 = (f32[8,1152]{1,0:T(8,128)S(1)}, f32[8,1152]{1,0:T(8,128)S(1)}, u32[]{:S(2)}, u32[]{:S(2)}) collective-permute-start(f32[8,1152]{1,0:T(8,128)S(1)} %get-tuple-element.52), channel_id=1, source_target_pairs={{0,192},{64,0},{128,64},{192,128},{1,193},{65,1},{129,65},{193,129... | collective-permute-start | bytes 110600 | tf_op jit(solution)/shard_map/ppermute | solution.py:22
  69.2 6.9 %collective-permute-start.11 = (bf16[64,1152]{1,0:T(8,128)(2,1)S(1)}, bf16[64,1152]{1,0:T(8,128)(2,1)S(1)}, u32[]{:S(2)}, u32[]{:S(2)}) collective-permute-start(bf16[64,1152]{1,0:T(8,128)(2,1)S(1)} %get-tuple-element.54), channel_id=1, source_target_pairs={{0,2},{2,4},{4,6},{6,0},{1,3},{3,5},{5,7},{7,1},{8,10},{10,12},{12... | collective-permute-start | bytes 442376 | tf_op jit(solution)/shard_map/ppermute | solution.py:22
  69.3 6.8 %collective-permute-start.12 = (bf16[64,1152]{1,0:T(8,128)(2,1)S(1)}, bf16[64,1152]{1,0:T(8,128)(2,1)S(1)}, u32[]{:S(2)}, u32[]{:S(2)}) collective-permute-start(bf16[64,1152]{1,0:T(8,128)(2,1)S(1)} %get-tuple-element.55), channel_id=1, source_target_pairs={{0,4},{2,6},{4,0},{6,2},{1,5},{3,7},{5,1},{7,3},{8,12},{10,14},{12... | collective-permute-start | bytes 442376 | tf_op jit(solution)/shard_map/ppermute | solution.py:22
  70.9 5.7 %collective-permute-start.13 = (bf16[64,1152]{1,0:T(8,128)(2,1)S(1)}, bf16[64,1152]{1,0:T(8,128)(2,1)S(1)}, u32[]{:S(2)}, u32[]{:S(2)}) collective-permute-start(bf16[64,1152]{1,0:T(8,128)(2,1)S(1)} %get-tuple-element.56), channel_id=1, source_target_pairs={{0,6},{2,0},{4,2},{6,4},{1,7},{3,1},{5,3},{7,5},{8,14},{10,8},{12,... | collective-permute-start | bytes 442376 | tf_op jit(solution)/shard_map/ppermute | solution.py:22
  81.4 7.1 %collective-permute-start.14 = (bf16[64,1152]{1,0:T(8,128)(2,1)S(1)}, bf16[64,1152]{1,0:T(8,128)(2,1)S(1)}, u32[]{:S(2)}, u32[]{:S(2)}) collective-permute-start(bf16[64,1152]{1,0:T(8,128)(2,1)S(1)} %get-tuple-element.58), channel_id=1, source_target_pairs={{0,6},{2,0},{4,2},{6,4},{1,7},{3,1},{5,3},{7,5},{8,14},{10,8},{12,... | collective-permute-start | bytes 442376 | tf_op jit(solution)/shard_map/ppermute | solution.py:22
  83.9 5.6 %collective-permute-start.15 = (bf16[64,1152]{1,0:T(8,128)(2,1)S(1)}, bf16[64,1152]{1,0:T(8,128)(2,1)S(1)}, u32[]{:S(2)}, u32[]{:S(2)}) collective-permute-start(bf16[64,1152]{1,0:T(8,128)(2,1)S(1)} %get-tuple-element.59), channel_id=1, source_target_pairs={{0,4},{2,6},{4,0},{6,2},{1,5},{3,7},{5,1},{7,3},{8,12},{10,14},{12... | collective-permute-start | bytes 442376 | tf_op jit(solution)/shard_map/ppermute | solution.py:22
  84.5 6.5 %collective-permute-start.16 = (bf16[64,1152]{1,0:T(8,128)(2,1)S(1)}, bf16[64,1152]{1,0:T(8,128)(2,1)S(1)}, u32[]{:S(2)}, u32[]{:S(2)}) collective-permute-start(bf16[64,1152]{1,0:T(8,128)(2,1)S(1)} %get-tuple-element.60), channel_id=1, source_target_pairs={{0,2},{2,4},{4,6},{6,0},{1,3},{3,5},{5,7},{7,1},{8,10},{10,12},{12... | collective-permute-start | bytes 442376 | tf_op jit(solution)/shard_map/ppermute | solution.py:22
  92.6 24.3 %collective-permute-start.18 = (f32[4,32,1152]{2,1,0:T(8,128)S(1)}, f32[4,32,1152]{2,1,0:T(8,128)S(1)}, u32[]{:S(2)}, u32[]{:S(2)}) collective-permute-start(f32[4,32,1152]{2,1,0:T(8,128)S(1)} %get-tuple-element.65), channel_id=1, source_target_pairs={{0,1},{1,0},{2,3},{3,2},{4,5},{5,4},{6,7},{7,6},{8,9},{9,8},{10,11... | collective-permute-start | bytes 1769480 | tf_op jit(solution)/shard_map/ppermute | solution.py:22
  110.6 6.3 %collective-permute-start.17 = (f32[8,1152]{1,0:T(8,128)S(1)}, f32[8,1152]{1,0:T(8,128)S(1)}, u32[]{:S(2)}, u32[]{:S(2)}) collective-permute-start(f32[8,1152]{1,0:T(8,128)S(1)} %get-tuple-element.64), channel_id=1, source_target_pairs={{0,64},{64,128},{128,192},{192,0},{1,65},{65,129},{129,193},{193,1... | collective-permute-start | bytes 110600 | tf_op jit(solution)/shard_map/ppermute | solution.py:22
  112.2 7.2 %collective-permute-start.19 = (f32[8,1152]{1,0:T(8,128)S(1)}, f32[8,1152]{1,0:T(8,128)S(1)}, u32[]{:S(2)}, u32[]{:S(2)}) collective-permute-start(f32[8,1152]{1,0:T(8,128)S(1)} %get-tuple-element.64), channel_id=1, source_target_pairs={{0,128},{64,192},{128,0},{192,64},{1,129},{65,193},{129,1},{193,65... | collective-permute-start | bytes 110600 | tf_op jit(solution)/shard_map/ppermute | solution.py:22
  116.3 4.5 %collective-permute-start.20 = (f32[8,1152]{1,0:T(8,128)S(1)}, f32[8,1152]{1,0:T(8,128)S(1)}, u32[]{:S(2)}, u32[]{:S(2)}) collective-permute-start(f32[8,1152]{1,0:T(8,128)S(1)} %get-tuple-element.64), channel_id=1, source_target_pairs={{0,192},{64,0},{128,64},{192,128},{1,193},{65,1},{129,65},{193,129... | collective-permute-start | bytes 110600 | tf_op jit(solution)/shard_map/ppermute | solution.py:22
  130.2 4.8 %collective-permute-start.21 = (f32[8,8,1152]{2,1,0:T(8,128)S(1)}, f32[8,8,1152]{2,1,0:T(8,128)S(1)}, u32[]{:S(2)}, u32[]{:S(2)}) collective-permute-start(f32[8,8,1152]{2,1,0:T(8,128)S(1)} %all_to_all.23.mine_lower), channel_id=1, source_target_pairs={{0,1},{1,0},{2,3},{3,2},{4,5},{5,4},{6,7},{7,6},{8,9},{9,8},{10,11... | collective-permute-start | bytes 884744 | tf_op jit(solution)/shard_map/ppermute | solution.py:22

commit v7 on v6

--- a/solution.py
+++ b/solution.py
@@ -215,15 +215,15 @@
     for q in range(held_ref.shape[0]):
         before_ref[q] = running
         running = running + held_ref[q]
-    all_ref[...] = running
-
-
-def below_body(where_ref, before_ref, *refs):
-    passed, out_ref = refs[:-1], refs[-1]
+    for g in range(all_ref.shape[0]):
+        all_ref[g] = running
+
+
+def below_body(where_ref, before_ref, totals_ref, out_ref):
     group = where_ref[1]
     below = jnp.zeros(before_ref.shape[1:], before_ref.dtype)
-    for shift, ref in enumerate(passed, 1):
-        below = below + jnp.where(shift <= group, ref[...], 0.0)
+    for g in range(totals_ref.shape[0] - 1):
+        below = below + jnp.where(g < group, totals_ref[g], 0.0)
     for q in range(before_ref.shape[0]):
         out_ref[q] = before_ref[q] + below
 
@@ -231,11 +231,12 @@
 def earlier_sum(where, shares, beside=None):
     held = lax.all_to_all(shares, SHARES, 0, 0, tiled=True)
     whole = jax.ShapeDtypeStruct(shares.shape, shares.dtype)
-    before, total = call(inside_body, [whole, jax.ShapeDtypeStruct(shares.shape[1:], shares.dtype)], [VMEM], held)
-    passed = spread([total] * (lax.axis_size(GROUPS) - 1), GROUPS)
+    copies = jax.ShapeDtypeStruct((lax.axis_size(GROUPS),) + shares.shape[1:], shares.dtype)
+    before, total = call(inside_body, [whole, copies], [VMEM], held)
+    totals = lax.all_to_all(total, GROUPS, 0, 0, tiled=True)
+    sums = call(below_body, whole, [SMEM] + [VMEM] * 2, where, before, totals)
     if beside is not None:
-        passed[0], beside = lax.optimization_barrier((passed[0], shifted(beside, "c", 1)))
-    sums = call(below_body, whole, [SMEM] + [VMEM] * (1 + len(passed)), where, before, *passed)
+        sums, beside = lax.optimization_barrier((sums, shifted(beside, "c", 1)))
     return lax.all_to_all(sums, SHARES, 0, 0, tiled=True), beside
 
 

time: 137 us -> 141 us (1.029)
  blocking collectives: 37.6 us -> 54.5 us
  starting transfers between devices: 46.2 us -> 37.3 us
  waiting for transfers between devices: 19 us -> 13.7 us
    all_to_all x0 -> x2, blocking collectives: none -> 24.8 us  [earlier_sum(): totals = lax.all_to_all(total, GROUPS, 0, 0, tiled=True)]
    ppermute x22 -> x16, starting transfers between devices: 46.2 us -> 33.8 us  [shifted(): lax.ppermute(value, axis, [(i, (i + shift) % size) for i in range(size)])]
    all_to_all x2 -> x1, blocking collectives: 19.6 us -> 9.6 us  [earlier_sum(): held = lax.all_to_all(shares, SHARES, 0, 0, tiled=True)]
    ppermute x22 -> x16, waiting for transfers between devices: 19 us -> 13.7 us  [shifted(): lax.ppermute(value, axis, [(i, (i + shift) % size) for i in range(size)])]
    all_to_all x0 -> x1, starting transfers between devices: none -> 3.42 us  [earlier_sum(): held = lax.all_to_all(shares, SHARES, 0, 0, tiled=True)]
    all_to_all x2, blocking collectives: 18.1 us -> 20.1 us  [earlier_sum(): return (lax.all_to_all(sums, SHARES, 0, 0, tiled=True), beside)]
  transfers between devices with their start and end apart: 22 -> 17, of which waited for: 14 -> 10; matrix products, arithmetic and copies ran while one was open for 0% -> 0% of each run, Pallas kernels for 11% -> 11%
where the time goes in v7:
time: 141 us; the launch traced here: 140 us
  blocking collectives  54.5 us (39%)
  starting transfers between devices  37.3 us (26%)
  Pallas kernels  29.2 us (21%)
  waiting for transfers between devices  13.7 us (10%)
  local copies, waits for them, and re-layouts  4.91 us (3%)
    ppermute x16, starting transfers between devices, shifted(): lax.ppermute(value, axis, [(i, (i + shift) % size) for i in range(size)])  33.8 us
    pallas_call x17, Pallas kernels, call(): pl.pallas_call(body, out_shape=outs, in_specs=specs, out_specs=jax.tree.m...  29.2 us
    all_to_all x2, blocking collectives, earlier_sum(): totals = lax.all_to_all(total, GROUPS, 0, 0, tiled=True)  24.8 us
    all_to_all x2, blocking collectives, earlier_sum(): return (lax.all_to_all(sums, SHARES, 0, 0, tiled=True), beside)  20.1 us
    ppermute x16, waiting for transfers between devices, shifted(): lax.ppermute(value, axis, [(i, (i + shift) % size) for i in range(size)])  13.7 us
    all_to_all x1, blocking collectives, earlier_sum(): held = lax.all_to_all(shares, SHARES, 0, 0, tiled=True)  9.6 us
    unnamed x20, local copies, waits for them, and re-layouts  3.45 us
    all_to_all x1, starting transfers between devices, earlier_sum(): held = lax.all_to_all(shares, SHARES, 0, 0, tiled=True)  3.42 us
  transfers between devices with their start and end apart: 17, of which 10 were waited for; matrix products, arithmetic and copies ran while one was open for 0% of the time, Pallas kernels for 11%

profile of v7, /device:TPU:1, one launch (start us, length us, event | category | flops | bytes accessed | tf_op | source)
XLA Modules:
  0.0 140.3 jit_solution(16040277153721404931)
XLA Ops:
  0.0 1.4 dynamic-slice_bitcast_fusion
  1.5 3.3 %collective-permute-start = (f32[5,32,1152]{2,1,0:T(8,128)S(1)}, f32[5,32,1152]{2,1,0:T(8,128)S(1)}, u32[]{:S(2)}, u32[]{:S(2)}) collective-permute-start(f32[5,32,1152]{2,1,0:T(8,128)S(1)} %pad_maximum_fusion), channel_id=1, source_target_pairs={{0,1},{1,0},{2,3},{3,2},{4,5},{5,4},{6,7},{7,6},{8,9},{9,8},{10,11... | collective-permute-start | bytes 2211848 | tf_op jit(solution)/shard_map/ppermute | solution.py:22
  5.0 0.1 fusion.1.mask_ref
  5.1 1.6 %collective-permute-done.peer_ref = f32[5,32,1152]{2,1,0:T(8,128)S(1)} collective-permute-done((f32[5,32,1152]{2,1,0:T(8,128)S(1)}, f32[5,32,1152]{2,1,0:T(8,128)S(1)}, u32[]{:S(2)}, u32[]{:S(2)}) %collective-permute-start) | collective-permute-done | bytes 737312 | tf_op jit(solution)/shard_map/ppermute | solution.py:22
  6.6 1.0 shard_map.91
  7.8 1.9 %collective-permute-start.2 = (bf16[64,1152]{1,0:T(8,128)(2,1)S(1)}, bf16[64,1152]{1,0:T(8,128)(2,1)S(1)}, u32[]{:S(2)}, u32[]{:S(2)}) collective-permute-start(bf16[64,1152]{1,0:T(8,128)(2,1)S(1)} %get-tuple-element.40), channel_id=1, source_target_pairs={{0,4},{2,6},{4,0},{6,2},{1,5},{3,7},{5,1},{7,3},{8,12},{10,14},{12... | collective-permute-start | bytes 442376 | tf_op jit(solution)/shard_map/ppermute | solution.py:22
  9.7 1.2 collective-permute-start.3
  10.9 3.3 %copy-done.1 = bf16[1152,3456]{1,0:T(8,128)(2,1)S(1)} copy-done((bf16[1152,3456]{1,0:T(8,128)(2,1)S(1)}, bf16[1152,3456]{1,0:T(8,128)(2,1)}, u32[]{:S(2)}) %copy-start.1) | copy-done | bytes 7962648
  14.1 1.4 shard_map.92.first_ref
  15.6 1.3 collective-permute-start.7
  16.9 0.6 collective-permute-done.3.a3
  17.5 0.1 copy-done.2
  17.6 4.8 %shard_map.93 = (bf16[64,1152]{1,0:T(8,128)(2,1)S(1)}, bf16[64,1152]{1,0:T(8,128)(2,1)S(1)}, bf16[64,1152]{1,0:T(8,128)(2,1)S(1)}, bf16[256,3456]{1,0:T(8,128)(2,1)S(1)}) custom-call(bf16[64,3456]{1,0:T(8,128)(2,1)S(1)} %shard_map.92.first_ref, bf16[64,1152]{1,0:T(8,128)(2,1)S(1)} %collective-permute-done.1.a1, ...), custom_call_target="tpu_custom_call" | custom-call | tf_op jit(solution)/shard_map/pallas_call | solution.py:33
  22.4 3.4 %collective-permute-start.4 = (bf16[64,1152]{1,0:T(8,128)(2,1)S(1)}, bf16[64,1152]{1,0:T(8,128)(2,1)S(1)}, u32[]{:S(2)}, u32[]{:S(2)}) collective-permute-start(bf16[64,1152]{1,0:T(8,128)(2,1)S(1)} %get-tuple-element.43), channel_id=1, source_target_pairs={{0,6},{2,0},{4,2},{6,4},{1,7},{3,1},{5,3},{7,5},{8,14},{10,8},{12,... | collective-permute-start | bytes 442376 | tf_op jit(solution)/shard_map/ppermute | solution.py:22
  25.8 0.7 collective-permute-start.6
  26.5 3.2 %shard_map.94.a0 = bf16[64,1152]{1,0:T(8,128)(2,1)S(1)} custom-call(bf16[64,3456]{1,0:T(8,128)(2,1)S(1)} %shard_map.92.first_ref, bf16[256,3456]{1,0:T(8,128)(2,1)S(1)} %get-tuple-element.42.qkv_ref, bf16[16,1152]{1,0:T(8,128)(2,1)S(1)} %fusion.1.mask_ref), custom_call_target="tpu_custom_call" | custom-call | tf_op jit(solution)/shard_map/pallas_call | solution.py:33
  29.7 0.8 shard_map.95.base_ref
  30.4 1.3 collective-permute-done.4.a1
  31.8 0.2 collective-permute-done.5.a2
  32.0 3.6 %collective-permute-done.6.a3 = bf16[64,1152]{1,0:T(8,128)(2,1)S(1)} collective-permute-done((bf16[64,1152]{1,0:T(8,128)(2,1)S(1)}, bf16[64,1152]{1,0:T(8,128)(2,1)S(1)}, u32[]{:S(2)}, u32[]{:S(2)}) %collective-permute-start.6) | collective-permute-done | bytes 147488 | tf_op jit(solution)/shard_map/ppermute | solution.py:22
  35.6 1.6 %shard_map.96 = (f32[4,32,1152]{2,1,0:T(8,128)S(1)}, f32[4,32,1152]{2,1,0:T(8,128)S(1)}, f32[8,8,1152]{2,1,0:T(8,128)S(1)}) custom-call(s32[7]{0:T(128)S(1)} %pad_add_fusion.where_ref, f32[3,4]{1,0:T(4,128)S(1)} %pad_maximum_fusion.1.coef_ref, bf16[64,1152]{1,0:T(8,128)(2,1)S(1)} %shard_map.94.a0, bf16[64,1152]{1,0:T(8,128)(2,1)S(1)} %collective-permute-done.4.a1, ...), custom_call_target="tpu_custom_call" | custom-call | tf_op jit(solution)/shard_map/pallas_call | solution.py:33
  37.3 9.6 %all_to_all.30.held_ref = f32[8,8,1152]{2,1,0:T(8,128)S(1)} all-to-all(f32[8,8,1152]{2,1,0:T(8,128)S(1)} %get-tuple-element.50), channel_id=1, replica_groups=mesh['w'=2,'v'=2,'u'=2,'y'=4,'x'=4,'c'=2] {'u','y'}, dimensions={0} | all-to-all | bytes 589824 | tf_op jit(solution)/shard_map/all_to_all | solution.py:232
  46.9 14.4 %all_to_all.31.totals_ref = f32[4,8,1152]{2,1,0:T(8,128)S(1)} all-to-all(f32[4,8,1152]{2,1,0:T(8,128)S(1)} %get-tuple-element.52), channel_id=1, replica_groups=mesh['w'=2,'v'=2,'u'=2,'y'=4,'x'=4,'c'=2] {'w','v'}, dimensions={0} | all-to-all | bytes 294912 | tf_op jit(solution)/shard_map/all_to_all | solution.py:236
  61.3 0.6 shard_map.98
  61.9 9.2 %all_to_all.32.lower_ref = f32[8,8,1152]{2,1,0:T(8,128)S(1)} all-to-all(f32[8,8,1152]{2,1,0:T(8,128)S(1)} %shard_map.98), channel_id=1, replica_groups=mesh['w'=2,'v'=2,'u'=2,'y'=4,'x'=4,'c'=2] {'u','y'}, dimensions={0} | all-to-all | bytes 589824 | tf_op jit(solution)/shard_map/all_to_all | solution.py:240
  71.1 1.1 shard_map.99
  72.3 1.4 collective-permute-start.9
  73.7 2.0 %collective-permute-start.10 = (bf16[64,1152]{1,0:T(8,128)(2,1)S(1)}, bf16[64,1152]{1,0:T(8,128)(2,1)S(1)}, u32[]{:S(2)}, u32[]{:S(2)}) collective-permute-start(bf16[64,1152]{1,0:T(8,128)(2,1)S(1)} %get-tuple-element.56), channel_id=1, source_target_pairs={{0,6},{2,0},{4,2},{6,4},{1,7},{3,1},{5,3},{7,5},{8,14},{10,8},{12,... | collective-permute-start | bytes 442376 | tf_op jit(solution)/shard_map/ppermute | solution.py:22
  75.7 1.3 shard_map.100.first_ref
  77.0 2.1 %collective-permute-done.8.a1 = bf16[64,1152]{1,0:T(8,128)(2,1)S(1)} collective-permute-done((bf16[64,1152]{1,0:T(8,128)(2,1)S(1)}, bf16[64,1152]{1,0:T(8,128)(2,1)S(1)}, u32[]{:S(2)}, u32[]{:S(2)}) %collective-permute-start.8) | collective-permute-done | bytes 147488 | tf_op jit(solution)/shard_map/ppermute | solution.py:22
  79.1 0.6 collective-permute-done.10.a3
  79.7 4.8 %shard_map.101 = (bf16[64,1152]{1,0:T(8,128)(2,1)S(1)}, bf16[64,1152]{1,0:T(8,128)(2,1)S(1)}, bf16[64,1152]{1,0:T(8,128)(2,1)S(1)}, bf16[256,3456]{1,0:T(8,128)(2,1)S(1)}) custom-call(bf16[64,3456]{1,0:T(8,128)(2,1)S(1)} %shard_map.100.first_ref, bf16[64,1152]{1,0:T(8,128)(2,1)S(1)} %collective-permute-done.8.a1, ...), custom_call_target="tpu_custom_call" | custom-call | tf_op jit(solution)/shard_map/pallas_call | solution.py:33
  84.5 2.5 %collective-permute-start.11 = (bf16[64,1152]{1,0:T(8,128)(2,1)S(1)}, bf16[64,1152]{1,0:T(8,128)(2,1)S(1)}, u32[]{:S(2)}, u32[]{:S(2)}) collective-permute-start(bf16[64,1152]{1,0:T(8,128)(2,1)S(1)} %get-tuple-element.58), channel_id=1, source_target_pairs={{0,6},{2,0},{4,2},{6,4},{1,7},{3,1},{5,3},{7,5},{8,14},{10,8},{12,... | collective-permute-start | bytes 442376 | tf_op jit(solution)/shard_map/ppermute | solution.py:22
  87.0 0.4 collective-permute-start.12
  87.4 0.3 collective-permute-start.13
  87.7 0.7 shard_map.103.base_ref
  88.4 3.2 %shard_map.102.a0 = bf16[64,1152]{1,0:T(8,128)(2,1)S(1)} custom-call(bf16[64,3456]{1,0:T(8,128)(2,1)S(1)} %shard_map.100.first_ref, bf16[256,3456]{1,0:T(8,128)(2,1)S(1)} %get-tuple-element.57.qkv_ref, bf16[16,1152]{1,0:T(8,128)(2,1)S(1)} %fusion.1.mask_ref), custom_call_target="tpu_custom_call" | custom-call | tf_op jit(solution)/shard_map/pallas_call | solution.py:33
  91.6 1.0 collective-permute-done.12.a2
  92.6 1.5 %collective-permute-done.13.a3 = bf16[64,1152]{1,0:T(8,128)(2,1)S(1)} collective-permute-done((bf16[64,1152]{1,0:T(8,128)(2,1)S(1)}, bf16[64,1152]{1,0:T(8,128)(2,1)S(1)}, u32[]{:S(2)}, u32[]{:S(2)}) %collective-permute-start.13) | collective-permute-done | bytes 147488 | tf_op jit(solution)/shard_map/ppermute | solution.py:22
  94.1 2.4 %shard_map.104 = (f32[4,32,1152]{2,1,0:T(8,128)S(1)}, f32[4,32,1152]{2,1,0:T(8,128)S(1)}, f32[8,8,1152]{2,1,0:T(8,128)}) custom-call(s32[7]{0:T(128)S(1)} %pad_add_fusion.where_ref, f32[3,4]{1,0:T(4,128)S(1)} %pad_maximum_fusion.1.coef_ref, bf16[64,1152]{1,0:T(8,128)(2,1)S(1)} %shard_map.102.a0, bf16[64,1152]{1,0:T(8,128)(2,1)S(1)} %collective-permute-done.11.a1, ...), custom_call_target="tpu_custom_call" | custom-call | tf_op jit(solution)/shard_map/pallas_call | solution.py:33
  96.4 3.4 %all-to-all-start.3 = ((f32[8,8,1152]{2,1,0:T(8,128)}), f32[8,8,1152]{2,1,0:T(8,128)S(1)}, u32[]{:S(2)}, u32[]{:S(2)}) async-start(f32[8,8,1152]{2,1,0:T(8,128)} %get-tuple-element.63), calls=%async_computation.3 | async-start | bytes 589824 | tf_op jit(solution)/shard_map/all_to_all | solution.py:232
  99.9 8.1 %collective-permute-start.14 = (f32[4,32,1152]{2,1,0:T(8,128)S(1)}, f32[4,32,1152]{2,1,0:T(8,128)S(1)}, u32[]{:S(2)}, u32[]{:S(2)}) collective-permute-start(f32[4,32,1152]{2,1,0:T(8,128)S(1)} %get-tuple-element.66), channel_id=1, source_target_pairs={{0,1},{1,0},{2,3},{3,2},{4,5},{5,4},{6,7},{7,6},{8,9},{9,8},{10,11... | collective-permute-start | bytes 1769480 | tf_op jit(solution)/shard_map/ppermute | solution.py:22
  108.0 10.4 %all_to_all.33.totals_ref = f32[4,8,1152]{2,1,0:T(8,128)S(1)} all-to-all(f32[4,8,1152]{2,1,0:T(8,128)S(1)} %get-tuple-element.65), channel_id=1, replica_groups=mesh['w'=2,'v'=2,'u'=2,'y'=4,'x'=4,'c'=2] {'w','v'}, dimensions={0} | all-to-all | bytes 294912 | tf_op jit(solution)/shard_map/all_to_all | solution.py:236
  118.4 0.6 shard_map.106
  118.9 10.9 %all_to_all.34.mine_lower = f32[8,8,1152]{2,1,0:T(8,128)S(1)} all-to-all(f32[8,8,1152]{2,1,0:T(8,128)S(1)} %shard_map.106), channel_id=1, replica_groups=mesh['w'=2,'v'=2,'u'=2,'y'=4,'x'=4,'c'=2] {'u','y'}, dimensions={0} | all-to-all | bytes 589824 | tf_op jit(solution)/shard_map/all_to_all | solution.py:240
  129.8 7.4 %collective-permute-start.15 = (f32[8,8,1152]{2,1,0:T(8,128)S(1)}, f32[8,8,1152]{2,1,0:T(8,128)S(1)}, u32[]{:S(2)}, u32[]{:S(2)}) collective-permute-start(f32[8,8,1152]{2,1,0:T(8,128)S(1)} %all_to_all.34.mine_lower), channel_id=1, source_target_pairs={{0,1},{1,0},{2,3},{3,2},{4,5},{5,4},{6,7},{7,6},{8,9},{9,8},{10,11... | collective-permute-start | bytes 884744 | tf_op jit(solution)/shard_map/ppermute | solution.py:22
  137.2 1.2 collective-permute-done.15.peer_lower
  138.4 1.6 %shard_map.107 = f32[4,2,32,1152]{3,2,1,0:T(8,128)} custom-call(s32[7]{0:T(128)S(1)} %pad_add_fusion.where_ref, f32[2,32,1152]{2,1,0:T(8,128)S(1)} %copy-done.4, f32[4,32,1152]{2,1,0:T(8,128)S(1)} %get-tuple-element.62.mine_before, f32[4,32,1152]{2,1,0:T(8,128)S(1)} %collective-permute-done.14.peer_before, f32[8,8,1152]{2,1,0:T(8,128)S(1)} %all_to_all.34.mine_lower, ...), custom_call_target="tpu_custom_call" | custom-call | tf_op jit(solution)/shard_map/pallas_call | solution.py:33
  (38 shorter events, 0.6 us)
Async XLA Ops:
  0.0 4.9 %copy-start = (s32[4,2]{0,1:T(2,128)S(1)}, s32[4,2]{0,1:T(2,128)}, u32[]{:S(2)}) copy-start(s32[4,2]{0,1:T(2,128)} %param.15) | copy-start | bytes 100
  0.0 1.4 copy-start.4
  1.4 3.4 %copy-start.7 = (f32[4,3,1152]{2,0,1:T(4,128)S(1)}, f32[4,3,1152]{2,0,1:T(4,128)}, u32[]{:S(2)}) copy-start(f32[4,3,1152]{2,0,1:T(4,128)} %param.13) | copy-start | bytes 165892
  1.4 3.4 %copy-start.6 = (f32[8,3,1152]{2,0,1:T(8,128)S(1)}, f32[8,3,1152]{2,0,1:T(8,128)}, u32[]{:S(2)}) copy-start(f32[8,3,1152]{2,0,1:T(8,128)} %param.14) | copy-start | bytes 331780
  1.5 5.1 %collective-permute-start = (f32[5,32,1152]{2,1,0:T(8,128)S(1)}, f32[5,32,1152]{2,1,0:T(8,128)S(1)}, u32[]{:S(2)}, u32[]{:S(2)}) collective-permute-start(f32[5,32,1152]{2,1,0:T(8,128)S(1)} %pad_maximum_fusion), channel_id=1, source_target_pairs={{0,1},{1,0},{2,3},{3,2},{4,5},{5,4},{6,7},{7,6},{8,9},{9,8},{10,11... | collective-permute-start | bytes 2211848 | tf_op jit(solution)/shard_map/ppermute | solution.py:22
  7.7 9.2 %collective-permute-start.1 = (bf16[64,1152]{1,0:T(8,128)(2,1)S(1)}, bf16[64,1152]{1,0:T(8,128)(2,1)S(1)}, u32[]{:S(2)}, u32[]{:S(2)}) collective-permute-start(bf16[64,1152]{1,0:T(8,128)(2,1)S(1)} %get-tuple-element.39), channel_id=1, source_target_pairs={{0,2},{2,4},{4,6},{6,0},{1,3},{3,5},{5,7},{7,1},{8,10},{10,12},{12... | collective-permute-start | bytes 442376 | tf_op jit(solution)/shard_map/ppermute | solution.py:22
  7.8 9.2 %collective-permute-start.2 = (bf16[64,1152]{1,0:T(8,128)(2,1)S(1)}, bf16[64,1152]{1,0:T(8,128)(2,1)S(1)}, u32[]{:S(2)}, u32[]{:S(2)}) collective-permute-start(bf16[64,1152]{1,0:T(8,128)(2,1)S(1)} %get-tuple-element.40), channel_id=1, source_target_pairs={{0,4},{2,6},{4,0},{6,2},{1,5},{3,7},{5,1},{7,3},{8,12},{10,14},{12... | collective-permute-start | bytes 442376 | tf_op jit(solution)/shard_map/ppermute | solution.py:22
  9.7 7.8 %collective-permute-start.3 = (bf16[64,1152]{1,0:T(8,128)(2,1)S(1)}, bf16[64,1152]{1,0:T(8,128)(2,1)S(1)}, u32[]{:S(2)}, u32[]{:S(2)}) collective-permute-start(bf16[64,1152]{1,0:T(8,128)(2,1)S(1)} %get-tuple-element.41), channel_id=1, source_target_pairs={{0,6},{2,0},{4,2},{6,4},{1,7},{3,1},{5,3},{7,5},{8,14},{10,8},{12,... | collective-permute-start | bytes 442376 | tf_op jit(solution)/shard_map/ppermute | solution.py:22
  10.9 3.3 %copy-start.1 = (bf16[1152,3456]{1,0:T(8,128)(2,1)S(1)}, bf16[1152,3456]{1,0:T(8,128)(2,1)}, u32[]{:S(2)}) copy-start(bf16[1152,3456]{1,0:T(8,128)(2,1)} %w_ref.10) | copy-start | bytes 23887876
  14.1 1.4 copy-start.5
  14.1 3.5 %copy-start.2 = (bf16[1152,3456]{1,0:T(8,128)(2,1)S(1)}, bf16[1152,3456]{1,0:T(8,128)(2,1)}, u32[]{:S(2)}) copy-start(bf16[1152,3456]{1,0:T(8,128)(2,1)} %w_ref.10) | copy-start | bytes 23887876
  15.6 10.9 %copy-start.8 = (s32[4]{0:T(128)S(1)}, s32[4]{0:T(128)}, u32[]{:S(2)}) copy-start(s32[4]{0:T(128)} %param.12) | copy-start | bytes 52
  15.6 14.1 %collective-permute-start.7 = (bf16[4,32,1152]{2,1,0:T(8,128)(2,1)S(1)}, bf16[4,32,1152]{2,1,0:T(8,128)(2,1)S(1)}, u32[]{:S(2)}, u32[]{:S(2)}) collective-permute-start(bf16[4,32,1152]{2,1,0:T(8,128)(2,1)S(1)} %get-tuple-element.71), channel_id=1, source_target_pairs={{0,1},{1,0},{2,3},{3,2},{4,5},{5,4},{6,7},{7,6},{8,9},{9,8},{10,11... | collective-permute-start | bytes 884744 | tf_op jit(solution)/shard_map/ppermute | solution.py:22
  22.4 9.4 %collective-permute-start.4 = (bf16[64,1152]{1,0:T(8,128)(2,1)S(1)}, bf16[64,1152]{1,0:T(8,128)(2,1)S(1)}, u32[]{:S(2)}, u32[]{:S(2)}) collective-permute-start(bf16[64,1152]{1,0:T(8,128)(2,1)S(1)} %get-tuple-element.43), channel_id=1, source_target_pairs={{0,6},{2,0},{4,2},{6,4},{1,7},{3,1},{5,3},{7,5},{8,14},{10,8},{12,... | collective-permute-start | bytes 442376 | tf_op jit(solution)/shard_map/ppermute | solution.py:22
  25.8 6.2 %collective-permute-start.5 = (bf16[64,1152]{1,0:T(8,128)(2,1)S(1)}, bf16[64,1152]{1,0:T(8,128)(2,1)S(1)}, u32[]{:S(2)}, u32[]{:S(2)}) collective-permute-start(bf16[64,1152]{1,0:T(8,128)(2,1)S(1)} %get-tuple-element.44), channel_id=1, source_target_pairs={{0,4},{2,6},{4,0},{6,2},{1,5},{3,7},{5,1},{7,3},{8,12},{10,14},{12... | collective-permute-start | bytes 442376 | tf_op jit(solution)/shard_map/ppermute | solution.py:22
  25.8 9.8 %collective-permute-start.6 = (bf16[64,1152]{1,0:T(8,128)(2,1)S(1)}, bf16[64,1152]{1,0:T(8,128)(2,1)S(1)}, u32[]{:S(2)}, u32[]{:S(2)}) collective-permute-start(bf16[64,1152]{1,0:T(8,128)(2,1)S(1)} %get-tuple-element.45), channel_id=1, source_target_pairs={{0,2},{2,4},{4,6},{6,0},{1,3},{3,5},{5,7},{7,1},{8,10},{10,12},{12... | collective-permute-start | bytes 442376 | tf_op jit(solution)/shard_map/ppermute | solution.py:22
  29.7 5.9 %copy-start.3 = (bf16[1152,1152]{1,0:T(8,128)(2,1)S(1)}, bf16[1152,1152]{1,0:T(8,128)(2,1)}, u32[]{:S(2)}) copy-start(bf16[1152,1152]{1,0:T(8,128)(2,1)} %w_ref.11) | copy-start | bytes 7962628
  72.2 6.9 %collective-permute-start.8 = (bf16[64,1152]{1,0:T(8,128)(2,1)S(1)}, bf16[64,1152]{1,0:T(8,128)(2,1)S(1)}, u32[]{:S(2)}, u32[]{:S(2)}) collective-permute-start(bf16[64,1152]{1,0:T(8,128)(2,1)S(1)} %get-tuple-element.54), channel_id=1, source_target_pairs={{0,2},{2,4},{4,6},{6,0},{1,3},{3,5},{5,7},{7,1},{8,10},{10,12},{12... | collective-permute-start | bytes 442376 | tf_op jit(solution)/shard_map/ppermute | solution.py:22
  72.3 6.8 %collective-permute-start.9 = (bf16[64,1152]{1,0:T(8,128)(2,1)S(1)}, bf16[64,1152]{1,0:T(8,128)(2,1)S(1)}, u32[]{:S(2)}, u32[]{:S(2)}) collective-permute-start(bf16[64,1152]{1,0:T(8,128)(2,1)S(1)} %get-tuple-element.55), channel_id=1, source_target_pairs={{0,4},{2,6},{4,0},{6,2},{1,5},{3,7},{5,1},{7,3},{8,12},{10,14},{12... | collective-permute-start | bytes 442376 | tf_op jit(solution)/shard_map/ppermute | solution.py:22
  73.7 6.0 %collective-permute-start.10 = (bf16[64,1152]{1,0:T(8,128)(2,1)S(1)}, bf16[64,1152]{1,0:T(8,128)(2,1)S(1)}, u32[]{:S(2)}, u32[]{:S(2)}) collective-permute-start(bf16[64,1152]{1,0:T(8,128)(2,1)S(1)} %get-tuple-element.56), channel_id=1, source_target_pairs={{0,6},{2,0},{4,2},{6,4},{1,7},{3,1},{5,3},{7,5},{8,14},{10,8},{12,... | collective-permute-start | bytes 442376 | tf_op jit(solution)/shard_map/ppermute | solution.py:22
  84.5 7.1 %collective-permute-start.11 = (bf16[64,1152]{1,0:T(8,128)(2,1)S(1)}, bf16[64,1152]{1,0:T(8,128)(2,1)S(1)}, u32[]{:S(2)}, u32[]{:S(2)}) collective-permute-start(bf16[64,1152]{1,0:T(8,128)(2,1)S(1)} %get-tuple-element.58), channel_id=1, source_target_pairs={{0,6},{2,0},{4,2},{6,4},{1,7},{3,1},{5,3},{7,5},{8,14},{10,8},{12,... | collective-permute-start | bytes 442376 | tf_op jit(solution)/shard_map/ppermute | solution.py:22
  87.0 5.6 %collective-permute-start.12 = (bf16[64,1152]{1,0:T(8,128)(2,1)S(1)}, bf16[64,1152]{1,0:T(8,128)(2,1)S(1)}, u32[]{:S(2)}, u32[]{:S(2)}) collective-permute-start(bf16[64,1152]{1,0:T(8,128)(2,1)S(1)} %get-tuple-element.59), channel_id=1, source_target_pairs={{0,4},{2,6},{4,0},{6,2},{1,5},{3,7},{5,1},{7,3},{8,12},{10,14},{12... | collective-permute-start | bytes 442376 | tf_op jit(solution)/shard_map/ppermute | solution.py:22
  87.4 6.7 %collective-permute-start.13 = (bf16[64,1152]{1,0:T(8,128)(2,1)S(1)}, bf16[64,1152]{1,0:T(8,128)(2,1)S(1)}, u32[]{:S(2)}, u32[]{:S(2)}) collective-permute-start(bf16[64,1152]{1,0:T(8,128)(2,1)S(1)} %get-tuple-element.60), channel_id=1, source_target_pairs={{0,2},{2,4},{4,6},{6,0},{1,3},{3,5},{5,7},{7,1},{8,10},{10,12},{12... | collective-permute-start | bytes 442376 | tf_op jit(solution)/shard_map/ppermute | solution.py:22
  96.4 11.5 %all-to-all-start.3 = ((f32[8,8,1152]{2,1,0:T(8,128)}), f32[8,8,1152]{2,1,0:T(8,128)S(1)}, u32[]{:S(2)}, u32[]{:S(2)}) async-start(f32[8,8,1152]{2,1,0:T(8,128)} %get-tuple-element.63), calls=%async_computation.3 | async-start | bytes 589824 | tf_op jit(solution)/shard_map/all_to_all | solution.py:232
  99.9 19.1 %collective-permute-start.14 = (f32[4,32,1152]{2,1,0:T(8,128)S(1)}, f32[4,32,1152]{2,1,0:T(8,128)S(1)}, u32[]{:S(2)}, u32[]{:S(2)}) collective-permute-start(f32[4,32,1152]{2,1,0:T(8,128)S(1)} %get-tuple-element.66), channel_id=1, source_target_pairs={{0,1},{1,0},{2,3},{3,2},{4,5},{5,4},{6,7},{7,6},{8,9},{9,8},{10,11... | collective-permute-start | bytes 1769480 | tf_op jit(solution)/shard_map/ppermute | solution.py:22
  129.8 8.6 %collective-permute-start.15 = (f32[8,8,1152]{2,1,0:T(8,128)S(1)}, f32[8,8,1152]{2,1,0:T(8,128)S(1)}, u32[]{:S(2)}, u32[]{:S(2)}) collective-permute-start(f32[8,8,1152]{2,1,0:T(8,128)S(1)} %all_to_all.34.mine_lower), channel_id=1, source_target_pairs={{0,1},{1,0},{2,3},{3,2},{4,5},{5,4},{6,7},{7,6},{8,9},{9,8},{10,11... | collective-permute-start | bytes 884744 | tf_op jit(solution)/shard_map/ppermute | solution.py:22

commit v8 on v6

--- a/solution.py
+++ b/solution.py
@@ -12,7 +12,7 @@
 LANES = 128
 LOG2E = 1.4426950408889634
 SHARES = ("u", "y")
-GROUPS = ("w", "v")
+PLANES = ("w", "v", "u")
 VMEM = pl.BlockSpec(memory_space=pltpu.VMEM)
 SMEM = pl.BlockSpec(memory_space=pltpu.SMEM)
 
@@ -49,7 +49,7 @@
 
 
 def modulation_row(where_ref, step_ref, view_ref, step, part):
-    return step_ref[step, part : part + 1, :] + view_ref[where_ref[3 + step], part : part + 1, :]
+    return step_ref[step, part : part + 1, :] + view_ref[where_ref[4 + step], part : part + 1, :]
 
 
 def enter_body(where_ref, mine_ref, start_mine, peer_ref, step_ref, view_ref, x_ref, start_ref, *mod_refs):
@@ -65,15 +65,20 @@
         mod_refs[r][...] = normed_rows(rows, shift, scale)
 
 
+def share_place(flip, q, places):
+    half = places // 2
+    return (q // half + flip * (1 - 2 * (q // half))) * half + q % half
+
+
 def resume_body(
     where_ref, start_ref, mine_before, peer_before, lower_ref, step_ref, view_ref, x_ref, *rest
 ):
     mod_refs, base_ref = rest[:-1], rest[-1]
-    place = where_ref[0]
+    place, flip = where_ref[0], where_ref[1]
     steps = mine_before.shape[0]
     places, share, _ = lower_ref.shape
     for q in range(places):
-        base_ref[q * share : (q + 1) * share, :] = lower_ref[q]
+        base_ref[q * share : (q + 1) * share, :] = lower_ref[share_place(flip, q, places)]
     for r in range(steps):
         step = lax.rem(place + r, steps)
         before = jnp.concatenate([mine_before[step], peer_before[step]], axis=0)
@@ -87,7 +92,7 @@
 def finish_body(
     where_ref, start_ref, mine_before, peer_before, mine_lower, peer_lower, out_ref, base_ref, rows_ref, sems
 ):
-    core = where_ref[2]
+    flip, core = where_ref[1], where_ref[2]
     places, share, _ = mine_lower.shape
     half = places // 2
     sides = ((core, 0, mine_before, mine_lower), (1 - core, half, peer_before, peer_lower))
@@ -95,7 +100,7 @@
     for side, (view, low, before_ref, lower_ref) in enumerate(sides):
         for q in range(half):
             rows = slice(q * share, (q + 1) * share)
-            base_ref[rows, :] = lower_ref[low + q]
+            base_ref[rows, :] = lower_ref[share_place(flip, low + q, places)]
         for step in range(before_ref.shape[0]):
             rows_ref[side, step] = start_ref[view] + (base_ref[...] + before_ref[step])
             copies.append(
@@ -180,7 +185,7 @@
     rows_ref,
     proj_ref,
 ):
-    place = where_ref[0]
+    place, flip = where_ref[0], where_ref[1]
     pieces = (a0, a1, a2, a3)
     part = a0.shape[0]
     half = part // 2
@@ -197,7 +202,7 @@
         running = running + (base_ref[step] + gate * proj_ref[step * part : (step + 1) * part, :])
     places, share, _ = total_ref.shape
     for q in range(places):
-        total_ref[q] = running[q * share : (q + 1) * share]
+        total_ref[share_place(flip, q, places)] = running[q * share : (q + 1) * share]
 
 
 def coefficients(steps_index):
@@ -218,12 +223,8 @@
     all_ref[...] = running
 
 
-def below_body(where_ref, before_ref, *refs):
-    passed, out_ref = refs[:-1], refs[-1]
-    group = where_ref[1]
-    below = jnp.zeros(before_ref.shape[1:], before_ref.dtype)
-    for shift, ref in enumerate(passed, 1):
-        below = below + jnp.where(shift <= group, ref[...], 0.0)
+def below_body(where_ref, before_ref, near_ref, far_ref, out_ref):
+    below = jnp.where(where_ref[3] == 1, near_ref[...], 0.0) + jnp.where(where_ref[1] == 1, far_ref[...], 0.0)
     for q in range(before_ref.shape[0]):
         out_ref[q] = before_ref[q] + below
 
@@ -232,16 +233,18 @@
     held = lax.all_to_all(shares, SHARES, 0, 0, tiled=True)
     whole = jax.ShapeDtypeStruct(shares.shape, shares.dtype)
     before, total = call(inside_body, [whole, jax.ShapeDtypeStruct(shares.shape[1:], shares.dtype)], [VMEM], held)
-    passed = spread([total] * (lax.axis_size(GROUPS) - 1), GROUPS)
+    near = shifted(total, "v", 1)
+    planes = lax.axis_size(PLANES)
+    far = lax.ppermute(total + near, PLANES, [(i, planes - 1 - i) for i in range(planes)])
     if beside is not None:
-        passed[0], beside = lax.optimization_barrier((passed[0], shifted(beside, "c", 1)))
-    sums = call(below_body, whole, [SMEM] + [VMEM] * (1 + len(passed)), where, before, *passed)
+        far, beside = lax.optimization_barrier((far, shifted(beside, "c", 1)))
+    sums = call(below_body, whole, [SMEM] + [VMEM] * 3, where, before, near, far)
     return lax.all_to_all(sums, SHARES, 0, 0, tiled=True), beside
 
 
 def device_program(states, noise, x_start, timesteps, step_mod, view_mod, view_ids, w_qkv, w_out):
     steps, views, part, width = states.shape
-    place, group, core = (lax.axis_index(a) for a in ("x", GROUPS, "c"))
+    place, flip, core, odd = (lax.axis_index(a) for a in ("x", "w", "c", "v"))
     other = 1 - core
     f32, bf16 = jnp.float32, jnp.bfloat16
     rows = 2 * part
@@ -257,7 +260,7 @@
 
     swapped = shifted(jnp.concatenate([given(states, 1), given(x_start, 0)[None]], axis=0), "c", 1)
     states_mine, start_mine = own(states, 1), own(x_start, 0)
-    where = jnp.concatenate([jnp.stack([place, group, core]).astype(jnp.int32), own(view_ids, 1)])
+    where = jnp.concatenate([jnp.stack([place, flip, core, odd]).astype(jnp.int32), own(view_ids, 1)])
     coefs = jnp.stack(coefficients(timesteps))
     size = width // HEADS
     column = jnp.arange(width, dtype=jnp.int32)[None, :]
@@ -361,6 +364,4 @@
         P(),
         P(),
     )
-    return jax.shard_map(
-        device_program, mesh=finer, in_specs=placed, out_specs=P(tm, None, tok, None), check_vma=False
-    )
+    return jax.shard_map(device_program, mesh=finer, in_specs=placed, out_specs=P(tm, None, tok, None), check_vma=False)

time: 137 us -> 138 us (level)
  blocking collectives: 37.6 us -> 31.6 us
  starting transfers between devices: 46.2 us -> 51.7 us
    all_to_all x2 -> x1, blocking collectives: 19.6 us -> 9.6 us  [earlier_sum(): held = lax.all_to_all(shares, SHARES, 0, 0, tiled=True)]
    ppermute x0 -> x2, starting transfers between devices: none -> 7.77 us  [earlier_sum(): lax.ppermute(total + near, PLANES, [(i, planes - 1 - i) for i in range(pl...]
    ppermute x22 -> x18, starting transfers between devices: 46.2 us -> 40.5 us  [shifted(): lax.ppermute(value, axis, [(i, (i + shift) % size) for i in range(size)])]
    all_to_all x2, blocking collectives: 18.1 us -> 21.9 us  [earlier_sum(): return (lax.all_to_all(sums, SHARES, 0, 0, tiled=True), beside)]
    all_to_all x0 -> x1, starting transfers between devices: none -> 3.42 us  [earlier_sum(): held = lax.all_to_all(shares, SHARES, 0, 0, tiled=True)]
    ppermute x0 -> x2, waiting for transfers between devices: none -> 2.69 us  [earlier_sum(): lax.ppermute(total + near, PLANES, [(i, planes - 1 - i) for i in range(pl...]
    ppermute x22 -> x18, waiting for transfers between devices: 19 us -> 17.1 us  [shifted(): lax.ppermute(value, axis, [(i, (i + shift) % size) for i in range(size)])]
  transfers between devices with their start and end apart: 22 -> 21, of which waited for: 14 -> 14; matrix products, arithmetic and copies ran while one was open for 0% -> 0% of each run, Pallas kernels for 11% -> 11%
where the time goes in v8:
time: 138 us
  starting transfers between devices  51.7 us (37%)
  blocking collectives  31.6 us (23%)
  Pallas kernels  29.2 us (21%)
  waiting for transfers between devices  19.8 us (14%)
  local copies, waits for them, and re-layouts  5 us (4%)
    ppermute x18, starting transfers between devices, shifted(): lax.ppermute(value, axis, [(i, (i + shift) % size) for i in range(size)])  40.5 us
    pallas_call x17, Pallas kernels, call(): pl.pallas_call(body, out_shape=outs, in_specs=specs, out_specs=jax.tree.m...  29.2 us
    all_to_all x2, blocking collectives, earlier_sum(): return (lax.all_to_all(sums, SHARES, 0, 0, tiled=True), beside)  21.9 us
    ppermute x18, waiting for transfers between devices, shifted(): lax.ppermute(value, axis, [(i, (i + shift) % size) for i in range(size)])  17.1 us
    all_to_all x1, blocking collectives, earlier_sum(): held = lax.all_to_all(shares, SHARES, 0, 0, tiled=True)  9.6 us
    ppermute x2, starting transfers between devices, earlier_sum(): lax.ppermute(total + near, PLANES, [(i, planes - 1 - i) for i in range(pl...  7.77 us
    unnamed x20, local copies, waits for them, and re-layouts  3.45 us
    all_to_all x1, starting transfers between devices, earlier_sum(): held = lax.all_to_all(shares, SHARES, 0, 0, tiled=True)  3.42 us
  transfers between devices with their start and end apart: 21, of which 14 were waited for; matrix products, arithmetic and copies ran while one was open for 0% of the time, Pallas kernels for 11%

profile of v8, /device:TPU:1, one launch (start us, length us, event | category | flops | bytes accessed | tf_op | source)
XLA Modules:
  0.0 137.9 jit_solution(299960538608170381)
XLA Ops:
  0.0 1.4 dynamic-slice_bitcast_fusion
  1.5 3.3 %collective-permute-start = (f32[5,32,1152]{2,1,0:T(8,128)S(1)}, f32[5,32,1152]{2,1,0:T(8,128)S(1)}, u32[]{:S(2)}, u32[]{:S(2)}) collective-permute-start(f32[5,32,1152]{2,1,0:T(8,128)S(1)} %pad_maximum_fusion), channel_id=1, source_target_pairs={{0,1},{1,0},{2,3},{3,2},{4,5},{5,4},{6,7},{7,6},{8,9},{9,8},{10,11... | collective-permute-start | bytes 2211848 | tf_op jit(solution)/shard_map/ppermute | solution.py:22
  5.1 1.6 %collective-permute-done.peer_ref = f32[5,32,1152]{2,1,0:T(8,128)S(1)} collective-permute-done((f32[5,32,1152]{2,1,0:T(8,128)S(1)}, f32[5,32,1152]{2,1,0:T(8,128)S(1)}, u32[]{:S(2)}, u32[]{:S(2)}) %collective-permute-start) | collective-permute-done | bytes 737312 | tf_op jit(solution)/shard_map/ppermute | solution.py:22
  6.6 1.0 shard_map.91
  7.8 1.9 %collective-permute-start.2 = (bf16[64,1152]{1,0:T(8,128)(2,1)S(1)}, bf16[64,1152]{1,0:T(8,128)(2,1)S(1)}, u32[]{:S(2)}, u32[]{:S(2)}) collective-permute-start(bf16[64,1152]{1,0:T(8,128)(2,1)S(1)} %get-tuple-element.40), channel_id=1, source_target_pairs={{0,4},{2,6},{4,0},{6,2},{1,5},{3,7},{5,1},{7,3},{8,12},{10,14},{12... | collective-permute-start | bytes 442376 | tf_op jit(solution)/shard_map/ppermute | solution.py:22
  9.7 1.2 collective-permute-start.3
  10.9 3.3 %copy-done.1 = bf16[1152,3456]{1,0:T(8,128)(2,1)S(1)} copy-done((bf16[1152,3456]{1,0:T(8,128)(2,1)S(1)}, bf16[1152,3456]{1,0:T(8,128)(2,1)}, u32[]{:S(2)}) %copy-start.1) | copy-done | bytes 7962648
  14.1 1.4 %shard_map.92.first_ref = bf16[64,3456]{1,0:T(8,128)(2,1)S(1)} custom-call(bf16[64,1152]{1,0:T(8,128)(2,1)S(1)} %get-tuple-element.38.a0, bf16[1152,3456]{1,0:T(8,128)(2,1)S(1)} %copy-done.1), custom_call_target="tpu_custom_call" | custom-call | tf_op jit(solution)/shard_map/pallas_call | solution.py:33
  15.6 1.3 collective-permute-start.7
  16.9 0.6 collective-permute-done.3.a3
  17.6 4.8 %shard_map.93 = (bf16[64,1152]{1,0:T(8,128)(2,1)S(1)}, bf16[64,1152]{1,0:T(8,128)(2,1)S(1)}, bf16[64,1152]{1,0:T(8,128)(2,1)S(1)}, bf16[256,3456]{1,0:T(8,128)(2,1)S(1)}) custom-call(bf16[64,3456]{1,0:T(8,128)(2,1)S(1)} %shard_map.92.first_ref, bf16[64,1152]{1,0:T(8,128)(2,1)S(1)} %collective-permute-done.1.a1, ...), custom_call_target="tpu_custom_call" | custom-call | tf_op jit(solution)/shard_map/pallas_call | solution.py:33
  22.4 3.4 %collective-permute-start.4 = (bf16[64,1152]{1,0:T(8,128)(2,1)S(1)}, bf16[64,1152]{1,0:T(8,128)(2,1)S(1)}, u32[]{:S(2)}, u32[]{:S(2)}) collective-permute-start(bf16[64,1152]{1,0:T(8,128)(2,1)S(1)} %get-tuple-element.43), channel_id=1, source_target_pairs={{0,6},{2,0},{4,2},{6,4},{1,7},{3,1},{5,3},{7,5},{8,14},{10,8},{12,... | collective-permute-start | bytes 442376 | tf_op jit(solution)/shard_map/ppermute | solution.py:22
  25.8 0.7 collective-permute-start.6
  26.5 3.2 %shard_map.94.a0 = bf16[64,1152]{1,0:T(8,128)(2,1)S(1)} custom-call(bf16[64,3456]{1,0:T(8,128)(2,1)S(1)} %shard_map.92.first_ref, bf16[256,3456]{1,0:T(8,128)(2,1)S(1)} %get-tuple-element.42.qkv_ref, bf16[16,1152]{1,0:T(8,128)(2,1)S(1)} %fusion.1.mask_ref), custom_call_target="tpu_custom_call" | custom-call | tf_op jit(solution)/shard_map/pallas_call | solution.py:33
  29.7 0.8 shard_map.95.base_ref
  30.4 1.3 collective-permute-done.4.a1
  32.0 3.6 %collective-permute-done.6.a3 = bf16[64,1152]{1,0:T(8,128)(2,1)S(1)} collective-permute-done((bf16[64,1152]{1,0:T(8,128)(2,1)S(1)}, bf16[64,1152]{1,0:T(8,128)(2,1)S(1)}, u32[]{:S(2)}, u32[]{:S(2)}) %collective-permute-start.6) | collective-permute-done | bytes 147488 | tf_op jit(solution)/shard_map/ppermute | solution.py:22
  35.6 1.6 %shard_map.96 = (f32[4,32,1152]{2,1,0:T(8,128)S(1)}, f32[4,32,1152]{2,1,0:T(8,128)S(1)}, f32[8,8,1152]{2,1,0:T(8,128)S(1)}) custom-call(s32[8]{0:T(128)S(1)} %concatenate.6.where_ref, f32[3,4]{1,0:T(4,128)S(1)} %pad_maximum_fusion.1.coef_ref, bf16[64,1152]{1,0:T(8,128)(2,1)S(1)} %shard_map.94.a0, bf16[64,1152]{1,0:T(8,128)(2,1)S(1)} %collective-permute-done.4.a1, ...), custom_call_target="tpu_custom_call" | custom-call | tf_op jit(solution)/shard_map/pallas_call | solution.py:33
  37.3 9.6 %all_to_all.20.held_ref = f32[8,8,1152]{2,1,0:T(8,128)S(1)} all-to-all(f32[8,8,1152]{2,1,0:T(8,128)S(1)} %get-tuple-element.50), channel_id=1, replica_groups=mesh['w'=2,'v'=2,'u'=2,'y'=4,'x'=4,'c'=2] {'u','y'}, dimensions={0} | all-to-all | bytes 589824 | tf_op jit(solution)/shard_map/all_to_all | solution.py:233
  46.9 3.1 %collective-permute-start.8 = (f32[8,1152]{1,0:T(8,128)S(1)}, f32[8,1152]{1,0:T(8,128)S(1)}, u32[]{:S(2)}, u32[]{:S(2)}) collective-permute-start(f32[8,1152]{1,0:T(8,128)S(1)} %get-tuple-element.52), channel_id=1, source_target_pairs={{0,64},{64,0},{1,65},{65,1},{2,66},{66,2},{3,67},{67,3},{4,68},{68... | collective-permute-start | bytes 110600 | tf_op jit(solution)/shard_map/ppermute | solution.py:22
  50.0 1.7 %collective-permute-done.8.near_ref = f32[8,1152]{1,0:T(8,128)S(1)} collective-permute-done((f32[8,1152]{1,0:T(8,128)S(1)}, f32[8,1152]{1,0:T(8,128)S(1)}, u32[]{:S(2)}, u32[]{:S(2)}) %collective-permute-start.8) | collective-permute-done | bytes 36896 | tf_op jit(solution)/shard_map/ppermute | solution.py:22
  51.7 3.2 %collective-permute-start.9 = (f32[8,1152]{1,0:T(8,128)S(1)}, f32[8,1152]{1,0:T(8,128)S(1)}, u32[]{:S(2)}, u32[]{:S(2)}) collective-permute-start(f32[8,1152]{1,0:T(8,128)S(1)} %add.47), channel_id=1, source_target_pairs={{0,224},{32,192},{64,160},{96,128},{128,96},{160,64},{192,32},{224... | collective-permute-start | bytes 110600 | tf_op jit(solution)/shard_map/ppermute | solution.py:238
  54.9 1.3 collective-permute-done.9.far_ref
  56.8 10.4 %all_to_all.21.lower_ref = f32[8,8,1152]{2,1,0:T(8,128)S(1)} all-to-all(f32[8,8,1152]{2,1,0:T(8,128)S(1)} %shard_map.98), channel_id=1, replica_groups=mesh['w'=2,'v'=2,'u'=2,'y'=4,'x'=4,'c'=2] {'u','y'}, dimensions={0} | all-to-all | bytes 589824 | tf_op jit(solution)/shard_map/all_to_all | solution.py:242
  67.2 1.1 shard_map.99
  68.4 1.8 %collective-permute-start.11 = (bf16[64,1152]{1,0:T(8,128)(2,1)S(1)}, bf16[64,1152]{1,0:T(8,128)(2,1)S(1)}, u32[]{:S(2)}, u32[]{:S(2)}) collective-permute-start(bf16[64,1152]{1,0:T(8,128)(2,1)S(1)} %get-tuple-element.55), channel_id=1, source_target_pairs={{0,4},{2,6},{4,0},{6,2},{1,5},{3,7},{5,1},{7,3},{8,12},{10,14},{12... | collective-permute-start | bytes 442376 | tf_op jit(solution)/shard_map/ppermute | solution.py:22
  70.2 2.0 %collective-permute-start.12 = (bf16[64,1152]{1,0:T(8,128)(2,1)S(1)}, bf16[64,1152]{1,0:T(8,128)(2,1)S(1)}, u32[]{:S(2)}, u32[]{:S(2)}) collective-permute-start(bf16[64,1152]{1,0:T(8,128)(2,1)S(1)} %get-tuple-element.56), channel_id=1, source_target_pairs={{0,6},{2,0},{4,2},{6,4},{1,7},{3,1},{5,3},{7,5},{8,14},{10,8},{12,... | collective-permute-start | bytes 442376 | tf_op jit(solution)/shard_map/ppermute | solution.py:22
  72.2 1.3 shard_map.100.first_ref
  73.5 1.6 %collective-permute-done.10.a1 = bf16[64,1152]{1,0:T(8,128)(2,1)S(1)} collective-permute-done((bf16[64,1152]{1,0:T(8,128)(2,1)S(1)}, bf16[64,1152]{1,0:T(8,128)(2,1)S(1)}, u32[]{:S(2)}, u32[]{:S(2)}) %collective-permute-start.10) | collective-permute-done | bytes 147488 | tf_op jit(solution)/shard_map/ppermute | solution.py:22
  75.2 0.6 collective-permute-done.12.a3
  75.7 4.8 %shard_map.101 = (bf16[64,1152]{1,0:T(8,128)(2,1)S(1)}, bf16[64,1152]{1,0:T(8,128)(2,1)S(1)}, bf16[64,1152]{1,0:T(8,128)(2,1)S(1)}, bf16[256,3456]{1,0:T(8,128)(2,1)S(1)}) custom-call(bf16[64,3456]{1,0:T(8,128)(2,1)S(1)} %shard_map.100.first_ref, bf16[64,1152]{1,0:T(8,128)(2,1)S(1)} %collective-permute-done.10.a1, ...), custom_call_target="tpu_custom_call" | custom-call | tf_op jit(solution)/shard_map/pallas_call | solution.py:33
  80.6 2.7 %collective-permute-start.13 = (bf16[64,1152]{1,0:T(8,128)(2,1)S(1)}, bf16[64,1152]{1,0:T(8,128)(2,1)S(1)}, u32[]{:S(2)}, u32[]{:S(2)}) collective-permute-start(bf16[64,1152]{1,0:T(8,128)(2,1)S(1)} %get-tuple-element.58), channel_id=1, source_target_pairs={{0,6},{2,0},{4,2},{6,4},{1,7},{3,1},{5,3},{7,5},{8,14},{10,8},{12,... | collective-permute-start | bytes 442376 | tf_op jit(solution)/shard_map/ppermute | solution.py:22
  83.9 0.7 shard_map.103.base_ref
  84.7 3.2 %shard_map.102.a0 = bf16[64,1152]{1,0:T(8,128)(2,1)S(1)} custom-call(bf16[64,3456]{1,0:T(8,128)(2,1)S(1)} %shard_map.100.first_ref, bf16[256,3456]{1,0:T(8,128)(2,1)S(1)} %get-tuple-element.57.qkv_ref, bf16[16,1152]{1,0:T(8,128)(2,1)S(1)} %fusion.1.mask_ref), custom_call_target="tpu_custom_call" | custom-call | tf_op jit(solution)/shard_map/pallas_call | solution.py:33
  87.9 1.0 collective-permute-done.14.a2
  88.9 1.5 %collective-permute-done.15.a3 = bf16[64,1152]{1,0:T(8,128)(2,1)S(1)} collective-permute-done((bf16[64,1152]{1,0:T(8,128)(2,1)S(1)}, bf16[64,1152]{1,0:T(8,128)(2,1)S(1)}, u32[]{:S(2)}, u32[]{:S(2)}) %collective-permute-start.15) | collective-permute-done | bytes 147488 | tf_op jit(solution)/shard_map/ppermute | solution.py:22
  90.3 2.4 %shard_map.104 = (f32[4,32,1152]{2,1,0:T(8,128)S(1)}, f32[4,32,1152]{2,1,0:T(8,128)S(1)}, f32[8,8,1152]{2,1,0:T(8,128)}) custom-call(s32[8]{0:T(128)S(1)} %concatenate.6.where_ref, f32[3,4]{1,0:T(4,128)S(1)} %pad_maximum_fusion.1.coef_ref, bf16[64,1152]{1,0:T(8,128)(2,1)S(1)} %shard_map.102.a0, bf16[64,1152]{1,0:T(8,128)(2,1)S(1)} %collective-permute-done.13.a1, ...), custom_call_target="tpu_custom_call" | custom-call | tf_op jit(solution)/shard_map/pallas_call | solution.py:33
  92.7 3.4 %all-to-all-start.2 = ((f32[8,8,1152]{2,1,0:T(8,128)}), f32[8,8,1152]{2,1,0:T(8,128)S(1)}, u32[]{:S(2)}, u32[]{:S(2)}) async-start(f32[8,8,1152]{2,1,0:T(8,128)} %get-tuple-element.63), calls=%async_computation.2 | async-start | bytes 589824 | tf_op jit(solution)/shard_map/all_to_all | solution.py:233
  96.1 8.7 %collective-permute-start.18 = (f32[4,32,1152]{2,1,0:T(8,128)S(1)}, f32[4,32,1152]{2,1,0:T(8,128)S(1)}, u32[]{:S(2)}, u32[]{:S(2)}) collective-permute-start(f32[4,32,1152]{2,1,0:T(8,128)S(1)} %get-tuple-element.65), channel_id=1, source_target_pairs={{0,1},{1,0},{2,3},{3,2},{4,5},{5,4},{6,7},{7,6},{8,9},{9,8},{10,11... | collective-permute-start | bytes 1769480 | tf_op jit(solution)/shard_map/ppermute | solution.py:22
  104.9 1.9 %collective-permute-start.16 = (f32[8,1152]{1,0:T(8,128)S(1)}, f32[8,1152]{1,0:T(8,128)S(1)}, u32[]{:S(2)}, u32[]{:S(2)}) collective-permute-start(f32[8,1152]{1,0:T(8,128)S(1)} %get-tuple-element.64), channel_id=1, source_target_pairs={{0,64},{64,0},{1,65},{65,1},{2,66},{66,2},{3,67},{67,3},{4,68},{68... | collective-permute-start | bytes 110600 | tf_op jit(solution)/shard_map/ppermute | solution.py:22
  106.8 2.2 %collective-permute-done.16.near_ref = f32[8,1152]{1,0:T(8,128)S(1)} collective-permute-done((f32[8,1152]{1,0:T(8,128)S(1)}, f32[8,1152]{1,0:T(8,128)S(1)}, u32[]{:S(2)}, u32[]{:S(2)}) %collective-permute-start.16) | collective-permute-done | bytes 36896 | tf_op jit(solution)/shard_map/ppermute | solution.py:22
  109.0 4.6 %collective-permute-start.17 = (f32[8,1152]{1,0:T(8,128)S(1)}, f32[8,1152]{1,0:T(8,128)S(1)}, u32[]{:S(2)}, u32[]{:S(2)}) collective-permute-start(f32[8,1152]{1,0:T(8,128)S(1)} %add.48), channel_id=1, source_target_pairs={{0,224},{32,192},{64,160},{96,128},{128,96},{160,64},{192,32},{224... | collective-permute-start | bytes 110600 | tf_op jit(solution)/shard_map/ppermute | solution.py:238
  113.5 1.3 collective-permute-done.17.far_ref
  114.9 0.6 shard_map.106
  115.5 11.6 %all_to_all.22.mine_lower = f32[8,8,1152]{2,1,0:T(8,128)S(1)} all-to-all(f32[8,8,1152]{2,1,0:T(8,128)S(1)} %shard_map.106), channel_id=1, replica_groups=mesh['w'=2,'v'=2,'u'=2,'y'=4,'x'=4,'c'=2] {'u','y'}, dimensions={0} | all-to-all | bytes 589824 | tf_op jit(solution)/shard_map/all_to_all | solution.py:242
  127.0 7.8 %collective-permute-start.19 = (f32[8,8,1152]{2,1,0:T(8,128)S(1)}, f32[8,8,1152]{2,1,0:T(8,128)S(1)}, u32[]{:S(2)}, u32[]{:S(2)}) collective-permute-start(f32[8,8,1152]{2,1,0:T(8,128)S(1)} %all_to_all.22.mine_lower), channel_id=1, source_target_pairs={{0,1},{1,0},{2,3},{3,2},{4,5},{5,4},{6,7},{7,6},{8,9},{9,8},{10,11... | collective-permute-start | bytes 884744 | tf_op jit(solution)/shard_map/ppermute | solution.py:22
  134.8 1.2 collective-permute-done.19.peer_lower
  136.0 1.6 %shard_map.107 = f32[4,2,32,1152]{3,2,1,0:T(8,128)} custom-call(s32[8]{0:T(128)S(1)} %concatenate.6.where_ref, f32[2,32,1152]{2,1,0:T(8,128)S(1)} %copy-done.4, f32[4,32,1152]{2,1,0:T(8,128)S(1)} %get-tuple-element.62.mine_before, f32[4,32,1152]{2,1,0:T(8,128)S(1)} %collective-permute-done.18.peer_before, f32[8,8,1152]{2,1,0:T(8,128)S(1)} %all_to_all.22.mine_lower, ...), custom_call_target="tpu_custom_call" | custom-call | tf_op jit(solution)/shard_map/pallas_call | solution.py:33
  (46 shorter events, 2.2 us)
Async XLA Ops:
  0.0 4.9 %copy-start = (s32[4,2]{0,1:T(2,128)S(1)}, s32[4,2]{0,1:T(2,128)}, u32[]{:S(2)}) copy-start(s32[4,2]{0,1:T(2,128)} %param.15) | copy-start | bytes 100
  0.0 1.4 copy-start.4
  1.4 3.4 %copy-start.7 = (f32[4,3,1152]{2,0,1:T(4,128)S(1)}, f32[4,3,1152]{2,0,1:T(4,128)}, u32[]{:S(2)}) copy-start(f32[4,3,1152]{2,0,1:T(4,128)} %param.13) | copy-start | bytes 165892
  1.4 3.4 %copy-start.6 = (f32[8,3,1152]{2,0,1:T(8,128)S(1)}, f32[8,3,1152]{2,0,1:T(8,128)}, u32[]{:S(2)}) copy-start(f32[8,3,1152]{2,0,1:T(8,128)} %param.14) | copy-start | bytes 331780
  1.5 5.1 %collective-permute-start = (f32[5,32,1152]{2,1,0:T(8,128)S(1)}, f32[5,32,1152]{2,1,0:T(8,128)S(1)}, u32[]{:S(2)}, u32[]{:S(2)}) collective-permute-start(f32[5,32,1152]{2,1,0:T(8,128)S(1)} %pad_maximum_fusion), channel_id=1, source_target_pairs={{0,1},{1,0},{2,3},{3,2},{4,5},{5,4},{6,7},{7,6},{8,9},{9,8},{10,11... | collective-permute-start | bytes 2211848 | tf_op jit(solution)/shard_map/ppermute | solution.py:22
  7.7 9.2 %collective-permute-start.1 = (bf16[64,1152]{1,0:T(8,128)(2,1)S(1)}, bf16[64,1152]{1,0:T(8,128)(2,1)S(1)}, u32[]{:S(2)}, u32[]{:S(2)}) collective-permute-start(bf16[64,1152]{1,0:T(8,128)(2,1)S(1)} %get-tuple-element.39), channel_id=1, source_target_pairs={{0,2},{2,4},{4,6},{6,0},{1,3},{3,5},{5,7},{7,1},{8,10},{10,12},{12... | collective-permute-start | bytes 442376 | tf_op jit(solution)/shard_map/ppermute | solution.py:22
  7.8 9.2 %collective-permute-start.2 = (bf16[64,1152]{1,0:T(8,128)(2,1)S(1)}, bf16[64,1152]{1,0:T(8,128)(2,1)S(1)}, u32[]{:S(2)}, u32[]{:S(2)}) collective-permute-start(bf16[64,1152]{1,0:T(8,128)(2,1)S(1)} %get-tuple-element.40), channel_id=1, source_target_pairs={{0,4},{2,6},{4,0},{6,2},{1,5},{3,7},{5,1},{7,3},{8,12},{10,14},{12... | collective-permute-start | bytes 442376 | tf_op jit(solution)/shard_map/ppermute | solution.py:22
  9.7 7.8 %collective-permute-start.3 = (bf16[64,1152]{1,0:T(8,128)(2,1)S(1)}, bf16[64,1152]{1,0:T(8,128)(2,1)S(1)}, u32[]{:S(2)}, u32[]{:S(2)}) collective-permute-start(bf16[64,1152]{1,0:T(8,128)(2,1)S(1)} %get-tuple-element.41), channel_id=1, source_target_pairs={{0,6},{2,0},{4,2},{6,4},{1,7},{3,1},{5,3},{7,5},{8,14},{10,8},{12,... | collective-permute-start | bytes 442376 | tf_op jit(solution)/shard_map/ppermute | solution.py:22
  10.9 3.3 %copy-start.1 = (bf16[1152,3456]{1,0:T(8,128)(2,1)S(1)}, bf16[1152,3456]{1,0:T(8,128)(2,1)}, u32[]{:S(2)}) copy-start(bf16[1152,3456]{1,0:T(8,128)(2,1)} %w_ref.10) | copy-start | bytes 23887876
  14.1 1.4 %copy-start.5 = (bf16[4,2,32,1152]{3,2,1,0:T(8,128)(2,1)S(1)}, bf16[4,2,32,1152]{3,2,1,0:T(8,128)(2,1)}, u32[]{:S(2)}) copy-start(bf16[4,2,32,1152]{3,2,1,0:T(8,128)(2,1)} %param.10) | copy-start | bytes 1769476
  14.1 3.5 %copy-start.2 = (bf16[1152,3456]{1,0:T(8,128)(2,1)S(1)}, bf16[1152,3456]{1,0:T(8,128)(2,1)}, u32[]{:S(2)}) copy-start(bf16[1152,3456]{1,0:T(8,128)(2,1)} %w_ref.10) | copy-start | bytes 23887876
  15.6 10.9 %copy-start.8 = (s32[4]{0:T(128)S(1)}, s32[4]{0:T(128)}, u32[]{:S(2)}) copy-start(s32[4]{0:T(128)} %param.12) | copy-start | bytes 52
  15.6 14.1 %collective-permute-start.7 = (bf16[4,32,1152]{2,1,0:T(8,128)(2,1)S(1)}, bf16[4,32,1152]{2,1,0:T(8,128)(2,1)S(1)}, u32[]{:S(2)}, u32[]{:S(2)}) collective-permute-start(bf16[4,32,1152]{2,1,0:T(8,128)(2,1)S(1)} %get-tuple-element.71), channel_id=1, source_target_pairs={{0,1},{1,0},{2,3},{3,2},{4,5},{5,4},{6,7},{7,6},{8,9},{9,8},{10,11... | collective-permute-start | bytes 884744 | tf_op jit(solution)/shard_map/ppermute | solution.py:22
  22.4 9.4 %collective-permute-start.4 = (bf16[64,1152]{1,0:T(8,128)(2,1)S(1)}, bf16[64,1152]{1,0:T(8,128)(2,1)S(1)}, u32[]{:S(2)}, u32[]{:S(2)}) collective-permute-start(bf16[64,1152]{1,0:T(8,128)(2,1)S(1)} %get-tuple-element.43), channel_id=1, source_target_pairs={{0,6},{2,0},{4,2},{6,4},{1,7},{3,1},{5,3},{7,5},{8,14},{10,8},{12,... | collective-permute-start | bytes 442376 | tf_op jit(solution)/shard_map/ppermute | solution.py:22
  25.8 6.2 %collective-permute-start.5 = (bf16[64,1152]{1,0:T(8,128)(2,1)S(1)}, bf16[64,1152]{1,0:T(8,128)(2,1)S(1)}, u32[]{:S(2)}, u32[]{:S(2)}) collective-permute-start(bf16[64,1152]{1,0:T(8,128)(2,1)S(1)} %get-tuple-element.44), channel_id=1, source_target_pairs={{0,4},{2,6},{4,0},{6,2},{1,5},{3,7},{5,1},{7,3},{8,12},{10,14},{12... | collective-permute-start | bytes 442376 | tf_op jit(solution)/shard_map/ppermute | solution.py:22
  25.8 9.8 %collective-permute-start.6 = (bf16[64,1152]{1,0:T(8,128)(2,1)S(1)}, bf16[64,1152]{1,0:T(8,128)(2,1)S(1)}, u32[]{:S(2)}, u32[]{:S(2)}) collective-permute-start(bf16[64,1152]{1,0:T(8,128)(2,1)S(1)} %get-tuple-element.45), channel_id=1, source_target_pairs={{0,2},{2,4},{4,6},{6,0},{1,3},{3,5},{5,7},{7,1},{8,10},{10,12},{12... | collective-permute-start | bytes 442376 | tf_op jit(solution)/shard_map/ppermute | solution.py:22
  29.7 5.9 %copy-start.3 = (bf16[1152,1152]{1,0:T(8,128)(2,1)S(1)}, bf16[1152,1152]{1,0:T(8,128)(2,1)}, u32[]{:S(2)}) copy-start(bf16[1152,1152]{1,0:T(8,128)(2,1)} %w_ref.11) | copy-start | bytes 7962628
  46.9 4.8 %collective-permute-start.8 = (f32[8,1152]{1,0:T(8,128)S(1)}, f32[8,1152]{1,0:T(8,128)S(1)}, u32[]{:S(2)}, u32[]{:S(2)}) collective-permute-start(f32[8,1152]{1,0:T(8,128)S(1)} %get-tuple-element.52), channel_id=1, source_target_pairs={{0,64},{64,0},{1,65},{65,1},{2,66},{66,2},{3,67},{67,3},{4,68},{68... | collective-permute-start | bytes 110600 | tf_op jit(solution)/shard_map/ppermute | solution.py:22
  51.7 4.5 %collective-permute-start.9 = (f32[8,1152]{1,0:T(8,128)S(1)}, f32[8,1152]{1,0:T(8,128)S(1)}, u32[]{:S(2)}, u32[]{:S(2)}) collective-permute-start(f32[8,1152]{1,0:T(8,128)S(1)} %add.47), channel_id=1, source_target_pairs={{0,224},{32,192},{64,160},{96,128},{128,96},{160,64},{192,32},{224... | collective-permute-start | bytes 110600 | tf_op jit(solution)/shard_map/ppermute | solution.py:238
  68.3 6.9 %collective-permute-start.10 = (bf16[64,1152]{1,0:T(8,128)(2,1)S(1)}, bf16[64,1152]{1,0:T(8,128)(2,1)S(1)}, u32[]{:S(2)}, u32[]{:S(2)}) collective-permute-start(bf16[64,1152]{1,0:T(8,128)(2,1)S(1)} %get-tuple-element.54), channel_id=1, source_target_pairs={{0,2},{2,4},{4,6},{6,0},{1,3},{3,5},{5,7},{7,1},{8,10},{10,12},{12... | collective-permute-start | bytes 442376 | tf_op jit(solution)/shard_map/ppermute | solution.py:22
  68.4 6.8 %collective-permute-start.11 = (bf16[64,1152]{1,0:T(8,128)(2,1)S(1)}, bf16[64,1152]{1,0:T(8,128)(2,1)S(1)}, u32[]{:S(2)}, u32[]{:S(2)}) collective-permute-start(bf16[64,1152]{1,0:T(8,128)(2,1)S(1)} %get-tuple-element.55), channel_id=1, source_target_pairs={{0,4},{2,6},{4,0},{6,2},{1,5},{3,7},{5,1},{7,3},{8,12},{10,14},{12... | collective-permute-start | bytes 442376 | tf_op jit(solution)/shard_map/ppermute | solution.py:22
  70.2 5.5 %collective-permute-start.12 = (bf16[64,1152]{1,0:T(8,128)(2,1)S(1)}, bf16[64,1152]{1,0:T(8,128)(2,1)S(1)}, u32[]{:S(2)}, u32[]{:S(2)}) collective-permute-start(bf16[64,1152]{1,0:T(8,128)(2,1)S(1)} %get-tuple-element.56), channel_id=1, source_target_pairs={{0,6},{2,0},{4,2},{6,4},{1,7},{3,1},{5,3},{7,5},{8,14},{10,8},{12,... | collective-permute-start | bytes 442376 | tf_op jit(solution)/shard_map/ppermute | solution.py:22
  80.6 7.3 %collective-permute-start.13 = (bf16[64,1152]{1,0:T(8,128)(2,1)S(1)}, bf16[64,1152]{1,0:T(8,128)(2,1)S(1)}, u32[]{:S(2)}, u32[]{:S(2)}) collective-permute-start(bf16[64,1152]{1,0:T(8,128)(2,1)S(1)} %get-tuple-element.58), channel_id=1, source_target_pairs={{0,6},{2,0},{4,2},{6,4},{1,7},{3,1},{5,3},{7,5},{8,14},{10,8},{12,... | collective-permute-start | bytes 442376 | tf_op jit(solution)/shard_map/ppermute | solution.py:22
  83.3 5.6 %collective-permute-start.14 = (bf16[64,1152]{1,0:T(8,128)(2,1)S(1)}, bf16[64,1152]{1,0:T(8,128)(2,1)S(1)}, u32[]{:S(2)}, u32[]{:S(2)}) collective-permute-start(bf16[64,1152]{1,0:T(8,128)(2,1)S(1)} %get-tuple-element.59), channel_id=1, source_target_pairs={{0,4},{2,6},{4,0},{6,2},{1,5},{3,7},{5,1},{7,3},{8,12},{10,14},{12... | collective-permute-start | bytes 442376 | tf_op jit(solution)/shard_map/ppermute | solution.py:22
  83.8 6.6 %collective-permute-start.15 = (bf16[64,1152]{1,0:T(8,128)(2,1)S(1)}, bf16[64,1152]{1,0:T(8,128)(2,1)S(1)}, u32[]{:S(2)}, u32[]{:S(2)}) collective-permute-start(bf16[64,1152]{1,0:T(8,128)(2,1)S(1)} %get-tuple-element.60), channel_id=1, source_target_pairs={{0,2},{2,4},{4,6},{6,0},{1,3},{3,5},{5,7},{7,1},{8,10},{10,12},{12... | collective-permute-start | bytes 442376 | tf_op jit(solution)/shard_map/ppermute | solution.py:22
  92.7 12.1 %all-to-all-start.2 = ((f32[8,8,1152]{2,1,0:T(8,128)}), f32[8,8,1152]{2,1,0:T(8,128)S(1)}, u32[]{:S(2)}, u32[]{:S(2)}) async-start(f32[8,8,1152]{2,1,0:T(8,128)} %get-tuple-element.63), calls=%async_computation.2 | async-start | bytes 589824 | tf_op jit(solution)/shard_map/all_to_all | solution.py:233
  96.1 18.8 %collective-permute-start.18 = (f32[4,32,1152]{2,1,0:T(8,128)S(1)}, f32[4,32,1152]{2,1,0:T(8,128)S(1)}, u32[]{:S(2)}, u32[]{:S(2)}) collective-permute-start(f32[4,32,1152]{2,1,0:T(8,128)S(1)} %get-tuple-element.65), channel_id=1, source_target_pairs={{0,1},{1,0},{2,3},{3,2},{4,5},{5,4},{6,7},{7,6},{8,9},{9,8},{10,11... | collective-permute-start | bytes 1769480 | tf_op jit(solution)/shard_map/ppermute | solution.py:22
  104.9 4.1 %collective-permute-start.16 = (f32[8,1152]{1,0:T(8,128)S(1)}, f32[8,1152]{1,0:T(8,128)S(1)}, u32[]{:S(2)}, u32[]{:S(2)}) collective-permute-start(f32[8,1152]{1,0:T(8,128)S(1)} %get-tuple-element.64), channel_id=1, source_target_pairs={{0,64},{64,0},{1,65},{65,1},{2,66},{66,2},{3,67},{67,3},{4,68},{68... | collective-permute-start | bytes 110600 | tf_op jit(solution)/shard_map/ppermute | solution.py:22
  109.0 5.9 %collective-permute-start.17 = (f32[8,1152]{1,0:T(8,128)S(1)}, f32[8,1152]{1,0:T(8,128)S(1)}, u32[]{:S(2)}, u32[]{:S(2)}) collective-permute-start(f32[8,1152]{1,0:T(8,128)S(1)} %add.48), channel_id=1, source_target_pairs={{0,224},{32,192},{64,160},{96,128},{128,96},{160,64},{192,32},{224... | collective-permute-start | bytes 110600 | tf_op jit(solution)/shard_map/ppermute | solution.py:238
  127.0 9.0 %collective-permute-start.19 = (f32[8,8,1152]{2,1,0:T(8,128)S(1)}, f32[8,8,1152]{2,1,0:T(8,128)S(1)}, u32[]{:S(2)}, u32[]{:S(2)}) collective-permute-start(f32[8,8,1152]{2,1,0:T(8,128)S(1)} %all_to_all.22.mine_lower), channel_id=1, source_target_pairs={{0,1},{1,0},{2,3},{3,2},{4,5},{5,4},{6,7},{7,6},{8,9},{9,8},{10,11... | collective-permute-start | bytes 884744 | tf_op jit(solution)/shard_map/ppermute | solution.py:22

commit v9 on v6

--- a/solution.py
+++ b/solution.py
@@ -8,6 +8,7 @@
 
 
 HEADS = 16
+HEAD_BATCH = 8
 SWEEPS = 2
 LANES = 128
 LOG2E = 1.4426950408889634
@@ -114,46 +115,70 @@
     qkv_ref[...] = project_rows(a0[...], w_ref)
 
 
-def attend(q_ref, kv_ref, mask_ref, outs):
+def attend(q_ref, kv_ref, mask_ref, outs, scores_ref, probs_ref):
     width = mask_ref.shape[1]
     part = outs[0].shape[0]
     size = width // HEADS
+    batch = scores_ref.shape[0]
     tiles = [None] * (width // LANES)
-    for h in range(HEADS):
+
+    def window(h):
         first = h * size // LANES
         last = ((h + 1) * size - 1) // LANES
-        low, high = first * LANES, (last + 1) * LANES
-        q = q_ref[:, low:high] * mask_ref[h : h + 1, low:high]
-        k = kv_ref[:, width + low : width + high]
-        v = kv_ref[:, 2 * width + low : 2 * width + high]
-        scores = lax.dot_general(q, k, (((1,), (1,)), ((), ())), preferred_element_type=jnp.float32)
-        top = jnp.max(scores, axis=-1, keepdims=True)
-        powers = jnp.exp2((scores - top) * (LOG2E / size**0.5))
-        share = 1.0 / jnp.sum(powers, axis=-1, keepdims=True)
-        out = jnp.dot(powers.astype(jnp.bfloat16), v, preferred_element_type=jnp.float32) * share
-        for t in range(first, last + 1):
-            piece = out[:, t * LANES - low : (t + 1) * LANES - low]
-            if tiles[t] is not None:
-                lane = lax.broadcasted_iota(jnp.int32, piece.shape, 1) + t * LANES
-                piece = jnp.where(lane >= h * size, piece, tiles[t])
-            tiles[t] = piece
-    for t, tile in enumerate(tiles):
-        tile = tile.astype(jnp.bfloat16)
-        for r, out in enumerate(outs):
-            out[:, t * LANES : (t + 1) * LANES] = tile[r * part : (r + 1) * part]
-
-
-def others_body(first_ref, a1, a2, a3, w_ref, mask_ref, o1, o2, o3, qkv_ref, rows_ref):
+        return first, last, first * LANES, (last + 1) * LANES
+
+    for start in range(0, HEADS, batch):
+        heads = range(start, start + batch)
+        shares = []
+        for h in heads:
+            _, _, low, high = window(h)
+            q = q_ref[:, low:high] * mask_ref[h : h + 1, low:high]
+            k = kv_ref[:, width + low : width + high]
+            scores_ref[h - start] = lax.dot_general(
+                q, k, (((1,), (1,)), ((), ())), preferred_element_type=jnp.float32
+            )
+        for h in heads:
+            scores = scores_ref[h - start]
+            top = jnp.max(scores, axis=-1, keepdims=True)
+            powers = jnp.exp2((scores - top) * (LOG2E / size**0.5))
+            shares.append(1.0 / jnp.sum(powers, axis=-1, keepdims=True))
+            probs_ref[h - start] = powers.astype(jnp.bfloat16)
+        for h in heads:
+            first, last, low, high = window(h)
+            v = kv_ref[:, 2 * width + low : 2 * width + high]
+            out = jnp.dot(probs_ref[h - start], v, preferred_element_type=jnp.float32) * shares[h - start]
+            for t in range(first, last + 1):
+                piece = out[:, t * LANES - low : (t + 1) * LANES - low]
+                if tiles[t] is not None:
+                    lane = lax.broadcasted_iota(jnp.int32, piece.shape, 1) + t * LANES
+                    piece = jnp.where(lane >= h * size, piece, tiles[t])
+                tiles[t] = piece
+                if (t + 1) * LANES <= (h + 1) * size:
+                    tile = piece.astype(jnp.bfloat16)
+                    for r, out_ref in enumerate(outs):
+                        out_ref[:, t * LANES : (t + 1) * LANES] = tile[r * part : (r + 1) * part]
+
+
+def stages(queries, keys):
+    return [
+        pltpu.VMEM((HEAD_BATCH, queries, keys), jnp.float32),
+        pltpu.VMEM((HEAD_BATCH, queries, keys), jnp.bfloat16),
+    ]
+
+
+def others_body(
+    first_ref, a1, a2, a3, w_ref, mask_ref, o1, o2, o3, qkv_ref, rows_ref, scores_ref, probs_ref
+):
     part = a1.shape[0]
     for r, piece in enumerate((a1, a2, a3)):
         rows_ref[r * part : (r + 1) * part, :] = piece[...]
     qkv_ref[: 3 * part, :] = project_rows(rows_ref[...], w_ref)
     qkv_ref[3 * part :, :] = first_ref[...]
-    attend(qkv_ref.at[: 3 * part], qkv_ref, mask_ref, (o1, o2, o3))
-
-
-def own_body(first_ref, qkv_ref, mask_ref, o0):
-    attend(first_ref, qkv_ref, mask_ref, (o0,))
+    attend(qkv_ref.at[: 3 * part], qkv_ref, mask_ref, (o1, o2, o3), scores_ref, probs_ref)
+
+
+def own_body(first_ref, qkv_ref, mask_ref, o0, scores_ref, probs_ref):
+    attend(first_ref, qkv_ref, mask_ref, (o0,), scores_ref, probs_ref)
 
 
 def base_body(coef_ref, x_ref, mine_ref, peer_ref, base_ref):
@@ -292,10 +317,12 @@
             *arrived,
             w_qkv,
             mask,
-            scratch=[pltpu.VMEM(((steps - 1) * rows, width), bf16)],
+            scratch=[pltpu.VMEM(((steps - 1) * rows, width), bf16)] + stages((steps - 1) * rows, steps * rows),
         )
         back = spread(attended, "x", -1)
-        kept = call(own_body, piece, [VMEM] * 3, first, qkv, mask)
+        kept = call(
+            own_body, piece, [VMEM] * 3, first, qkv, mask, scratch=stages(rows, steps * rows)
+        )
         base = call(base_body, x_shape, [SMEM] + [VMEM] * 3, coefs, x, noise_mine, noise_peer)
         mine_before, peer_before, total = call(
             project_body,
@@ -361,6 +388,4 @@
         P(),
         P(),
     )
-    return jax.shard_map(
-        device_program, mesh=finer, in_specs=placed, out_specs=P(tm, None, tok, None), check_vma=False
-    )
+    return jax.shard_map(device_program, mesh=finer, in_specs=placed, out_specs=P(tm, None, tok, None), check_vma=False)

time: 137 us -> 134 us (0.978)
  Pallas kernels: 28.5 us -> 21.2 us
  waiting for transfers between devices: 19 us -> 23.2 us
    pallas_call x17, Pallas kernels: 28.5 us -> 21.2 us  [call(): pl.pallas_call(body, out_shape=outs, in_specs=specs, out_specs=jax.tree.m...]
    ppermute x22, waiting for transfers between devices: 19 us -> 23.2 us  [shifted(): lax.ppermute(value, axis, [(i, (i + shift) % size) for i in range(size)])]
  transfers between devices with their start and end apart: 22 -> 22, of which waited for: 14 -> 15; matrix products, arithmetic and copies ran while one was open for 0% -> 0% of each run, Pallas kernels for 11% -> 7%
where the time goes in v9:
time: 134 us
  starting transfers between devices  46.1 us (34%)
  blocking collectives  37.8 us (28%)
  waiting for transfers between devices  23.2 us (17%)
  Pallas kernels  21.2 us (16%)
  local copies, waits for them, and re-layouts  4.91 us (4%)
    ppermute x22, starting transfers between devices, shifted(): lax.ppermute(value, axis, [(i, (i + shift) % size) for i in range(size)])  46.1 us
    ppermute x22, waiting for transfers between devices, shifted(): lax.ppermute(value, axis, [(i, (i + shift) % size) for i in range(size)])  23.2 us
    pallas_call x17, Pallas kernels, call(): pl.pallas_call(body, out_shape=outs, in_specs=specs, out_specs=jax.tree.m...  21.2 us
    all_to_all x2, blocking collectives, earlier_sum(): held = lax.all_to_all(shares, SHARES, 0, 0, tiled=True)  19.5 us
    all_to_all x2, blocking collectives, earlier_sum(): return (lax.all_to_all(sums, SHARES, 0, 0, tiled=True), beside)  18.2 us
    unnamed x20, local copies, waits for them, and re-layouts  3.45 us
  transfers between devices with their start and end apart: 22, of which 15 were waited for; matrix products, arithmetic and copies ran while one was open for 0% of the time, Pallas kernels for 7%

profile of v9, /device:TPU:1, one launch (start us, length us, event | category | flops | bytes accessed | tf_op | source)
XLA Modules:
  0.0 133.8 jit_solution(6040719547488713992)
XLA Ops:
  0.0 1.4 %dynamic-slice_bitcast_fusion = (f32[4,32,1152]{2,1,0:T(8,128)S(1)}, f32[4,32,1152]{2,1,0:T(8,128)S(1)}) fusion(f32[4,2,32,1152]{3,2,1,0:T(8,128)} %param.9, s32[]{:T(128)S(6)} %select_n.16, s32[]{:T(128)S(6)} %select_n.15), kind=kLoop, calls=%fused_computation.1 | loop fusion | bytes 2359304 | tf_op jit(solution)/shard_map/jit(dynamic_index_in_dim)/squeeze | solution.py:278
  1.5 3.3 %collective-permute-start = (f32[5,32,1152]{2,1,0:T(8,128)S(1)}, f32[5,32,1152]{2,1,0:T(8,128)S(1)}, u32[]{:S(2)}, u32[]{:S(2)}) collective-permute-start(f32[5,32,1152]{2,1,0:T(8,128)S(1)} %pad_maximum_fusion), channel_id=1, source_target_pairs={{0,1},{1,0},{2,3},{3,2},{4,5},{5,4},{6,7},{7,6},{8,9},{9,8},{10,11... | collective-permute-start | bytes 2211848 | tf_op jit(solution)/shard_map/ppermute | solution.py:23
  5.1 1.6 %collective-permute-done.peer_ref = f32[5,32,1152]{2,1,0:T(8,128)S(1)} collective-permute-done((f32[5,32,1152]{2,1,0:T(8,128)S(1)}, f32[5,32,1152]{2,1,0:T(8,128)S(1)}, u32[]{:S(2)}, u32[]{:S(2)}) %collective-permute-start) | collective-permute-done | bytes 737312 | tf_op jit(solution)/shard_map/ppermute | solution.py:23
  6.6 1.0 shard_map.91
  7.8 1.9 %collective-permute-start.2 = (bf16[64,1152]{1,0:T(8,128)(2,1)S(1)}, bf16[64,1152]{1,0:T(8,128)(2,1)S(1)}, u32[]{:S(2)}, u32[]{:S(2)}) collective-permute-start(bf16[64,1152]{1,0:T(8,128)(2,1)S(1)} %get-tuple-element.40), channel_id=1, source_target_pairs={{0,4},{2,6},{4,0},{6,2},{1,5},{3,7},{5,1},{7,3},{8,12},{10,14},{12... | collective-permute-start | bytes 442376 | tf_op jit(solution)/shard_map/ppermute | solution.py:23
  9.7 1.2 collective-permute-start.3
  10.9 3.3 %copy-done.1 = bf16[1152,3456]{1,0:T(8,128)(2,1)S(1)} copy-done((bf16[1152,3456]{1,0:T(8,128)(2,1)S(1)}, bf16[1152,3456]{1,0:T(8,128)(2,1)}, u32[]{:S(2)}) %copy-start.1) | copy-done | bytes 7962648
  14.1 1.4 %shard_map.92.first_ref = bf16[64,3456]{1,0:T(8,128)(2,1)S(1)} custom-call(bf16[64,1152]{1,0:T(8,128)(2,1)S(1)} %get-tuple-element.38.a0, bf16[1152,3456]{1,0:T(8,128)(2,1)S(1)} %copy-done.1), custom_call_target="tpu_custom_call" | custom-call | tf_op jit(solution)/shard_map/pallas_call | solution.py:34
  15.6 1.3 collective-permute-start.7
  17.6 3.2 %shard_map.93 = (bf16[64,1152]{1,0:T(8,128)(2,1)S(1)}, bf16[64,1152]{1,0:T(8,128)(2,1)S(1)}, bf16[64,1152]{1,0:T(8,128)(2,1)S(1)}, bf16[256,3456]{1,0:T(8,128)(2,1)S(1)}) custom-call(bf16[64,3456]{1,0:T(8,128)(2,1)S(1)} %shard_map.92.first_ref, bf16[64,1152]{1,0:T(8,128)(2,1)S(1)} %collective-permute-done.1.a1, ...), custom_call_target="tpu_custom_call" | custom-call | tf_op jit(solution)/shard_map/pallas_call | solution.py:34
  20.8 3.4 %collective-permute-start.4 = (bf16[64,1152]{1,0:T(8,128)(2,1)S(1)}, bf16[64,1152]{1,0:T(8,128)(2,1)S(1)}, u32[]{:S(2)}, u32[]{:S(2)}) collective-permute-start(bf16[64,1152]{1,0:T(8,128)(2,1)S(1)} %get-tuple-element.43), channel_id=1, source_target_pairs={{0,6},{2,0},{4,2},{6,4},{1,7},{3,1},{5,3},{7,5},{8,14},{10,8},{12,... | collective-permute-start | bytes 442376 | tf_op jit(solution)/shard_map/ppermute | solution.py:23
  24.2 0.7 collective-permute-start.6
  24.9 1.1 shard_map.94.a0
  26.1 0.8 shard_map.95.base_ref
  26.8 3.4 %collective-permute-done.4.a1 = bf16[64,1152]{1,0:T(8,128)(2,1)S(1)} collective-permute-done((bf16[64,1152]{1,0:T(8,128)(2,1)S(1)}, bf16[64,1152]{1,0:T(8,128)(2,1)S(1)}, u32[]{:S(2)}, u32[]{:S(2)}) %collective-permute-start.4) | collective-permute-done | bytes 147488 | tf_op jit(solution)/shard_map/ppermute | solution.py:23
  30.4 3.6 %collective-permute-done.6.a3 = bf16[64,1152]{1,0:T(8,128)(2,1)S(1)} collective-permute-done((bf16[64,1152]{1,0:T(8,128)(2,1)S(1)}, bf16[64,1152]{1,0:T(8,128)(2,1)S(1)}, u32[]{:S(2)}, u32[]{:S(2)}) %collective-permute-start.6) | collective-permute-done | bytes 147488 | tf_op jit(solution)/shard_map/ppermute | solution.py:23
  34.1 1.6 %shard_map.96 = (f32[4,32,1152]{2,1,0:T(8,128)S(1)}, f32[4,32,1152]{2,1,0:T(8,128)S(1)}, f32[8,8,1152]{2,1,0:T(8,128)S(1)}) custom-call(s32[7]{0:T(128)S(1)} %pad_add_fusion.where_ref, f32[3,4]{1,0:T(4,128)S(1)} %pad_maximum_fusion.1.coef_ref, bf16[64,1152]{1,0:T(8,128)(2,1)S(1)} %shard_map.94.a0, bf16[64,1152]{1,0:T(8,128)(2,1)S(1)} %collective-permute-done.4.a1, ...), custom_call_target="tpu_custom_call" | custom-call | tf_op jit(solution)/shard_map/pallas_call | solution.py:34
  35.7 9.6 %all_to_all.20.held_ref = f32[8,8,1152]{2,1,0:T(8,128)S(1)} all-to-all(f32[8,8,1152]{2,1,0:T(8,128)S(1)} %get-tuple-element.50), channel_id=1, replica_groups=mesh['w'=2,'v'=2,'u'=2,'y'=4,'x'=4,'c'=2] {'u','y'}, dimensions={0} | all-to-all | bytes 589824 | tf_op jit(solution)/shard_map/all_to_all | solution.py:257
  45.3 3.1 %collective-permute-start.8 = (f32[8,1152]{1,0:T(8,128)S(1)}, f32[8,1152]{1,0:T(8,128)S(1)}, u32[]{:S(2)}, u32[]{:S(2)}) collective-permute-start(f32[8,1152]{1,0:T(8,128)S(1)} %get-tuple-element.52), channel_id=1, source_target_pairs={{0,64},{64,128},{128,192},{192,0},{1,65},{65,129},{129,193},{193,1... | collective-permute-start | bytes 110600 | tf_op jit(solution)/shard_map/ppermute | solution.py:23
  48.4 4.2 %collective-permute-start.9 = (f32[8,1152]{1,0:T(8,128)S(1)}, f32[8,1152]{1,0:T(8,128)S(1)}, u32[]{:S(2)}, u32[]{:S(2)}) collective-permute-start(f32[8,1152]{1,0:T(8,128)S(1)} %get-tuple-element.52), channel_id=1, source_target_pairs={{0,128},{64,192},{128,0},{192,64},{1,129},{65,193},{129,1},{193,65... | collective-permute-start | bytes 110600 | tf_op jit(solution)/shard_map/ppermute | solution.py:23
  52.6 2.4 %collective-permute-start.10 = (f32[8,1152]{1,0:T(8,128)S(1)}, f32[8,1152]{1,0:T(8,128)S(1)}, u32[]{:S(2)}, u32[]{:S(2)}) collective-permute-start(f32[8,1152]{1,0:T(8,128)S(1)} %get-tuple-element.52), channel_id=1, source_target_pairs={{0,192},{64,0},{128,64},{192,128},{1,193},{65,1},{129,65},{193,129... | collective-permute-start | bytes 110600 | tf_op jit(solution)/shard_map/ppermute | solution.py:23
  55.5 1.3 collective-permute-done.10.refs_2_
  57.4 9.1 %all_to_all.21.lower_ref = f32[8,8,1152]{2,1,0:T(8,128)S(1)} all-to-all(f32[8,8,1152]{2,1,0:T(8,128)S(1)} %shard_map.98), channel_id=1, replica_groups=mesh['w'=2,'v'=2,'u'=2,'y'=4,'x'=4,'c'=2] {'u','y'}, dimensions={0} | all-to-all | bytes 589824 | tf_op jit(solution)/shard_map/all_to_all | solution.py:264
  66.5 1.1 shard_map.99
  67.7 1.6 %collective-permute-start.12 = (bf16[64,1152]{1,0:T(8,128)(2,1)S(1)}, bf16[64,1152]{1,0:T(8,128)(2,1)S(1)}, u32[]{:S(2)}, u32[]{:S(2)}) collective-permute-start(bf16[64,1152]{1,0:T(8,128)(2,1)S(1)} %get-tuple-element.55), channel_id=1, source_target_pairs={{0,4},{2,6},{4,0},{6,2},{1,5},{3,7},{5,1},{7,3},{8,12},{10,14},{12... | collective-permute-start | bytes 442376 | tf_op jit(solution)/shard_map/ppermute | solution.py:23
  69.3 2.0 %collective-permute-start.13 = (bf16[64,1152]{1,0:T(8,128)(2,1)S(1)}, bf16[64,1152]{1,0:T(8,128)(2,1)S(1)}, u32[]{:S(2)}, u32[]{:S(2)}) collective-permute-start(bf16[64,1152]{1,0:T(8,128)(2,1)S(1)} %get-tuple-element.56), channel_id=1, source_target_pairs={{0,6},{2,0},{4,2},{6,4},{1,7},{3,1},{5,3},{7,5},{8,14},{10,8},{12,... | collective-permute-start | bytes 442376 | tf_op jit(solution)/shard_map/ppermute | solution.py:23
  71.3 1.3 shard_map.100.first_ref
  72.6 1.9 %collective-permute-done.11.a1 = bf16[64,1152]{1,0:T(8,128)(2,1)S(1)} collective-permute-done((bf16[64,1152]{1,0:T(8,128)(2,1)S(1)}, bf16[64,1152]{1,0:T(8,128)(2,1)S(1)}, u32[]{:S(2)}, u32[]{:S(2)}) %collective-permute-start.11) | collective-permute-done | bytes 147488 | tf_op jit(solution)/shard_map/ppermute | solution.py:23
  75.1 3.3 %shard_map.101 = (bf16[64,1152]{1,0:T(8,128)(2,1)S(1)}, bf16[64,1152]{1,0:T(8,128)(2,1)S(1)}, bf16[64,1152]{1,0:T(8,128)(2,1)S(1)}, bf16[256,3456]{1,0:T(8,128)(2,1)S(1)}) custom-call(bf16[64,3456]{1,0:T(8,128)(2,1)S(1)} %shard_map.100.first_ref, bf16[64,1152]{1,0:T(8,128)(2,1)S(1)} %collective-permute-done.11.a1, ...), custom_call_target="tpu_custom_call" | custom-call | tf_op jit(solution)/shard_map/pallas_call | solution.py:34
  78.3 2.5 %collective-permute-start.14 = (bf16[64,1152]{1,0:T(8,128)(2,1)S(1)}, bf16[64,1152]{1,0:T(8,128)(2,1)S(1)}, u32[]{:S(2)}, u32[]{:S(2)}) collective-permute-start(bf16[64,1152]{1,0:T(8,128)(2,1)S(1)} %get-tuple-element.58), channel_id=1, source_target_pairs={{0,6},{2,0},{4,2},{6,4},{1,7},{3,1},{5,3},{7,5},{8,14},{10,8},{12,... | collective-permute-start | bytes 442376 | tf_op jit(solution)/shard_map/ppermute | solution.py:23
  80.8 0.6 collective-permute-start.15
  81.5 0.7 shard_map.103.base_ref
  82.2 1.1 shard_map.102.a0
  83.3 1.1 collective-permute-done.14.a1
  84.5 1.9 %collective-permute-done.15.a2 = bf16[64,1152]{1,0:T(8,128)(2,1)S(1)} collective-permute-done((bf16[64,1152]{1,0:T(8,128)(2,1)S(1)}, bf16[64,1152]{1,0:T(8,128)(2,1)S(1)}, u32[]{:S(2)}, u32[]{:S(2)}) %collective-permute-start.15) | collective-permute-done | bytes 147488 | tf_op jit(solution)/shard_map/ppermute | solution.py:23
  86.4 1.5 %collective-permute-done.16.a3 = bf16[64,1152]{1,0:T(8,128)(2,1)S(1)} collective-permute-done((bf16[64,1152]{1,0:T(8,128)(2,1)S(1)}, bf16[64,1152]{1,0:T(8,128)(2,1)S(1)}, u32[]{:S(2)}, u32[]{:S(2)}) %collective-permute-start.16) | collective-permute-done | bytes 147488 | tf_op jit(solution)/shard_map/ppermute | solution.py:23
  87.9 1.6 %shard_map.104 = (f32[4,32,1152]{2,1,0:T(8,128)S(1)}, f32[4,32,1152]{2,1,0:T(8,128)S(1)}, f32[8,8,1152]{2,1,0:T(8,128)S(1)}) custom-call(s32[7]{0:T(128)S(1)} %pad_add_fusion.where_ref, f32[3,4]{1,0:T(4,128)S(1)} %pad_maximum_fusion.1.coef_ref, bf16[64,1152]{1,0:T(8,128)(2,1)S(1)} %shard_map.102.a0, bf16[64,1152]{1,0:T(8,128)(2,1)S(1)} %collective-permute-done.14.a1, ...), custom_call_target="tpu_custom_call" | custom-call | tf_op jit(solution)/shard_map/pallas_call | solution.py:34
  89.5 7.9 %collective-permute-start.18 = (f32[4,32,1152]{2,1,0:T(8,128)S(1)}, f32[4,32,1152]{2,1,0:T(8,128)S(1)}, u32[]{:S(2)}, u32[]{:S(2)}) collective-permute-start(f32[4,32,1152]{2,1,0:T(8,128)S(1)} %get-tuple-element.65), channel_id=1, source_target_pairs={{0,1},{1,0},{2,3},{3,2},{4,5},{5,4},{6,7},{7,6},{8,9},{9,8},{10,11... | collective-permute-start | bytes 1769480 | tf_op jit(solution)/shard_map/ppermute | solution.py:23
  97.5 10.0 %all_to_all.22.held_ref = f32[8,8,1152]{2,1,0:T(8,128)S(1)} all-to-all(f32[8,8,1152]{2,1,0:T(8,128)S(1)} %get-tuple-element.63), channel_id=1, replica_groups=mesh['w'=2,'v'=2,'u'=2,'y'=4,'x'=4,'c'=2] {'u','y'}, dimensions={0} | all-to-all | bytes 589824 | tf_op jit(solution)/shard_map/all_to_all | solution.py:257
  107.5 1.7 %collective-permute-start.17 = (f32[8,1152]{1,0:T(8,128)S(1)}, f32[8,1152]{1,0:T(8,128)S(1)}, u32[]{:S(2)}, u32[]{:S(2)}) collective-permute-start(f32[8,1152]{1,0:T(8,128)S(1)} %get-tuple-element.64), channel_id=1, source_target_pairs={{0,64},{64,128},{128,192},{192,0},{1,65},{65,129},{129,193},{193,1... | collective-permute-start | bytes 110600 | tf_op jit(solution)/shard_map/ppermute | solution.py:23
  109.2 3.9 %collective-permute-start.19 = (f32[8,1152]{1,0:T(8,128)S(1)}, f32[8,1152]{1,0:T(8,128)S(1)}, u32[]{:S(2)}, u32[]{:S(2)}) collective-permute-start(f32[8,1152]{1,0:T(8,128)S(1)} %get-tuple-element.64), channel_id=1, source_target_pairs={{0,128},{64,192},{128,0},{192,64},{1,129},{65,193},{129,1},{193,65... | collective-permute-start | bytes 110600 | tf_op jit(solution)/shard_map/ppermute | solution.py:23
  113.1 0.6 collective-permute-start.20
  113.7 2.5 %collective-permute-done.19.refs_1_ = f32[8,1152]{1,0:T(8,128)S(1)} collective-permute-done((f32[8,1152]{1,0:T(8,128)S(1)}, f32[8,1152]{1,0:T(8,128)S(1)}, u32[]{:S(2)}, u32[]{:S(2)}) %collective-permute-start.19) | collective-permute-done | bytes 36896 | tf_op jit(solution)/shard_map/ppermute | solution.py:23
  116.2 1.4 %collective-permute-done.20.refs_2_ = f32[8,1152]{1,0:T(8,128)S(1)} collective-permute-done((f32[8,1152]{1,0:T(8,128)S(1)}, f32[8,1152]{1,0:T(8,128)S(1)}, u32[]{:S(2)}, u32[]{:S(2)}) %collective-permute-start.20) | collective-permute-done | bytes 36896 | tf_op jit(solution)/shard_map/ppermute | solution.py:23
  118.2 9.1 %all_to_all.23.mine_lower = f32[8,8,1152]{2,1,0:T(8,128)S(1)} all-to-all(f32[8,8,1152]{2,1,0:T(8,128)S(1)} %shard_map.106), channel_id=1, replica_groups=mesh['w'=2,'v'=2,'u'=2,'y'=4,'x'=4,'c'=2] {'u','y'}, dimensions={0} | all-to-all | bytes 589824 | tf_op jit(solution)/shard_map/all_to_all | solution.py:264
  127.2 3.6 %collective-permute-start.21 = (f32[8,8,1152]{2,1,0:T(8,128)S(1)}, f32[8,8,1152]{2,1,0:T(8,128)S(1)}, u32[]{:S(2)}, u32[]{:S(2)}) collective-permute-start(f32[8,8,1152]{2,1,0:T(8,128)S(1)} %all_to_all.23.mine_lower), channel_id=1, source_target_pairs={{0,1},{1,0},{2,3},{3,2},{4,5},{5,4},{6,7},{7,6},{8,9},{9,8},{10,11... | collective-permute-start | bytes 884744 | tf_op jit(solution)/shard_map/ppermute | solution.py:23
  130.8 1.2 collective-permute-done.21.peer_lower
  132.0 1.6 %shard_map.107 = f32[4,2,32,1152]{3,2,1,0:T(8,128)} custom-call(s32[7]{0:T(128)S(1)} %pad_add_fusion.where_ref, f32[2,32,1152]{2,1,0:T(8,128)S(1)} %copy-done.4, f32[4,32,1152]{2,1,0:T(8,128)S(1)} %get-tuple-element.62.mine_before, f32[4,32,1152]{2,1,0:T(8,128)S(1)} %collective-permute-done.18.peer_before, f32[8,8,1152]{2,1,0:T(8,128)S(1)} %all_to_all.23.mine_lower, ...), custom_call_target="tpu_custom_call" | custom-call | tf_op jit(solution)/shard_map/pallas_call | solution.py:34
  (47 shorter events, 3.9 us)
Async XLA Ops:
  0.0 4.9 %copy-start = (s32[4,2]{0,1:T(2,128)S(1)}, s32[4,2]{0,1:T(2,128)}, u32[]{:S(2)}) copy-start(s32[4,2]{0,1:T(2,128)} %param.15) | copy-start | bytes 100
  0.0 1.4 %copy-start.4 = (f32[2,32,1152]{2,1,0:T(8,128)S(1)}, f32[2,32,1152]{2,1,0:T(8,128)}, u32[]{:S(2)}) copy-start(f32[2,32,1152]{2,1,0:T(8,128)} %start_ref.1) | copy-start | bytes 884740
  1.4 3.4 %copy-start.7 = (f32[4,3,1152]{2,0,1:T(4,128)S(1)}, f32[4,3,1152]{2,0,1:T(4,128)}, u32[]{:S(2)}) copy-start(f32[4,3,1152]{2,0,1:T(4,128)} %param.13) | copy-start | bytes 165892
  1.4 3.4 %copy-start.6 = (f32[8,3,1152]{2,0,1:T(8,128)S(1)}, f32[8,3,1152]{2,0,1:T(8,128)}, u32[]{:S(2)}) copy-start(f32[8,3,1152]{2,0,1:T(8,128)} %param.14) | copy-start | bytes 331780
  1.5 5.1 %collective-permute-start = (f32[5,32,1152]{2,1,0:T(8,128)S(1)}, f32[5,32,1152]{2,1,0:T(8,128)S(1)}, u32[]{:S(2)}, u32[]{:S(2)}) collective-permute-start(f32[5,32,1152]{2,1,0:T(8,128)S(1)} %pad_maximum_fusion), channel_id=1, source_target_pairs={{0,1},{1,0},{2,3},{3,2},{4,5},{5,4},{6,7},{7,6},{8,9},{9,8},{10,11... | collective-permute-start | bytes 2211848 | tf_op jit(solution)/shard_map/ppermute | solution.py:23
  7.7 9.2 %collective-permute-start.1 = (bf16[64,1152]{1,0:T(8,128)(2,1)S(1)}, bf16[64,1152]{1,0:T(8,128)(2,1)S(1)}, u32[]{:S(2)}, u32[]{:S(2)}) collective-permute-start(bf16[64,1152]{1,0:T(8,128)(2,1)S(1)} %get-tuple-element.39), channel_id=1, source_target_pairs={{0,2},{2,4},{4,6},{6,0},{1,3},{3,5},{5,7},{7,1},{8,10},{10,12},{12... | collective-permute-start | bytes 442376 | tf_op jit(solution)/shard_map/ppermute | solution.py:23
  7.8 9.2 %collective-permute-start.2 = (bf16[64,1152]{1,0:T(8,128)(2,1)S(1)}, bf16[64,1152]{1,0:T(8,128)(2,1)S(1)}, u32[]{:S(2)}, u32[]{:S(2)}) collective-permute-start(bf16[64,1152]{1,0:T(8,128)(2,1)S(1)} %get-tuple-element.40), channel_id=1, source_target_pairs={{0,4},{2,6},{4,0},{6,2},{1,5},{3,7},{5,1},{7,3},{8,12},{10,14},{12... | collective-permute-start | bytes 442376 | tf_op jit(solution)/shard_map/ppermute | solution.py:23
  9.7 7.8 %collective-permute-start.3 = (bf16[64,1152]{1,0:T(8,128)(2,1)S(1)}, bf16[64,1152]{1,0:T(8,128)(2,1)S(1)}, u32[]{:S(2)}, u32[]{:S(2)}) collective-permute-start(bf16[64,1152]{1,0:T(8,128)(2,1)S(1)} %get-tuple-element.41), channel_id=1, source_target_pairs={{0,6},{2,0},{4,2},{6,4},{1,7},{3,1},{5,3},{7,5},{8,14},{10,8},{12,... | collective-permute-start | bytes 442376 | tf_op jit(solution)/shard_map/ppermute | solution.py:23
  10.9 3.3 %copy-start.1 = (bf16[1152,3456]{1,0:T(8,128)(2,1)S(1)}, bf16[1152,3456]{1,0:T(8,128)(2,1)}, u32[]{:S(2)}) copy-start(bf16[1152,3456]{1,0:T(8,128)(2,1)} %w_ref.10) | copy-start | bytes 23887876
  14.1 1.4 %copy-start.5 = (bf16[4,2,32,1152]{3,2,1,0:T(8,128)(2,1)S(1)}, bf16[4,2,32,1152]{3,2,1,0:T(8,128)(2,1)}, u32[]{:S(2)}) copy-start(bf16[4,2,32,1152]{3,2,1,0:T(8,128)(2,1)} %param.10) | copy-start | bytes 1769476
  14.1 3.5 %copy-start.2 = (bf16[1152,3456]{1,0:T(8,128)(2,1)S(1)}, bf16[1152,3456]{1,0:T(8,128)(2,1)}, u32[]{:S(2)}) copy-start(bf16[1152,3456]{1,0:T(8,128)(2,1)} %w_ref.10) | copy-start | bytes 23887876
  15.6 9.3 %copy-start.8 = (s32[4]{0:T(128)S(1)}, s32[4]{0:T(128)}, u32[]{:S(2)}) copy-start(s32[4]{0:T(128)} %param.12) | copy-start | bytes 52
  15.6 10.4 %collective-permute-start.7 = (bf16[4,32,1152]{2,1,0:T(8,128)(2,1)S(1)}, bf16[4,32,1152]{2,1,0:T(8,128)(2,1)S(1)}, u32[]{:S(2)}, u32[]{:S(2)}) collective-permute-start(bf16[4,32,1152]{2,1,0:T(8,128)(2,1)S(1)} %get-tuple-element.71), channel_id=1, source_target_pairs={{0,1},{1,0},{2,3},{3,2},{4,5},{5,4},{6,7},{7,6},{8,9},{9,8},{10,11... | collective-permute-start | bytes 884744 | tf_op jit(solution)/shard_map/ppermute | solution.py:23
  20.8 9.4 %collective-permute-start.4 = (bf16[64,1152]{1,0:T(8,128)(2,1)S(1)}, bf16[64,1152]{1,0:T(8,128)(2,1)S(1)}, u32[]{:S(2)}, u32[]{:S(2)}) collective-permute-start(bf16[64,1152]{1,0:T(8,128)(2,1)S(1)} %get-tuple-element.43), channel_id=1, source_target_pairs={{0,6},{2,0},{4,2},{6,4},{1,7},{3,1},{5,3},{7,5},{8,14},{10,8},{12,... | collective-permute-start | bytes 442376 | tf_op jit(solution)/shard_map/ppermute | solution.py:23
  24.2 6.2 %collective-permute-start.5 = (bf16[64,1152]{1,0:T(8,128)(2,1)S(1)}, bf16[64,1152]{1,0:T(8,128)(2,1)S(1)}, u32[]{:S(2)}, u32[]{:S(2)}) collective-permute-start(bf16[64,1152]{1,0:T(8,128)(2,1)S(1)} %get-tuple-element.44), channel_id=1, source_target_pairs={{0,4},{2,6},{4,0},{6,2},{1,5},{3,7},{5,1},{7,3},{8,12},{10,14},{12... | collective-permute-start | bytes 442376 | tf_op jit(solution)/shard_map/ppermute | solution.py:23
  24.2 9.8 %collective-permute-start.6 = (bf16[64,1152]{1,0:T(8,128)(2,1)S(1)}, bf16[64,1152]{1,0:T(8,128)(2,1)S(1)}, u32[]{:S(2)}, u32[]{:S(2)}) collective-permute-start(bf16[64,1152]{1,0:T(8,128)(2,1)S(1)} %get-tuple-element.45), channel_id=1, source_target_pairs={{0,2},{2,4},{4,6},{6,0},{1,3},{3,5},{5,7},{7,1},{8,10},{10,12},{12... | collective-permute-start | bytes 442376 | tf_op jit(solution)/shard_map/ppermute | solution.py:23
  26.0 8.0 %copy-start.3 = (bf16[1152,1152]{1,0:T(8,128)(2,1)S(1)}, bf16[1152,1152]{1,0:T(8,128)(2,1)}, u32[]{:S(2)}) copy-start(bf16[1152,1152]{1,0:T(8,128)(2,1)} %w_ref.11) | copy-start | bytes 7962628
  45.3 9.7 %collective-permute-start.8 = (f32[8,1152]{1,0:T(8,128)S(1)}, f32[8,1152]{1,0:T(8,128)S(1)}, u32[]{:S(2)}, u32[]{:S(2)}) collective-permute-start(f32[8,1152]{1,0:T(8,128)S(1)} %get-tuple-element.52), channel_id=1, source_target_pairs={{0,64},{64,128},{128,192},{192,0},{1,65},{65,129},{129,193},{193,1... | collective-permute-start | bytes 110600 | tf_op jit(solution)/shard_map/ppermute | solution.py:23
  48.4 7.1 %collective-permute-start.9 = (f32[8,1152]{1,0:T(8,128)S(1)}, f32[8,1152]{1,0:T(8,128)S(1)}, u32[]{:S(2)}, u32[]{:S(2)}) collective-permute-start(f32[8,1152]{1,0:T(8,128)S(1)} %get-tuple-element.52), channel_id=1, source_target_pairs={{0,128},{64,192},{128,0},{192,64},{1,129},{65,193},{129,1},{193,65... | collective-permute-start | bytes 110600 | tf_op jit(solution)/shard_map/ppermute | solution.py:23
  52.6 4.2 %collective-permute-start.10 = (f32[8,1152]{1,0:T(8,128)S(1)}, f32[8,1152]{1,0:T(8,128)S(1)}, u32[]{:S(2)}, u32[]{:S(2)}) collective-permute-start(f32[8,1152]{1,0:T(8,128)S(1)} %get-tuple-element.52), channel_id=1, source_target_pairs={{0,192},{64,0},{128,64},{192,128},{1,193},{65,1},{129,65},{193,129... | collective-permute-start | bytes 110600 | tf_op jit(solution)/shard_map/ppermute | solution.py:23
  67.6 6.9 %collective-permute-start.11 = (bf16[64,1152]{1,0:T(8,128)(2,1)S(1)}, bf16[64,1152]{1,0:T(8,128)(2,1)S(1)}, u32[]{:S(2)}, u32[]{:S(2)}) collective-permute-start(bf16[64,1152]{1,0:T(8,128)(2,1)S(1)} %get-tuple-element.54), channel_id=1, source_target_pairs={{0,2},{2,4},{4,6},{6,0},{1,3},{3,5},{5,7},{7,1},{8,10},{10,12},{12... | collective-permute-start | bytes 442376 | tf_op jit(solution)/shard_map/ppermute | solution.py:23
  67.7 6.8 %collective-permute-start.12 = (bf16[64,1152]{1,0:T(8,128)(2,1)S(1)}, bf16[64,1152]{1,0:T(8,128)(2,1)S(1)}, u32[]{:S(2)}, u32[]{:S(2)}) collective-permute-start(bf16[64,1152]{1,0:T(8,128)(2,1)S(1)} %get-tuple-element.55), channel_id=1, source_target_pairs={{0,4},{2,6},{4,0},{6,2},{1,5},{3,7},{5,1},{7,3},{8,12},{10,14},{12... | collective-permute-start | bytes 442376 | tf_op jit(solution)/shard_map/ppermute | solution.py:23
  69.3 5.7 %collective-permute-start.13 = (bf16[64,1152]{1,0:T(8,128)(2,1)S(1)}, bf16[64,1152]{1,0:T(8,128)(2,1)S(1)}, u32[]{:S(2)}, u32[]{:S(2)}) collective-permute-start(bf16[64,1152]{1,0:T(8,128)(2,1)S(1)} %get-tuple-element.56), channel_id=1, source_target_pairs={{0,6},{2,0},{4,2},{6,4},{1,7},{3,1},{5,3},{7,5},{8,14},{10,8},{12,... | collective-permute-start | bytes 442376 | tf_op jit(solution)/shard_map/ppermute | solution.py:23
  78.3 6.1 %collective-permute-start.14 = (bf16[64,1152]{1,0:T(8,128)(2,1)S(1)}, bf16[64,1152]{1,0:T(8,128)(2,1)S(1)}, u32[]{:S(2)}, u32[]{:S(2)}) collective-permute-start(bf16[64,1152]{1,0:T(8,128)(2,1)S(1)} %get-tuple-element.58), channel_id=1, source_target_pairs={{0,6},{2,0},{4,2},{6,4},{1,7},{3,1},{5,3},{7,5},{8,14},{10,8},{12,... | collective-permute-start | bytes 442376 | tf_op jit(solution)/shard_map/ppermute | solution.py:23
  80.8 5.6 %collective-permute-start.15 = (bf16[64,1152]{1,0:T(8,128)(2,1)S(1)}, bf16[64,1152]{1,0:T(8,128)(2,1)S(1)}, u32[]{:S(2)}, u32[]{:S(2)}) collective-permute-start(bf16[64,1152]{1,0:T(8,128)(2,1)S(1)} %get-tuple-element.59), channel_id=1, source_target_pairs={{0,4},{2,6},{4,0},{6,2},{1,5},{3,7},{5,1},{7,3},{8,12},{10,14},{12... | collective-permute-start | bytes 442376 | tf_op jit(solution)/shard_map/ppermute | solution.py:23
  81.4 6.5 %collective-permute-start.16 = (bf16[64,1152]{1,0:T(8,128)(2,1)S(1)}, bf16[64,1152]{1,0:T(8,128)(2,1)S(1)}, u32[]{:S(2)}, u32[]{:S(2)}) collective-permute-start(bf16[64,1152]{1,0:T(8,128)(2,1)S(1)} %get-tuple-element.60), channel_id=1, source_target_pairs={{0,2},{2,4},{4,6},{6,0},{1,3},{3,5},{5,7},{7,1},{8,10},{10,12},{12... | collective-permute-start | bytes 442376 | tf_op jit(solution)/shard_map/ppermute | solution.py:23
  89.5 24.2 %collective-permute-start.18 = (f32[4,32,1152]{2,1,0:T(8,128)S(1)}, f32[4,32,1152]{2,1,0:T(8,128)S(1)}, u32[]{:S(2)}, u32[]{:S(2)}) collective-permute-start(f32[4,32,1152]{2,1,0:T(8,128)S(1)} %get-tuple-element.65), channel_id=1, source_target_pairs={{0,1},{1,0},{2,3},{3,2},{4,5},{5,4},{6,7},{7,6},{8,9},{9,8},{10,11... | collective-permute-start | bytes 1769480 | tf_op jit(solution)/shard_map/ppermute | solution.py:23
  107.5 6.3 %collective-permute-start.17 = (f32[8,1152]{1,0:T(8,128)S(1)}, f32[8,1152]{1,0:T(8,128)S(1)}, u32[]{:S(2)}, u32[]{:S(2)}) collective-permute-start(f32[8,1152]{1,0:T(8,128)S(1)} %get-tuple-element.64), channel_id=1, source_target_pairs={{0,64},{64,128},{128,192},{192,0},{1,65},{65,129},{129,193},{193,1... | collective-permute-start | bytes 110600 | tf_op jit(solution)/shard_map/ppermute | solution.py:23
  109.2 7.0 %collective-permute-start.19 = (f32[8,1152]{1,0:T(8,128)S(1)}, f32[8,1152]{1,0:T(8,128)S(1)}, u32[]{:S(2)}, u32[]{:S(2)}) collective-permute-start(f32[8,1152]{1,0:T(8,128)S(1)} %get-tuple-element.64), channel_id=1, source_target_pairs={{0,128},{64,192},{128,0},{192,64},{1,129},{65,193},{129,1},{193,65... | collective-permute-start | bytes 110600 | tf_op jit(solution)/shard_map/ppermute | solution.py:23
  113.1 4.5 %collective-permute-start.20 = (f32[8,1152]{1,0:T(8,128)S(1)}, f32[8,1152]{1,0:T(8,128)S(1)}, u32[]{:S(2)}, u32[]{:S(2)}) collective-permute-start(f32[8,1152]{1,0:T(8,128)S(1)} %get-tuple-element.64), channel_id=1, source_target_pairs={{0,192},{64,0},{128,64},{192,128},{1,193},{65,1},{129,65},{193,129... | collective-permute-start | bytes 110600 | tf_op jit(solution)/shard_map/ppermute | solution.py:23
  127.2 4.8 %collective-permute-start.21 = (f32[8,8,1152]{2,1,0:T(8,128)S(1)}, f32[8,8,1152]{2,1,0:T(8,128)S(1)}, u32[]{:S(2)}, u32[]{:S(2)}) collective-permute-start(f32[8,8,1152]{2,1,0:T(8,128)S(1)} %all_to_all.23.mine_lower), channel_id=1, source_target_pairs={{0,1},{1,0},{2,3},{3,2},{4,5},{5,4},{6,7},{7,6},{8,9},{9,8},{10,11... | collective-permute-start | bytes 884744 | tf_op jit(solution)/shard_map/ppermute | solution.py:23

commit v10 on v9

--- a/solution.py
+++ b/solution.py
@@ -53,15 +53,23 @@
     return step_ref[step, part : part + 1, :] + view_ref[where_ref[3 + step], part : part + 1, :]
 
 
-def enter_body(where_ref, mine_ref, start_mine, peer_ref, step_ref, view_ref, x_ref, start_ref, *mod_refs):
-    place = where_ref[0]
-    start_ref[...] = jnp.concatenate([start_mine[...], peer_ref[mine_ref.shape[0]]], axis=0)
-    steps = mine_ref.shape[0]
+def give_body(core_ref, states_ref, start_ref, out_ref):
+    other = 1 - core_ref[0]
+    steps = states_ref.shape[0]
+    for step in range(steps):
+        out_ref[step] = states_ref[step, other]
+    out_ref[steps] = start_ref[other]
+
+
+def enter_body(where_ref, states_ref, all_start, peer_ref, step_ref, view_ref, x_ref, start_ref, *mod_refs):
+    place, core = where_ref[0], where_ref[2]
+    steps = states_ref.shape[0]
+    start_ref[...] = jnp.concatenate([all_start[core], peer_ref[steps]], axis=0)
     for r in range(steps):
         step = lax.rem(place + r, steps)
         shift = modulation_row(where_ref, step_ref, view_ref, step, 0)
         scale = modulation_row(where_ref, step_ref, view_ref, step, 1)
-        rows = jnp.concatenate([mine_ref[step], peer_ref[step]], axis=0)
+        rows = jnp.concatenate([states_ref[step, core], peer_ref[step]], axis=0)
         x_ref[step] = rows
         mod_refs[r][...] = normed_rows(rows, shift, scale)
 
@@ -280,8 +288,9 @@
     def shape(*dims, kind=f32):
         return jax.ShapeDtypeStruct(dims, kind)
 
-    swapped = shifted(jnp.concatenate([given(states, 1), given(x_start, 0)[None]], axis=0), "c", 1)
-    states_mine, start_mine = own(states, 1), own(x_start, 0)
+    cores = jnp.reshape(core, (1,)).astype(jnp.int32)
+    given_rows = call(give_body, shape(steps + 1, part, width), [SMEM] + [VMEM] * 2, cores, states, x_start)
+    swapped = shifted(given_rows, "c", 1)
     where = jnp.concatenate([jnp.stack([place, group, core]).astype(jnp.int32), own(view_ids, 1)])
     coefs = jnp.stack(coefficients(timesteps))
     size = width // HEADS
@@ -298,8 +307,8 @@
         [x_shape, shape(rows, width)] + [piece] * steps,
         [SMEM] + [VMEM] * 5,
         where,
-        states_mine,
-        start_mine,
+        states,
+        x_start,
         swapped,
         step_mod,
         view_mod,

time: 134 us -> 135 us (level)
    unnamed x20 -> x26, local copies, waits for them, and re-layouts: 3.45 us -> 5.69 us
    squeeze x2 -> x1, local copies, waits for them, and re-layouts: 1.42 us -> 0.06 us  [given(): return lax.dynamic_index_in_dim(a, other, axis, keepdims=False)]
    pallas_call x17 -> x18, Pallas kernels: 21.2 us -> 21.3 us  [call(): pl.pallas_call(body, out_shape=outs, in_specs=specs, out_specs=jax.tree.m...]
where the time goes in v10:
time: 135 us
  starting transfers between devices  46.7 us (35%)
  blocking collectives  37.5 us (28%)
  waiting for transfers between devices  22.8 us (17%)
  Pallas kernels  21.3 us (16%)
  local copies, waits for them, and re-layouts  5.76 us (4%)
    ppermute x22, starting transfers between devices, shifted(): lax.ppermute(value, axis, [(i, (i + shift) % size) for i in range(size)])  46.7 us
    ppermute x22, waiting for transfers between devices, shifted(): lax.ppermute(value, axis, [(i, (i + shift) % size) for i in range(size)])  22.8 us
    pallas_call x18, Pallas kernels, call(): pl.pallas_call(body, out_shape=outs, in_specs=specs, out_specs=jax.tree.m...  21.3 us
    all_to_all x2, blocking collectives, earlier_sum(): held = lax.all_to_all(shares, SHARES, 0, 0, tiled=True)  19.6 us
    all_to_all x2, blocking collectives, earlier_sum(): return (lax.all_to_all(sums, SHARES, 0, 0, tiled=True), beside)  18 us
    unnamed x26, local copies, waits for them, and re-layouts  5.69 us
  transfers between devices with their start and end apart: 22, of which 15 were waited for; matrix products, arithmetic and copies ran while one was open for 0% of the time, Pallas kernels for 7%

profile of v10, /device:TPU:1, one launch (start us, length us, event | category | flops | bytes accessed | tf_op | source)
XLA Modules:
  0.0 134.7 jit_solution(15737048015567277235)
XLA Ops:
  0.0 1.3 copy-done.4
  1.3 1.0 copy-done.6
  2.3 3.3 %collective-permute-start = (f32[5,32,1152]{2,1,0:T(8,128)S(1)}, f32[5,32,1152]{2,1,0:T(8,128)S(1)}, u32[]{:S(2)}, u32[]{:S(2)}) collective-permute-start(f32[5,32,1152]{2,1,0:T(8,128)S(1)} %shard_map.91), channel_id=1, source_target_pairs={{0,1},{1,0},{2,3},{3,2},{4,5},{5,4},{6,7},{7,6},{8,9},{9,8},{10,11... | collective-permute-start | bytes 2211848 | tf_op jit(solution)/shard_map/ppermute | solution.py:23
  5.9 1.6 %collective-permute-done.peer_ref = f32[5,32,1152]{2,1,0:T(8,128)S(1)} collective-permute-done((f32[5,32,1152]{2,1,0:T(8,128)S(1)}, f32[5,32,1152]{2,1,0:T(8,128)S(1)}, u32[]{:S(2)}, u32[]{:S(2)}) %collective-permute-start) | collective-permute-done | bytes 737312 | tf_op jit(solution)/shard_map/ppermute | solution.py:23
  7.5 1.1 shard_map.92
  8.6 1.9 %collective-permute-start.2 = (bf16[64,1152]{1,0:T(8,128)(2,1)S(1)}, bf16[64,1152]{1,0:T(8,128)(2,1)S(1)}, u32[]{:S(2)}, u32[]{:S(2)}) collective-permute-start(bf16[64,1152]{1,0:T(8,128)(2,1)S(1)} %get-tuple-element.40), channel_id=1, source_target_pairs={{0,4},{2,6},{4,0},{6,2},{1,5},{3,7},{5,1},{7,3},{8,12},{10,14},{12... | collective-permute-start | bytes 442376 | tf_op jit(solution)/shard_map/ppermute | solution.py:23
  10.5 1.2 collective-permute-start.3
  11.7 3.3 %copy-done.1 = bf16[1152,3456]{1,0:T(8,128)(2,1)S(1)} copy-done((bf16[1152,3456]{1,0:T(8,128)(2,1)S(1)}, bf16[1152,3456]{1,0:T(8,128)(2,1)}, u32[]{:S(2)}) %copy-start.1) | copy-done | bytes 7962648
  15.0 1.3 shard_map.93.first_ref
  16.4 1.3 collective-permute-start.7
  18.4 3.2 %shard_map.94 = (bf16[64,1152]{1,0:T(8,128)(2,1)S(1)}, bf16[64,1152]{1,0:T(8,128)(2,1)S(1)}, bf16[64,1152]{1,0:T(8,128)(2,1)S(1)}, bf16[256,3456]{1,0:T(8,128)(2,1)S(1)}) custom-call(bf16[64,3456]{1,0:T(8,128)(2,1)S(1)} %shard_map.93.first_ref, bf16[64,1152]{1,0:T(8,128)(2,1)S(1)} %collective-permute-done.1.a1, ...), custom_call_target="tpu_custom_call" | custom-call | tf_op jit(solution)/shard_map/pallas_call | solution.py:34
  21.7 3.4 %collective-permute-start.4 = (bf16[64,1152]{1,0:T(8,128)(2,1)S(1)}, bf16[64,1152]{1,0:T(8,128)(2,1)S(1)}, u32[]{:S(2)}, u32[]{:S(2)}) collective-permute-start(bf16[64,1152]{1,0:T(8,128)(2,1)S(1)} %get-tuple-element.43), channel_id=1, source_target_pairs={{0,6},{2,0},{4,2},{6,4},{1,7},{3,1},{5,3},{7,5},{8,14},{10,8},{12,... | collective-permute-start | bytes 442376 | tf_op jit(solution)/shard_map/ppermute | solution.py:23
  25.0 0.7 collective-permute-start.6
  25.8 1.1 shard_map.95.a0
  26.9 0.8 shard_map.96.base_ref
  27.6 3.4 %collective-permute-done.4.a1 = bf16[64,1152]{1,0:T(8,128)(2,1)S(1)} collective-permute-done((bf16[64,1152]{1,0:T(8,128)(2,1)S(1)}, bf16[64,1152]{1,0:T(8,128)(2,1)S(1)}, u32[]{:S(2)}, u32[]{:S(2)}) %collective-permute-start.4) | collective-permute-done | bytes 147488 | tf_op jit(solution)/shard_map/ppermute | solution.py:23
  31.3 3.6 %collective-permute-done.6.a3 = bf16[64,1152]{1,0:T(8,128)(2,1)S(1)} collective-permute-done((bf16[64,1152]{1,0:T(8,128)(2,1)S(1)}, bf16[64,1152]{1,0:T(8,128)(2,1)S(1)}, u32[]{:S(2)}, u32[]{:S(2)}) %collective-permute-start.6) | collective-permute-done | bytes 147488 | tf_op jit(solution)/shard_map/ppermute | solution.py:23
  34.9 1.6 %shard_map.97 = (f32[4,32,1152]{2,1,0:T(8,128)S(1)}, f32[4,32,1152]{2,1,0:T(8,128)S(1)}, f32[8,8,1152]{2,1,0:T(8,128)S(1)}) custom-call(s32[7]{0:T(128)S(1)} %pad_add_fusion.where_ref, f32[3,4]{1,0:T(4,128)S(1)} %pad_maximum_fusion.coef_ref, bf16[64,1152]{1,0:T(8,128)(2,1)S(1)} %shard_map.95.a0, bf16[64,1152]{1,0:T(8,128)(2,1)S(1)} %collective-permute-done.4.a1, ...), custom_call_target="tpu_custom_call" | custom-call | tf_op jit(solution)/shard_map/pallas_call | solution.py:34
  36.6 9.6 %all_to_all.20.held_ref = f32[8,8,1152]{2,1,0:T(8,128)S(1)} all-to-all(f32[8,8,1152]{2,1,0:T(8,128)S(1)} %get-tuple-element.50), channel_id=1, replica_groups=mesh['w'=2,'v'=2,'u'=2,'y'=4,'x'=4,'c'=2] {'u','y'}, dimensions={0} | all-to-all | bytes 589824 | tf_op jit(solution)/shard_map/all_to_all | solution.py:265
  46.2 3.1 %collective-permute-start.8 = (f32[8,1152]{1,0:T(8,128)S(1)}, f32[8,1152]{1,0:T(8,128)S(1)}, u32[]{:S(2)}, u32[]{:S(2)}) collective-permute-start(f32[8,1152]{1,0:T(8,128)S(1)} %get-tuple-element.52), channel_id=1, source_target_pairs={{0,64},{64,128},{128,192},{192,0},{1,65},{65,129},{129,193},{193,1... | collective-permute-start | bytes 110600 | tf_op jit(solution)/shard_map/ppermute | solution.py:23
  49.3 4.2 %collective-permute-start.9 = (f32[8,1152]{1,0:T(8,128)S(1)}, f32[8,1152]{1,0:T(8,128)S(1)}, u32[]{:S(2)}, u32[]{:S(2)}) collective-permute-start(f32[8,1152]{1,0:T(8,128)S(1)} %get-tuple-element.52), channel_id=1, source_target_pairs={{0,128},{64,192},{128,0},{192,64},{1,129},{65,193},{129,1},{193,65... | collective-permute-start | bytes 110600 | tf_op jit(solution)/shard_map/ppermute | solution.py:23
  53.4 2.4 %collective-permute-start.10 = (f32[8,1152]{1,0:T(8,128)S(1)}, f32[8,1152]{1,0:T(8,128)S(1)}, u32[]{:S(2)}, u32[]{:S(2)}) collective-permute-start(f32[8,1152]{1,0:T(8,128)S(1)} %get-tuple-element.52), channel_id=1, source_target_pairs={{0,192},{64,0},{128,64},{192,128},{1,193},{65,1},{129,65},{193,129... | collective-permute-start | bytes 110600 | tf_op jit(solution)/shard_map/ppermute | solution.py:23
  56.4 1.2 collective-permute-done.10.refs_2_
  58.2 8.9 %all_to_all.21.lower_ref = f32[8,8,1152]{2,1,0:T(8,128)S(1)} all-to-all(f32[8,8,1152]{2,1,0:T(8,128)S(1)} %shard_map.99), channel_id=1, replica_groups=mesh['w'=2,'v'=2,'u'=2,'y'=4,'x'=4,'c'=2] {'u','y'}, dimensions={0} | all-to-all | bytes 589824 | tf_op jit(solution)/shard_map/all_to_all | solution.py:272
  67.1 1.1 shard_map.100
  68.3 1.8 %collective-permute-start.12 = (bf16[64,1152]{1,0:T(8,128)(2,1)S(1)}, bf16[64,1152]{1,0:T(8,128)(2,1)S(1)}, u32[]{:S(2)}, u32[]{:S(2)}) collective-permute-start(bf16[64,1152]{1,0:T(8,128)(2,1)S(1)} %get-tuple-element.55), channel_id=1, source_target_pairs={{0,4},{2,6},{4,0},{6,2},{1,5},{3,7},{5,1},{7,3},{8,12},{10,14},{12... | collective-permute-start | bytes 442376 | tf_op jit(solution)/shard_map/ppermute | solution.py:23
  70.1 2.0 %collective-permute-start.13 = (bf16[64,1152]{1,0:T(8,128)(2,1)S(1)}, bf16[64,1152]{1,0:T(8,128)(2,1)S(1)}, u32[]{:S(2)}, u32[]{:S(2)}) collective-permute-start(bf16[64,1152]{1,0:T(8,128)(2,1)S(1)} %get-tuple-element.56), channel_id=1, source_target_pairs={{0,6},{2,0},{4,2},{6,4},{1,7},{3,1},{5,3},{7,5},{8,14},{10,8},{12,... | collective-permute-start | bytes 442376 | tf_op jit(solution)/shard_map/ppermute | solution.py:23
  72.1 1.4 %shard_map.101.first_ref = bf16[64,3456]{1,0:T(8,128)(2,1)S(1)} custom-call(bf16[64,1152]{1,0:T(8,128)(2,1)S(1)} %get-tuple-element.53.a0, bf16[1152,3456]{1,0:T(8,128)(2,1)S(1)} %copy-done.2), custom_call_target="tpu_custom_call" | custom-call | tf_op jit(solution)/shard_map/pallas_call | solution.py:34
  73.5 1.6 %collective-permute-done.11.a1 = bf16[64,1152]{1,0:T(8,128)(2,1)S(1)} collective-permute-done((bf16[64,1152]{1,0:T(8,128)(2,1)S(1)}, bf16[64,1152]{1,0:T(8,128)(2,1)S(1)}, u32[]{:S(2)}, u32[]{:S(2)}) %collective-permute-start.11) | collective-permute-done | bytes 147488 | tf_op jit(solution)/shard_map/ppermute | solution.py:23
  75.7 3.3 %shard_map.102 = (bf16[64,1152]{1,0:T(8,128)(2,1)S(1)}, bf16[64,1152]{1,0:T(8,128)(2,1)S(1)}, bf16[64,1152]{1,0:T(8,128)(2,1)S(1)}, bf16[256,3456]{1,0:T(8,128)(2,1)S(1)}) custom-call(bf16[64,3456]{1,0:T(8,128)(2,1)S(1)} %shard_map.101.first_ref, bf16[64,1152]{1,0:T(8,128)(2,1)S(1)} %collective-permute-done.11.a1, ...), custom_call_target="tpu_custom_call" | custom-call | tf_op jit(solution)/shard_map/pallas_call | solution.py:34
  78.9 2.5 %collective-permute-start.14 = (bf16[64,1152]{1,0:T(8,128)(2,1)S(1)}, bf16[64,1152]{1,0:T(8,128)(2,1)S(1)}, u32[]{:S(2)}, u32[]{:S(2)}) collective-permute-start(bf16[64,1152]{1,0:T(8,128)(2,1)S(1)} %get-tuple-element.58), channel_id=1, source_target_pairs={{0,6},{2,0},{4,2},{6,4},{1,7},{3,1},{5,3},{7,5},{8,14},{10,8},{12,... | collective-permute-start | bytes 442376 | tf_op jit(solution)/shard_map/ppermute | solution.py:23
  81.4 0.8 collective-permute-start.15
  82.2 0.7 shard_map.104.base_ref
  83.0 1.1 shard_map.103.a0
  84.1 1.0 collective-permute-done.14.a1
  85.1 1.9 %collective-permute-done.15.a2 = bf16[64,1152]{1,0:T(8,128)(2,1)S(1)} collective-permute-done((bf16[64,1152]{1,0:T(8,128)(2,1)S(1)}, bf16[64,1152]{1,0:T(8,128)(2,1)S(1)}, u32[]{:S(2)}, u32[]{:S(2)}) %collective-permute-start.15) | collective-permute-done | bytes 147488 | tf_op jit(solution)/shard_map/ppermute | solution.py:23
  87.0 1.5 %collective-permute-done.16.a3 = bf16[64,1152]{1,0:T(8,128)(2,1)S(1)} collective-permute-done((bf16[64,1152]{1,0:T(8,128)(2,1)S(1)}, bf16[64,1152]{1,0:T(8,128)(2,1)S(1)}, u32[]{:S(2)}, u32[]{:S(2)}) %collective-permute-start.16) | collective-permute-done | bytes 147488 | tf_op jit(solution)/shard_map/ppermute | solution.py:23
  88.5 1.6 %shard_map.105 = (f32[4,32,1152]{2,1,0:T(8,128)S(1)}, f32[4,32,1152]{2,1,0:T(8,128)S(1)}, f32[8,8,1152]{2,1,0:T(8,128)S(1)}) custom-call(s32[7]{0:T(128)S(1)} %pad_add_fusion.where_ref, f32[3,4]{1,0:T(4,128)S(1)} %pad_maximum_fusion.coef_ref, bf16[64,1152]{1,0:T(8,128)(2,1)S(1)} %shard_map.103.a0, bf16[64,1152]{1,0:T(8,128)(2,1)S(1)} %collective-permute-done.14.a1, ...), custom_call_target="tpu_custom_call" | custom-call | tf_op jit(solution)/shard_map/pallas_call | solution.py:34
  90.1 8.2 %collective-permute-start.18 = (f32[4,32,1152]{2,1,0:T(8,128)S(1)}, f32[4,32,1152]{2,1,0:T(8,128)S(1)}, u32[]{:S(2)}, u32[]{:S(2)}) collective-permute-start(f32[4,32,1152]{2,1,0:T(8,128)S(1)} %get-tuple-element.65), channel_id=1, source_target_pairs={{0,1},{1,0},{2,3},{3,2},{4,5},{5,4},{6,7},{7,6},{8,9},{9,8},{10,11... | collective-permute-start | bytes 1769480 | tf_op jit(solution)/shard_map/ppermute | solution.py:23
  98.3 10.0 %all_to_all.22.held_ref = f32[8,8,1152]{2,1,0:T(8,128)S(1)} all-to-all(f32[8,8,1152]{2,1,0:T(8,128)S(1)} %get-tuple-element.63), channel_id=1, replica_groups=mesh['w'=2,'v'=2,'u'=2,'y'=4,'x'=4,'c'=2] {'u','y'}, dimensions={0} | all-to-all | bytes 589824 | tf_op jit(solution)/shard_map/all_to_all | solution.py:265
  108.3 1.7 %collective-permute-start.17 = (f32[8,1152]{1,0:T(8,128)S(1)}, f32[8,1152]{1,0:T(8,128)S(1)}, u32[]{:S(2)}, u32[]{:S(2)}) collective-permute-start(f32[8,1152]{1,0:T(8,128)S(1)} %get-tuple-element.64), channel_id=1, source_target_pairs={{0,64},{64,128},{128,192},{192,0},{1,65},{65,129},{129,193},{193,1... | collective-permute-start | bytes 110600 | tf_op jit(solution)/shard_map/ppermute | solution.py:23
  110.0 3.9 %collective-permute-start.19 = (f32[8,1152]{1,0:T(8,128)S(1)}, f32[8,1152]{1,0:T(8,128)S(1)}, u32[]{:S(2)}, u32[]{:S(2)}) collective-permute-start(f32[8,1152]{1,0:T(8,128)S(1)} %get-tuple-element.64), channel_id=1, source_target_pairs={{0,128},{64,192},{128,0},{192,64},{1,129},{65,193},{129,1},{193,65... | collective-permute-start | bytes 110600 | tf_op jit(solution)/shard_map/ppermute | solution.py:23
  114.6 2.5 %collective-permute-done.19.refs_1_ = f32[8,1152]{1,0:T(8,128)S(1)} collective-permute-done((f32[8,1152]{1,0:T(8,128)S(1)}, f32[8,1152]{1,0:T(8,128)S(1)}, u32[]{:S(2)}, u32[]{:S(2)}) %collective-permute-start.19) | collective-permute-done | bytes 36896 | tf_op jit(solution)/shard_map/ppermute | solution.py:23
  117.1 1.3 collective-permute-done.20.refs_2_
  119.0 9.1 %all_to_all.23.mine_lower = f32[8,8,1152]{2,1,0:T(8,128)S(1)} all-to-all(f32[8,8,1152]{2,1,0:T(8,128)S(1)} %shard_map.107), channel_id=1, replica_groups=mesh['w'=2,'v'=2,'u'=2,'y'=4,'x'=4,'c'=2] {'u','y'}, dimensions={0} | all-to-all | bytes 589824 | tf_op jit(solution)/shard_map/all_to_all | solution.py:272
  128.1 3.6 %collective-permute-start.21 = (f32[8,8,1152]{2,1,0:T(8,128)S(1)}, f32[8,8,1152]{2,1,0:T(8,128)S(1)}, u32[]{:S(2)}, u32[]{:S(2)}) collective-permute-start(f32[8,8,1152]{2,1,0:T(8,128)S(1)} %all_to_all.23.mine_lower), channel_id=1, source_target_pairs={{0,1},{1,0},{2,3},{3,2},{4,5},{5,4},{6,7},{7,6},{8,9},{9,8},{10,11... | collective-permute-start | bytes 884744 | tf_op jit(solution)/shard_map/ppermute | solution.py:23
  131.7 1.2 collective-permute-done.21.peer_lower
  132.9 1.6 %shard_map.108 = f32[4,2,32,1152]{3,2,1,0:T(8,128)} custom-call(s32[7]{0:T(128)S(1)} %pad_add_fusion.where_ref, f32[2,32,1152]{2,1,0:T(8,128)S(1)} %copy-done.7, f32[4,32,1152]{2,1,0:T(8,128)S(1)} %get-tuple-element.62.mine_before, f32[4,32,1152]{2,1,0:T(8,128)S(1)} %collective-permute-done.18.peer_before, f32[8,8,1152]{2,1,0:T(8,128)S(1)} %all_to_all.23.mine_lower, ...), custom_call_target="tpu_custom_call" | custom-call | tf_op jit(solution)/shard_map/pallas_call | solution.py:34
  (51 shorter events, 4.4 us)
Async XLA Ops:
  0.0 5.7 %copy-start = (s32[4,2]{0,1:T(2,128)S(1)}, s32[4,2]{0,1:T(2,128)}, u32[]{:S(2)}) copy-start(s32[4,2]{0,1:T(2,128)} %param.15) | copy-start | bytes 100
  0.0 1.3 copy-start.4
  1.3 1.0 copy-start.6
  2.2 3.4 %copy-start.10 = (f32[4,3,1152]{2,0,1:T(4,128)S(1)}, f32[4,3,1152]{2,0,1:T(4,128)}, u32[]{:S(2)}) copy-start(f32[4,3,1152]{2,0,1:T(4,128)} %param.13) | copy-start | bytes 165892
  2.3 3.4 %copy-start.9 = (f32[8,3,1152]{2,0,1:T(8,128)S(1)}, f32[8,3,1152]{2,0,1:T(8,128)}, u32[]{:S(2)}) copy-start(f32[8,3,1152]{2,0,1:T(8,128)} %param.14) | copy-start | bytes 331780
  2.3 5.2 %copy-start.5 = (f32[4,2,32,1152]{3,2,1,0:T(8,128)S(1)}, f32[4,2,32,1152]{3,2,1,0:T(8,128)}, u32[]{:S(2)}) copy-start(f32[4,2,32,1152]{3,2,1,0:T(8,128)} %states_ref.3) | copy-start | bytes 3538948
  2.3 5.2 %copy-start.7 = (f32[2,32,1152]{2,1,0:T(8,128)S(1)}, f32[2,32,1152]{2,1,0:T(8,128)}, u32[]{:S(2)}) copy-start(f32[2,32,1152]{2,1,0:T(8,128)} %start_ref.3) | copy-start | bytes 884740
  2.3 5.1 %collective-permute-start = (f32[5,32,1152]{2,1,0:T(8,128)S(1)}, f32[5,32,1152]{2,1,0:T(8,128)S(1)}, u32[]{:S(2)}, u32[]{:S(2)}) collective-permute-start(f32[5,32,1152]{2,1,0:T(8,128)S(1)} %shard_map.91), channel_id=1, source_target_pairs={{0,1},{1,0},{2,3},{3,2},{4,5},{5,4},{6,7},{7,6},{8,9},{9,8},{10,11... | collective-permute-start | bytes 2211848 | tf_op jit(solution)/shard_map/ppermute | solution.py:23
  8.5 9.2 %collective-permute-start.1 = (bf16[64,1152]{1,0:T(8,128)(2,1)S(1)}, bf16[64,1152]{1,0:T(8,128)(2,1)S(1)}, u32[]{:S(2)}, u32[]{:S(2)}) collective-permute-start(bf16[64,1152]{1,0:T(8,128)(2,1)S(1)} %get-tuple-element.39), channel_id=1, source_target_pairs={{0,2},{2,4},{4,6},{6,0},{1,3},{3,5},{5,7},{7,1},{8,10},{10,12},{12... | collective-permute-start | bytes 442376 | tf_op jit(solution)/shard_map/ppermute | solution.py:23
  8.6 9.1 %collective-permute-start.2 = (bf16[64,1152]{1,0:T(8,128)(2,1)S(1)}, bf16[64,1152]{1,0:T(8,128)(2,1)S(1)}, u32[]{:S(2)}, u32[]{:S(2)}) collective-permute-start(bf16[64,1152]{1,0:T(8,128)(2,1)S(1)} %get-tuple-element.40), channel_id=1, source_target_pairs={{0,4},{2,6},{4,0},{6,2},{1,5},{3,7},{5,1},{7,3},{8,12},{10,14},{12... | collective-permute-start | bytes 442376 | tf_op jit(solution)/shard_map/ppermute | solution.py:23
  10.5 7.8 %collective-permute-start.3 = (bf16[64,1152]{1,0:T(8,128)(2,1)S(1)}, bf16[64,1152]{1,0:T(8,128)(2,1)S(1)}, u32[]{:S(2)}, u32[]{:S(2)}) collective-permute-start(bf16[64,1152]{1,0:T(8,128)(2,1)S(1)} %get-tuple-element.41), channel_id=1, source_target_pairs={{0,6},{2,0},{4,2},{6,4},{1,7},{3,1},{5,3},{7,5},{8,14},{10,8},{12,... | collective-permute-start | bytes 442376 | tf_op jit(solution)/shard_map/ppermute | solution.py:23
  11.7 3.3 %copy-start.1 = (bf16[1152,3456]{1,0:T(8,128)(2,1)S(1)}, bf16[1152,3456]{1,0:T(8,128)(2,1)}, u32[]{:S(2)}) copy-start(bf16[1152,3456]{1,0:T(8,128)(2,1)} %w_ref.10) | copy-start | bytes 23887876
  15.0 1.3 %copy-start.8 = (bf16[4,2,32,1152]{3,2,1,0:T(8,128)(2,1)S(1)}, bf16[4,2,32,1152]{3,2,1,0:T(8,128)(2,1)}, u32[]{:S(2)}) copy-start(bf16[4,2,32,1152]{3,2,1,0:T(8,128)(2,1)} %param.10) | copy-start | bytes 1769476
  15.0 3.5 %copy-start.2 = (bf16[1152,3456]{1,0:T(8,128)(2,1)S(1)}, bf16[1152,3456]{1,0:T(8,128)(2,1)}, u32[]{:S(2)}) copy-start(bf16[1152,3456]{1,0:T(8,128)(2,1)} %w_ref.10) | copy-start | bytes 23887876
  16.4 9.3 %copy-start.11 = (s32[4]{0:T(128)S(1)}, s32[4]{0:T(128)}, u32[]{:S(2)}) copy-start(s32[4]{0:T(128)} %param.12) | copy-start | bytes 52
  16.4 10.5 %collective-permute-start.7 = (bf16[4,32,1152]{2,1,0:T(8,128)(2,1)S(1)}, bf16[4,32,1152]{2,1,0:T(8,128)(2,1)S(1)}, u32[]{:S(2)}, u32[]{:S(2)}) collective-permute-start(bf16[4,32,1152]{2,1,0:T(8,128)(2,1)S(1)} %get-tuple-element.69), channel_id=1, source_target_pairs={{0,1},{1,0},{2,3},{3,2},{4,5},{5,4},{6,7},{7,6},{8,9},{9,8},{10,11... | collective-permute-start | bytes 884744 | tf_op jit(solution)/shard_map/ppermute | solution.py:23
  21.7 9.4 %collective-permute-start.4 = (bf16[64,1152]{1,0:T(8,128)(2,1)S(1)}, bf16[64,1152]{1,0:T(8,128)(2,1)S(1)}, u32[]{:S(2)}, u32[]{:S(2)}) collective-permute-start(bf16[64,1152]{1,0:T(8,128)(2,1)S(1)} %get-tuple-element.43), channel_id=1, source_target_pairs={{0,6},{2,0},{4,2},{6,4},{1,7},{3,1},{5,3},{7,5},{8,14},{10,8},{12,... | collective-permute-start | bytes 442376 | tf_op jit(solution)/shard_map/ppermute | solution.py:23
  25.0 6.2 %collective-permute-start.5 = (bf16[64,1152]{1,0:T(8,128)(2,1)S(1)}, bf16[64,1152]{1,0:T(8,128)(2,1)S(1)}, u32[]{:S(2)}, u32[]{:S(2)}) collective-permute-start(bf16[64,1152]{1,0:T(8,128)(2,1)S(1)} %get-tuple-element.44), channel_id=1, source_target_pairs={{0,4},{2,6},{4,0},{6,2},{1,5},{3,7},{5,1},{7,3},{8,12},{10,14},{12... | collective-permute-start | bytes 442376 | tf_op jit(solution)/shard_map/ppermute | solution.py:23
  25.0 9.8 %collective-permute-start.6 = (bf16[64,1152]{1,0:T(8,128)(2,1)S(1)}, bf16[64,1152]{1,0:T(8,128)(2,1)S(1)}, u32[]{:S(2)}, u32[]{:S(2)}) collective-permute-start(bf16[64,1152]{1,0:T(8,128)(2,1)S(1)} %get-tuple-element.45), channel_id=1, source_target_pairs={{0,2},{2,4},{4,6},{6,0},{1,3},{3,5},{5,7},{7,1},{8,10},{10,12},{12... | collective-permute-start | bytes 442376 | tf_op jit(solution)/shard_map/ppermute | solution.py:23
  26.9 8.0 %copy-start.3 = (bf16[1152,1152]{1,0:T(8,128)(2,1)S(1)}, bf16[1152,1152]{1,0:T(8,128)(2,1)}, u32[]{:S(2)}) copy-start(bf16[1152,1152]{1,0:T(8,128)(2,1)} %w_ref.11) | copy-start | bytes 7962628
  46.2 9.7 %collective-permute-start.8 = (f32[8,1152]{1,0:T(8,128)S(1)}, f32[8,1152]{1,0:T(8,128)S(1)}, u32[]{:S(2)}, u32[]{:S(2)}) collective-permute-start(f32[8,1152]{1,0:T(8,128)S(1)} %get-tuple-element.52), channel_id=1, source_target_pairs={{0,64},{64,128},{128,192},{192,0},{1,65},{65,129},{129,193},{193,1... | collective-permute-start | bytes 110600 | tf_op jit(solution)/shard_map/ppermute | solution.py:23
  49.3 7.1 %collective-permute-start.9 = (f32[8,1152]{1,0:T(8,128)S(1)}, f32[8,1152]{1,0:T(8,128)S(1)}, u32[]{:S(2)}, u32[]{:S(2)}) collective-permute-start(f32[8,1152]{1,0:T(8,128)S(1)} %get-tuple-element.52), channel_id=1, source_target_pairs={{0,128},{64,192},{128,0},{192,64},{1,129},{65,193},{129,1},{193,65... | collective-permute-start | bytes 110600 | tf_op jit(solution)/shard_map/ppermute | solution.py:23
  53.4 4.2 %collective-permute-start.10 = (f32[8,1152]{1,0:T(8,128)S(1)}, f32[8,1152]{1,0:T(8,128)S(1)}, u32[]{:S(2)}, u32[]{:S(2)}) collective-permute-start(f32[8,1152]{1,0:T(8,128)S(1)} %get-tuple-element.52), channel_id=1, source_target_pairs={{0,192},{64,0},{128,64},{192,128},{1,193},{65,1},{129,65},{193,129... | collective-permute-start | bytes 110600 | tf_op jit(solution)/shard_map/ppermute | solution.py:23
  68.2 6.9 %collective-permute-start.11 = (bf16[64,1152]{1,0:T(8,128)(2,1)S(1)}, bf16[64,1152]{1,0:T(8,128)(2,1)S(1)}, u32[]{:S(2)}, u32[]{:S(2)}) collective-permute-start(bf16[64,1152]{1,0:T(8,128)(2,1)S(1)} %get-tuple-element.54), channel_id=1, source_target_pairs={{0,2},{2,4},{4,6},{6,0},{1,3},{3,5},{5,7},{7,1},{8,10},{10,12},{12... | collective-permute-start | bytes 442376 | tf_op jit(solution)/shard_map/ppermute | solution.py:23
  68.3 6.8 %collective-permute-start.12 = (bf16[64,1152]{1,0:T(8,128)(2,1)S(1)}, bf16[64,1152]{1,0:T(8,128)(2,1)S(1)}, u32[]{:S(2)}, u32[]{:S(2)}) collective-permute-start(bf16[64,1152]{1,0:T(8,128)(2,1)S(1)} %get-tuple-element.55), channel_id=1, source_target_pairs={{0,4},{2,6},{4,0},{6,2},{1,5},{3,7},{5,1},{7,3},{8,12},{10,14},{12... | collective-permute-start | bytes 442376 | tf_op jit(solution)/shard_map/ppermute | solution.py:23
  70.1 5.5 %collective-permute-start.13 = (bf16[64,1152]{1,0:T(8,128)(2,1)S(1)}, bf16[64,1152]{1,0:T(8,128)(2,1)S(1)}, u32[]{:S(2)}, u32[]{:S(2)}) collective-permute-start(bf16[64,1152]{1,0:T(8,128)(2,1)S(1)} %get-tuple-element.56), channel_id=1, source_target_pairs={{0,6},{2,0},{4,2},{6,4},{1,7},{3,1},{5,3},{7,5},{8,14},{10,8},{12,... | collective-permute-start | bytes 442376 | tf_op jit(solution)/shard_map/ppermute | solution.py:23
  78.9 6.1 %collective-permute-start.14 = (bf16[64,1152]{1,0:T(8,128)(2,1)S(1)}, bf16[64,1152]{1,0:T(8,128)(2,1)S(1)}, u32[]{:S(2)}, u32[]{:S(2)}) collective-permute-start(bf16[64,1152]{1,0:T(8,128)(2,1)S(1)} %get-tuple-element.58), channel_id=1, source_target_pairs={{0,6},{2,0},{4,2},{6,4},{1,7},{3,1},{5,3},{7,5},{8,14},{10,8},{12,... | collective-permute-start | bytes 442376 | tf_op jit(solution)/shard_map/ppermute | solution.py:23
  81.4 5.6 %collective-permute-start.15 = (bf16[64,1152]{1,0:T(8,128)(2,1)S(1)}, bf16[64,1152]{1,0:T(8,128)(2,1)S(1)}, u32[]{:S(2)}, u32[]{:S(2)}) collective-permute-start(bf16[64,1152]{1,0:T(8,128)(2,1)S(1)} %get-tuple-element.59), channel_id=1, source_target_pairs={{0,4},{2,6},{4,0},{6,2},{1,5},{3,7},{5,1},{7,3},{8,12},{10,14},{12... | collective-permute-start | bytes 442376 | tf_op jit(solution)/shard_map/ppermute | solution.py:23
  82.2 6.2 %collective-permute-start.16 = (bf16[64,1152]{1,0:T(8,128)(2,1)S(1)}, bf16[64,1152]{1,0:T(8,128)(2,1)S(1)}, u32[]{:S(2)}, u32[]{:S(2)}) collective-permute-start(bf16[64,1152]{1,0:T(8,128)(2,1)S(1)} %get-tuple-element.60), channel_id=1, source_target_pairs={{0,2},{2,4},{4,6},{6,0},{1,3},{3,5},{5,7},{7,1},{8,10},{10,12},{12... | collective-permute-start | bytes 442376 | tf_op jit(solution)/shard_map/ppermute | solution.py:23
  90.1 24.5 %collective-permute-start.18 = (f32[4,32,1152]{2,1,0:T(8,128)S(1)}, f32[4,32,1152]{2,1,0:T(8,128)S(1)}, u32[]{:S(2)}, u32[]{:S(2)}) collective-permute-start(f32[4,32,1152]{2,1,0:T(8,128)S(1)} %get-tuple-element.65), channel_id=1, source_target_pairs={{0,1},{1,0},{2,3},{3,2},{4,5},{5,4},{6,7},{7,6},{8,9},{9,8},{10,11... | collective-permute-start | bytes 1769480 | tf_op jit(solution)/shard_map/ppermute | solution.py:23
  108.3 6.3 %collective-permute-start.17 = (f32[8,1152]{1,0:T(8,128)S(1)}, f32[8,1152]{1,0:T(8,128)S(1)}, u32[]{:S(2)}, u32[]{:S(2)}) collective-permute-start(f32[8,1152]{1,0:T(8,128)S(1)} %get-tuple-element.64), channel_id=1, source_target_pairs={{0,64},{64,128},{128,192},{192,0},{1,65},{65,129},{129,193},{193,1... | collective-permute-start | bytes 110600 | tf_op jit(solution)/shard_map/ppermute | solution.py:23
  110.0 7.1 %collective-permute-start.19 = (f32[8,1152]{1,0:T(8,128)S(1)}, f32[8,1152]{1,0:T(8,128)S(1)}, u32[]{:S(2)}, u32[]{:S(2)}) collective-permute-start(f32[8,1152]{1,0:T(8,128)S(1)} %get-tuple-element.64), channel_id=1, source_target_pairs={{0,128},{64,192},{128,0},{192,64},{1,129},{65,193},{129,1},{193,65... | collective-permute-start | bytes 110600 | tf_op jit(solution)/shard_map/ppermute | solution.py:23
  114.0 4.5 %collective-permute-start.20 = (f32[8,1152]{1,0:T(8,128)S(1)}, f32[8,1152]{1,0:T(8,128)S(1)}, u32[]{:S(2)}, u32[]{:S(2)}) collective-permute-start(f32[8,1152]{1,0:T(8,128)S(1)} %get-tuple-element.64), channel_id=1, source_target_pairs={{0,192},{64,0},{128,64},{192,128},{1,193},{65,1},{129,65},{193,129... | collective-permute-start | bytes 110600 | tf_op jit(solution)/shard_map/ppermute | solution.py:23
  128.1 4.8 %collective-permute-start.21 = (f32[8,8,1152]{2,1,0:T(8,128)S(1)}, f32[8,8,1152]{2,1,0:T(8,128)S(1)}, u32[]{:S(2)}, u32[]{:S(2)}) collective-permute-start(f32[8,8,1152]{2,1,0:T(8,128)S(1)} %all_to_all.23.mine_lower), channel_id=1, source_target_pairs={{0,1},{1,0},{2,3},{3,2},{4,5},{5,4},{6,7},{7,6},{8,9},{9,8},{10,11... | collective-permute-start | bytes 884744 | tf_op jit(solution)/shard_map/ppermute | solution.py:23

commit v11 on v9

--- a/solution.py
+++ b/solution.py
@@ -53,9 +53,8 @@
     return step_ref[step, part : part + 1, :] + view_ref[where_ref[3 + step], part : part + 1, :]
 
 
-def enter_body(where_ref, mine_ref, start_mine, peer_ref, step_ref, view_ref, x_ref, start_ref, *mod_refs):
+def enter_body(where_ref, mine_ref, peer_ref, step_ref, view_ref, x_ref, *mod_refs):
     place = where_ref[0]
-    start_ref[...] = jnp.concatenate([start_mine[...], peer_ref[mine_ref.shape[0]]], axis=0)
     steps = mine_ref.shape[0]
     for r in range(steps):
         step = lax.rem(place + r, steps)
@@ -67,7 +66,7 @@
 
 
 def resume_body(
-    where_ref, start_ref, mine_before, peer_before, lower_ref, step_ref, view_ref, x_ref, *rest
+    where_ref, mine_start, peer_start, mine_before, peer_before, lower_ref, step_ref, view_ref, x_ref, *rest
 ):
     mod_refs, base_ref = rest[:-1], rest[-1]
     place = where_ref[0]
@@ -75,10 +74,11 @@
     places, share, _ = lower_ref.shape
     for q in range(places):
         base_ref[q * share : (q + 1) * share, :] = lower_ref[q]
+    start = jnp.concatenate([mine_start[...], peer_start[...]], axis=0)
     for r in range(steps):
         step = lax.rem(place + r, steps)
         before = jnp.concatenate([mine_before[step], peer_before[step]], axis=0)
-        rows = start_ref[...] + (base_ref[...] + before)
+        rows = start + (base_ref[...] + before)
         x_ref[step] = rows
         shift = modulation_row(where_ref, step_ref, view_ref, step, 0)
         scale = modulation_row(where_ref, step_ref, view_ref, step, 1)
@@ -280,8 +280,8 @@
     def shape(*dims, kind=f32):
         return jax.ShapeDtypeStruct(dims, kind)
 
-    swapped = shifted(jnp.concatenate([given(states, 1), given(x_start, 0)[None]], axis=0), "c", 1)
-    states_mine, start_mine = own(states, 1), own(x_start, 0)
+    swapped = shifted(given(states, 1), "c", 1)
+    states_mine = own(states, 1)
     where = jnp.concatenate([jnp.stack([place, group, core]).astype(jnp.int32), own(view_ids, 1)])
     coefs = jnp.stack(coefficients(timesteps))
     size = width // HEADS
@@ -293,19 +293,20 @@
     half = shape(steps, part, width)
     places = lax.axis_size(SHARES)
     piece = shape(rows, width, kind=bf16)
-    x, start, *mods = call(
+    x, *mods = call(
         enter_body,
-        [x_shape, shape(rows, width)] + [piece] * steps,
-        [SMEM] + [VMEM] * 5,
+        [x_shape] + [piece] * steps,
+        [SMEM] + [VMEM] * 4,
         where,
         states_mine,
-        start_mine,
         swapped,
         step_mod,
         view_mod,
     )
-    drawn, _ = lax.optimization_barrier((noise, mods[0]))
-    noise_mine, noise_peer = own(drawn, 1), shifted(given(drawn, 1), "c", 1)
+    drawn, late, _ = lax.optimization_barrier((noise, x_start, mods[0]))
+    start_mine, start_peer, noise_mine, noise_peer = lax.optimization_barrier(
+        (own(late, 0), shifted(given(late, 0), "c", 1), own(drawn, 1), shifted(given(drawn, 1), "c", 1))
+    )
     for sweep in range(SWEEPS):
         arrived = spread(mods[1:], "x")
         first = call(first_body, shape(rows, 3 * width, kind=bf16), [VMEM] * 2, mods[0], w_qkv)
@@ -344,9 +345,10 @@
         x, *mods = call(
             resume_body,
             [x_shape] + [piece] * steps,
-            [SMEM] + [VMEM] * 6,
+            [SMEM] + [VMEM] * 7,
             where,
-            start,
+            start_mine,
+            start_peer,
             mine_before,
             peer_before,
             lower,

time: 134 us -> 136 us (1.015)
  starting transfers between devices: 46.1 us -> 44.6 us
    ppermute x22 -> x23, starting transfers between devices: 46.1 us -> 44.6 us  [shifted(): lax.ppermute(value, axis, [(i, (i + shift) % size) for i in range(size)])]
    ppermute x22 -> x23, waiting for transfers between devices: 23.2 us -> 23.7 us  [shifted(): lax.ppermute(value, axis, [(i, (i + shift) % size) for i in range(size)])]
  transfers between devices with their start and end apart: 22 -> 23, of which waited for: 15 -> 13; matrix products, arithmetic and copies ran while one was open for 0% -> 0% of each run, Pallas kernels for 7% -> 7%
where the time goes in v11:
time: 136 us; the launch traced here: 135 us
  starting transfers between devices  44.6 us (33%)
  blocking collectives  38.8 us (29%)
  waiting for transfers between devices  23.7 us (17%)
  Pallas kernels  21.2 us (16%)
  local copies, waits for them, and re-layouts  6.24 us (5%)
    ppermute x23, starting transfers between devices, shifted(): lax.ppermute(value, axis, [(i, (i + shift) % size) for i in range(size)])  44.6 us
    ppermute x23, waiting for transfers between devices, shifted(): lax.ppermute(value, axis, [(i, (i + shift) % size) for i in range(size)])  23.7 us
    pallas_call x17, Pallas kernels, call(): pl.pallas_call(body, out_shape=outs, in_specs=specs, out_specs=jax.tree.m...  21.2 us
    all_to_all x2, blocking collectives, earlier_sum(): held = lax.all_to_all(shares, SHARES, 0, 0, tiled=True)  20 us
    all_to_all x2, blocking collectives, earlier_sum(): return (lax.all_to_all(sums, SHARES, 0, 0, tiled=True), beside)  18.8 us
    unnamed x20, local copies, waits for them, and re-layouts  4.78 us
  transfers between devices with their start and end apart: 23, of which 13 were waited for; matrix products, arithmetic and copies ran while one was open for 0% of the time, Pallas kernels for 7%

profile of v11, /device:TPU:1, one launch (start us, length us, event | category | flops | bytes accessed | tf_op | source)
XLA Modules:
  0.0 135.3 jit_solution(5281486479875295353)
XLA Ops:
  0.0 1.4 %dynamic-slice_bitcast_fusion = (f32[4,32,1152]{2,1,0:T(8,128)S(1)}, f32[4,32,1152]{2,1,0:T(8,128)S(1)}) fusion(f32[4,2,32,1152]{3,2,1,0:T(8,128)} %param.9, s32[]{:T(128)S(6)} %select_n.16, s32[]{:T(128)S(6)} %select_n.15), kind=kLoop, calls=%fused_computation | loop fusion | bytes 2359304 | tf_op jit(solution)/shard_map/jit(dynamic_index_in_dim)/squeeze | solution.py:278
  1.4 3.3 %collective-permute-start = (f32[4,32,1152]{2,1,0:T(8,128)S(1)}, f32[4,32,1152]{2,1,0:T(8,128)S(1)}, u32[]{:S(2)}, u32[]{:S(2)}) collective-permute-start(f32[4,32,1152]{2,1,0:T(8,128)S(1)} %get-tuple-element.77), channel_id=1, source_target_pairs={{0,1},{1,0},{2,3},{3,2},{4,5},{5,4},{6,7},{7,6},{8,9},{9,8},{10,11... | collective-permute-start | bytes 1769480 | tf_op jit(solution)/shard_map/ppermute | solution.py:23
  4.9 1.4 %collective-permute-done.peer_ref = f32[4,32,1152]{2,1,0:T(8,128)S(1)} collective-permute-done((f32[4,32,1152]{2,1,0:T(8,128)S(1)}, f32[4,32,1152]{2,1,0:T(8,128)S(1)}, u32[]{:S(2)}, u32[]{:S(2)}) %collective-permute-start) | collective-permute-done | bytes 589856 | tf_op jit(solution)/shard_map/ppermute | solution.py:23
  6.3 1.0 shard_map.91
  7.4 2.0 %collective-permute-start.4 = (bf16[64,1152]{1,0:T(8,128)(2,1)S(1)}, bf16[64,1152]{1,0:T(8,128)(2,1)S(1)}, u32[]{:S(2)}, u32[]{:S(2)}) collective-permute-start(bf16[64,1152]{1,0:T(8,128)(2,1)S(1)} %get-tuple-element.47), channel_id=1, source_target_pairs={{0,4},{2,6},{4,0},{6,2},{1,5},{3,7},{5,1},{7,3},{8,12},{10,14},{12... | collective-permute-start | bytes 442376 | tf_op jit(solution)/shard_map/ppermute | solution.py:23
  9.4 1.2 collective-permute-start.5
  10.6 1.3 collective-permute-start.1
  11.9 3.3 %copy-done.1 = bf16[1152,3456]{1,0:T(8,128)(2,1)S(1)} copy-done((bf16[1152,3456]{1,0:T(8,128)(2,1)S(1)}, bf16[1152,3456]{1,0:T(8,128)(2,1)}, u32[]{:S(2)}) %copy-start.1) | copy-done | bytes 7962648
  15.1 1.4 %shard_map.92.first_ref = bf16[64,3456]{1,0:T(8,128)(2,1)S(1)} custom-call(bf16[64,1152]{1,0:T(8,128)(2,1)S(1)} %get-tuple-element.41.a0, bf16[1152,3456]{1,0:T(8,128)(2,1)S(1)} %copy-done.1), custom_call_target="tpu_custom_call" | custom-call | tf_op jit(solution)/shard_map/pallas_call | solution.py:34
  17.2 1.4 %copy-done.2 = bf16[1152,3456]{1,0:T(8,128)(2,1)S(1)} copy-done((bf16[1152,3456]{1,0:T(8,128)(2,1)S(1)}, bf16[1152,3456]{1,0:T(8,128)(2,1)}, u32[]{:S(2)}) %copy-start.2) | copy-done | bytes 7962648
  18.6 3.3 %shard_map.93 = (bf16[64,1152]{1,0:T(8,128)(2,1)S(1)}, bf16[64,1152]{1,0:T(8,128)(2,1)S(1)}, bf16[64,1152]{1,0:T(8,128)(2,1)S(1)}, bf16[256,3456]{1,0:T(8,128)(2,1)S(1)}) custom-call(bf16[64,3456]{1,0:T(8,128)(2,1)S(1)} %shard_map.92.first_ref, bf16[64,1152]{1,0:T(8,128)(2,1)S(1)} %collective-permute-done.3.a1, ...), custom_call_target="tpu_custom_call" | custom-call | tf_op jit(solution)/shard_map/pallas_call | solution.py:34
  21.8 2.0 %collective-permute-start.6 = (bf16[64,1152]{1,0:T(8,128)(2,1)S(1)}, bf16[64,1152]{1,0:T(8,128)(2,1)S(1)}, u32[]{:S(2)}, u32[]{:S(2)}) collective-permute-start(bf16[64,1152]{1,0:T(8,128)(2,1)S(1)} %get-tuple-element.50), channel_id=1, source_target_pairs={{0,6},{2,0},{4,2},{6,4},{1,7},{3,1},{5,3},{7,5},{8,14},{10,8},{12,... | collective-permute-start | bytes 442376 | tf_op jit(solution)/shard_map/ppermute | solution.py:23
  24.0 0.7 collective-permute-start.8
  24.7 1.1 shard_map.94.a0
  25.9 0.8 shard_map.95.base_ref
  26.6 0.6 collective-permute-done.6.a1
  27.2 2.8 %collective-permute-done.7.a2 = bf16[64,1152]{1,0:T(8,128)(2,1)S(1)} collective-permute-done((bf16[64,1152]{1,0:T(8,128)(2,1)S(1)}, bf16[64,1152]{1,0:T(8,128)(2,1)S(1)}, u32[]{:S(2)}, u32[]{:S(2)}) %collective-permute-start.7) | collective-permute-done | bytes 147488 | tf_op jit(solution)/shard_map/ppermute | solution.py:23
  30.1 3.9 %collective-permute-done.8.a3 = bf16[64,1152]{1,0:T(8,128)(2,1)S(1)} collective-permute-done((bf16[64,1152]{1,0:T(8,128)(2,1)S(1)}, bf16[64,1152]{1,0:T(8,128)(2,1)S(1)}, u32[]{:S(2)}, u32[]{:S(2)}) %collective-permute-start.8) | collective-permute-done | bytes 147488 | tf_op jit(solution)/shard_map/ppermute | solution.py:23
  34.0 1.6 %shard_map.96 = (f32[4,32,1152]{2,1,0:T(8,128)S(1)}, f32[4,32,1152]{2,1,0:T(8,128)S(1)}, f32[8,8,1152]{2,1,0:T(8,128)S(1)}) custom-call(s32[7]{0:T(128)S(1)} %pad_add_fusion.where_ref, f32[3,4]{1,0:T(4,128)S(1)} %pad_maximum_fusion.coef_ref, bf16[64,1152]{1,0:T(8,128)(2,1)S(1)} %shard_map.94.a0, bf16[64,1152]{1,0:T(8,128)(2,1)S(1)} %collective-permute-done.6.a1, ...), custom_call_target="tpu_custom_call" | custom-call | tf_op jit(solution)/shard_map/pallas_call | solution.py:34
  35.7 10.1 %all_to_all.20.held_ref = f32[8,8,1152]{2,1,0:T(8,128)S(1)} all-to-all(f32[8,8,1152]{2,1,0:T(8,128)S(1)} %get-tuple-element.58), channel_id=1, replica_groups=mesh['w'=2,'v'=2,'u'=2,'y'=4,'x'=4,'c'=2] {'u','y'}, dimensions={0} | all-to-all | bytes 589824 | tf_op jit(solution)/shard_map/all_to_all | solution.py:257
  45.8 5.2 %collective-permute-start.11 = (f32[8,1152]{1,0:T(8,128)S(1)}, f32[8,1152]{1,0:T(8,128)S(1)}, u32[]{:S(2)}, u32[]{:S(2)}) collective-permute-start(f32[8,1152]{1,0:T(8,128)S(1)} %get-tuple-element.60), channel_id=1, source_target_pairs={{0,192},{64,0},{128,64},{192,128},{1,193},{65,1},{129,65},{193,129... | collective-permute-start | bytes 110600 | tf_op jit(solution)/shard_map/ppermute | solution.py:23
  51.0 1.2 collective-permute-start.10
  52.1 2.1 %collective-permute-start.9 = (f32[8,1152]{1,0:T(8,128)S(1)}, f32[8,1152]{1,0:T(8,128)S(1)}, u32[]{:S(2)}, u32[]{:S(2)}) collective-permute-start(f32[8,1152]{1,0:T(8,128)S(1)} %get-tuple-element.60), channel_id=1, source_target_pairs={{0,64},{64,128},{128,192},{192,0},{1,65},{65,129},{129,193},{193,1... | collective-permute-start | bytes 110600 | tf_op jit(solution)/shard_map/ppermute | solution.py:23
  54.2 3.5 %collective-permute-done.10.refs_1_ = f32[8,1152]{1,0:T(8,128)S(1)} collective-permute-done((f32[8,1152]{1,0:T(8,128)S(1)}, f32[8,1152]{1,0:T(8,128)S(1)}, u32[]{:S(2)}, u32[]{:S(2)}) %collective-permute-start.10) | collective-permute-done | bytes 36896 | tf_op jit(solution)/shard_map/ppermute | solution.py:23
  58.3 9.0 %all_to_all.21.lower_ref = f32[8,8,1152]{2,1,0:T(8,128)S(1)} all-to-all(f32[8,8,1152]{2,1,0:T(8,128)S(1)} %shard_map.98), channel_id=1, replica_groups=mesh['w'=2,'v'=2,'u'=2,'y'=4,'x'=4,'c'=2] {'u','y'}, dimensions={0} | all-to-all | bytes 589824 | tf_op jit(solution)/shard_map/all_to_all | solution.py:264
  67.3 1.1 shard_map.99
  68.6 1.8 %collective-permute-start.13 = (bf16[64,1152]{1,0:T(8,128)(2,1)S(1)}, bf16[64,1152]{1,0:T(8,128)(2,1)S(1)}, u32[]{:S(2)}, u32[]{:S(2)}) collective-permute-start(bf16[64,1152]{1,0:T(8,128)(2,1)S(1)} %get-tuple-element.63), channel_id=1, source_target_pairs={{0,4},{2,6},{4,0},{6,2},{1,5},{3,7},{5,1},{7,3},{8,12},{10,14},{12... | collective-permute-start | bytes 442376 | tf_op jit(solution)/shard_map/ppermute | solution.py:23
  70.4 1.4 %collective-permute-start.14 = (bf16[64,1152]{1,0:T(8,128)(2,1)S(1)}, bf16[64,1152]{1,0:T(8,128)(2,1)S(1)}, u32[]{:S(2)}, u32[]{:S(2)}) collective-permute-start(bf16[64,1152]{1,0:T(8,128)(2,1)S(1)} %get-tuple-element.64), channel_id=1, source_target_pairs={{0,6},{2,0},{4,2},{6,4},{1,7},{3,1},{5,3},{7,5},{8,14},{10,8},{12,... | collective-permute-start | bytes 442376 | tf_op jit(solution)/shard_map/ppermute | solution.py:23
  71.8 1.4 %shard_map.100.first_ref = bf16[64,3456]{1,0:T(8,128)(2,1)S(1)} custom-call(bf16[64,1152]{1,0:T(8,128)(2,1)S(1)} %get-tuple-element.61.a0, bf16[1152,3456]{1,0:T(8,128)(2,1)S(1)} %copy-done.2), custom_call_target="tpu_custom_call" | custom-call | tf_op jit(solution)/shard_map/pallas_call | solution.py:34
  73.2 2.0 %collective-permute-done.12.a1 = bf16[64,1152]{1,0:T(8,128)(2,1)S(1)} collective-permute-done((bf16[64,1152]{1,0:T(8,128)(2,1)S(1)}, bf16[64,1152]{1,0:T(8,128)(2,1)S(1)}, u32[]{:S(2)}, u32[]{:S(2)}) %collective-permute-start.12) | collective-permute-done | bytes 147488 | tf_op jit(solution)/shard_map/ppermute | solution.py:23
  75.8 3.3 %shard_map.101 = (bf16[64,1152]{1,0:T(8,128)(2,1)S(1)}, bf16[64,1152]{1,0:T(8,128)(2,1)S(1)}, bf16[64,1152]{1,0:T(8,128)(2,1)S(1)}, bf16[256,3456]{1,0:T(8,128)(2,1)S(1)}) custom-call(bf16[64,3456]{1,0:T(8,128)(2,1)S(1)} %shard_map.100.first_ref, bf16[64,1152]{1,0:T(8,128)(2,1)S(1)} %collective-permute-done.12.a1, ...), custom_call_target="tpu_custom_call" | custom-call | tf_op jit(solution)/shard_map/pallas_call | solution.py:34
  79.1 2.5 %collective-permute-start.15 = (bf16[64,1152]{1,0:T(8,128)(2,1)S(1)}, bf16[64,1152]{1,0:T(8,128)(2,1)S(1)}, u32[]{:S(2)}, u32[]{:S(2)}) collective-permute-start(bf16[64,1152]{1,0:T(8,128)(2,1)S(1)} %get-tuple-element.66), channel_id=1, source_target_pairs={{0,6},{2,0},{4,2},{6,4},{1,7},{3,1},{5,3},{7,5},{8,14},{10,8},{12,... | collective-permute-start | bytes 442376 | tf_op jit(solution)/shard_map/ppermute | solution.py:23
  81.6 0.6 collective-permute-start.17
  82.3 0.7 shard_map.103.base_ref
  83.0 1.1 shard_map.102.a0
  84.1 1.1 collective-permute-done.15.a1
  85.2 1.9 %collective-permute-done.16.a2 = bf16[64,1152]{1,0:T(8,128)(2,1)S(1)} collective-permute-done((bf16[64,1152]{1,0:T(8,128)(2,1)S(1)}, bf16[64,1152]{1,0:T(8,128)(2,1)S(1)}, u32[]{:S(2)}, u32[]{:S(2)}) %collective-permute-start.16) | collective-permute-done | bytes 147488 | tf_op jit(solution)/shard_map/ppermute | solution.py:23
  87.2 1.2 collective-permute-done.17.a3
  88.4 1.6 %shard_map.104 = (f32[4,32,1152]{2,1,0:T(8,128)S(1)}, f32[4,32,1152]{2,1,0:T(8,128)S(1)}, f32[8,8,1152]{2,1,0:T(8,128)S(1)}) custom-call(s32[7]{0:T(128)S(1)} %pad_add_fusion.where_ref, f32[3,4]{1,0:T(4,128)S(1)} %pad_maximum_fusion.coef_ref, bf16[64,1152]{1,0:T(8,128)(2,1)S(1)} %shard_map.102.a0, bf16[64,1152]{1,0:T(8,128)(2,1)S(1)} %collective-permute-done.15.a1, ...), custom_call_target="tpu_custom_call" | custom-call | tf_op jit(solution)/shard_map/pallas_call | solution.py:34
  90.1 7.9 %collective-permute-start.19 = (f32[4,32,1152]{2,1,0:T(8,128)S(1)}, f32[4,32,1152]{2,1,0:T(8,128)S(1)}, u32[]{:S(2)}, u32[]{:S(2)}) collective-permute-start(f32[4,32,1152]{2,1,0:T(8,128)S(1)} %get-tuple-element.73), channel_id=1, source_target_pairs={{0,1},{1,0},{2,3},{3,2},{4,5},{5,4},{6,7},{7,6},{8,9},{9,8},{10,11... | collective-permute-start | bytes 1769480 | tf_op jit(solution)/shard_map/ppermute | solution.py:23
  98.0 10.0 %all_to_all.22.held_ref = f32[8,8,1152]{2,1,0:T(8,128)S(1)} all-to-all(f32[8,8,1152]{2,1,0:T(8,128)S(1)} %get-tuple-element.71), channel_id=1, replica_groups=mesh['w'=2,'v'=2,'u'=2,'y'=4,'x'=4,'c'=2] {'u','y'}, dimensions={0} | all-to-all | bytes 589824 | tf_op jit(solution)/shard_map/all_to_all | solution.py:257
  108.5 3.1 %collective-permute-start.21 = (f32[8,1152]{1,0:T(8,128)S(1)}, f32[8,1152]{1,0:T(8,128)S(1)}, u32[]{:S(2)}, u32[]{:S(2)}) collective-permute-start(f32[8,1152]{1,0:T(8,128)S(1)} %get-tuple-element.72), channel_id=1, source_target_pairs={{0,192},{64,0},{128,64},{192,128},{1,193},{65,1},{129,65},{193,129... | collective-permute-start | bytes 110600 | tf_op jit(solution)/shard_map/ppermute | solution.py:23
  111.6 3.8 %collective-permute-start.20 = (f32[8,1152]{1,0:T(8,128)S(1)}, f32[8,1152]{1,0:T(8,128)S(1)}, u32[]{:S(2)}, u32[]{:S(2)}) collective-permute-start(f32[8,1152]{1,0:T(8,128)S(1)} %get-tuple-element.72), channel_id=1, source_target_pairs={{0,128},{64,192},{128,0},{192,64},{1,129},{65,193},{129,1},{193,65... | collective-permute-start | bytes 110600 | tf_op jit(solution)/shard_map/ppermute | solution.py:23
  115.4 2.9 %collective-permute-done.20.refs_1_ = f32[8,1152]{1,0:T(8,128)S(1)} collective-permute-done((f32[8,1152]{1,0:T(8,128)S(1)}, f32[8,1152]{1,0:T(8,128)S(1)}, u32[]{:S(2)}, u32[]{:S(2)}) %collective-permute-start.20) | collective-permute-done | bytes 36896 | tf_op jit(solution)/shard_map/ppermute | solution.py:23
  118.9 9.8 %all_to_all.23.mine_lower = f32[8,8,1152]{2,1,0:T(8,128)S(1)} all-to-all(f32[8,8,1152]{2,1,0:T(8,128)S(1)} %shard_map.106), channel_id=1, replica_groups=mesh['w'=2,'v'=2,'u'=2,'y'=4,'x'=4,'c'=2] {'u','y'}, dimensions={0} | all-to-all | bytes 589824 | tf_op jit(solution)/shard_map/all_to_all | solution.py:264
  128.7 3.5 %collective-permute-start.22 = (f32[8,8,1152]{2,1,0:T(8,128)S(1)}, f32[8,8,1152]{2,1,0:T(8,128)S(1)}, u32[]{:S(2)}, u32[]{:S(2)}) collective-permute-start(f32[8,8,1152]{2,1,0:T(8,128)S(1)} %all_to_all.23.mine_lower), channel_id=1, source_target_pairs={{0,1},{1,0},{2,3},{3,2},{4,5},{5,4},{6,7},{7,6},{8,9},{9,8},{10,11... | collective-permute-start | bytes 884744 | tf_op jit(solution)/shard_map/ppermute | solution.py:23
  132.2 1.2 collective-permute-done.22.peer_lower
  133.4 1.6 %shard_map.107 = f32[4,2,32,1152]{3,2,1,0:T(8,128)} custom-call(s32[7]{0:T(128)S(1)} %pad_add_fusion.where_ref, f32[2,32,1152]{2,1,0:T(8,128)S(1)} %copy-done.4, f32[4,32,1152]{2,1,0:T(8,128)S(1)} %get-tuple-element.70.mine_before, f32[4,32,1152]{2,1,0:T(8,128)S(1)} %collective-permute-done.19.peer_before, f32[8,8,1152]{2,1,0:T(8,128)S(1)} %all_to_all.23.mine_lower, ...), custom_call_target="tpu_custom_call" | custom-call | tf_op jit(solution)/shard_map/pallas_call | solution.py:34
  (48 shorter events, 3.8 us)
Async XLA Ops:
  0.0 4.7 %copy-start = (s32[4,2]{0,1:T(2,128)S(1)}, s32[4,2]{0,1:T(2,128)}, u32[]{:S(2)}) copy-start(s32[4,2]{0,1:T(2,128)} %param.15) | copy-start | bytes 100
  0.0 4.8 %copy-start.7 = (f32[4,3,1152]{2,0,1:T(4,128)S(1)}, f32[4,3,1152]{2,0,1:T(4,128)}, u32[]{:S(2)}) copy-start(f32[4,3,1152]{2,0,1:T(4,128)} %param.13) | copy-start | bytes 165892
  0.0 4.8 %copy-start.6 = (f32[8,3,1152]{2,0,1:T(8,128)S(1)}, f32[8,3,1152]{2,0,1:T(8,128)}, u32[]{:S(2)}) copy-start(f32[8,3,1152]{2,0,1:T(8,128)} %param.14) | copy-start | bytes 331780
  1.4 9.1 %copy-start.4 = (f32[2,32,1152]{2,1,0:T(8,128)S(1)}, f32[2,32,1152]{2,1,0:T(8,128)}, u32[]{:S(2)}) copy-start(f32[2,32,1152]{2,1,0:T(8,128)} %start_ref.1) | copy-start | bytes 884740
  1.4 4.9 %collective-permute-start = (f32[4,32,1152]{2,1,0:T(8,128)S(1)}, f32[4,32,1152]{2,1,0:T(8,128)S(1)}, u32[]{:S(2)}, u32[]{:S(2)}) collective-permute-start(f32[4,32,1152]{2,1,0:T(8,128)S(1)} %get-tuple-element.77), channel_id=1, source_target_pairs={{0,1},{1,0},{2,3},{3,2},{4,5},{5,4},{6,7},{7,6},{8,9},{9,8},{10,11... | collective-permute-start | bytes 1769480 | tf_op jit(solution)/shard_map/ppermute | solution.py:23
  7.3 9.4 %collective-permute-start.3 = (bf16[64,1152]{1,0:T(8,128)(2,1)S(1)}, bf16[64,1152]{1,0:T(8,128)(2,1)S(1)}, u32[]{:S(2)}, u32[]{:S(2)}) collective-permute-start(bf16[64,1152]{1,0:T(8,128)(2,1)S(1)} %get-tuple-element.46), channel_id=1, source_target_pairs={{0,2},{2,4},{4,6},{6,0},{1,3},{3,5},{5,7},{7,1},{8,10},{10,12},{12... | collective-permute-start | bytes 442376 | tf_op jit(solution)/shard_map/ppermute | solution.py:23
  7.4 9.3 %collective-permute-start.4 = (bf16[64,1152]{1,0:T(8,128)(2,1)S(1)}, bf16[64,1152]{1,0:T(8,128)(2,1)S(1)}, u32[]{:S(2)}, u32[]{:S(2)}) collective-permute-start(bf16[64,1152]{1,0:T(8,128)(2,1)S(1)} %get-tuple-element.47), channel_id=1, source_target_pairs={{0,4},{2,6},{4,0},{6,2},{1,5},{3,7},{5,1},{7,3},{8,12},{10,14},{12... | collective-permute-start | bytes 442376 | tf_op jit(solution)/shard_map/ppermute | solution.py:23
  9.4 7.8 %collective-permute-start.5 = (bf16[64,1152]{1,0:T(8,128)(2,1)S(1)}, bf16[64,1152]{1,0:T(8,128)(2,1)S(1)}, u32[]{:S(2)}, u32[]{:S(2)}) collective-permute-start(bf16[64,1152]{1,0:T(8,128)(2,1)S(1)} %get-tuple-element.48), channel_id=1, source_target_pairs={{0,6},{2,0},{4,2},{6,4},{1,7},{3,1},{5,3},{7,5},{8,14},{10,8},{12,... | collective-permute-start | bytes 442376 | tf_op jit(solution)/shard_map/ppermute | solution.py:23
  10.6 15.3 %collective-permute-start.1 = (f32[32,1152]{1,0:T(8,128)S(1)}, f32[32,1152]{1,0:T(8,128)S(1)}, u32[]{:S(2)}, u32[]{:S(2)}) collective-permute-start(f32[32,1152]{1,0:T(8,128)S(1)} %get-tuple-element.81), channel_id=1, source_target_pairs={{0,1},{1,0},{2,3},{3,2},{4,5},{5,4},{6,7},{7,6},{8,9},{9,8},{10,11... | collective-permute-start | bytes 442376 | tf_op jit(solution)/shard_map/ppermute | solution.py:23
  11.9 3.3 %copy-start.1 = (bf16[1152,3456]{1,0:T(8,128)(2,1)S(1)}, bf16[1152,3456]{1,0:T(8,128)(2,1)}, u32[]{:S(2)}) copy-start(bf16[1152,3456]{1,0:T(8,128)(2,1)} %w_ref.10) | copy-start | bytes 23887876
  15.1 1.4 %copy-start.5 = (bf16[4,2,32,1152]{3,2,1,0:T(8,128)(2,1)S(1)}, bf16[4,2,32,1152]{3,2,1,0:T(8,128)(2,1)}, u32[]{:S(2)}) copy-start(bf16[4,2,32,1152]{3,2,1,0:T(8,128)(2,1)} %param.10) | copy-start | bytes 1769476
  15.1 3.5 %copy-start.2 = (bf16[1152,3456]{1,0:T(8,128)(2,1)S(1)}, bf16[1152,3456]{1,0:T(8,128)(2,1)}, u32[]{:S(2)}) copy-start(bf16[1152,3456]{1,0:T(8,128)(2,1)} %w_ref.10) | copy-start | bytes 23887876
  16.6 8.1 %copy-start.8 = (s32[4]{0:T(128)S(1)}, s32[4]{0:T(128)}, u32[]{:S(2)}) copy-start(s32[4]{0:T(128)} %param.12) | copy-start | bytes 52
  16.6 9.3 %collective-permute-start.2 = (bf16[4,32,1152]{2,1,0:T(8,128)(2,1)S(1)}, bf16[4,32,1152]{2,1,0:T(8,128)(2,1)S(1)}, u32[]{:S(2)}, u32[]{:S(2)}) collective-permute-start(bf16[4,32,1152]{2,1,0:T(8,128)(2,1)S(1)} %get-tuple-element.79), channel_id=1, source_target_pairs={{0,1},{1,0},{2,3},{3,2},{4,5},{5,4},{6,7},{7,6},{8,9},{9,8},{10,11... | collective-permute-start | bytes 884744 | tf_op jit(solution)/shard_map/ppermute | solution.py:23
  21.8 5.4 %collective-permute-start.6 = (bf16[64,1152]{1,0:T(8,128)(2,1)S(1)}, bf16[64,1152]{1,0:T(8,128)(2,1)S(1)}, u32[]{:S(2)}, u32[]{:S(2)}) collective-permute-start(bf16[64,1152]{1,0:T(8,128)(2,1)S(1)} %get-tuple-element.50), channel_id=1, source_target_pairs={{0,6},{2,0},{4,2},{6,4},{1,7},{3,1},{5,3},{7,5},{8,14},{10,8},{12,... | collective-permute-start | bytes 442376 | tf_op jit(solution)/shard_map/ppermute | solution.py:23
  23.9 6.2 %collective-permute-start.7 = (bf16[64,1152]{1,0:T(8,128)(2,1)S(1)}, bf16[64,1152]{1,0:T(8,128)(2,1)S(1)}, u32[]{:S(2)}, u32[]{:S(2)}) collective-permute-start(bf16[64,1152]{1,0:T(8,128)(2,1)S(1)} %get-tuple-element.51), channel_id=1, source_target_pairs={{0,4},{2,6},{4,0},{6,2},{1,5},{3,7},{5,1},{7,3},{8,12},{10,14},{12... | collective-permute-start | bytes 442376 | tf_op jit(solution)/shard_map/ppermute | solution.py:23
  24.0 10.0 %collective-permute-start.8 = (bf16[64,1152]{1,0:T(8,128)(2,1)S(1)}, bf16[64,1152]{1,0:T(8,128)(2,1)S(1)}, u32[]{:S(2)}, u32[]{:S(2)}) collective-permute-start(bf16[64,1152]{1,0:T(8,128)(2,1)S(1)} %get-tuple-element.52), channel_id=1, source_target_pairs={{0,2},{2,4},{4,6},{6,0},{1,3},{3,5},{5,7},{7,1},{8,10},{10,12},{12... | collective-permute-start | bytes 442376 | tf_op jit(solution)/shard_map/ppermute | solution.py:23
  25.9 8.2 %copy-start.3 = (bf16[1152,1152]{1,0:T(8,128)(2,1)S(1)}, bf16[1152,1152]{1,0:T(8,128)(2,1)}, u32[]{:S(2)}) copy-start(bf16[1152,1152]{1,0:T(8,128)(2,1)} %w_ref.11) | copy-start | bytes 7962628
  45.8 8.4 %collective-permute-start.11 = (f32[8,1152]{1,0:T(8,128)S(1)}, f32[8,1152]{1,0:T(8,128)S(1)}, u32[]{:S(2)}, u32[]{:S(2)}) collective-permute-start(f32[8,1152]{1,0:T(8,128)S(1)} %get-tuple-element.60), channel_id=1, source_target_pairs={{0,192},{64,0},{128,64},{192,128},{1,193},{65,1},{129,65},{193,129... | collective-permute-start | bytes 110600 | tf_op jit(solution)/shard_map/ppermute | solution.py:23
  51.0 6.7 %collective-permute-start.10 = (f32[8,1152]{1,0:T(8,128)S(1)}, f32[8,1152]{1,0:T(8,128)S(1)}, u32[]{:S(2)}, u32[]{:S(2)}) collective-permute-start(f32[8,1152]{1,0:T(8,128)S(1)} %get-tuple-element.60), channel_id=1, source_target_pairs={{0,128},{64,192},{128,0},{192,64},{1,129},{65,193},{129,1},{193,65... | collective-permute-start | bytes 110600 | tf_op jit(solution)/shard_map/ppermute | solution.py:23
  52.1 5.6 %collective-permute-start.9 = (f32[8,1152]{1,0:T(8,128)S(1)}, f32[8,1152]{1,0:T(8,128)S(1)}, u32[]{:S(2)}, u32[]{:S(2)}) collective-permute-start(f32[8,1152]{1,0:T(8,128)S(1)} %get-tuple-element.60), channel_id=1, source_target_pairs={{0,64},{64,128},{128,192},{192,0},{1,65},{65,129},{129,193},{193,1... | collective-permute-start | bytes 110600 | tf_op jit(solution)/shard_map/ppermute | solution.py:23
  68.4 6.9 %collective-permute-start.12 = (bf16[64,1152]{1,0:T(8,128)(2,1)S(1)}, bf16[64,1152]{1,0:T(8,128)(2,1)S(1)}, u32[]{:S(2)}, u32[]{:S(2)}) collective-permute-start(bf16[64,1152]{1,0:T(8,128)(2,1)S(1)} %get-tuple-element.62), channel_id=1, source_target_pairs={{0,2},{2,4},{4,6},{6,0},{1,3},{3,5},{5,7},{7,1},{8,10},{10,12},{12... | collective-permute-start | bytes 442376 | tf_op jit(solution)/shard_map/ppermute | solution.py:23
  68.6 6.7 %collective-permute-start.13 = (bf16[64,1152]{1,0:T(8,128)(2,1)S(1)}, bf16[64,1152]{1,0:T(8,128)(2,1)S(1)}, u32[]{:S(2)}, u32[]{:S(2)}) collective-permute-start(bf16[64,1152]{1,0:T(8,128)(2,1)S(1)} %get-tuple-element.63), channel_id=1, source_target_pairs={{0,4},{2,6},{4,0},{6,2},{1,5},{3,7},{5,1},{7,3},{8,12},{10,14},{12... | collective-permute-start | bytes 442376 | tf_op jit(solution)/shard_map/ppermute | solution.py:23
  70.4 5.4 %collective-permute-start.14 = (bf16[64,1152]{1,0:T(8,128)(2,1)S(1)}, bf16[64,1152]{1,0:T(8,128)(2,1)S(1)}, u32[]{:S(2)}, u32[]{:S(2)}) collective-permute-start(bf16[64,1152]{1,0:T(8,128)(2,1)S(1)} %get-tuple-element.64), channel_id=1, source_target_pairs={{0,6},{2,0},{4,2},{6,4},{1,7},{3,1},{5,3},{7,5},{8,14},{10,8},{12,... | collective-permute-start | bytes 442376 | tf_op jit(solution)/shard_map/ppermute | solution.py:23
  79.1 6.1 %collective-permute-start.15 = (bf16[64,1152]{1,0:T(8,128)(2,1)S(1)}, bf16[64,1152]{1,0:T(8,128)(2,1)S(1)}, u32[]{:S(2)}, u32[]{:S(2)}) collective-permute-start(bf16[64,1152]{1,0:T(8,128)(2,1)S(1)} %get-tuple-element.66), channel_id=1, source_target_pairs={{0,6},{2,0},{4,2},{6,4},{1,7},{3,1},{5,3},{7,5},{8,14},{10,8},{12,... | collective-permute-start | bytes 442376 | tf_op jit(solution)/shard_map/ppermute | solution.py:23
  81.6 5.6 %collective-permute-start.16 = (bf16[64,1152]{1,0:T(8,128)(2,1)S(1)}, bf16[64,1152]{1,0:T(8,128)(2,1)S(1)}, u32[]{:S(2)}, u32[]{:S(2)}) collective-permute-start(bf16[64,1152]{1,0:T(8,128)(2,1)S(1)} %get-tuple-element.67), channel_id=1, source_target_pairs={{0,4},{2,6},{4,0},{6,2},{1,5},{3,7},{5,1},{7,3},{8,12},{10,14},{12... | collective-permute-start | bytes 442376 | tf_op jit(solution)/shard_map/ppermute | solution.py:23
  81.6 6.8 %collective-permute-start.17 = (bf16[64,1152]{1,0:T(8,128)(2,1)S(1)}, bf16[64,1152]{1,0:T(8,128)(2,1)S(1)}, u32[]{:S(2)}, u32[]{:S(2)}) collective-permute-start(bf16[64,1152]{1,0:T(8,128)(2,1)S(1)} %get-tuple-element.68), channel_id=1, source_target_pairs={{0,2},{2,4},{4,6},{6,0},{1,3},{3,5},{5,7},{7,1},{8,10},{10,12},{12... | collective-permute-start | bytes 442376 | tf_op jit(solution)/shard_map/ppermute | solution.py:23
  90.1 25.4 %collective-permute-start.19 = (f32[4,32,1152]{2,1,0:T(8,128)S(1)}, f32[4,32,1152]{2,1,0:T(8,128)S(1)}, u32[]{:S(2)}, u32[]{:S(2)}) collective-permute-start(f32[4,32,1152]{2,1,0:T(8,128)S(1)} %get-tuple-element.73), channel_id=1, source_target_pairs={{0,1},{1,0},{2,3},{3,2},{4,5},{5,4},{6,7},{7,6},{8,9},{9,8},{10,11... | collective-permute-start | bytes 1769480 | tf_op jit(solution)/shard_map/ppermute | solution.py:23
  108.0 7.5 %collective-permute-start.18 = (f32[8,1152]{1,0:T(8,128)S(1)}, f32[8,1152]{1,0:T(8,128)S(1)}, u32[]{:S(2)}, u32[]{:S(2)}) collective-permute-start(f32[8,1152]{1,0:T(8,128)S(1)} %get-tuple-element.72), channel_id=1, source_target_pairs={{0,64},{64,128},{128,192},{192,0},{1,65},{65,129},{129,193},{193,1... | collective-permute-start | bytes 110600 | tf_op jit(solution)/shard_map/ppermute | solution.py:23
  108.5 6.9 %collective-permute-start.21 = (f32[8,1152]{1,0:T(8,128)S(1)}, f32[8,1152]{1,0:T(8,128)S(1)}, u32[]{:S(2)}, u32[]{:S(2)}) collective-permute-start(f32[8,1152]{1,0:T(8,128)S(1)} %get-tuple-element.72), channel_id=1, source_target_pairs={{0,192},{64,0},{128,64},{192,128},{1,193},{65,1},{129,65},{193,129... | collective-permute-start | bytes 110600 | tf_op jit(solution)/shard_map/ppermute | solution.py:23
  111.6 6.7 %collective-permute-start.20 = (f32[8,1152]{1,0:T(8,128)S(1)}, f32[8,1152]{1,0:T(8,128)S(1)}, u32[]{:S(2)}, u32[]{:S(2)}) collective-permute-start(f32[8,1152]{1,0:T(8,128)S(1)} %get-tuple-element.72), channel_id=1, source_target_pairs={{0,128},{64,192},{128,0},{192,64},{1,129},{65,193},{129,1},{193,65... | collective-permute-start | bytes 110600 | tf_op jit(solution)/shard_map/ppermute | solution.py:23
  128.7 4.7 %collective-permute-start.22 = (f32[8,8,1152]{2,1,0:T(8,128)S(1)}, f32[8,8,1152]{2,1,0:T(8,128)S(1)}, u32[]{:S(2)}, u32[]{:S(2)}) collective-permute-start(f32[8,8,1152]{2,1,0:T(8,128)S(1)} %all_to_all.23.mine_lower), channel_id=1, source_target_pairs={{0,1},{1,0},{2,3},{3,2},{4,5},{5,4},{6,7},{7,6},{8,9},{9,8},{10,11... | collective-permute-start | bytes 884744 | tf_op jit(solution)/shard_map/ppermute | solution.py:23
